TPU v7x, 32 devices: a whole 2x2x4 slice. The times are simulated.
32 devices in a mesh: groups: 2 (over y), patch: 8 (over z, x), sub: 2 (over core).
Axes of the slice: x: 2, y: 2, z: 4, core: 2. Of those that a mesh axis runs over, the one named last changes fastest.
Arguments:
- block_cols: int32 [64, 3], P(('groups', 'patch', 'sub')), parts along dimension 0, may hold values from 0 to 31, as said below
- step_tiles: float32 [64, 3, 128, 128], P(('groups', 'patch', 'sub')), parts along dimension 0, as said below
- mass: float32 [8192], P(('groups', 'patch', 'sub')), parts along dimension 0, as said below
- warm_start: float32 [8192, 128], P(('groups', 'patch', 'sub')), parts along dimension 0, may hold values from -2.5 to 2.5
- source_ids: int32 [256], P('groups'), parts along dimension 0, may hold values from 0 to 4095
Outputs:
- solution: float32 [8192, 128], P(('groups', 'patch', 'sub')), parts along dimension 0
There are 2 independent parts, one for each index of `groups`. A program takes and returns all parts, laid end to end along the dimension named above; each array names one. Nothing has to cross between parts.
Inputs may be any that keep to these rules, and one draw needn't show every extreme that they name: `block_cols`: slot lists of block row g name g itself and blocks within 1 of g coupled to it; coupling is symmetric (g names h exactly when h names g). Unused slots name g and carry a zero tile. `step_tiles`: entries are not negative. The tile of block row h toward g is the transpose of the tile of row g toward h; the tile of a row toward itself is symmetric with a zero diagonal. `mass`: between 0.1 and 1.2.
All inputs are finite; a program needn't handle non-finite values.
Results may differ from a plain program's by a relative error of at most 0.00023.
Values sent between devices are 32-bit elements; how exact they have to be, the bound alone decides.
No kernel may reach another device: no remote copies, remote signals or barrier semaphores. Data moves between devices by JAX's collectives and lax.ppermute only.
A program may use at most 64 MiB of HBM per device.

v0:
```python
import jax
import jax.numpy as jnp
from jax import lax
from jax.sharding import PartitionSpec as P

REACH = 1
ITERS = 2


def extended_2(shard, sides, width):
    for axis, dim in sides:
        size, length = (lax.axis_size(axis), shard.shape[dim])
        up = [(i, (i + 1) % size) for i in range(size - 1)]
        down = [(j, i) for i, j in up]
        last = lax.slice_in_dim(shard, length - width, length, axis=dim)
        leading = lax.slice_in_dim(shard, 0, width, axis=dim)
        before = lax.ppermute(last, axis, up)
        after = lax.ppermute(leading, axis, down)
        shard = jnp.concatenate([before, shard, after], axis=dim)
    return shard


def apply_operator(operand, extend, local_cols, step_tiles, diag_total):
    tile_size = step_tiles.shape[-1]
    extended = extend(operand)
    blocks = extended.reshape(-1, tile_size, operand.shape[1])
    picked = blocks[local_cols]
    coupled = jnp.einsum(
        "bkij,bkjs->bis",
        step_tiles,
        picked,
        precision=lax.Precision.HIGHEST,
        preferred_element_type=jnp.float32,
    )
    return diag_total * operand - coupled.reshape(operand.shape)


def paired_products(residual, image_vec):
    return lax.psum(
        (jnp.sum(residual * residual, axis=0), jnp.sum(residual * image_vec, axis=0)),
        ("patch", "sub"),
    )


def body(block_cols, step_tiles, mass, warm_start, source_ids):
    blocks_here = block_cols.shape[0]
    tile_size = step_tiles.shape[-1]
    rim_rows = REACH * tile_size
    rows_here = blocks_here * tile_size
    position = lax.axis_index(("patch", "sub"))
    local_cols = block_cols - (position * blocks_here - REACH)
    degree = jnp.sum(step_tiles, axis=(1, 3)).reshape(rows_here)
    diag_total = (mass + degree)[:, None]
    vertex_ids = position * rows_here + jnp.arange(rows_here, dtype=jnp.int32)
    rhs = (vertex_ids[:, None] == source_ids[None, :]).astype(jnp.float32)

    def extend(operand):
        return extended_2(operand, ((("patch", "sub"), 0),), rim_rows)

    def operator(operand):
        return apply_operator(operand, extend, local_cols, step_tiles, diag_total)

    solution = warm_start
    residual = rhs - operator(warm_start)
    image_vec = operator(residual)
    norm_now, product = paired_products(residual, image_vec)
    alpha_step = norm_now / product
    direction = residual
    along = image_vec
    for iteration in range(ITERS):
        solution = solution + alpha_step * direction
        residual = residual - alpha_step * along
        if iteration + 1 < ITERS:
            image_vec = operator(residual)
            norm_next, product = paired_products(residual, image_vec)
            ratio = norm_next / norm_now
            alpha_step = norm_next / (product - ratio * norm_next / alpha_step)
            direction = residual + ratio * direction
            along = image_vec + ratio * along
            norm_now = norm_next
    return solution


def solution(mesh):
    in_specs = (
        P(("groups", "patch", "sub"), None),
        P(("groups", "patch", "sub"), None, None, None),
        P(("groups", "patch", "sub")),
        P(("groups", "patch", "sub"), None),
        P("groups"),
    )
    out_specs = P(("groups", "patch", "sub"), None)
    return jax.shard_map(body, mesh=mesh, in_specs=in_specs, out_specs=out_specs, check_vma=False)
```

profile of v0, /device:TPU:0, one launch (start us, length us, event | category | flops | bytes accessed | tf_op | source)
XLA Modules:
  0.0 89.1 jit_solution(11889256737454881527)
XLA Ops:
  0.0 0.9 fusion.5
  0.9 2.4 %collective-permute-start = (f32[128,128]{1,0:T(8,128)S(1)}, f32[128,128]{1,0:T(8,128)S(1)}, u32[]{:S(2)}, u32[]{:S(2)}) collective-permute-start(f32[128,128]{1,0:T(8,128)S(1)} %get-tuple-element.19), channel_id=1, source_target_pairs={{0,1},{1,2},{2,3},{3,4},{4,5},{5,6},{6,7},{7,8},{8,9},{9,10},{10,1... | collective-permute-start | bytes 196616 | tf_op jit(solution)/shard_map/ppermute | solution.py:17
  3.3 1.3 %collective-permute-start.1 = (f32[128,128]{1,0:T(8,128)S(1)}, f32[128,128]{1,0:T(8,128)S(1)}, u32[]{:S(2)}, u32[]{:S(2)}) collective-permute-start(f32[128,128]{1,0:T(8,128)S(1)} %get-tuple-element.20), channel_id=1, source_target_pairs={{1,0},{2,1},{3,2},{4,3},{5,4},{6,5},{7,6},{8,7},{9,8},{10,9},{11,1... | collective-permute-start | bytes 196616 | tf_op jit(solution)/shard_map/ppermute | solution.py:18
  4.6 0.0 copy-start.3
  4.6 0.7 copy-done.3
  5.3 0.1 reshape.39
  5.4 1.1 %reduce_sum.45 = f32[2,128]{1,0:T(2,128)S(1)} reduce(f32[2,3,128,128]{3,2,1,0:T(8,128)} %param.6, f32[]{:T(128)} %constant.7.clone.1), dimensions={1,3}, to_apply=%region_0.0 | reduce | flops 98048 | bytes 394244 | tf_op jit(solution)/shard_map/reduce_sum | solution.py:52
  6.6 0.0 collective-permute-done
  6.6 1.9 %collective-permute-done.1 = f32[128,128]{1,0:T(8,128)S(1)} collective-permute-done((f32[128,128]{1,0:T(8,128)S(1)}, f32[128,128]{1,0:T(8,128)S(1)}, u32[]{:S(2)}, u32[]{:S(2)}) %collective-permute-start.1) | collective-permute-done | bytes 65568 | tf_op jit(solution)/shard_map/ppermute | solution.py:18
  8.6 0.0 copy-start
  8.6 0.6 gather_fusion
  9.2 0.4 copy-done
  9.6 0.5 fusion.6
  10.1 0.1 copy-done.4
  10.2 0.1 fusion.2
  10.4 4.8 %collective-permute-start.2 = (f32[128,128]{1,0:T(8,128)S(1)}, f32[128,128]{1,0:T(8,128)S(1)}, u32[]{:S(2)}, u32[]{:S(2)}) collective-permute-start(f32[128,128]{1,0:T(8,128)S(1)} %get-tuple-element.17), channel_id=1, source_target_pairs={{0,1},{1,2},{2,3},{3,4},{4,5},{5,6},{6,7},{7,8},{8,9},{9,10},{10,1... | collective-permute-start | bytes 196616 | tf_op jit(solution)/shard_map/ppermute | solution.py:17
  15.2 1.3 %collective-permute-start.3 = (f32[128,128]{1,0:T(8,128)S(1)}, f32[128,128]{1,0:T(8,128)S(1)}, u32[]{:S(2)}, u32[]{:S(2)}) collective-permute-start(f32[128,128]{1,0:T(8,128)S(1)} %get-tuple-element.18), channel_id=1, source_target_pairs={{1,0},{2,1},{3,2},{4,3},{5,4},{6,5},{7,6},{8,7},{9,8},{10,9},{11,1... | collective-permute-start | bytes 196616 | tf_op jit(solution)/shard_map/ppermute | solution.py:18
  16.5 0.0 collective-permute-done.2
  16.5 1.8 %collective-permute-done.3 = f32[128,128]{1,0:T(8,128)S(1)} collective-permute-done((f32[128,128]{1,0:T(8,128)S(1)}, f32[128,128]{1,0:T(8,128)S(1)}, u32[]{:S(2)}, u32[]{:S(2)}) %collective-permute-start.3) | collective-permute-done | bytes 65568 | tf_op jit(solution)/shard_map/ppermute | solution.py:18
  18.4 0.6 gather_fusion.1
  19.0 0.5 fusion.7
  19.5 0.1 multiply_reduce_fusion.1
  19.6 32.8 %all-reduce.1 = (f32[128]{0:T(128)S(1)}, f32[128]{0:T(128)S(1)}) all-reduce(f32[128]{0:T(128)S(1)} %get-tuple-element.8, f32[128]{0:T(128)S(1)} %get-tuple-element.7), channel_id=1, replica_groups=mesh['groups'=2,'patch'=8,'sub'=2] {'patch','sub'}, use_global_device_ids=true, to_apply=%region_2.0 | all-reduce | flops 256 | bytes 2048 | tf_op jit(solution)/shard_map/psum | solution.py:39
  52.4 0.1 multiply_subtract_fusion
  52.5 1.3 %collective-permute-start.4 = (f32[128,128]{1,0:T(8,128)S(1)}, f32[128,128]{1,0:T(8,128)S(1)}, u32[]{:S(2)}, u32[]{:S(2)}) collective-permute-start(f32[128,128]{1,0:T(8,128)S(1)} %get-tuple-element.15), channel_id=1, source_target_pairs={{0,1},{1,2},{2,3},{3,4},{4,5},{5,6},{6,7},{7,8},{8,9},{9,10},{10,1... | collective-permute-start | bytes 196616 | tf_op jit(solution)/shard_map/ppermute | solution.py:17
  53.8 1.3 %collective-permute-start.5 = (f32[128,128]{1,0:T(8,128)S(1)}, f32[128,128]{1,0:T(8,128)S(1)}, u32[]{:S(2)}, u32[]{:S(2)}) collective-permute-start(f32[128,128]{1,0:T(8,128)S(1)} %get-tuple-element.16), channel_id=1, source_target_pairs={{1,0},{2,1},{3,2},{4,3},{5,4},{6,5},{7,6},{8,7},{9,8},{10,9},{11,1... | collective-permute-start | bytes 196616 | tf_op jit(solution)/shard_map/ppermute | solution.py:18
  55.1 1.8 %collective-permute-done.5 = f32[128,128]{1,0:T(8,128)S(1)} collective-permute-done((f32[128,128]{1,0:T(8,128)S(1)}, f32[128,128]{1,0:T(8,128)S(1)}, u32[]{:S(2)}, u32[]{:S(2)}) %collective-permute-start.5) | collective-permute-done | bytes 65568 | tf_op jit(solution)/shard_map/ppermute | solution.py:18
  57.0 0.6 gather_fusion.2
  57.6 0.5 fusion.8
  58.1 0.1 fusion.1
  58.2 30.2 %all-reduce = (f32[128]{0:T(128)S(1)}, f32[128]{0:T(128)S(1)}) all-reduce(f32[128]{0:T(128)S(1)} %get-tuple-element.6, f32[128]{0:T(128)S(1)} %get-tuple-element.5), channel_id=1, replica_groups=mesh['groups'=2,'patch'=8,'sub'=2] {'patch','sub'}, use_global_device_ids=true, to_apply=%region_6.0 | all-reduce | flops 256 | bytes 2048 | tf_op jit(solution)/shard_map/psum | solution.py:39
  88.4 0.7 multiply_add_fusion
  (17 shorter events, 0.1 us)
Async XLA Ops:
  0.9 5.7 %collective-permute-start = (f32[128,128]{1,0:T(8,128)S(1)}, f32[128,128]{1,0:T(8,128)S(1)}, u32[]{:S(2)}, u32[]{:S(2)}) collective-permute-start(f32[128,128]{1,0:T(8,128)S(1)} %get-tuple-element.19), channel_id=1, source_target_pairs={{0,1},{1,2},{2,3},{3,4},{4,5},{5,6},{6,7},{7,8},{8,9},{9,10},{10,1... | collective-permute-start | bytes 196616 | tf_op jit(solution)/shard_map/ppermute | solution.py:17
  3.3 5.2 %collective-permute-start.1 = (f32[128,128]{1,0:T(8,128)S(1)}, f32[128,128]{1,0:T(8,128)S(1)}, u32[]{:S(2)}, u32[]{:S(2)}) collective-permute-start(f32[128,128]{1,0:T(8,128)S(1)} %get-tuple-element.20), channel_id=1, source_target_pairs={{1,0},{2,1},{3,2},{4,3},{5,4},{6,5},{7,6},{8,7},{9,8},{10,9},{11,1... | collective-permute-start | bytes 196616 | tf_op jit(solution)/shard_map/ppermute | solution.py:18
  4.6 0.7 copy-start.3
  5.4 1.2 %copy-start.2 = (f32[256]{0:T(256)S(1)}, f32[256]{0:T(256)}, u32[]{:S(2)}) copy-start(f32[256]{0:T(256)} %param.7) | copy-start | bytes 3076
  5.4 3.2 %copy-start.1 = (f32[256,128]{1,0:T(8,128)S(1)}, f32[256,128]{1,0:T(8,128)}, u32[]{:S(2)}) copy-start(f32[256,128]{1,0:T(8,128)} %param.8) | copy-start | bytes 393220
  8.6 1.0 %copy-start = (f32[2,3,128,128]{3,2,1,0:T(8,128)S(1)}, f32[2,3,128,128]{3,2,1,0:T(8,128)}, u32[]{:S(2)}) copy-start(f32[2,3,128,128]{3,2,1,0:T(8,128)} %param.6) | copy-start | bytes 1179652
  9.6 0.7 copy-start.4
  10.4 6.2 %collective-permute-start.2 = (f32[128,128]{1,0:T(8,128)S(1)}, f32[128,128]{1,0:T(8,128)S(1)}, u32[]{:S(2)}, u32[]{:S(2)}) collective-permute-start(f32[128,128]{1,0:T(8,128)S(1)} %get-tuple-element.17), channel_id=1, source_target_pairs={{0,1},{1,2},{2,3},{3,4},{4,5},{5,6},{6,7},{7,8},{8,9},{9,10},{10,1... | collective-permute-start | bytes 196616 | tf_op jit(solution)/shard_map/ppermute | solution.py:17
  15.2 3.1 %collective-permute-start.3 = (f32[128,128]{1,0:T(8,128)S(1)}, f32[128,128]{1,0:T(8,128)S(1)}, u32[]{:S(2)}, u32[]{:S(2)}) collective-permute-start(f32[128,128]{1,0:T(8,128)S(1)} %get-tuple-element.18), channel_id=1, source_target_pairs={{1,0},{2,1},{3,2},{4,3},{5,4},{6,5},{7,6},{8,7},{9,8},{10,9},{11,1... | collective-permute-start | bytes 196616 | tf_op jit(solution)/shard_map/ppermute | solution.py:18
  52.5 2.6 %collective-permute-start.4 = (f32[128,128]{1,0:T(8,128)S(1)}, f32[128,128]{1,0:T(8,128)S(1)}, u32[]{:S(2)}, u32[]{:S(2)}) collective-permute-start(f32[128,128]{1,0:T(8,128)S(1)} %get-tuple-element.15), channel_id=1, source_target_pairs={{0,1},{1,2},{2,3},{3,4},{4,5},{5,6},{6,7},{7,8},{8,9},{9,10},{10,1... | collective-permute-start | bytes 196616 | tf_op jit(solution)/shard_map/ppermute | solution.py:17
  53.8 3.1 %collective-permute-start.5 = (f32[128,128]{1,0:T(8,128)S(1)}, f32[128,128]{1,0:T(8,128)S(1)}, u32[]{:S(2)}, u32[]{:S(2)}) collective-permute-start(f32[128,128]{1,0:T(8,128)S(1)} %get-tuple-element.16), channel_id=1, source_target_pairs={{1,0},{2,1},{3,2},{4,3},{5,4},{6,5},{7,6},{8,7},{9,8},{10,9},{11,1... | collective-permute-start | bytes 196616 | tf_op jit(solution)/shard_map/ppermute | solution.py:18
where the time goes:
time: 89.5 us; the launch traced here: 89.1 us
  blocking collectives  63 us (70%)
  starting transfers between devices  12.4 us (14%)
  waiting for transfers between devices  5.63 us (6%)
  local copies, waits for them, and re-layouts  3.94 us (4%)
  other arithmetic  2.43 us (3%)
  matrix products  1.52 us (2%)
    psum x2, blocking collectives, paired_products(): lax.psum((jnp.sum(residual * residual, axis=0), jnp.sum(residual * image_...  63 us
    ppermute x3, starting transfers between devices, extended_2(): before = lax.ppermute(last, axis, up)  8.53 us
    ppermute x3, waiting for transfers between devices, extended_2(): after = lax.ppermute(leading, axis, down)  5.62 us
    ppermute x3, starting transfers between devices, extended_2(): after = lax.ppermute(leading, axis, down)  3.88 us
  transfers between devices with their start and end apart: 6, of which 3 were waited for; matrix products, arithmetic and copies ran while one was open for 1% of the time, Pallas kernels for 0%

commit v1 on v0

v1 whole, which is shorter than its diff:
```python
import functools

import jax
import jax.numpy as jnp
from jax import lax
from jax.experimental import pallas as pl
from jax.experimental.pallas import tpu as pltpu
from jax.sharding import PartitionSpec as P

AXES = ("patch", "sub")
LEAST_EIGENVALUE = 0.0999
VMEM = pl.BlockSpec(memory_space=pltpu.VMEM)
SMEM = pl.BlockSpec(memory_space=pltpu.SMEM)


def dot(a, b):
    return jnp.dot(a, b, precision=lax.Precision.HIGHEST, preferred_element_type=jnp.float32)


def place():
    return lax.axis_index("patch") * lax.axis_size("sub") + lax.axis_index("sub")


def outer_block(tile):
    side = lax.rem(place(), 2)
    outer = pl.ds(pl.multiple_of(side * tile, tile), tile)
    inner = pl.ds(pl.multiple_of((1 - side) * tile, tile), tile)
    return outer, inner


def local_kernel(cols, tiles, mass, x, sources, local, t_in, t_out, t_out_t, base, push):
    tile = tiles.shape[-1]
    slots = tiles.shape[1]
    position = place()
    side = lax.rem(position, 2)
    first = position * 2
    above, below = first - 1, first + 2
    eye = lax.broadcasted_iota(jnp.int32, (tile, tile), 0) == lax.broadcasted_iota(jnp.int32, (tile, tile), 1)

    def toward(row, block):
        total = jnp.where(cols[row, 0] == block, tiles[row, 0], 0.0)
        for slot in range(1, slots):
            total += jnp.where(cols[row, slot] == block, tiles[row, slot], 0.0)
        return total

    for row in range(2):
        whole = tiles[row, 0]
        for slot in range(1, slots):
            whole += tiles[row, slot]
        masses = mass[pl.ds(row * tile, tile)][None, :]
        total = jnp.sum(whole + jnp.where(eye, masses, 0.0), axis=1, keepdims=True)
        own = jnp.where(eye, total, 0.0) - toward(row, first + row)
        cross = -toward(row, first + 1 - row)
        local[pl.ds(row * tile, tile), pl.ds(row * tile, tile)] = own
        local[pl.ds(row * tile, tile), pl.ds((1 - row) * tile, tile)] = cross
    outer, _ = outer_block(tile)
    outward = toward(side, jnp.where(side == 0, above, below))
    outward_t = outward.T
    t_in[...] = toward(1 - side, jnp.where(side == 0, below, above))
    t_out[...] = outward
    t_out_t[...] = outward_t
    vertices = position * (2 * tile) + lax.broadcasted_iota(jnp.int32, x.shape, 0)
    rhs = jnp.where(vertices == sources[...][None, :], 1.0, 0.0)
    base[...] = rhs - dot(local[...], x[...])
    push[...] = dot(outward_t, x[outer, :])


def start_kernel(local, t_in, base, push, other_x, t, q, send):
    tile = t_in.shape[0]
    outer, inner = outer_block(tile)
    t[outer, :] = base[outer, :]
    t[inner, :] = base[inner, :] + dot(t_in[...], other_x[outer, :])
    q[...] = dot(local[...], t[...])
    send[0:tile, :] = t[outer, :]
    send[tile : 2 * tile, :] = q[outer, :]
    send[2 * tile : 3 * tile, :] = push[...]
    send[3 * tile :, :] = local[outer, outer_columns(tile)]


def outer_columns(tile):
    side = lax.rem(place(), 2)
    return pl.ds(pl.multiple_of(side * tile, tile), tile)


def image_kernel(local, t_in, t_out, t, q, push, other_t, got, r, w, w_in):
    tile = t_in.shape[0]
    outer, inner = outer_block(tile)
    push_here = got[2 * tile : 3 * tile, :]
    r[inner, :] = t[inner, :]
    r[outer, :] = t[outer, :] + push_here
    change = dot(local[:, outer_columns(tile)], push_here)
    w[...] = q[...] + change
    beyond = got[0:tile, :] + push[...]
    w[outer, :] = w[outer, :] - dot(t_out[...], beyond)
    w_inner = w[inner, :] - dot(t_in[...], other_t[outer, :])
    w[inner, :] = w_inner
    w_in[...] = w_inner


def moment_kernel(local, t_in, t_out, t_out_t, push, got, r, w, moments, edge):
    tile = t_in.shape[0]
    outer, inner = outer_block(tile)
    w_now, r_now = w[...], r[...]
    w_beyond = (
        got[tile : 2 * tile, :] + dot(got[3 * tile :, :], push[...]) - dot(t_out_t[...], r[outer, :])
    )
    r_r = jnp.sum(r_now * r_now, axis=0, keepdims=True)
    r_w = jnp.sum(r_now * w_now, axis=0, keepdims=True)
    left = w_now - jnp.where(r_r > 0, r_w / r_r, 0.0) * r_now
    w_aw = jnp.sum(w_now * dot(local[...], w_now), axis=0, keepdims=True)
    w_aw -= jnp.sum(w[outer, :] * dot(t_out[...], w_beyond), axis=0, keepdims=True)
    moments[0:1, :] = r_r
    moments[1:2, :] = r_w
    moments[2:3, :] = jnp.sum(left * left, axis=0, keepdims=True)
    moments[3:4, :] = w_aw
    edge[...] = dot(t_in[...].T, w[inner, :])


def share_kernel(moments, edge, other_w, out):
    coupling = jnp.sum(edge[...] * other_w[...], axis=0, keepdims=True)
    row = lax.broadcasted_iota(jnp.int32, moments.shape, 0)
    total = moments[...] - jnp.where(row == 3, coupling, 0.0)
    out[...] = jnp.broadcast_to(total[None], out.shape)


def finish_kernel(shares, x, r, w, out):
    r_rs, r_ws = shares[:, 0, :], shares[:, 1, :]
    r_r = jnp.sum(r_rs, axis=0, keepdims=True)
    r_w = jnp.sum(r_ws, axis=0, keepdims=True)
    theta = r_w / r_r
    off = jnp.where(r_rs > 0, r_ws / r_rs, 0.0) - theta
    spread = jnp.sum(shares[:, 2, :] + r_rs * off * off, axis=0, keepdims=True)
    w_aw = jnp.sum(shares[:, 3, :], axis=0, keepdims=True)
    ratio = spread / (theta * theta * r_r)
    energy = w_aw - 2.0 * theta * spread - theta * theta * r_w
    energy = jnp.maximum(energy - ratio * theta * spread, LEAST_EIGENVALUE * spread * (1.0 + ratio))
    step = jnp.where(spread > 0, spread / energy, 0.0)
    first = 1.0 / theta
    out[...] = x[...] + (first + step * (1.0 + ratio)) * r[...] - (step * first) * w[...]


def call(kernel, shapes, in_specs):
    outs = [jax.ShapeDtypeStruct(shape, jnp.float32) for shape in shapes]
    return pl.pallas_call(
        kernel,
        out_shape=outs if len(outs) > 1 else outs[0],
        in_specs=in_specs,
        out_specs=[VMEM] * len(outs) if len(outs) > 1 else VMEM,
        name=kernel.__name__,
    )


def body(block_cols, step_tiles, mass, warm_start, source_ids):
    tile = step_tiles.shape[-1]
    rows, columns = warm_start.shape
    assert block_cols.shape[0] == 2
    devices = lax.axis_size("patch") * lax.axis_size("sub")
    partner = [(i, i ^ 1) for i in range(devices)]
    across = [(i, i + 1) for i in range(1, devices - 1, 2)]
    across += [(j, i) for i, j in across]
    field, block = (rows, columns), (tile, columns)
    square = (tile, tile)

    other_x = lax.ppermute(warm_start, AXES, partner)
    local, t_in, t_out, t_out_t, base, push = call(
        local_kernel, [(rows, rows), square, square, square, field, block], [SMEM] + [VMEM] * 4
    )(block_cols, step_tiles, mass, warm_start, source_ids)
    t, q, send = call(start_kernel, [field, field, (4 * tile, columns)], [VMEM] * 5)(
        local, t_in, base, push, other_x
    )
    other_t = lax.ppermute(t, AXES, partner)
    got = lax.ppermute(send, AXES, across)
    r, w, w_in = call(image_kernel, [field, field, block], [VMEM] * 8)(
        local, t_in, t_out, t, q, push, other_t, got
    )
    other_w = lax.ppermute(w_in, AXES, partner)
    moments, edge = call(moment_kernel, [(4, columns), block], [VMEM] * 8)(
        local, t_in, t_out, t_out_t, push, got, r, w
    )
    shares = call(share_kernel, [(devices, 4, columns)], [VMEM] * 3)(moments, edge, other_w)
    shares = lax.all_to_all(shares, AXES, 0, 0)
    return call(finish_kernel, [field], [VMEM] * 4)(shares, warm_start, r, w)


def solution(mesh):
    in_specs = (
        P(("groups", "patch", "sub"), None),
        P(("groups", "patch", "sub"), None, None, None),
        P(("groups", "patch", "sub")),
        P(("groups", "patch", "sub"), None),
        P("groups"),
    )
    out_specs = P(("groups", "patch", "sub"), None)
    return jax.shard_map(body, mesh=mesh, in_specs=in_specs, out_specs=out_specs, check_vma=False)
```

time: 89.5 us -> 39.6 us (0.44)
  blocking collectives: 63 us -> 13 us
  Pallas kernels: 0 us -> 12.9 us
  waiting for transfers between devices: 5.63 us -> 1.2 us
  other arithmetic: 2.43 us -> 0 us
  starting transfers between devices: 12.4 us -> 10.2 us
  local copies, waits for them, and re-layouts: 3.94 us -> 1.99 us
  matrix products: 1.52 us -> 0 us
    psum x2 -> x0, blocking collectives: 63 us -> none  [paired_products(): lax.psum((jnp.sum(residual * residual, axis=0), jnp.sum(residual * image_...]
    all_to_all x0 -> x1, blocking collectives: none -> 13 us  [body(): shares = lax.all_to_all(shares, AXES, 0, 0)]
    pallas_call x0 -> x6, Pallas kernels: none -> 12.9 us  [the longest x1 2.57 us: body(): call(start_kernel, [field, field, (4 * tile, columns)], [VMEM] * 5)]
    ppermute x6 -> x4, waiting for transfers between devices: 5.63 us -> 1.2 us  [the longest x1 1.2 us: body(): other_t = lax.ppermute(t, AXES, partner)]
    ppermute x6 -> x4, starting transfers between devices: 12.4 us -> 10.2 us  [the longest x1 5.11 us: body(): other_w = lax.ppermute(w_in, AXES, partner)]
    gather x3 -> x0, local copies, waits for them, and re-layouts: 1.72 us -> none  [apply_operator(): picked = blocks[local_cols]]
    dot_general x3 -> x0, matrix products: 1.52 us -> none  [apply_operator(): jnp.einsum('bkij,bkjs->bis', step_tiles, picked, precision=lax.Precision....]
    reduce_sum x3 -> x0, other arithmetic: 1.39 us -> none  [the longest x1 1.15 us: body(): degree = jnp.sum(step_tiles, axis=(1, 3)).reshape(rows_here)]
  transfers between devices with their start and end apart: 6 -> 4, of which waited for: 3 -> 1; matrix products, arithmetic and copies ran while one was open for 1% -> 0% of each run, Pallas kernels for 0% -> 12%
where the time goes in v1:
time: 39.6 us; the launch traced here: 39.2 us
  blocking collectives  13 us (33%)
  Pallas kernels  12.9 us (33%)
  starting transfers between devices  10.2 us (26%)
  local copies, waits for them, and re-layouts  1.99 us (5%)
  waiting for transfers between devices  1.2 us (3%)
    all_to_all x1, blocking collectives, body(): shares = lax.all_to_all(shares, AXES, 0, 0)  13 us
    ppermute x1, starting transfers between devices, body(): other_w = lax.ppermute(w_in, AXES, partner)  5.11 us
    ppermute x1, starting transfers between devices, body(): other_t = lax.ppermute(t, AXES, partner)  3.89 us
    pallas_call x1, Pallas kernels, body(): call(start_kernel, [field, field, (4 * tile, columns)], [VMEM] * 5)  2.57 us
    pallas_call x1, Pallas kernels, body(): call(moment_kernel, [(4, columns), block], [VMEM] * 8)  2.44 us
    pallas_call x1, Pallas kernels, body(): call(image_kernel, [field, field, block], [VMEM] * 8)  2.35 us
    pallas_call x1, Pallas kernels, body(): call(local_kernel, [(rows, rows), square, square, square, field, block],...  2.21 us
    unnamed x8, local copies, waits for them, and re-layouts  1.99 us
  transfers between devices with their start and end apart: 4, of which 1 were waited for; matrix products, arithmetic and copies ran while one was open for 0% of the time, Pallas kernels for 12%

profile of v1, /device:TPU:0, one launch (start us, length us, event | category | flops | bytes accessed | tf_op | source)
XLA Modules:
  0.0 39.2 jit_solution(12693034530163775795)
XLA Ops:
  0.0 0.5 %collective-permute-start = (f32[256,128]{1,0:T(8,128)}, f32[256,128]{1,0:T(8,128)S(1)}, u32[]{:S(2)}, u32[]{:S(2)}) collective-permute-start(f32[256,128]{1,0:T(8,128)} %x.3), channel_id=1, source_target_pairs={{0,1},{1,0},{2,3},{3,2},{4,5},{5,4},{6,7},{7,6},{8,9},{9,8},{10,11... | collective-permute-start | bytes 393224 | tf_op jit(solution)/shard_map/ppermute | solution.py:164
  0.5 2.2 %local_kernel.1 = (f32[256,256]{1,0:T(8,128)}, f32[128,128]{1,0:T(8,128)}, f32[128,128]{1,0:T(8,128)}, f32[128,128]{1,0:T(8,128)}, f32[256,128]{1,0:T(8,128)}, /*index=5*/f32[128,128]{1,0:T(8,128)}) custom-call(s32[2,3]{1,0:T(2,128)} %cols.1, f32[2,3,128,128]{3,2,1,0:T(8,128)} %tiles.1, f32[256]{0:T(256)} %mass.1, f32[256,128]{1,0:T(8,128)} %x.3, s32[128]{0:T(128)} %sources.1), custom_call_target="tpu_custom_call" | custom-call | tf_op jit(solution)/shard_map/local_kernel/pallas_call | solution.py:165
  2.7 0.0 collective-permute-done.other_x
  2.7 0.0 copy-start.1
  2.7 0.6 %copy-done.1 = f32[256,128]{1,0:T(8,128)} copy-done((f32[256,128]{1,0:T(8,128)}, f32[256,128]{1,0:T(8,128)S(1)}, u32[]{:S(2)}) %copy-start.1) | copy-done | bytes 131096
  3.4 2.6 %start_kernel.1 = (f32[256,128]{1,0:T(8,128)}, f32[256,128]{1,0:T(8,128)}, f32[512,128]{1,0:T(8,128)}) custom-call(f32[256,256]{1,0:T(8,128)} %get-tuple-element.19.local, f32[128,128]{1,0:T(8,128)} %get-tuple-element.20.t_in, f32[256,128]{1,0:T(8,128)} %get-tuple-element.24.base, f32[128,128]{1,0:T(8,128)} %get-tuple-element.23.push, f32[256,128]{1,0:T(8,128)} %copy-done.1), custom_call_target="tpu_custom_call" | custom-call | tf_op jit(solution)/shard_map/start_kernel/pallas_call | solution.py:168
  5.9 0.7 %collective-permute-start.1 = (f32[512,128]{1,0:T(8,128)}, f32[512,128]{1,0:T(8,128)S(1)}, u32[]{:S(2)}, u32[]{:S(2)}) collective-permute-start(f32[512,128]{1,0:T(8,128)} %get-tuple-element.25), channel_id=1, source_target_pairs={{1,2},{3,4},{5,6},{7,8},{9,10},{11,12},{13,14},{2,1},{4,3},{6,5},{... | collective-permute-start | bytes 786440 | tf_op jit(solution)/shard_map/ppermute | solution.py:172
  6.6 3.9 %collective-permute-start.2 = (f32[256,128]{1,0:T(8,128)}, f32[256,128]{1,0:T(8,128)S(1)}, u32[]{:S(2)}, u32[]{:S(2)}) collective-permute-start(f32[256,128]{1,0:T(8,128)} %get-tuple-element.26.t), channel_id=1, source_target_pairs={{0,1},{1,0},{2,3},{3,2},{4,5},{5,4},{6,7},{7,6},{8,9},{9,8},{10,11... | collective-permute-start | bytes 393224 | tf_op jit(solution)/shard_map/ppermute | solution.py:171
  10.5 1.2 %collective-permute-done.2.other_t = f32[256,128]{1,0:T(8,128)S(1)} collective-permute-done((f32[256,128]{1,0:T(8,128)}, f32[256,128]{1,0:T(8,128)S(1)}, u32[]{:S(2)}, u32[]{:S(2)}) %collective-permute-start.2) | collective-permute-done | bytes 131104 | tf_op jit(solution)/shard_map/ppermute | solution.py:171
  11.7 0.0 copy-start.2
  11.7 0.0 collective-permute-done.1.got
  11.7 0.0 copy-start
  11.7 0.6 %copy-done.2 = f32[256,128]{1,0:T(8,128)} copy-done((f32[256,128]{1,0:T(8,128)}, f32[256,128]{1,0:T(8,128)S(1)}, u32[]{:S(2)}) %copy-start.2) | copy-done | bytes 131096
  12.3 0.1 copy-done
  12.4 2.3 %image_kernel.1 = (f32[256,128]{1,0:T(8,128)}, f32[256,128]{1,0:T(8,128)}, f32[128,128]{1,0:T(8,128)}) custom-call(f32[256,256]{1,0:T(8,128)} %get-tuple-element.19.local, f32[128,128]{1,0:T(8,128)} %get-tuple-element.20.t_in, f32[128,128]{1,0:T(8,128)} %get-tuple-element.21.t_out, f32[256,128]{1,0:T(8,128)} %get-tuple-element.26.t, ...), custom_call_target="tpu_custom_call" | custom-call | tf_op jit(solution)/shard_map/image_kernel/pallas_call | solution.py:173
  14.8 5.1 %collective-permute-start.3 = (f32[128,128]{1,0:T(8,128)}, f32[128,128]{1,0:T(8,128)S(1)}, u32[]{:S(2)}, u32[]{:S(2)}) collective-permute-start(f32[128,128]{1,0:T(8,128)} %get-tuple-element.32), channel_id=1, source_target_pairs={{0,1},{1,0},{2,3},{3,2},{4,5},{5,4},{6,7},{7,6},{8,9},{9,8},{10,11... | collective-permute-start | bytes 196616 | tf_op jit(solution)/shard_map/ppermute | solution.py:176
  19.9 2.4 %moment_kernel.1 = (f32[4,128]{1,0:T(4,128)}, f32[128,128]{1,0:T(8,128)}) custom-call(f32[256,256]{1,0:T(8,128)} %get-tuple-element.19.local, f32[128,128]{1,0:T(8,128)} %get-tuple-element.20.t_in, f32[128,128]{1,0:T(8,128)} %get-tuple-element.21.t_out, f32[128,128]{1,0:T(8,128)} %get-tuple-element.22.t_out_t, f32[128,128]{1,0:T(8,128)} %get-tuple-element.23.push, ...), custom_call_target="tpu_custom_call" | custom-call | tf_op jit(solution)/shard_map/moment_kernel/pallas_call | solution.py:177
  22.3 0.0 collective-permute-done.3.other_w
  22.3 0.0 copy-start.3
  22.3 0.6 %copy-done.3 = f32[128,128]{1,0:T(8,128)} copy-done((f32[128,128]{1,0:T(8,128)}, f32[128,128]{1,0:T(8,128)S(1)}, u32[]{:S(2)}) %copy-start.3) | copy-done | bytes 65560
  22.9 1.5 %share_kernel.1 = f32[16,4,128]{2,1,0:T(4,128)} custom-call(f32[4,128]{1,0:T(4,128)} %get-tuple-element.30.moments, f32[128,128]{1,0:T(8,128)} %get-tuple-element.31.edge, f32[128,128]{1,0:T(8,128)} %copy-done.3), custom_call_target="tpu_custom_call" | custom-call | tf_op jit(solution)/shard_map/share_kernel/pallas_call | solution.py:180
  24.4 13.0 %all_to_all.5.shares = f32[16,4,128]{2,1,0:T(4,128)} all-to-all(f32[16,4,128]{2,1,0:T(4,128)} %share_kernel.1), channel_id=1, replica_groups=mesh['groups'=2,'patch'=8,'sub'=2] {'patch','sub'}, dimensions={0} | all-to-all | bytes 65536 | tf_op jit(solution)/shard_map/all_to_all | solution.py:181
  37.5 1.8 %finish_kernel.1 = f32[256,128]{1,0:T(8,128)} custom-call(f32[16,4,128]{2,1,0:T(4,128)} %all_to_all.5.shares, f32[256,128]{1,0:T(8,128)} %x.3, f32[256,128]{1,0:T(8,128)} %get-tuple-element.28.r, f32[256,128]{1,0:T(8,128)} %get-tuple-element.29.w), custom_call_target="tpu_custom_call" | custom-call | tf_op jit(solution)/shard_map/finish_kernel/pallas_call | solution.py:182
Async XLA Ops:
  0.0 2.7 %collective-permute-start = (f32[256,128]{1,0:T(8,128)}, f32[256,128]{1,0:T(8,128)S(1)}, u32[]{:S(2)}, u32[]{:S(2)}) collective-permute-start(f32[256,128]{1,0:T(8,128)} %x.3), channel_id=1, source_target_pairs={{0,1},{1,0},{2,3},{3,2},{4,5},{5,4},{6,7},{7,6},{8,9},{9,8},{10,11... | collective-permute-start | bytes 393224 | tf_op jit(solution)/shard_map/ppermute | solution.py:164
  2.7 0.6 %copy-start.1 = (f32[256,128]{1,0:T(8,128)}, f32[256,128]{1,0:T(8,128)S(1)}, u32[]{:S(2)}) copy-start(f32[256,128]{1,0:T(8,128)S(1)} %collective-permute-done.other_x) | copy-start | bytes 393220
  5.9 5.8 %collective-permute-start.1 = (f32[512,128]{1,0:T(8,128)}, f32[512,128]{1,0:T(8,128)S(1)}, u32[]{:S(2)}, u32[]{:S(2)}) collective-permute-start(f32[512,128]{1,0:T(8,128)} %get-tuple-element.25), channel_id=1, source_target_pairs={{1,2},{3,4},{5,6},{7,8},{9,10},{11,12},{13,14},{2,1},{4,3},{6,5},{... | collective-permute-start | bytes 786440 | tf_op jit(solution)/shard_map/ppermute | solution.py:172
  6.6 5.1 %collective-permute-start.2 = (f32[256,128]{1,0:T(8,128)}, f32[256,128]{1,0:T(8,128)S(1)}, u32[]{:S(2)}, u32[]{:S(2)}) collective-permute-start(f32[256,128]{1,0:T(8,128)} %get-tuple-element.26.t), channel_id=1, source_target_pairs={{0,1},{1,0},{2,3},{3,2},{4,5},{5,4},{6,7},{7,6},{8,9},{9,8},{10,11... | collective-permute-start | bytes 393224 | tf_op jit(solution)/shard_map/ppermute | solution.py:171
  11.7 0.7 %copy-start.2 = (f32[256,128]{1,0:T(8,128)}, f32[256,128]{1,0:T(8,128)S(1)}, u32[]{:S(2)}) copy-start(f32[256,128]{1,0:T(8,128)S(1)} %collective-permute-done.2.other_t) | copy-start | bytes 393220
  11.7 0.7 %copy-start = (f32[512,128]{1,0:T(8,128)}, f32[512,128]{1,0:T(8,128)S(1)}, u32[]{:S(2)}) copy-start(f32[512,128]{1,0:T(8,128)S(1)} %collective-permute-done.1.got) | copy-start | bytes 786436
  14.8 7.6 %collective-permute-start.3 = (f32[128,128]{1,0:T(8,128)}, f32[128,128]{1,0:T(8,128)S(1)}, u32[]{:S(2)}, u32[]{:S(2)}) collective-permute-start(f32[128,128]{1,0:T(8,128)} %get-tuple-element.32), channel_id=1, source_target_pairs={{0,1},{1,0},{2,3},{3,2},{4,5},{5,4},{6,7},{7,6},{8,9},{9,8},{10,11... | collective-permute-start | bytes 196616 | tf_op jit(solution)/shard_map/ppermute | solution.py:176
  22.3 0.6 %copy-start.3 = (f32[128,128]{1,0:T(8,128)}, f32[128,128]{1,0:T(8,128)S(1)}, u32[]{:S(2)}) copy-start(f32[128,128]{1,0:T(8,128)S(1)} %collective-permute-done.3.other_w) | copy-start | bytes 196612

commit v2 on v1

--- a/solution.py
+++ b/solution.py
@@ -139,21 +139,27 @@
     out[...] = x[...] + (first + step * (1.0 + ratio)) * r[...] - (step * first) * w[...]
 
 
-def call(kernel, shapes, in_specs):
-    outs = [jax.ShapeDtypeStruct(shape, jnp.float32) for shape in shapes]
+def call(kernel, shapes, *operands, first=False, last=False):
+    place_out = jax.ShapeDtypeStruct if last else pltpu.VMEM
+    outs = [place_out(shape, jnp.float32) for shape in shapes]
+    in_specs, placed = [], []
+    for operand in operands:
+        scalars = operand.dtype == jnp.int32 and operand.ndim > 1
+        in_specs.append(SMEM if scalars else VMEM)
+        placed.append(operand if first else pltpu.with_memory_space_constraint(operand, pltpu.VMEM))
     return pl.pallas_call(
         kernel,
         out_shape=outs if len(outs) > 1 else outs[0],
         in_specs=in_specs,
         out_specs=[VMEM] * len(outs) if len(outs) > 1 else VMEM,
         name=kernel.__name__,
-    )
+    )(*placed)
 
 
 def body(block_cols, step_tiles, mass, warm_start, source_ids):
     tile = step_tiles.shape[-1]
     rows, columns = warm_start.shape
-    assert block_cols.shape[0] == 2
+    assert block_cols.shape[0] == 2 and columns == tile
     devices = lax.axis_size("patch") * lax.axis_size("sub")
     partner = [(i, i ^ 1) for i in range(devices)]
     across = [(i, i + 1) for i in range(1, devices - 1, 2)]
@@ -163,23 +169,24 @@
 
     other_x = lax.ppermute(warm_start, AXES, partner)
     local, t_in, t_out, t_out_t, base, push = call(
-        local_kernel, [(rows, rows), square, square, square, field, block], [SMEM] + [VMEM] * 4
-    )(block_cols, step_tiles, mass, warm_start, source_ids)
-    t, q, send = call(start_kernel, [field, field, (4 * tile, columns)], [VMEM] * 5)(
-        local, t_in, base, push, other_x
+        local_kernel, [(rows, rows), square, square, square, field, block],
+        block_cols, step_tiles, mass, warm_start, source_ids, first=True,
+    )
+    t, q, send = call(
+        start_kernel, [field, field, (4 * tile, columns)], local, t_in, base, push, other_x
     )
     other_t = lax.ppermute(t, AXES, partner)
     got = lax.ppermute(send, AXES, across)
-    r, w, w_in = call(image_kernel, [field, field, block], [VMEM] * 8)(
-        local, t_in, t_out, t, q, push, other_t, got
+    r, w, w_in = call(
+        image_kernel, [field, field, block], local, t_in, t_out, t, q, push, other_t, got
     )
     other_w = lax.ppermute(w_in, AXES, partner)
-    moments, edge = call(moment_kernel, [(4, columns), block], [VMEM] * 8)(
-        local, t_in, t_out, t_out_t, push, got, r, w
-    )
-    shares = call(share_kernel, [(devices, 4, columns)], [VMEM] * 3)(moments, edge, other_w)
+    moments, edge = call(
+        moment_kernel, [(4, columns), block], local, t_in, t_out, t_out_t, push, got, r, w
+    )
+    shares = call(share_kernel, [(devices, 4, columns)], moments, edge, other_w)
     shares = lax.all_to_all(shares, AXES, 0, 0)
-    return call(finish_kernel, [field], [VMEM] * 4)(shares, warm_start, r, w)
+    return call(finish_kernel, [field], shares, warm_start, r, w, last=True)
 
 
 def solution(mesh):

time: 39.6 us -> 28.5 us (0.72)
  Pallas kernels: 12.9 us -> 3.99 us
  local copies, waits for them, and re-layouts: 1.99 us -> 0.01 us
    pallas_call x6, Pallas kernels: 12.9 us -> 3.99 us  [call(): pl.pallas_call(kernel, out_shape=outs if len(outs) > 1 else outs[0], in_s...]
    unnamed x8 -> x2, local copies, waits for them, and re-layouts: 1.99 us -> 0.01 us
  transfers between devices with their start and end apart: 4 -> 4, of which waited for: 1 -> 2; matrix products, arithmetic and copies ran while one was open for 0% -> 0% of each run, Pallas kernels for 12% -> 8%
where the time goes in v2:
time: 28.5 us; the launch traced here: 28.3 us
  blocking collectives  12.8 us (45%)
  starting transfers between devices  10.2 us (36%)
  Pallas kernels  3.99 us (14%)
  waiting for transfers between devices  1.29 us (5%)
    all_to_all x1, blocking collectives, body(): shares = lax.all_to_all(shares, AXES, 0, 0)  12.8 us
    ppermute x1, starting transfers between devices, body(): other_w = lax.ppermute(w_in, AXES, partner)  5.12 us
    pallas_call x6, Pallas kernels, call(): pl.pallas_call(kernel, out_shape=outs if len(outs) > 1 else outs[0], in_s...  3.99 us
    ppermute x1, starting transfers between devices, body(): other_t = lax.ppermute(t, AXES, partner)  3.89 us
    ppermute x1, waiting for transfers between devices, body(): other_t = lax.ppermute(t, AXES, partner)  0.99 us
    ppermute x1, starting transfers between devices, body(): got = lax.ppermute(send, AXES, across)  0.68 us
  transfers between devices with their start and end apart: 4, of which 2 were waited for; matrix products, arithmetic and copies ran while one was open for 0% of the time, Pallas kernels for 8%

profile of v2, /device:TPU:0, one launch (start us, length us, event | category | flops | bytes accessed | tf_op | source)
XLA Modules:
  0.0 28.3 jit_solution(9099107314052215859)
XLA Ops:
  0.0 0.5 %collective-permute-start = (f32[256,128]{1,0:T(8,128)}, f32[256,128]{1,0:T(8,128)S(1)}, u32[]{:S(2)}, u32[]{:S(2)}) collective-permute-start(f32[256,128]{1,0:T(8,128)} %x.3), channel_id=1, source_target_pairs={{0,1},{1,0},{2,3},{3,2},{4,5},{5,4},{6,7},{7,6},{8,9},{9,8},{10,11... | collective-permute-start | bytes 393224 | tf_op jit(solution)/shard_map/ppermute | solution.py:170
  0.5 1.5 %local_kernel.1 = (f32[256,256]{1,0:T(8,128)S(1)}, f32[128,128]{1,0:T(8,128)S(1)}, f32[128,128]{1,0:T(8,128)S(1)}, f32[128,128]{1,0:T(8,128)S(1)}, f32[256,128]{1,0:T(8,128)S(1)}, /*index=5*/f32[128,128]{1,0:T(8,128)S(1)}) custom-call(s32[2,3]{1,0:T(2,128)} %cols.1, f32[2,3,128,128]{3,2,1,0:T(8,128)} %tiles.1, f32[256]{0:T(256)} %mass.1, f32[256,128]{1,0:T(8,128)} %x.3, ...), custom_call_target="tpu_custom_call" | custom-call | tf_op jit(solution)/shard_map/local_kernel/pallas_call | solution.py:150
  2.0 0.0 collective-permute-done.other_x
  2.0 0.7 %start_kernel.1 = (f32[256,128]{1,0:T(8,128)S(1)}, f32[256,128]{1,0:T(8,128)S(1)}, f32[512,128]{1,0:T(8,128)S(1)}) custom-call(f32[256,256]{1,0:T(8,128)S(1)} %get-tuple-element.19.local, f32[128,128]{1,0:T(8,128)S(1)} %get-tuple-element.20.t_in, f32[256,128]{1,0:T(8,128)S(1)} %get-tuple-element.24.base, f32[128,128]{1,0:T(8,128)S(1)} %get-tuple-element.23.push, ...), custom_call_target="tpu_custom_call" | custom-call | tf_op jit(solution)/shard_map/start_kernel/pallas_call | solution.py:150
  2.8 0.7 %collective-permute-start.1 = (f32[512,128]{1,0:T(8,128)S(1)}, f32[512,128]{1,0:T(8,128)S(1)}, u32[]{:S(2)}, u32[]{:S(2)}) collective-permute-start(f32[512,128]{1,0:T(8,128)S(1)} %get-tuple-element.25), channel_id=1, source_target_pairs={{1,2},{3,4},{5,6},{7,8},{9,10},{11,12},{13,14},{2,1},{4,3},{6,5},{... | collective-permute-start | bytes 786440 | tf_op jit(solution)/shard_map/ppermute | solution.py:179
  3.4 3.9 %collective-permute-start.2 = (f32[256,128]{1,0:T(8,128)S(1)}, f32[256,128]{1,0:T(8,128)S(1)}, u32[]{:S(2)}, u32[]{:S(2)}) collective-permute-start(f32[256,128]{1,0:T(8,128)S(1)} %get-tuple-element.26.t), channel_id=1, source_target_pairs={{0,1},{1,0},{2,3},{3,2},{4,5},{5,4},{6,7},{7,6},{8,9},{9,8},{10,11... | collective-permute-start | bytes 393224 | tf_op jit(solution)/shard_map/ppermute | solution.py:178
  7.3 1.0 %collective-permute-done.2.other_t = f32[256,128]{1,0:T(8,128)S(1)} collective-permute-done((f32[256,128]{1,0:T(8,128)S(1)}, f32[256,128]{1,0:T(8,128)S(1)}, u32[]{:S(2)}, u32[]{:S(2)}) %collective-permute-start.2) | collective-permute-done | bytes 131104 | tf_op jit(solution)/shard_map/ppermute | solution.py:178
  8.3 0.0 collective-permute-done.1.got
  8.3 0.4 %image_kernel.1 = (f32[256,128]{1,0:T(8,128)S(1)}, f32[256,128]{1,0:T(8,128)S(1)}, f32[128,128]{1,0:T(8,128)S(1)}) custom-call(f32[256,256]{1,0:T(8,128)S(1)} %get-tuple-element.19.local, f32[128,128]{1,0:T(8,128)S(1)} %get-tuple-element.20.t_in, f32[128,128]{1,0:T(8,128)S(1)} %get-tuple-element.21.t_out, f32[256,128]{1,0:T(8,128)S(1)} %get-tuple-element.26.t, ...), custom_call_target="tpu_custom_call" | custom-call | tf_op jit(solution)/shard_map/image_kernel/pallas_call | solution.py:150
  8.7 5.1 %collective-permute-start.3 = (f32[128,128]{1,0:T(8,128)S(1)}, f32[128,128]{1,0:T(8,128)S(1)}, u32[]{:S(2)}, u32[]{:S(2)}) collective-permute-start(f32[128,128]{1,0:T(8,128)S(1)} %get-tuple-element.32), channel_id=1, source_target_pairs={{0,1},{1,0},{2,3},{3,2},{4,5},{5,4},{6,7},{7,6},{8,9},{9,8},{10,11... | collective-permute-start | bytes 196616 | tf_op jit(solution)/shard_map/ppermute | solution.py:183
  13.9 0.6 %moment_kernel.1 = (f32[4,128]{1,0:T(4,128)S(1)}, f32[128,128]{1,0:T(8,128)S(1)}) custom-call(f32[256,256]{1,0:T(8,128)S(1)} %get-tuple-element.19.local, f32[128,128]{1,0:T(8,128)S(1)} %get-tuple-element.20.t_in, f32[128,128]{1,0:T(8,128)S(1)} %get-tuple-element.21.t_out, f32[128,128]{1,0:T(8,128)S(1)} %get-tuple-element.22.t_out_t, ...), custom_call_target="tpu_custom_call" | custom-call | tf_op jit(solution)/shard_map/moment_kernel/pallas_call | solution.py:150
  14.4 0.0 copy-start
  14.5 0.3 %collective-permute-done.3.other_w = f32[128,128]{1,0:T(8,128)S(1)} collective-permute-done((f32[128,128]{1,0:T(8,128)S(1)}, f32[128,128]{1,0:T(8,128)S(1)}, u32[]{:S(2)}, u32[]{:S(2)}) %collective-permute-start.3) | collective-permute-done | bytes 65568 | tf_op jit(solution)/shard_map/ppermute | solution.py:183
  14.8 12.8 %all_to_all.5.shares = f32[16,4,128]{2,1,0:T(4,128)S(1)} all-to-all(f32[16,4,128]{2,1,0:T(4,128)S(1)} %share_kernel.1), channel_id=1, replica_groups=mesh['groups'=2,'patch'=8,'sub'=2] {'patch','sub'}, dimensions={0} | all-to-all | bytes 65536 | tf_op jit(solution)/shard_map/all_to_all | solution.py:188
  27.6 0.0 copy-done
  27.6 0.7 %finish_kernel.1 = f32[256,128]{1,0:T(8,128)} custom-call(f32[16,4,128]{2,1,0:T(4,128)S(1)} %all_to_all.5.shares, f32[256,128]{1,0:T(8,128)S(1)} %copy-done, f32[256,128]{1,0:T(8,128)S(1)} %get-tuple-element.28.r, f32[256,128]{1,0:T(8,128)S(1)} %get-tuple-element.29.w), custom_call_target="tpu_custom_call" | custom-call | tf_op jit(solution)/shard_map/finish_kernel/pallas_call | solution.py:150
  (1 shorter events, 0.0 us)
Async XLA Ops:
  0.0 2.0 %collective-permute-start = (f32[256,128]{1,0:T(8,128)}, f32[256,128]{1,0:T(8,128)S(1)}, u32[]{:S(2)}, u32[]{:S(2)}) collective-permute-start(f32[256,128]{1,0:T(8,128)} %x.3), channel_id=1, source_target_pairs={{0,1},{1,0},{2,3},{3,2},{4,5},{5,4},{6,7},{7,6},{8,9},{9,8},{10,11... | collective-permute-start | bytes 393224 | tf_op jit(solution)/shard_map/ppermute | solution.py:170
  2.8 5.6 %collective-permute-start.1 = (f32[512,128]{1,0:T(8,128)S(1)}, f32[512,128]{1,0:T(8,128)S(1)}, u32[]{:S(2)}, u32[]{:S(2)}) collective-permute-start(f32[512,128]{1,0:T(8,128)S(1)} %get-tuple-element.25), channel_id=1, source_target_pairs={{1,2},{3,4},{5,6},{7,8},{9,10},{11,12},{13,14},{2,1},{4,3},{6,5},{... | collective-permute-start | bytes 786440 | tf_op jit(solution)/shard_map/ppermute | solution.py:179
  3.4 4.9 %collective-permute-start.2 = (f32[256,128]{1,0:T(8,128)S(1)}, f32[256,128]{1,0:T(8,128)S(1)}, u32[]{:S(2)}, u32[]{:S(2)}) collective-permute-start(f32[256,128]{1,0:T(8,128)S(1)} %get-tuple-element.26.t), channel_id=1, source_target_pairs={{0,1},{1,0},{2,3},{3,2},{4,5},{5,4},{6,7},{7,6},{8,9},{9,8},{10,11... | collective-permute-start | bytes 393224 | tf_op jit(solution)/shard_map/ppermute | solution.py:178
  8.7 6.0 %collective-permute-start.3 = (f32[128,128]{1,0:T(8,128)S(1)}, f32[128,128]{1,0:T(8,128)S(1)}, u32[]{:S(2)}, u32[]{:S(2)}) collective-permute-start(f32[128,128]{1,0:T(8,128)S(1)} %get-tuple-element.32), channel_id=1, source_target_pairs={{0,1},{1,0},{2,3},{3,2},{4,5},{5,4},{6,7},{7,6},{8,9},{9,8},{10,11... | collective-permute-start | bytes 196616 | tf_op jit(solution)/shard_map/ppermute | solution.py:183
  14.4 13.1 %copy-start = (f32[256,128]{1,0:T(8,128)S(1)}, f32[256,128]{1,0:T(8,128)}, u32[]{:S(2)}) copy-start(f32[256,128]{1,0:T(8,128)} %x.3) | copy-start | bytes 393220

commit v3 on v2

--- a/solution.py
+++ b/solution.py
@@ -28,14 +28,23 @@
     return outer, inner
 
 
-def local_kernel(cols, tiles, mass, x, sources, local, t_in, t_out, t_out_t, base, push):
+def flip(x):
+    return pltpu.roll(x, x.shape[1] // 2, 1)
+
+
+def index_of(shape, dimension):
+    return lax.broadcasted_iota(jnp.int32, shape, dimension)
+
+
+def local_kernel(cols, tiles, mass, x, sources, local, t_in, t_out, t_out_t, base, push, packed):
     tile = tiles.shape[-1]
+    half = tile // 2
     slots = tiles.shape[1]
     position = place()
     side = lax.rem(position, 2)
     first = position * 2
     above, below = first - 1, first + 2
-    eye = lax.broadcasted_iota(jnp.int32, (tile, tile), 0) == lax.broadcasted_iota(jnp.int32, (tile, tile), 1)
+    eye = index_of((tile, tile), 0) == index_of((tile, tile), 1)
 
     def toward(row, block):
         total = jnp.where(cols[row, 0] == block, tiles[row, 0], 0.0)
@@ -59,61 +68,97 @@
     t_in[...] = toward(1 - side, jnp.where(side == 0, below, above))
     t_out[...] = outward
     t_out_t[...] = outward_t
-    vertices = position * (2 * tile) + lax.broadcasted_iota(jnp.int32, x.shape, 0)
+    vertices = position * (2 * tile) + index_of(x.shape, 0)
     rhs = jnp.where(vertices == sources[...][None, :], 1.0, 0.0)
     base[...] = rhs - dot(local[...], x[...])
     push[...] = dot(outward_t, x[outer, :])
-
-
-def start_kernel(local, t_in, base, push, other_x, t, q, send):
+    own = local[outer, outer_columns(tile)]
+    above_diagonal = index_of((half, tile), 1) > index_of((half, tile), 0)
+    packed[0:half, :] = jnp.where(above_diagonal, own[:half], flip(own[half:]))
+    diagonal = jnp.sum(jnp.where(eye, own, 0.0), axis=0, keepdims=True)
+    packed[half:, :] = jnp.broadcast_to(diagonal, (8, tile))
+
+
+def unpack(packed):
+    tile = packed.shape[1]
+    half = tile // 2
+    rows = packed[0:half, :]
+    row, column = index_of((half, tile), 0), index_of((half, tile), 1)
+    upper = jnp.where(column > row, rows, 0.0)
+    lower = flip(jnp.where(column < row, rows, 0.0))
+    triangles = jnp.concatenate([upper, lower], axis=0)
+    eye = index_of((tile, tile), 0) == index_of((tile, tile), 1)
+    return triangles + triangles.T + jnp.where(eye, packed[half : half + 1, :], 0.0)
+
+
+def outer_columns(tile):
+    side = lax.rem(place(), 2)
+    return pl.ds(pl.multiple_of(side * tile, tile), tile)
+
+
+def start_kernel(local, t_in, base, push, packed, other_x, t, q_outer, send):
     tile = t_in.shape[0]
+    half = tile // 2
+    side = lax.rem(place(), 2)
     outer, inner = outer_block(tile)
     t[outer, :] = base[outer, :]
     t[inner, :] = base[inner, :] + dot(t_in[...], other_x[outer, :])
-    q[...] = dot(local[...], t[...])
-    send[0:tile, :] = t[outer, :]
-    send[tile : 2 * tile, :] = q[outer, :]
-    send[2 * tile : 3 * tile, :] = push[...]
-    send[3 * tile :, :] = local[outer, outer_columns(tile)]
-
-
-def outer_columns(tile):
-    side = lax.rem(place(), 2)
-    return pl.ds(pl.multiple_of(side * tile, tile), tile)
-
-
-def image_kernel(local, t_in, t_out, t, q, push, other_t, got, r, w, w_in):
+    q = dot(local[outer, :], t[...])
+    q_outer[...] = q
+    q = jnp.where(side == 0, flip(q), q)
+    first_half = index_of((half, tile), 1) < half
+    send[0:tile, :] = base[outer, :]
+    send[tile : 2 * tile, :] = push[...]
+    send[2 * tile : 2 * tile + half, :] = jnp.where(first_half, q[:half], flip(q[half:]))
+    send[2 * tile + half :, :] = packed[...]
+
+
+def inner_kernel(local, t_in, t, other_t, q_inner):
+    outer, inner = outer_block(t_in.shape[0])
+    q_inner[...] = dot(local[inner, :], t[...]) - dot(t_in[...], other_t[outer, :])
+
+
+def image_kernel(local, q_inner, got, w_inner):
+    tile = q_inner.shape[0]
+    _, inner = outer_block(tile)
+    w_inner[...] = q_inner[...] + dot(local[inner, outer_columns(tile)], got[tile : 2 * tile, :])
+
+
+def moment_kernel(local, t_in, t_out, t_out_t, t, q_outer, push, got, w_inner, r, w, moments, edge):
     tile = t_in.shape[0]
+    half = tile // 2
+    side = lax.rem(place(), 2)
     outer, inner = outer_block(tile)
-    push_here = got[2 * tile : 3 * tile, :]
+    push_here, push_there = got[tile : 2 * tile, :], push[...]
+    r_outer = t[outer, :] + push_here
+    w_outer = (
+        q_outer[...]
+        + dot(local[outer, outer_columns(tile)], push_here)
+        - dot(t_out[...], got[0:tile, :] + push_there)
+    )
+    r[outer, :] = r_outer
     r[inner, :] = t[inner, :]
-    r[outer, :] = t[outer, :] + push_here
-    change = dot(local[:, outer_columns(tile)], push_here)
-    w[...] = q[...] + change
-    beyond = got[0:tile, :] + push[...]
-    w[outer, :] = w[outer, :] - dot(t_out[...], beyond)
-    w_inner = w[inner, :] - dot(t_in[...], other_t[outer, :])
-    w[inner, :] = w_inner
-    w_in[...] = w_inner
-
-
-def moment_kernel(local, t_in, t_out, t_out_t, push, got, r, w, moments, edge):
-    tile = t_in.shape[0]
-    outer, inner = outer_block(tile)
+    w[outer, :] = w_outer
+    w[inner, :] = w_inner[...]
     w_now, r_now = w[...], r[...]
-    w_beyond = (
-        got[tile : 2 * tile, :] + dot(got[3 * tile :, :], push[...]) - dot(t_out_t[...], r[outer, :])
-    )
+    q_half = got[2 * tile : 2 * tile + half, :]
+    q_flip = flip(q_half)
+    q_there = jnp.concatenate(
+        [jnp.where(side == 0, q_half, q_flip), jnp.where(side == 0, q_flip, q_half)], axis=0
+    )
+    own_there = unpack(got[2 * tile + half :, :])
+    w_there = q_there + dot(own_there, push_there) - dot(t_out_t[...], r_outer)
+    coupling = jnp.sum(w_outer * dot(t_out[...], w_there), axis=0, keepdims=True)
+    mine = (index_of(coupling.shape, 1) >= half) == (side == 1)
     r_r = jnp.sum(r_now * r_now, axis=0, keepdims=True)
     r_w = jnp.sum(r_now * w_now, axis=0, keepdims=True)
     left = w_now - jnp.where(r_r > 0, r_w / r_r, 0.0) * r_now
     w_aw = jnp.sum(w_now * dot(local[...], w_now), axis=0, keepdims=True)
-    w_aw -= jnp.sum(w[outer, :] * dot(t_out[...], w_beyond), axis=0, keepdims=True)
     moments[0:1, :] = r_r
     moments[1:2, :] = r_w
     moments[2:3, :] = jnp.sum(left * left, axis=0, keepdims=True)
-    moments[3:4, :] = w_aw
-    edge[...] = dot(t_in[...].T, w[inner, :])
+    moments[3:4, :] = w_aw - jnp.where(mine, 2.0 * coupling, 0.0)
+    edge[...] = dot(t_in[...].T, w_inner[...])
 
 
 def share_kernel(moments, edge, other_w, out):
@@ -165,24 +210,24 @@
     across = [(i, i + 1) for i in range(1, devices - 1, 2)]
     across += [(j, i) for i, j in across]
     field, block = (rows, columns), (tile, columns)
-    square = (tile, tile)
+    square, packing = (tile, tile), (tile // 2 + 8, columns)
 
     other_x = lax.ppermute(warm_start, AXES, partner)
-    local, t_in, t_out, t_out_t, base, push = call(
-        local_kernel, [(rows, rows), square, square, square, field, block],
+    local, t_in, t_out, t_out_t, base, push, packed = call(
+        local_kernel, [(rows, rows), square, square, square, field, block, packing],
         block_cols, step_tiles, mass, warm_start, source_ids, first=True,
     )
-    t, q, send = call(
-        start_kernel, [field, field, (4 * tile, columns)], local, t_in, base, push, other_x
-    )
+    t, q_outer, send = call(
+        start_kernel, [field, block, (3 * tile + 8, columns)], local, t_in, base, push, packed, other_x
+    )
+    got = lax.ppermute(send, AXES, across)
     other_t = lax.ppermute(t, AXES, partner)
-    got = lax.ppermute(send, AXES, across)
-    r, w, w_in = call(
-        image_kernel, [field, field, block], local, t_in, t_out, t, q, push, other_t, got
-    )
-    other_w = lax.ppermute(w_in, AXES, partner)
-    moments, edge = call(
-        moment_kernel, [(4, columns), block], local, t_in, t_out, t_out_t, push, got, r, w
+    q_inner = call(inner_kernel, [block], local, t_in, t, other_t)
+    w_inner = call(image_kernel, [block], local, q_inner, got)
+    other_w = lax.ppermute(w_inner, AXES, partner)
+    r, w, moments, edge = call(
+        moment_kernel, [field, field, (4, columns), block],
+        local, t_in, t_out, t_out_t, t, q_outer, push, got, w_inner,
     )
     shares = call(share_kernel, [(devices, 4, columns)], moments, edge, other_w)
     shares = lax.all_to_all(shares, AXES, 0, 0)

time: 28.5 us -> 27 us (0.947)
  starting transfers between devices: 10.2 us -> 8.53 us
  Pallas kernels: 3.99 us -> 4.4 us
  waiting for transfers between devices: 1.29 us -> 0.99 us
    ppermute x1, starting transfers between devices: 5.12 us -> 3.47 us  [body(): other_w = lax.ppermute(w_inner, AXES, partner)]
    pallas_call x6 -> x7, Pallas kernels: 3.99 us -> 4.4 us  [call(): pl.pallas_call(kernel, out_shape=outs if len(outs) > 1 else outs[0], in_s...]
    ppermute x1, waiting for transfers between devices: 0.3 us -> 0.01 us  [body(): other_w = lax.ppermute(w_inner, AXES, partner)]
  transfers between devices with their start and end apart: 4 -> 4, of which waited for: 2 -> 1; matrix products, arithmetic and copies ran while one was open for 0% -> 0% of each run, Pallas kernels for 8% -> 10%
where the time goes in v3:
time: 27 us; the launch traced here: 26.8 us
  blocking collectives  12.8 us (47%)
  starting transfers between devices  8.53 us (32%)
  Pallas kernels  4.4 us (16%)
  waiting for transfers between devices  0.99 us (4%)
    all_to_all x1, blocking collectives, body(): shares = lax.all_to_all(shares, AXES, 0, 0)  12.8 us
    pallas_call x7, Pallas kernels, call(): pl.pallas_call(kernel, out_shape=outs if len(outs) > 1 else outs[0], in_s...  4.4 us
    ppermute x1, starting transfers between devices, body(): other_t = lax.ppermute(t, AXES, partner)  3.89 us
    ppermute x1, starting transfers between devices, body(): other_w = lax.ppermute(w_inner, AXES, partner)  3.47 us
    ppermute x1, waiting for transfers between devices, body(): other_t = lax.ppermute(t, AXES, partner)  0.99 us
    ppermute x1, starting transfers between devices, body(): got = lax.ppermute(send, AXES, across)  0.67 us
  transfers between devices with their start and end apart: 4, of which 1 were waited for; matrix products, arithmetic and copies ran while one was open for 0% of the time, Pallas kernels for 10%

profile of v3, /device:TPU:0, one launch (start us, length us, event | category | flops | bytes accessed | tf_op | source)
XLA Modules:
  0.0 26.8 jit_solution(6917358894803662175)
XLA Ops:
  0.0 0.5 %collective-permute-start = (f32[256,128]{1,0:T(8,128)}, f32[256,128]{1,0:T(8,128)S(1)}, u32[]{:S(2)}, u32[]{:S(2)}) collective-permute-start(f32[256,128]{1,0:T(8,128)} %x.3), channel_id=1, source_target_pairs={{0,1},{1,0},{2,3},{3,2},{4,5},{5,4},{6,7},{7,6},{8,9},{9,8},{10,11... | collective-permute-start | bytes 393224 | tf_op jit(solution)/shard_map/ppermute | solution.py:215
  0.5 1.5 %local_kernel.1 = (f32[256,256]{1,0:T(8,128)S(1)}, f32[128,128]{1,0:T(8,128)S(1)}, f32[128,128]{1,0:T(8,128)S(1)}, f32[128,128]{1,0:T(8,128)S(1)}, f32[256,128]{...) custom-call(s32[2,3]{1,0:T(2,128)} %cols.1, f32[2,3,128,128]{3,2,1,0:T(8,128)} %tiles.1, f32[256]{0:T(256)} %mass.1, ...), custom_call_target="tpu_custom_call" | custom-call | tf_op jit(solution)/shard_map/local_kernel/pallas_call | solution.py:195
  2.0 0.0 collective-permute-done.other_x
  2.1 0.7 %start_kernel.1 = (f32[256,128]{1,0:T(8,128)S(1)}, f32[128,128]{1,0:T(8,128)S(1)}, f32[392,128]{1,0:T(8,128)S(1)}) custom-call(f32[256,256]{1,0:T(8,128)S(1)} %get-tuple-element.19.local, f32[128,128]{1,0:T(8,128)S(1)} %get-tuple-element.20.t_in, f32[256,128]{1,0:T(8,128)S(1)} %get-tuple-element.23.base, f32[128,128]{1,0:T(8,128)S(1)} %get-tuple-element.24.push, ...), custom_call_target="tpu_custom_call" | custom-call | tf_op jit(solution)/shard_map/start_kernel/pallas_call | solution.py:195
  2.8 0.7 %collective-permute-start.1 = (f32[392,128]{1,0:T(8,128)S(1)}, f32[392,128]{1,0:T(8,128)S(1)}, u32[]{:S(2)}, u32[]{:S(2)}) collective-permute-start(f32[392,128]{1,0:T(8,128)S(1)} %get-tuple-element.28), channel_id=1, source_target_pairs={{1,2},{3,4},{5,6},{7,8},{9,10},{11,12},{13,14},{2,1},{4,3},{6,5},{... | collective-permute-start | bytes 602120 | tf_op jit(solution)/shard_map/ppermute | solution.py:223
  3.4 3.9 %collective-permute-start.2 = (f32[256,128]{1,0:T(8,128)S(1)}, f32[256,128]{1,0:T(8,128)S(1)}, u32[]{:S(2)}, u32[]{:S(2)}) collective-permute-start(f32[256,128]{1,0:T(8,128)S(1)} %get-tuple-element.26.t), channel_id=1, source_target_pairs={{0,1},{1,0},{2,3},{3,2},{4,5},{5,4},{6,7},{7,6},{8,9},{9,8},{10,11... | collective-permute-start | bytes 393224 | tf_op jit(solution)/shard_map/ppermute | solution.py:224
  7.3 1.0 %collective-permute-done.2.other_t = f32[256,128]{1,0:T(8,128)S(1)} collective-permute-done((f32[256,128]{1,0:T(8,128)S(1)}, f32[256,128]{1,0:T(8,128)S(1)}, u32[]{:S(2)}, u32[]{:S(2)}) %collective-permute-start.2) | collective-permute-done | bytes 131104 | tf_op jit(solution)/shard_map/ppermute | solution.py:224
  8.3 0.3 %inner_kernel.1.q_inner = f32[128,128]{1,0:T(8,128)S(1)} custom-call(f32[256,256]{1,0:T(8,128)S(1)} %get-tuple-element.19.local, f32[128,128]{1,0:T(8,128)S(1)} %get-tuple-element.20.t_in, f32[256,128]{1,0:T(8,128)S(1)} %get-tuple-element.26.t, f32[256,128]{1,0:T(8,128)S(1)} %collective-permute-done.2.other_t), custom_call_target="tpu_custom_call" | custom-call | tf_op jit(solution)/shard_map/inner_kernel/pallas_call | solution.py:195
  8.6 0.0 collective-permute-done.1.got
  8.6 0.2 image_kernel.1.w_inner
  8.9 3.5 %collective-permute-start.3 = (f32[128,128]{1,0:T(8,128)S(1)}, f32[128,128]{1,0:T(8,128)S(1)}, u32[]{:S(2)}, u32[]{:S(2)}) collective-permute-start(f32[128,128]{1,0:T(8,128)S(1)} %image_kernel.1.w_inner), channel_id=1, source_target_pairs={{0,1},{1,0},{2,3},{3,2},{4,5},{5,4},{6,7},{7,6},{8,9},{9,8},{10,11... | collective-permute-start | bytes 196616 | tf_op jit(solution)/shard_map/ppermute | solution.py:227
  12.3 0.9 %moment_kernel.1 = (f32[256,128]{1,0:T(8,128)S(1)}, f32[256,128]{1,0:T(8,128)S(1)}, f32[4,128]{1,0:T(4,128)S(1)}, f32[128,128]{1,0:T(8,128)S(1)}) custom-call(f32[256,256]{1,0:T(8,128)S(1)} %get-tuple-element.19.local, f32[128,128]{1,0:T(8,128)S(1)} %get-tuple-element.20.t_in, f32[128,128]{1,0:T(8,128)S(1)} %get-tuple-element.21.t_out, ...), custom_call_target="tpu_custom_call" | custom-call | tf_op jit(solution)/shard_map/moment_kernel/pallas_call | solution.py:195
  13.2 0.0 copy-start
  13.2 0.0 collective-permute-done.3.other_w
  13.3 12.8 %all_to_all.5.shares = f32[16,4,128]{2,1,0:T(4,128)S(1)} all-to-all(f32[16,4,128]{2,1,0:T(4,128)S(1)} %share_kernel.1), channel_id=1, replica_groups=mesh['groups'=2,'patch'=8,'sub'=2] {'patch','sub'}, dimensions={0} | all-to-all | bytes 65536 | tf_op jit(solution)/shard_map/all_to_all | solution.py:233
  26.1 0.0 copy-done
  26.1 0.7 %finish_kernel.1 = f32[256,128]{1,0:T(8,128)} custom-call(f32[16,4,128]{2,1,0:T(4,128)S(1)} %all_to_all.5.shares, f32[256,128]{1,0:T(8,128)S(1)} %copy-done, f32[256,128]{1,0:T(8,128)S(1)} %get-tuple-element.31.r, f32[256,128]{1,0:T(8,128)S(1)} %get-tuple-element.32.w), custom_call_target="tpu_custom_call" | custom-call | tf_op jit(solution)/shard_map/finish_kernel/pallas_call | solution.py:195
  (1 shorter events, 0.0 us)
Async XLA Ops:
  0.0 2.0 %collective-permute-start = (f32[256,128]{1,0:T(8,128)}, f32[256,128]{1,0:T(8,128)S(1)}, u32[]{:S(2)}, u32[]{:S(2)}) collective-permute-start(f32[256,128]{1,0:T(8,128)} %x.3), channel_id=1, source_target_pairs={{0,1},{1,0},{2,3},{3,2},{4,5},{5,4},{6,7},{7,6},{8,9},{9,8},{10,11... | collective-permute-start | bytes 393224 | tf_op jit(solution)/shard_map/ppermute | solution.py:215
  2.8 5.9 %collective-permute-start.1 = (f32[392,128]{1,0:T(8,128)S(1)}, f32[392,128]{1,0:T(8,128)S(1)}, u32[]{:S(2)}, u32[]{:S(2)}) collective-permute-start(f32[392,128]{1,0:T(8,128)S(1)} %get-tuple-element.28), channel_id=1, source_target_pairs={{1,2},{3,4},{5,6},{7,8},{9,10},{11,12},{13,14},{2,1},{4,3},{6,5},{... | collective-permute-start | bytes 602120 | tf_op jit(solution)/shard_map/ppermute | solution.py:223
  3.4 4.9 %collective-permute-start.2 = (f32[256,128]{1,0:T(8,128)S(1)}, f32[256,128]{1,0:T(8,128)S(1)}, u32[]{:S(2)}, u32[]{:S(2)}) collective-permute-start(f32[256,128]{1,0:T(8,128)S(1)} %get-tuple-element.26.t), channel_id=1, source_target_pairs={{0,1},{1,0},{2,3},{3,2},{4,5},{5,4},{6,7},{7,6},{8,9},{9,8},{10,11... | collective-permute-start | bytes 393224 | tf_op jit(solution)/shard_map/ppermute | solution.py:224
  8.9 4.4 %collective-permute-start.3 = (f32[128,128]{1,0:T(8,128)S(1)}, f32[128,128]{1,0:T(8,128)S(1)}, u32[]{:S(2)}, u32[]{:S(2)}) collective-permute-start(f32[128,128]{1,0:T(8,128)S(1)} %image_kernel.1.w_inner), channel_id=1, source_target_pairs={{0,1},{1,0},{2,3},{3,2},{4,5},{5,4},{6,7},{7,6},{8,9},{9,8},{10,11... | collective-permute-start | bytes 196616 | tf_op jit(solution)/shard_map/ppermute | solution.py:227
  13.2 12.9 %copy-start = (f32[256,128]{1,0:T(8,128)S(1)}, f32[256,128]{1,0:T(8,128)}, u32[]{:S(2)}) copy-start(f32[256,128]{1,0:T(8,128)} %x.3) | copy-start | bytes 393220

commit v4 on v3

--- a/solution.py
+++ b/solution.py
@@ -13,8 +13,19 @@
 SMEM = pl.BlockSpec(memory_space=pltpu.SMEM)
 
 
+def halves(a):
+    high = a.astype(jnp.bfloat16)
+    return high, (a - high.astype(jnp.float32)).astype(jnp.bfloat16)
+
+
 def dot(a, b):
-    return jnp.dot(a, b, precision=lax.Precision.HIGHEST, preferred_element_type=jnp.float32)
+    a_high, a_low = a[0], a[1]
+    b_high, b_low = halves(b)
+
+    def product(p, q):
+        return jnp.dot(p, q, preferred_element_type=jnp.float32)
+
+    return product(a_high, b_high) + (product(a_high, b_low) + product(a_low, b_high))
 
 
 def place():
@@ -36,7 +47,7 @@
     return lax.broadcasted_iota(jnp.int32, shape, dimension)
 
 
-def local_kernel(cols, tiles, mass, x, sources, local, t_in, t_out, t_out_t, base, push, packed):
+def local_kernel(cols, tiles, mass, x, sources, local, diag, t_in, t_out, t_out_t, base, push, packed):
     tile = tiles.shape[-1]
     half = tile // 2
     slots = tiles.shape[1]
@@ -53,29 +64,29 @@
         return total
 
     for row in range(2):
+        here = pl.ds(row * tile, tile)
         whole = tiles[row, 0]
         for slot in range(1, slots):
             whole += tiles[row, slot]
-        masses = mass[pl.ds(row * tile, tile)][None, :]
+        masses = mass[here][None, :]
         total = jnp.sum(whole + jnp.where(eye, masses, 0.0), axis=1, keepdims=True)
-        own = jnp.where(eye, total, 0.0) - toward(row, first + row)
-        cross = -toward(row, first + 1 - row)
-        local[pl.ds(row * tile, tile), pl.ds(row * tile, tile)] = own
-        local[pl.ds(row * tile, tile), pl.ds((1 - row) * tile, tile)] = cross
+        diag[here, :] = jnp.broadcast_to(total, (tile, x.shape[1]))
+        for column in range(2):
+            there = pl.ds(column * tile, tile)
+            local[0, here, there], local[1, here, there] = halves(-toward(row, first + column))
     outer, _ = outer_block(tile)
     outward = toward(side, jnp.where(side == 0, above, below))
-    outward_t = outward.T
-    t_in[...] = toward(1 - side, jnp.where(side == 0, below, above))
-    t_out[...] = outward
-    t_out_t[...] = outward_t
+    t_in[0], t_in[1] = halves(toward(1 - side, jnp.where(side == 0, below, above)))
+    t_out[0], t_out[1] = halves(outward)
+    t_out_t[0], t_out_t[1] = halves(outward.T)
     vertices = position * (2 * tile) + index_of(x.shape, 0)
     rhs = jnp.where(vertices == sources[...][None, :], 1.0, 0.0)
-    base[...] = rhs - dot(local[...], x[...])
-    push[...] = dot(outward_t, x[outer, :])
-    own = local[outer, outer_columns(tile)]
+    base[...] = rhs - diag[...] * x[...] - dot(local, x[...])
+    push[...] = dot(t_out_t, x[outer, :])
+    own = toward(side, first + side)
     above_diagonal = index_of((half, tile), 1) > index_of((half, tile), 0)
     packed[0:half, :] = jnp.where(above_diagonal, own[:half], flip(own[half:]))
-    diagonal = jnp.sum(jnp.where(eye, own, 0.0), axis=0, keepdims=True)
+    diagonal = jnp.sum(jnp.where(eye, diag[outer, :], 0.0), axis=0, keepdims=True)
     packed[half:, :] = jnp.broadcast_to(diagonal, (8, tile))
 
 
@@ -88,7 +99,8 @@
     lower = flip(jnp.where(column < row, rows, 0.0))
     triangles = jnp.concatenate([upper, lower], axis=0)
     eye = index_of((tile, tile), 0) == index_of((tile, tile), 1)
-    return triangles + triangles.T + jnp.where(eye, packed[half : half + 1, :], 0.0)
+    diagonal = jnp.sum(jnp.where(eye, packed[half : half + 1, :], 0.0), axis=1, keepdims=True)
+    return triangles + triangles.T, diagonal
 
 
 def outer_columns(tile):
@@ -96,14 +108,18 @@
     return pl.ds(pl.multiple_of(side * tile, tile), tile)
 
 
-def start_kernel(local, t_in, base, push, packed, other_x, t, q_outer, send):
-    tile = t_in.shape[0]
+def part(pair, *index):
+    return pair[(0, *index)], pair[(1, *index)]
+
+
+def start_kernel(local, diag, t_in, base, push, packed, other_x, t, q_outer, send):
+    tile = t_in.shape[-1]
     half = tile // 2
     side = lax.rem(place(), 2)
     outer, inner = outer_block(tile)
     t[outer, :] = base[outer, :]
-    t[inner, :] = base[inner, :] + dot(t_in[...], other_x[outer, :])
-    q = dot(local[outer, :], t[...])
+    t[inner, :] = base[inner, :] + dot(t_in, other_x[outer, :])
+    q = diag[outer, :] * base[outer, :] + dot(part(local, outer), t[...])
     q_outer[...] = q
     q = jnp.where(side == 0, flip(q), q)
     first_half = index_of((half, tile), 1) < half
@@ -113,19 +129,21 @@
     send[2 * tile + half :, :] = packed[...]
 
 
-def inner_kernel(local, t_in, t, other_t, q_inner):
-    outer, inner = outer_block(t_in.shape[0])
-    q_inner[...] = dot(local[inner, :], t[...]) - dot(t_in[...], other_t[outer, :])
+def inner_kernel(local, diag, t_in, t, other_t, q_inner):
+    outer, inner = outer_block(t_in.shape[-1])
+    q_inner[...] = (
+        diag[inner, :] * t[inner, :] + dot(part(local, inner), t[...]) - dot(t_in, other_t[outer, :])
+    )
 
 
 def image_kernel(local, q_inner, got, w_inner):
     tile = q_inner.shape[0]
     _, inner = outer_block(tile)
-    w_inner[...] = q_inner[...] + dot(local[inner, outer_columns(tile)], got[tile : 2 * tile, :])
-
-
-def moment_kernel(local, t_in, t_out, t_out_t, t, q_outer, push, got, w_inner, r, w, moments, edge):
-    tile = t_in.shape[0]
+    w_inner[...] = q_inner[...] + dot(part(local, inner, outer_columns(tile)), got[tile : 2 * tile, :])
+
+
+def moment_kernel(local, diag, t_in, t_out, t_out_t, t, q_outer, push, got, w_inner, r, w, moments, edge):
+    tile = t_in.shape[-1]
     half = tile // 2
     side = lax.rem(place(), 2)
     outer, inner = outer_block(tile)
@@ -133,8 +151,9 @@
     r_outer = t[outer, :] + push_here
     w_outer = (
         q_outer[...]
-        + dot(local[outer, outer_columns(tile)], push_here)
-        - dot(t_out[...], got[0:tile, :] + push_there)
+        + diag[outer, :] * push_here
+        + dot(part(local, outer, outer_columns(tile)), push_here)
+        - dot(t_out, got[0:tile, :] + push_there)
     )
     r[outer, :] = r_outer
     r[inner, :] = t[inner, :]
@@ -146,19 +165,19 @@
     q_there = jnp.concatenate(
         [jnp.where(side == 0, q_half, q_flip), jnp.where(side == 0, q_flip, q_half)], axis=0
     )
-    own_there = unpack(got[2 * tile + half :, :])
-    w_there = q_there + dot(own_there, push_there) - dot(t_out_t[...], r_outer)
-    coupling = jnp.sum(w_outer * dot(t_out[...], w_there), axis=0, keepdims=True)
+    own_there, diag_there = unpack(got[2 * tile + half :, :])
+    w_there = q_there + diag_there * push_there - dot(halves(own_there), push_there) - dot(t_out_t, r_outer)
+    coupling = jnp.sum(w_outer * dot(t_out, w_there), axis=0, keepdims=True)
     mine = (index_of(coupling.shape, 1) >= half) == (side == 1)
     r_r = jnp.sum(r_now * r_now, axis=0, keepdims=True)
     r_w = jnp.sum(r_now * w_now, axis=0, keepdims=True)
     left = w_now - jnp.where(r_r > 0, r_w / r_r, 0.0) * r_now
-    w_aw = jnp.sum(w_now * dot(local[...], w_now), axis=0, keepdims=True)
+    w_aw = jnp.sum(w_now * (diag[...] * w_now + dot(local, w_now)), axis=0, keepdims=True)
     moments[0:1, :] = r_r
     moments[1:2, :] = r_w
     moments[2:3, :] = jnp.sum(left * left, axis=0, keepdims=True)
     moments[3:4, :] = w_aw - jnp.where(mine, 2.0 * coupling, 0.0)
-    edge[...] = dot(t_in[...].T, w_inner[...])
+    edge[...] = dot((t_in[0].T, t_in[1].T), w_inner[...])
 
 
 def share_kernel(moments, edge, other_w, out):
@@ -186,7 +205,7 @@
 
 def call(kernel, shapes, *operands, first=False, last=False):
     place_out = jax.ShapeDtypeStruct if last else pltpu.VMEM
-    outs = [place_out(shape, jnp.float32) for shape in shapes]
+    outs = [place_out(shape[1:], shape[0]) for shape in shapes]
     in_specs, placed = [], []
     for operand in operands:
         scalars = operand.dtype == jnp.int32 and operand.ndim > 1
@@ -209,27 +228,29 @@
     partner = [(i, i ^ 1) for i in range(devices)]
     across = [(i, i + 1) for i in range(1, devices - 1, 2)]
     across += [(j, i) for i, j in across]
-    field, block = (rows, columns), (tile, columns)
-    square, packing = (tile, tile), (tile // 2 + 8, columns)
+    single = jnp.float32
+    field, block = (single, rows, columns), (single, tile, columns)
+    square, packing = (jnp.bfloat16, 2, tile, tile), (single, tile // 2 + 8, columns)
 
     other_x = lax.ppermute(warm_start, AXES, partner)
-    local, t_in, t_out, t_out_t, base, push, packed = call(
-        local_kernel, [(rows, rows), square, square, square, field, block, packing],
+    local, diag, t_in, t_out, t_out_t, base, push, packed = call(
+        local_kernel, [(jnp.bfloat16, 2, rows, rows), field, square, square, square, field, block, packing],
         block_cols, step_tiles, mass, warm_start, source_ids, first=True,
     )
     t, q_outer, send = call(
-        start_kernel, [field, block, (3 * tile + 8, columns)], local, t_in, base, push, packed, other_x
+        start_kernel, [field, block, (single, 3 * tile + 8, columns)],
+        local, diag, t_in, base, push, packed, other_x,
     )
     got = lax.ppermute(send, AXES, across)
     other_t = lax.ppermute(t, AXES, partner)
-    q_inner = call(inner_kernel, [block], local, t_in, t, other_t)
+    q_inner = call(inner_kernel, [block], local, diag, t_in, t, other_t)
     w_inner = call(image_kernel, [block], local, q_inner, got)
     other_w = lax.ppermute(w_inner, AXES, partner)
     r, w, moments, edge = call(
-        moment_kernel, [field, field, (4, columns), block],
-        local, t_in, t_out, t_out_t, t, q_outer, push, got, w_inner,
-    )
-    shares = call(share_kernel, [(devices, 4, columns)], moments, edge, other_w)
+        moment_kernel, [field, field, (single, 4, columns), block],
+        local, diag, t_in, t_out, t_out_t, t, q_outer, push, got, w_inner,
+    )
+    shares = call(share_kernel, [(single, devices, 4, columns)], moments, edge, other_w)
     shares = lax.all_to_all(shares, AXES, 0, 0)
     return call(finish_kernel, [field], shares, warm_start, r, w, last=True)
 

time: 27 us -> 26.7 us (0.989)
  Pallas kernels: 4.4 us -> 3.83 us
    pallas_call x7, Pallas kernels: 4.4 us -> 3.83 us  [call(): pl.pallas_call(kernel, out_shape=outs if len(outs) > 1 else outs[0], in_s...]
  transfers between devices with their start and end apart: 4 -> 4, of which waited for: 1 -> 2; matrix products, arithmetic and copies ran while one was open for 0% -> 0% of each run, Pallas kernels for 10% -> 9%
where the time goes in v4:
time: 26.7 us; the launch traced here: 26.5 us
  blocking collectives  12.7 us (48%)
  starting transfers between devices  8.68 us (33%)
  Pallas kernels  3.83 us (14%)
  waiting for transfers between devices  1.23 us (5%)
    all_to_all x1, blocking collectives, body(): shares = lax.all_to_all(shares, AXES, 0, 0)  12.7 us
    ppermute x1, starting transfers between devices, body(): other_t = lax.ppermute(t, AXES, partner)  3.97 us
    pallas_call x7, Pallas kernels, call(): pl.pallas_call(kernel, out_shape=outs if len(outs) > 1 else outs[0], in_s...  3.83 us
    ppermute x1, starting transfers between devices, body(): other_w = lax.ppermute(w_inner, AXES, partner)  3.54 us
    ppermute x1, waiting for transfers between devices, body(): other_t = lax.ppermute(t, AXES, partner)  0.99 us
    ppermute x1, starting transfers between devices, body(): got = lax.ppermute(send, AXES, across)  0.67 us
  transfers between devices with their start and end apart: 4, of which 2 were waited for; matrix products, arithmetic and copies ran while one was open for 0% of the time, Pallas kernels for 9%

profile of v4, /device:TPU:0, one launch (start us, length us, event | category | flops | bytes accessed | tf_op | source)
XLA Modules:
  0.0 26.5 jit_solution(10268922431798008702)
XLA Ops:
  0.0 0.5 %collective-permute-start = (f32[256,128]{1,0:T(8,128)}, f32[256,128]{1,0:T(8,128)S(1)}, u32[]{:S(2)}, u32[]{:S(2)}) collective-permute-start(f32[256,128]{1,0:T(8,128)} %x.3), channel_id=1, source_target_pairs={{0,1},{1,0},{2,3},{3,2},{4,5},{5,4},{6,7},{7,6},{8,9},{9,8},{10,11... | collective-permute-start | bytes 393224 | tf_op jit(solution)/shard_map/ppermute | solution.py:235
  0.5 1.4 %local_kernel.1 = (bf16[2,256,256]{2,1,0:T(8,128)(2,1)S(1)}, f32[256,128]{1,0:T(8,128)S(1)}, bf16[2,128,128]{2,1,0:T(8,128)(2,1)S(1)}, bf16[2,128,128]{2,1,0:T(8...) custom-call(s32[2,3]{1,0:T(2,128)} %cols.1, ...), custom_call_target="tpu_custom_call" | custom-call | tf_op jit(solution)/shard_map/local_kernel/pallas_call | solution.py:214
  1.9 0.0 collective-permute-done.other_x
  2.0 0.6 %start_kernel.1 = (f32[256,128]{1,0:T(8,128)S(1)}, f32[128,128]{1,0:T(8,128)S(1)}, f32[392,128]{1,0:T(8,128)S(1)}) custom-call(bf16[2,256,256]{2,1,0:T(8,128)(2,1)S(1)} %get-tuple-element.20.local, f32[256,128]{1,0:T(8,128)S(1)} %get-tuple-element.21.diag, bf16[2,128,128]{2,1,0:T(8,128)(2,1)S(1)} %get-tuple-element.22.t_in, ...), custom_call_target="tpu_custom_call" | custom-call | tf_op jit(solution)/shard_map/start_kernel/pallas_call | solution.py:214
  2.5 0.7 %collective-permute-start.1 = (f32[392,128]{1,0:T(8,128)S(1)}, f32[392,128]{1,0:T(8,128)S(1)}, u32[]{:S(2)}, u32[]{:S(2)}) collective-permute-start(f32[392,128]{1,0:T(8,128)S(1)} %get-tuple-element.30), channel_id=1, source_target_pairs={{1,2},{3,4},{5,6},{7,8},{9,10},{11,12},{13,14},{2,1},{4,3},{6,5},{... | collective-permute-start | bytes 602120 | tf_op jit(solution)/shard_map/ppermute | solution.py:244
  3.2 4.0 %collective-permute-start.2 = (f32[256,128]{1,0:T(8,128)S(1)}, f32[256,128]{1,0:T(8,128)S(1)}, u32[]{:S(2)}, u32[]{:S(2)}) collective-permute-start(f32[256,128]{1,0:T(8,128)S(1)} %get-tuple-element.28.t), channel_id=1, source_target_pairs={{0,1},{1,0},{2,3},{3,2},{4,5},{5,4},{6,7},{7,6},{8,9},{9,8},{10,11... | collective-permute-start | bytes 393224 | tf_op jit(solution)/shard_map/ppermute | solution.py:245
  7.2 1.0 %collective-permute-done.2.other_t = f32[256,128]{1,0:T(8,128)S(1)} collective-permute-done((f32[256,128]{1,0:T(8,128)S(1)}, f32[256,128]{1,0:T(8,128)S(1)}, u32[]{:S(2)}, u32[]{:S(2)}) %collective-permute-start.2) | collective-permute-done | bytes 131104 | tf_op jit(solution)/shard_map/ppermute | solution.py:245
  8.2 0.2 inner_kernel.1.q_inner
  8.4 0.0 collective-permute-done.1.got
  8.4 0.2 image_kernel.1.w_inner
  8.6 3.5 %collective-permute-start.3 = (f32[128,128]{1,0:T(8,128)S(1)}, f32[128,128]{1,0:T(8,128)S(1)}, u32[]{:S(2)}, u32[]{:S(2)}) collective-permute-start(f32[128,128]{1,0:T(8,128)S(1)} %image_kernel.1.w_inner), channel_id=1, source_target_pairs={{0,1},{1,0},{2,3},{3,2},{4,5},{5,4},{6,7},{7,6},{8,9},{9,8},{10,11... | collective-permute-start | bytes 196616 | tf_op jit(solution)/shard_map/ppermute | solution.py:248
  12.1 0.7 %moment_kernel.1 = (f32[256,128]{1,0:T(8,128)S(1)}, f32[256,128]{1,0:T(8,128)S(1)}, f32[4,128]{1,0:T(4,128)S(1)}, f32[128,128]{1,0:T(8,128)S(1)}) custom-call(bf16[2,256,256]{2,1,0:T(8,128)(2,1)S(1)} %get-tuple-element.20.local, f32[256,128]{1,0:T(8,128)S(1)} %get-tuple-element.21.diag, bf16[2,128,128]{2,1,0:T(8,128)(2,1)S(1)} %get-tuple-element.22.t_in, ...), custom_call_target="tpu_custom_call" | custom-call | tf_op jit(solution)/shard_map/moment_kernel/pallas_call | solution.py:214
  12.8 0.0 copy-start
  12.8 0.2 collective-permute-done.3.other_w
  13.1 12.7 %all_to_all.5.shares = f32[16,4,128]{2,1,0:T(4,128)S(1)} all-to-all(f32[16,4,128]{2,1,0:T(4,128)S(1)} %share_kernel.1), channel_id=1, replica_groups=mesh['groups'=2,'patch'=8,'sub'=2] {'patch','sub'}, dimensions={0} | all-to-all | bytes 65536 | tf_op jit(solution)/shard_map/all_to_all | solution.py:254
  25.8 0.0 copy-done
  25.8 0.7 %finish_kernel.1 = f32[256,128]{1,0:T(8,128)} custom-call(f32[16,4,128]{2,1,0:T(4,128)S(1)} %all_to_all.5.shares, f32[256,128]{1,0:T(8,128)S(1)} %copy-done, f32[256,128]{1,0:T(8,128)S(1)} %get-tuple-element.33.r, f32[256,128]{1,0:T(8,128)S(1)} %get-tuple-element.34.w), custom_call_target="tpu_custom_call" | custom-call | tf_op jit(solution)/shard_map/finish_kernel/pallas_call | solution.py:214
  (1 shorter events, 0.0 us)
Async XLA Ops:
  0.0 1.9 %collective-permute-start = (f32[256,128]{1,0:T(8,128)}, f32[256,128]{1,0:T(8,128)S(1)}, u32[]{:S(2)}, u32[]{:S(2)}) collective-permute-start(f32[256,128]{1,0:T(8,128)} %x.3), channel_id=1, source_target_pairs={{0,1},{1,0},{2,3},{3,2},{4,5},{5,4},{6,7},{7,6},{8,9},{9,8},{10,11... | collective-permute-start | bytes 393224 | tf_op jit(solution)/shard_map/ppermute | solution.py:235
  2.5 5.9 %collective-permute-start.1 = (f32[392,128]{1,0:T(8,128)S(1)}, f32[392,128]{1,0:T(8,128)S(1)}, u32[]{:S(2)}, u32[]{:S(2)}) collective-permute-start(f32[392,128]{1,0:T(8,128)S(1)} %get-tuple-element.30), channel_id=1, source_target_pairs={{1,2},{3,4},{5,6},{7,8},{9,10},{11,12},{13,14},{2,1},{4,3},{6,5},{... | collective-permute-start | bytes 602120 | tf_op jit(solution)/shard_map/ppermute | solution.py:244
  3.2 5.0 %collective-permute-start.2 = (f32[256,128]{1,0:T(8,128)S(1)}, f32[256,128]{1,0:T(8,128)S(1)}, u32[]{:S(2)}, u32[]{:S(2)}) collective-permute-start(f32[256,128]{1,0:T(8,128)S(1)} %get-tuple-element.28.t), channel_id=1, source_target_pairs={{0,1},{1,0},{2,3},{3,2},{4,5},{5,4},{6,7},{7,6},{8,9},{9,8},{10,11... | collective-permute-start | bytes 393224 | tf_op jit(solution)/shard_map/ppermute | solution.py:245
  8.6 4.4 %collective-permute-start.3 = (f32[128,128]{1,0:T(8,128)S(1)}, f32[128,128]{1,0:T(8,128)S(1)}, u32[]{:S(2)}, u32[]{:S(2)}) collective-permute-start(f32[128,128]{1,0:T(8,128)S(1)} %image_kernel.1.w_inner), channel_id=1, source_target_pairs={{0,1},{1,0},{2,3},{3,2},{4,5},{5,4},{6,7},{7,6},{8,9},{9,8},{10,11... | collective-permute-start | bytes 196616 | tf_op jit(solution)/shard_map/ppermute | solution.py:248
  12.8 13.0 %copy-start = (f32[256,128]{1,0:T(8,128)S(1)}, f32[256,128]{1,0:T(8,128)}, u32[]{:S(2)}) copy-start(f32[256,128]{1,0:T(8,128)} %x.3) | copy-start | bytes 393220

commit v5 on v4

--- a/solution.py
+++ b/solution.py
@@ -142,24 +142,35 @@
     w_inner[...] = q_inner[...] + dot(part(local, inner, outer_columns(tile)), got[tile : 2 * tile, :])
 
 
-def moment_kernel(local, diag, t_in, t_out, t_out_t, t, q_outer, push, got, w_inner, r, w, moments, edge):
+def moment_kernel(
+    local, diag, t_in, t_out, t_out_t, t, q_outer, push, got, w_inner, r, w, moments, edge, edge_r
+):
     tile = t_in.shape[-1]
     half = tile // 2
     side = lax.rem(place(), 2)
     outer, inner = outer_block(tile)
+
+    def total(value):
+        return jnp.sum(value, axis=0, keepdims=True)
+
     push_here, push_there = got[tile : 2 * tile, :], push[...]
-    r_outer = t[outer, :] + push_here
+    r_outer, r_there = t[outer, :] + push_here, got[0:tile, :] + push_there
+    pull_r = dot(t_out, r_there)
     w_outer = (
         q_outer[...]
         + diag[outer, :] * push_here
         + dot(part(local, outer, outer_columns(tile)), push_here)
-        - dot(t_out, got[0:tile, :] + push_there)
+        - pull_r
     )
     r[outer, :] = r_outer
     r[inner, :] = t[inner, :]
     w[outer, :] = w_outer
     w[inner, :] = w_inner[...]
     w_now, r_now = w[...], r[...]
+    r_r, r_w = total(r_now * r_now), total(r_now * w_now)
+    shift = jnp.where(r_r > 0, r_w / r_r, 0.0)
+    y = w_now - shift * r_now
+    y_outer = w_outer - shift * r_outer
     q_half = got[2 * tile : 2 * tile + half, :]
     q_flip = flip(q_half)
     q_there = jnp.concatenate(
@@ -167,36 +178,41 @@
     )
     own_there, diag_there = unpack(got[2 * tile + half :, :])
     w_there = q_there + diag_there * push_there - dot(halves(own_there), push_there) - dot(t_out_t, r_outer)
-    coupling = jnp.sum(w_outer * dot(t_out, w_there), axis=0, keepdims=True)
-    mine = (index_of(coupling.shape, 1) >= half) == (side == 1)
-    r_r = jnp.sum(r_now * r_now, axis=0, keepdims=True)
-    r_w = jnp.sum(r_now * w_now, axis=0, keepdims=True)
-    left = w_now - jnp.where(r_r > 0, r_w / r_r, 0.0) * r_now
-    w_aw = jnp.sum(w_now * (diag[...] * w_now + dot(local, w_now)), axis=0, keepdims=True)
-    moments[0:1, :] = r_r
-    moments[1:2, :] = r_w
-    moments[2:3, :] = jnp.sum(left * left, axis=0, keepdims=True)
-    moments[3:4, :] = w_aw - jnp.where(mine, 2.0 * coupling, 0.0)
-    edge[...] = dot((t_in[0].T, t_in[1].T), w_inner[...])
-
-
-def share_kernel(moments, edge, other_w, out):
-    coupling = jnp.sum(edge[...] * other_w[...], axis=0, keepdims=True)
-    row = lax.broadcasted_iota(jnp.int32, moments.shape, 0)
-    total = moments[...] - jnp.where(row == 3, coupling, 0.0)
+    pull_y = dot(t_out, w_there - shift * r_there)
+    mine = (index_of((1, r_now.shape[1]), 1) >= half) == (side == 1)
+    weight = jnp.where(mine, 2.0, 0.0)
+    a_y = diag[...] * y + dot(local, y)
+    y_ay = total(y * a_y) - weight * total(y_outer * pull_y)
+    r_ay = total(r_now * a_y + y * w_now) + total(y_outer * pull_r)
+    r_ay -= weight * total(r_outer * pull_y + y_outer * pull_r)
+    r_ar = r_w + (1.0 - weight) * total(r_outer * pull_r)
+    moments[...] = jnp.concatenate([r_r, r_w, total(y * y), y_ay, r_ay, r_ar, shift, shift], axis=0)
+    t_in_t = (t_in[0].T, t_in[1].T)
+    edge[...] = dot(t_in_t, w_inner[...] - shift * r[inner, :])
+    edge_r[...] = dot(t_in_t, r[inner, :])
+
+
+def share_kernel(moments, edge, edge_r, other_t, other_w, out):
+    outer, _ = outer_block(edge.shape[0])
+    y_there = other_w[...] - moments[6:7, :] * other_t[outer, :]
+    y_ay = jnp.sum(edge[...] * y_there, axis=0, keepdims=True)
+    r_ay = jnp.sum(edge_r[...] * y_there, axis=0, keepdims=True)
+    row = index_of(moments.shape, 0)
+    total = moments[...] - jnp.where(row == 3, y_ay, 0.0) - jnp.where(row == 4, r_ay, 0.0)
     out[...] = jnp.broadcast_to(total[None], out.shape)
 
 
 def finish_kernel(shares, x, r, w, out):
-    r_rs, r_ws = shares[:, 0, :], shares[:, 1, :]
+    r_rs = shares[:, 0, :]
     r_r = jnp.sum(r_rs, axis=0, keepdims=True)
-    r_w = jnp.sum(r_ws, axis=0, keepdims=True)
+    r_w = jnp.sum(shares[:, 1, :], axis=0, keepdims=True)
     theta = r_w / r_r
-    off = jnp.where(r_rs > 0, r_ws / r_rs, 0.0) - theta
+    off = shares[:, 6, :] - theta
     spread = jnp.sum(shares[:, 2, :] + r_rs * off * off, axis=0, keepdims=True)
-    w_aw = jnp.sum(shares[:, 3, :], axis=0, keepdims=True)
+    energy = jnp.sum(
+        shares[:, 3, :] + off * (shares[:, 4, :] + off * shares[:, 5, :]), axis=0, keepdims=True
+    )
     ratio = spread / (theta * theta * r_r)
-    energy = w_aw - 2.0 * theta * spread - theta * theta * r_w
     energy = jnp.maximum(energy - ratio * theta * spread, LEAST_EIGENVALUE * spread * (1.0 + ratio))
     step = jnp.where(spread > 0, spread / energy, 0.0)
     first = 1.0 / theta
@@ -246,11 +262,11 @@
     q_inner = call(inner_kernel, [block], local, diag, t_in, t, other_t)
     w_inner = call(image_kernel, [block], local, q_inner, got)
     other_w = lax.ppermute(w_inner, AXES, partner)
-    r, w, moments, edge = call(
-        moment_kernel, [field, field, (single, 4, columns), block],
+    r, w, moments, edge, edge_r = call(
+        moment_kernel, [field, field, (single, 8, columns), block, block],
         local, diag, t_in, t_out, t_out_t, t, q_outer, push, got, w_inner,
     )
-    shares = call(share_kernel, [(single, devices, 4, columns)], moments, edge, other_w)
+    shares = call(share_kernel, [(single, devices, 8, columns)], moments, edge, edge_r, other_t, other_w)
     shares = lax.all_to_all(shares, AXES, 0, 0)
     return call(finish_kernel, [field], shares, warm_start, r, w, last=True)
 

time: 26.7 us -> 27.1 us (1.015)
  blocking collectives: 12.7 us -> 13.1 us
    all_to_all x1, blocking collectives: 12.7 us -> 13.1 us  [body(): shares = lax.all_to_all(shares, AXES, 0, 0)]
where the time goes in v5:
time: 27.1 us; the launch traced here: 26.9 us
  blocking collectives  13.1 us (48%)
  starting transfers between devices  8.68 us (32%)
  Pallas kernels  3.86 us (14%)
  waiting for transfers between devices  1.21 us (4%)
    all_to_all x1, blocking collectives, body(): shares = lax.all_to_all(shares, AXES, 0, 0)  13.1 us
    ppermute x1, starting transfers between devices, body(): other_t = lax.ppermute(t, AXES, partner)  3.98 us
    pallas_call x7, Pallas kernels, call(): pl.pallas_call(kernel, out_shape=outs if len(outs) > 1 else outs[0], in_s...  3.86 us
    ppermute x1, starting transfers between devices, body(): other_w = lax.ppermute(w_inner, AXES, partner)  3.54 us
    ppermute x1, waiting for transfers between devices, body(): other_t = lax.ppermute(t, AXES, partner)  0.99 us
    ppermute x1, starting transfers between devices, body(): got = lax.ppermute(send, AXES, across)  0.67 us
  transfers between devices with their start and end apart: 4, of which 2 were waited for; matrix products, arithmetic and copies ran while one was open for 0% of the time, Pallas kernels for 9%

profile of v5, /device:TPU:0, one launch (start us, length us, event | category | flops | bytes accessed | tf_op | source)
XLA Modules:
  0.0 26.9 jit_solution(12327821251102734356)
XLA Ops:
  0.0 0.5 %collective-permute-start = (f32[256,128]{1,0:T(8,128)}, f32[256,128]{1,0:T(8,128)S(1)}, u32[]{:S(2)}, u32[]{:S(2)}) collective-permute-start(f32[256,128]{1,0:T(8,128)} %x.3), channel_id=1, source_target_pairs={{0,1},{1,0},{2,3},{3,2},{4,5},{5,4},{6,7},{7,6},{8,9},{9,8},{10,11... | collective-permute-start | bytes 393224 | tf_op jit(solution)/shard_map/ppermute | solution.py:251
  0.5 1.4 %local_kernel.1 = (bf16[2,256,256]{2,1,0:T(8,128)(2,1)S(1)}, f32[256,128]{1,0:T(8,128)S(1)}, bf16[2,128,128]{2,1,0:T(8,128)(2,1)S(1)}, bf16[2,128,128]{2,1,0:T(8...) custom-call(s32[2,3]{1,0:T(2,128)} %cols.1, ...), custom_call_target="tpu_custom_call" | custom-call | tf_op jit(solution)/shard_map/local_kernel/pallas_call | solution.py:230
  1.9 0.0 collective-permute-done.other_x
  2.0 0.6 %start_kernel.1 = (f32[256,128]{1,0:T(8,128)S(1)}, f32[128,128]{1,0:T(8,128)S(1)}, f32[392,128]{1,0:T(8,128)S(1)}) custom-call(bf16[2,256,256]{2,1,0:T(8,128)(2,1)S(1)} %get-tuple-element.21.local, f32[256,128]{1,0:T(8,128)S(1)} %get-tuple-element.22.diag, bf16[2,128,128]{2,1,0:T(8,128)(2,1)S(1)} %get-tuple-element.23.t_in, ...), custom_call_target="tpu_custom_call" | custom-call | tf_op jit(solution)/shard_map/start_kernel/pallas_call | solution.py:230
  2.5 0.7 %collective-permute-start.1 = (f32[392,128]{1,0:T(8,128)S(1)}, f32[392,128]{1,0:T(8,128)S(1)}, u32[]{:S(2)}, u32[]{:S(2)}) collective-permute-start(f32[392,128]{1,0:T(8,128)S(1)} %get-tuple-element.31), channel_id=1, source_target_pairs={{1,2},{3,4},{5,6},{7,8},{9,10},{11,12},{13,14},{2,1},{4,3},{6,5},{... | collective-permute-start | bytes 602120 | tf_op jit(solution)/shard_map/ppermute | solution.py:260
  3.2 4.0 %collective-permute-start.2 = (f32[256,128]{1,0:T(8,128)S(1)}, f32[256,128]{1,0:T(8,128)S(1)}, u32[]{:S(2)}, u32[]{:S(2)}) collective-permute-start(f32[256,128]{1,0:T(8,128)S(1)} %get-tuple-element.29.t), channel_id=1, source_target_pairs={{0,1},{1,0},{2,3},{3,2},{4,5},{5,4},{6,7},{7,6},{8,9},{9,8},{10,11... | collective-permute-start | bytes 393224 | tf_op jit(solution)/shard_map/ppermute | solution.py:261
  7.2 1.0 %collective-permute-done.2.other_t = f32[256,128]{1,0:T(8,128)S(1)} collective-permute-done((f32[256,128]{1,0:T(8,128)S(1)}, f32[256,128]{1,0:T(8,128)S(1)}, u32[]{:S(2)}, u32[]{:S(2)}) %collective-permute-start.2) | collective-permute-done | bytes 131104 | tf_op jit(solution)/shard_map/ppermute | solution.py:261
  8.2 0.2 inner_kernel.1.q_inner
  8.4 0.0 collective-permute-done.1.got
  8.4 0.2 image_kernel.1.w_inner
  8.6 3.5 %collective-permute-start.3 = (f32[128,128]{1,0:T(8,128)S(1)}, f32[128,128]{1,0:T(8,128)S(1)}, u32[]{:S(2)}, u32[]{:S(2)}) collective-permute-start(f32[128,128]{1,0:T(8,128)S(1)} %image_kernel.1.w_inner), channel_id=1, source_target_pairs={{0,1},{1,0},{2,3},{3,2},{4,5},{5,4},{6,7},{7,6},{8,9},{9,8},{10,11... | collective-permute-start | bytes 196616 | tf_op jit(solution)/shard_map/ppermute | solution.py:264
  12.1 0.7 %moment_kernel.1 = (f32[256,128]{1,0:T(8,128)S(1)}, f32[256,128]{1,0:T(8,128)S(1)}, f32[8,128]{1,0:T(8,128)S(1)}, f32[128,128]{1,0:T(8,128)S(1)}, f32[128,128]{1,0:T(8,128)S(1)}) custom-call(bf16[2,256,256]{2,1,0:T(8,128)(2,1)S(1)} %get-tuple-element.21.local, f32[256,128]{1,0:T(8,128)S(1)} %get-tuple-element.22.diag, ...), custom_call_target="tpu_custom_call" | custom-call | tf_op jit(solution)/shard_map/moment_kernel/pallas_call | solution.py:230
  12.8 0.2 collective-permute-done.3.other_w
  13.1 0.0 copy-start
  13.1 13.1 %all_to_all.5.shares = f32[16,8,128]{2,1,0:T(8,128)S(1)} all-to-all(f32[16,8,128]{2,1,0:T(8,128)S(1)} %share_kernel.1), channel_id=1, replica_groups=mesh['groups'=2,'patch'=8,'sub'=2] {'patch','sub'}, dimensions={0} | all-to-all | bytes 131072 | tf_op jit(solution)/shard_map/all_to_all | solution.py:270
  26.2 0.0 copy-done
  26.2 0.7 %finish_kernel.1 = f32[256,128]{1,0:T(8,128)} custom-call(f32[16,8,128]{2,1,0:T(8,128)S(1)} %all_to_all.5.shares, f32[256,128]{1,0:T(8,128)S(1)} %copy-done, f32[256,128]{1,0:T(8,128)S(1)} %get-tuple-element.35.r, f32[256,128]{1,0:T(8,128)S(1)} %get-tuple-element.36.w), custom_call_target="tpu_custom_call" | custom-call | tf_op jit(solution)/shard_map/finish_kernel/pallas_call | solution.py:230
  (1 shorter events, 0.0 us)
Async XLA Ops:
  0.0 1.9 %collective-permute-start = (f32[256,128]{1,0:T(8,128)}, f32[256,128]{1,0:T(8,128)S(1)}, u32[]{:S(2)}, u32[]{:S(2)}) collective-permute-start(f32[256,128]{1,0:T(8,128)} %x.3), channel_id=1, source_target_pairs={{0,1},{1,0},{2,3},{3,2},{4,5},{5,4},{6,7},{7,6},{8,9},{9,8},{10,11... | collective-permute-start | bytes 393224 | tf_op jit(solution)/shard_map/ppermute | solution.py:251
  2.5 5.9 %collective-permute-start.1 = (f32[392,128]{1,0:T(8,128)S(1)}, f32[392,128]{1,0:T(8,128)S(1)}, u32[]{:S(2)}, u32[]{:S(2)}) collective-permute-start(f32[392,128]{1,0:T(8,128)S(1)} %get-tuple-element.31), channel_id=1, source_target_pairs={{1,2},{3,4},{5,6},{7,8},{9,10},{11,12},{13,14},{2,1},{4,3},{6,5},{... | collective-permute-start | bytes 602120 | tf_op jit(solution)/shard_map/ppermute | solution.py:260
  3.2 5.0 %collective-permute-start.2 = (f32[256,128]{1,0:T(8,128)S(1)}, f32[256,128]{1,0:T(8,128)S(1)}, u32[]{:S(2)}, u32[]{:S(2)}) collective-permute-start(f32[256,128]{1,0:T(8,128)S(1)} %get-tuple-element.29.t), channel_id=1, source_target_pairs={{0,1},{1,0},{2,3},{3,2},{4,5},{5,4},{6,7},{7,6},{8,9},{9,8},{10,11... | collective-permute-start | bytes 393224 | tf_op jit(solution)/shard_map/ppermute | solution.py:261
  8.6 4.4 %collective-permute-start.3 = (f32[128,128]{1,0:T(8,128)S(1)}, f32[128,128]{1,0:T(8,128)S(1)}, u32[]{:S(2)}, u32[]{:S(2)}) collective-permute-start(f32[128,128]{1,0:T(8,128)S(1)} %image_kernel.1.w_inner), channel_id=1, source_target_pairs={{0,1},{1,0},{2,3},{3,2},{4,5},{5,4},{6,7},{7,6},{8,9},{9,8},{10,11... | collective-permute-start | bytes 196616 | tf_op jit(solution)/shard_map/ppermute | solution.py:264
  13.1 13.1 %copy-start = (f32[256,128]{1,0:T(8,128)S(1)}, f32[256,128]{1,0:T(8,128)}, u32[]{:S(2)}) copy-start(f32[256,128]{1,0:T(8,128)} %x.3) | copy-start | bytes 393220

commit v6 on v5

--- a/solution.py
+++ b/solution.py
@@ -47,7 +47,9 @@
     return lax.broadcasted_iota(jnp.int32, shape, dimension)
 
 
-def local_kernel(cols, tiles, mass, x, sources, local, diag, t_in, t_out, t_out_t, base, push, packed):
+def local_kernel(
+    cols, tiles, mass, x, sources, local, diag, t_in, t_out_t, base, push, q_base, send
+):
     tile = tiles.shape[-1]
     half = tile // 2
     slots = tiles.shape[1]
@@ -57,34 +59,40 @@
     above, below = first - 1, first + 2
     eye = index_of((tile, tile), 0) == index_of((tile, tile), 1)
 
-    def toward(row, block):
-        total = jnp.where(cols[row, 0] == block, tiles[row, 0], 0.0)
-        for slot in range(1, slots):
-            total += jnp.where(cols[row, slot] == block, tiles[row, slot], 0.0)
-        return total
-
+    def toward(row, block, sign=1.0):
+        slot, scale = jnp.int32(0), 0.0
+        for k in range(slots):
+            named = cols[row, k] == block
+            slot, scale = jnp.where(named, k, slot), jnp.where(named, sign, scale)
+        return scale * tiles[row, slot]
+
+    owns = []
     for row in range(2):
-        here = pl.ds(row * tile, tile)
-        whole = tiles[row, 0]
-        for slot in range(1, slots):
-            whole += tiles[row, slot]
+        here, there = pl.ds(row * tile, tile), pl.ds((1 - row) * tile, tile)
+        whole, own = tiles[row, 0], jnp.where(cols[row, 0] == first + row, tiles[row, 0], 0.0)
+        for k in range(1, slots):
+            whole += tiles[row, k]
+            own += jnp.where(cols[row, k] == first + row, tiles[row, k], 0.0)
         masses = mass[here][None, :]
         total = jnp.sum(whole + jnp.where(eye, masses, 0.0), axis=1, keepdims=True)
         diag[here, :] = jnp.broadcast_to(total, (tile, x.shape[1]))
-        for column in range(2):
-            there = pl.ds(column * tile, tile)
-            local[0, here, there], local[1, here, there] = halves(-toward(row, first + column))
+        local[0, here, here], local[1, here, here] = halves(-own)
+        local[0, here, there], local[1, here, there] = halves(toward(row, first + 1 - row, -1.0))
+        owns.append(own)
     outer, _ = outer_block(tile)
-    outward = toward(side, jnp.where(side == 0, above, below))
+    outward_t = toward(side, jnp.where(side == 0, above, below)).T
     t_in[0], t_in[1] = halves(toward(1 - side, jnp.where(side == 0, below, above)))
-    t_out[0], t_out[1] = halves(outward)
-    t_out_t[0], t_out_t[1] = halves(outward.T)
+    t_out_t[0], t_out_t[1] = halves(outward_t)
     vertices = position * (2 * tile) + index_of(x.shape, 0)
     rhs = jnp.where(vertices == sources[...][None, :], 1.0, 0.0)
     base[...] = rhs - diag[...] * x[...] - dot(local, x[...])
     push[...] = dot(t_out_t, x[outer, :])
-    own = toward(side, first + side)
+    q_base[...] = diag[outer, :] * base[outer, :] + dot(part(local, outer), base[...])
+    send[0:tile, :] = base[outer, :]
+    send[tile : 2 * tile, :] = push[...]
+    own = jnp.where(side == 0, owns[0], owns[1])
     above_diagonal = index_of((half, tile), 1) > index_of((half, tile), 0)
+    packed = send.at[2 * tile + half :]
     packed[0:half, :] = jnp.where(above_diagonal, own[:half], flip(own[half:]))
     diagonal = jnp.sum(jnp.where(eye, diag[outer, :], 0.0), axis=0, keepdims=True)
     packed[half:, :] = jnp.broadcast_to(diagonal, (8, tile))
@@ -108,29 +116,35 @@
     return pl.ds(pl.multiple_of(side * tile, tile), tile)
 
 
+def inner_columns(tile):
+    side = lax.rem(place(), 2)
+    return pl.ds(pl.multiple_of((1 - side) * tile, tile), tile)
+
+
 def part(pair, *index):
     return pair[(0, *index)], pair[(1, *index)]
 
 
-def start_kernel(local, diag, t_in, base, push, packed, other_x, t, q_outer, send):
+def start_kernel(local, t_in, base, q_base, other_x, send_in, t, q_outer, send):
     tile = t_in.shape[-1]
     half = tile // 2
     side = lax.rem(place(), 2)
     outer, inner = outer_block(tile)
+    pull = dot(t_in, other_x[outer, :])
+    q = q_base[...] + dot(part(local, outer, inner_columns(tile)), pull)
+    turned = jnp.where(side == 0, flip(q), q)
+    first_half = index_of((half, tile), 1) < half
+    send[2 * tile : 2 * tile + half, :] = jnp.where(first_half, turned[:half], flip(turned[half:]))
+    q_outer[...] = q
     t[outer, :] = base[outer, :]
-    t[inner, :] = base[inner, :] + dot(t_in, other_x[outer, :])
-    q = diag[outer, :] * base[outer, :] + dot(part(local, outer), t[...])
-    q_outer[...] = q
-    q = jnp.where(side == 0, flip(q), q)
-    first_half = index_of((half, tile), 1) < half
-    send[0:tile, :] = base[outer, :]
-    send[tile : 2 * tile, :] = push[...]
-    send[2 * tile : 2 * tile + half, :] = jnp.where(first_half, q[:half], flip(q[half:]))
-    send[2 * tile + half :, :] = packed[...]
-
-
-def inner_kernel(local, diag, t_in, t, other_t, q_inner):
+    t[inner, :] = base[inner, :] + pull
+
+
+def inner_kernel(local, diag, t_in, t_out_t, t, other_t, q_inner, t_in_t, t_out):
     outer, inner = outer_block(t_in.shape[-1])
+    for half in range(2):
+        t_in_t[half] = t_in[half].T
+        t_out[half] = t_out_t[half].T
     q_inner[...] = (
         diag[inner, :] * t[inner, :] + dot(part(local, inner), t[...]) - dot(t_in, other_t[outer, :])
     )
@@ -143,9 +157,9 @@
 
 
 def moment_kernel(
-    local, diag, t_in, t_out, t_out_t, t, q_outer, push, got, w_inner, r, w, moments, edge, edge_r
+    local, diag, t_in_t, t_out, t_out_t, t, q_outer, push, got, w_inner, r, w, moments, edge, edge_r
 ):
-    tile = t_in.shape[-1]
+    tile = t_out.shape[-1]
     half = tile // 2
     side = lax.rem(place(), 2)
     outer, inner = outer_block(tile)
@@ -187,7 +201,6 @@
     r_ay -= weight * total(r_outer * pull_y + y_outer * pull_r)
     r_ar = r_w + (1.0 - weight) * total(r_outer * pull_r)
     moments[...] = jnp.concatenate([r_r, r_w, total(y * y), y_ay, r_ay, r_ar, shift, shift], axis=0)
-    t_in_t = (t_in[0].T, t_in[1].T)
     edge[...] = dot(t_in_t, w_inner[...] - shift * r[inner, :])
     edge_r[...] = dot(t_in_t, r[inner, :])
 
@@ -199,19 +212,18 @@
     r_ay = jnp.sum(edge_r[...] * y_there, axis=0, keepdims=True)
     row = index_of(moments.shape, 0)
     total = moments[...] - jnp.where(row == 3, y_ay, 0.0) - jnp.where(row == 4, r_ay, 0.0)
-    out[...] = jnp.broadcast_to(total[None], out.shape)
+    for pair in range(out.shape[1]):
+        out[:, pair] = jnp.broadcast_to(total[None, 2 * pair : 2 * pair + 2], out[:, pair].shape)
 
 
 def finish_kernel(shares, x, r, w, out):
-    r_rs = shares[:, 0, :]
+    r_rs, r_ws, spreads, y_ay, r_ay, r_ar = [shares[:, row // 2, row % 2, :] for row in range(6)]
     r_r = jnp.sum(r_rs, axis=0, keepdims=True)
-    r_w = jnp.sum(shares[:, 1, :], axis=0, keepdims=True)
+    r_w = jnp.sum(r_ws, axis=0, keepdims=True)
     theta = r_w / r_r
-    off = shares[:, 6, :] - theta
-    spread = jnp.sum(shares[:, 2, :] + r_rs * off * off, axis=0, keepdims=True)
-    energy = jnp.sum(
-        shares[:, 3, :] + off * (shares[:, 4, :] + off * shares[:, 5, :]), axis=0, keepdims=True
-    )
+    off = jnp.where(r_rs > 0, r_ws / r_rs, 0.0) - theta
+    spread = jnp.sum(spreads + r_rs * off * off, axis=0, keepdims=True)
+    energy = jnp.sum(y_ay + off * (r_ay + off * r_ar), axis=0, keepdims=True)
     ratio = spread / (theta * theta * r_r)
     energy = jnp.maximum(energy - ratio * theta * spread, LEAST_EIGENVALUE * spread * (1.0 + ratio))
     step = jnp.where(spread > 0, spread / energy, 0.0)
@@ -219,7 +231,7 @@
     out[...] = x[...] + (first + step * (1.0 + ratio)) * r[...] - (step * first) * w[...]
 
 
-def call(kernel, shapes, *operands, first=False, last=False):
+def call(kernel, shapes, *operands, first=False, last=False, aliases={}):
     place_out = jax.ShapeDtypeStruct if last else pltpu.VMEM
     outs = [place_out(shape[1:], shape[0]) for shape in shapes]
     in_specs, placed = [], []
@@ -232,6 +244,7 @@
         out_shape=outs if len(outs) > 1 else outs[0],
         in_specs=in_specs,
         out_specs=[VMEM] * len(outs) if len(outs) > 1 else VMEM,
+        input_output_aliases=aliases,
         name=kernel.__name__,
     )(*placed)
 
@@ -246,27 +259,29 @@
     across += [(j, i) for i, j in across]
     single = jnp.float32
     field, block = (single, rows, columns), (single, tile, columns)
-    square, packing = (jnp.bfloat16, 2, tile, tile), (single, tile // 2 + 8, columns)
+    square, sending = (jnp.bfloat16, 2, tile, tile), (single, 3 * tile + 8, columns)
 
     other_x = lax.ppermute(warm_start, AXES, partner)
-    local, diag, t_in, t_out, t_out_t, base, push, packed = call(
-        local_kernel, [(jnp.bfloat16, 2, rows, rows), field, square, square, square, field, block, packing],
+    local, diag, t_in, t_out_t, base, push, q_base, send = call(
+        local_kernel,
+        [(jnp.bfloat16, 2, rows, rows), field, square, square, field, block, block, sending],
         block_cols, step_tiles, mass, warm_start, source_ids, first=True,
     )
     t, q_outer, send = call(
-        start_kernel, [field, block, (single, 3 * tile + 8, columns)],
-        local, diag, t_in, base, push, packed, other_x,
+        start_kernel, [field, block, sending], local, t_in, base, q_base, other_x, send, aliases={5: 2}
     )
     got = lax.ppermute(send, AXES, across)
     other_t = lax.ppermute(t, AXES, partner)
-    q_inner = call(inner_kernel, [block], local, diag, t_in, t, other_t)
+    q_inner, t_in_t, t_out = call(
+        inner_kernel, [block, square, square], local, diag, t_in, t_out_t, t, other_t
+    )
     w_inner = call(image_kernel, [block], local, q_inner, got)
     other_w = lax.ppermute(w_inner, AXES, partner)
     r, w, moments, edge, edge_r = call(
         moment_kernel, [field, field, (single, 8, columns), block, block],
-        local, diag, t_in, t_out, t_out_t, t, q_outer, push, got, w_inner,
-    )
-    shares = call(share_kernel, [(single, devices, 8, columns)], moments, edge, edge_r, other_t, other_w)
+        local, diag, t_in_t, t_out, t_out_t, t, q_outer, push, got, w_inner,
+    )
+    shares = call(share_kernel, [(single, devices, 3, 2, columns)], moments, edge, edge_r, other_t, other_w)
     shares = lax.all_to_all(shares, AXES, 0, 0)
     return call(finish_kernel, [field], shares, warm_start, r, w, last=True)
 

time: 27.1 us -> 27.1 us (level)
  no operation moved by 1% of the time
where the time goes in v6:
time: 27.1 us; the launch traced here: 26.9 us
  blocking collectives  13.1 us (48%)
  starting transfers between devices  8.6 us (32%)
  Pallas kernels  3.99 us (15%)
  waiting for transfers between devices  1.22 us (5%)
    all_to_all x1, blocking collectives, body(): shares = lax.all_to_all(shares, AXES, 0, 0)  13.1 us
    pallas_call x7, Pallas kernels, call(): pl.pallas_call(kernel, out_shape=outs if len(outs) > 1 else outs[0], in_s...  3.99 us
    ppermute x1, starting transfers between devices, body(): other_t = lax.ppermute(t, AXES, partner)  3.89 us
    ppermute x1, starting transfers between devices, body(): other_w = lax.ppermute(w_inner, AXES, partner)  3.55 us
    ppermute x1, waiting for transfers between devices, body(): other_t = lax.ppermute(t, AXES, partner)  0.99 us
    ppermute x1, starting transfers between devices, body(): got = lax.ppermute(send, AXES, across)  0.67 us
  transfers between devices with their start and end apart: 4, of which 2 were waited for; matrix products, arithmetic and copies ran while one was open for 0% of the time, Pallas kernels for 9%

profile of v6, /device:TPU:0, one launch (start us, length us, event | category | flops | bytes accessed | tf_op | source)
XLA Modules:
  0.0 26.9 jit_solution(4143538308168143887)
XLA Ops:
  0.0 0.5 %collective-permute-start = (f32[256,128]{1,0:T(8,128)}, f32[256,128]{1,0:T(8,128)S(1)}, u32[]{:S(2)}, u32[]{:S(2)}) collective-permute-start(f32[256,128]{1,0:T(8,128)} %x.3), channel_id=1, source_target_pairs={{0,1},{1,0},{2,3},{3,2},{4,5},{5,4},{6,7},{7,6},{8,9},{9,8},{10,11... | collective-permute-start | bytes 393224 | tf_op jit(solution)/shard_map/ppermute | solution.py:264
  0.5 1.6 %local_kernel.1 = (bf16[2,256,256]{2,1,0:T(8,128)(2,1)S(1)}, f32[256,128]{1,0:T(8,128)S(1)}, bf16[2,128,128]{2,1,0:T(8,128)(2,1)S(1)}, bf16[2,128,128]{2,1,0:T(8...) custom-call(s32[2,3]{1,0:T(2,128)} %cols.1, ...), custom_call_target="tpu_custom_call" | custom-call | tf_op jit(solution)/shard_map/local_kernel/pallas_call | solution.py:242
  2.1 0.0 collective-permute-done.other_x
  2.1 0.5 %start_kernel.1 = (f32[256,128]{1,0:T(8,128)S(1)}, f32[128,128]{1,0:T(8,128)S(1)}, f32[392,128]{1,0:T(8,128)S(1)}) custom-call(bf16[2,256,256]{2,1,0:T(8,128)(2,1)S(1)} %get-tuple-element.24.local, bf16[2,128,128]{2,1,0:T(8,128)(2,1)S(1)} %get-tuple-element.26.t_in, f32[256,128]{1,0:T(8,128)S(1)} %get-tuple-element.28.base, ...), custom_call_target="tpu_custom_call", output_to_operand_aliasing={{2}: (5, {})} | custom-call | tf_op jit(solution)/shard_map/start_kernel/pallas_call | solution.py:242
  2.6 0.7 %collective-permute-start.2 = (f32[392,128]{1,0:T(8,128)S(1)}, f32[392,128]{1,0:T(8,128)S(1)}, u32[]{:S(2)}, u32[]{:S(2)}) collective-permute-start(f32[392,128]{1,0:T(8,128)S(1)} %get-tuple-element.36), channel_id=1, source_target_pairs={{1,2},{3,4},{5,6},{7,8},{9,10},{11,12},{13,14},{2,1},{4,3},{6,5},{... | collective-permute-start | bytes 602120 | tf_op jit(solution)/shard_map/ppermute | solution.py:273
  3.3 3.9 %collective-permute-start.1 = (f32[256,128]{1,0:T(8,128)S(1)}, f32[256,128]{1,0:T(8,128)S(1)}, u32[]{:S(2)}, u32[]{:S(2)}) collective-permute-start(f32[256,128]{1,0:T(8,128)S(1)} %get-tuple-element.31.t), channel_id=1, source_target_pairs={{0,1},{1,0},{2,3},{3,2},{4,5},{5,4},{6,7},{7,6},{8,9},{9,8},{10,11... | collective-permute-start | bytes 393224 | tf_op jit(solution)/shard_map/ppermute | solution.py:274
  7.2 1.0 %collective-permute-done.1.other_t = f32[256,128]{1,0:T(8,128)S(1)} collective-permute-done((f32[256,128]{1,0:T(8,128)S(1)}, f32[256,128]{1,0:T(8,128)S(1)}, u32[]{:S(2)}, u32[]{:S(2)}) %collective-permute-start.1) | collective-permute-done | bytes 131104 | tf_op jit(solution)/shard_map/ppermute | solution.py:274
  8.2 0.2 inner_kernel.1
  8.4 0.0 collective-permute-done.2.got
  8.4 0.2 image_kernel.1.w_inner
  8.6 3.5 %collective-permute-start.3 = (f32[128,128]{1,0:T(8,128)S(1)}, f32[128,128]{1,0:T(8,128)S(1)}, u32[]{:S(2)}, u32[]{:S(2)}) collective-permute-start(f32[128,128]{1,0:T(8,128)S(1)} %image_kernel.1.w_inner), channel_id=1, source_target_pairs={{0,1},{1,0},{2,3},{3,2},{4,5},{5,4},{6,7},{7,6},{8,9},{9,8},{10,11... | collective-permute-start | bytes 196616 | tf_op jit(solution)/shard_map/ppermute | solution.py:279
  12.2 0.7 %moment_kernel.1 = (f32[256,128]{1,0:T(8,128)S(1)}, f32[256,128]{1,0:T(8,128)S(1)}, f32[8,128]{1,0:T(8,128)S(1)}, f32[128,128]{1,0:T(8,128)S(1)}, f32[128,128]{1,0:T(8,128)S(1)}) custom-call(bf16[2,256,256]{2,1,0:T(8,128)(2,1)S(1)} %get-tuple-element.24.local, f32[256,128]{1,0:T(8,128)S(1)} %get-tuple-element.25.diag, ...), custom_call_target="tpu_custom_call" | custom-call | tf_op jit(solution)/shard_map/moment_kernel/pallas_call | solution.py:242
  12.8 0.2 collective-permute-done.3.other_w
  13.1 0.0 copy-start
  13.1 13.1 %all_to_all.5.shares = f32[16,3,2,128]{3,2,1,0:T(2,128)S(1)} all-to-all(f32[16,3,2,128]{3,2,1,0:T(2,128)S(1)} %share_kernel.1), channel_id=1, replica_groups=mesh['groups'=2,'patch'=8,'sub'=2] {'patch','sub'}, dimensions={0} | all-to-all | bytes 98304 | tf_op jit(solution)/shard_map/all_to_all | solution.py:285
  26.2 0.0 copy-done
  26.2 0.8 %finish_kernel.1 = f32[256,128]{1,0:T(8,128)} custom-call(f32[16,3,2,128]{3,2,1,0:T(2,128)S(1)} %all_to_all.5.shares, f32[256,128]{1,0:T(8,128)S(1)} %copy-done, f32[256,128]{1,0:T(8,128)S(1)} %get-tuple-element.41.r, f32[256,128]{1,0:T(8,128)S(1)} %get-tuple-element.42.w), custom_call_target="tpu_custom_call" | custom-call | tf_op jit(solution)/shard_map/finish_kernel/pallas_call | solution.py:242
  (1 shorter events, 0.0 us)
Async XLA Ops:
  0.0 2.1 %collective-permute-start = (f32[256,128]{1,0:T(8,128)}, f32[256,128]{1,0:T(8,128)S(1)}, u32[]{:S(2)}, u32[]{:S(2)}) collective-permute-start(f32[256,128]{1,0:T(8,128)} %x.3), channel_id=1, source_target_pairs={{0,1},{1,0},{2,3},{3,2},{4,5},{5,4},{6,7},{7,6},{8,9},{9,8},{10,11... | collective-permute-start | bytes 393224 | tf_op jit(solution)/shard_map/ppermute | solution.py:264
  2.6 5.8 %collective-permute-start.2 = (f32[392,128]{1,0:T(8,128)S(1)}, f32[392,128]{1,0:T(8,128)S(1)}, u32[]{:S(2)}, u32[]{:S(2)}) collective-permute-start(f32[392,128]{1,0:T(8,128)S(1)} %get-tuple-element.36), channel_id=1, source_target_pairs={{1,2},{3,4},{5,6},{7,8},{9,10},{11,12},{13,14},{2,1},{4,3},{6,5},{... | collective-permute-start | bytes 602120 | tf_op jit(solution)/shard_map/ppermute | solution.py:273
  3.3 4.9 %collective-permute-start.1 = (f32[256,128]{1,0:T(8,128)S(1)}, f32[256,128]{1,0:T(8,128)S(1)}, u32[]{:S(2)}, u32[]{:S(2)}) collective-permute-start(f32[256,128]{1,0:T(8,128)S(1)} %get-tuple-element.31.t), channel_id=1, source_target_pairs={{0,1},{1,0},{2,3},{3,2},{4,5},{5,4},{6,7},{7,6},{8,9},{9,8},{10,11... | collective-permute-start | bytes 393224 | tf_op jit(solution)/shard_map/ppermute | solution.py:274
  8.6 4.5 %collective-permute-start.3 = (f32[128,128]{1,0:T(8,128)S(1)}, f32[128,128]{1,0:T(8,128)S(1)}, u32[]{:S(2)}, u32[]{:S(2)}) collective-permute-start(f32[128,128]{1,0:T(8,128)S(1)} %image_kernel.1.w_inner), channel_id=1, source_target_pairs={{0,1},{1,0},{2,3},{3,2},{4,5},{5,4},{6,7},{7,6},{8,9},{9,8},{10,11... | collective-permute-start | bytes 196616 | tf_op jit(solution)/shard_map/ppermute | solution.py:279
  13.1 13.1 %copy-start = (f32[256,128]{1,0:T(8,128)S(1)}, f32[256,128]{1,0:T(8,128)}, u32[]{:S(2)}) copy-start(f32[256,128]{1,0:T(8,128)} %x.3) | copy-start | bytes 393220

commit v7 on v6

--- a/solution.py
+++ b/solution.py
@@ -48,7 +48,7 @@
 
 
 def local_kernel(
-    cols, tiles, mass, x, sources, local, diag, t_in, t_out_t, base, push, q_base, send
+    cols, tiles, mass, x, sources, local, diag, t_in, t_out_t, base, push, send
 ):
     tile = tiles.shape[-1]
     half = tile // 2
@@ -87,7 +87,6 @@
     rhs = jnp.where(vertices == sources[...][None, :], 1.0, 0.0)
     base[...] = rhs - diag[...] * x[...] - dot(local, x[...])
     push[...] = dot(t_out_t, x[outer, :])
-    q_base[...] = diag[outer, :] * base[outer, :] + dot(part(local, outer), base[...])
     send[0:tile, :] = base[outer, :]
     send[tile : 2 * tile, :] = push[...]
     own = jnp.where(side == 0, owns[0], owns[1])
@@ -116,38 +115,32 @@
     return pl.ds(pl.multiple_of(side * tile, tile), tile)
 
 
-def inner_columns(tile):
-    side = lax.rem(place(), 2)
-    return pl.ds(pl.multiple_of((1 - side) * tile, tile), tile)
-
-
 def part(pair, *index):
     return pair[(0, *index)], pair[(1, *index)]
 
 
-def start_kernel(local, t_in, base, q_base, other_x, send_in, t, q_outer, send):
+def start_kernel(local, diag, t_in, base, other_x, send_in, t, q_outer, send):
     tile = t_in.shape[-1]
     half = tile // 2
     side = lax.rem(place(), 2)
     outer, inner = outer_block(tile)
-    pull = dot(t_in, other_x[outer, :])
-    q = q_base[...] + dot(part(local, outer, inner_columns(tile)), pull)
+    t[outer, :] = base[outer, :]
+    t[inner, :] = base[inner, :] + dot(t_in, other_x[outer, :])
+    q = diag[outer, :] * base[outer, :] + dot(part(local, outer), t[...])
     turned = jnp.where(side == 0, flip(q), q)
     first_half = index_of((half, tile), 1) < half
     send[2 * tile : 2 * tile + half, :] = jnp.where(first_half, turned[:half], flip(turned[half:]))
     q_outer[...] = q
-    t[outer, :] = base[outer, :]
-    t[inner, :] = base[inner, :] + pull
-
-
-def inner_kernel(local, diag, t_in, t_out_t, t, other_t, q_inner, t_in_t, t_out):
+
+
+def inner_kernel(local, diag, t_in, t_out_t, t, other_t, q_inner, pull_in, t_in_t, t_out):
     outer, inner = outer_block(t_in.shape[-1])
     for half in range(2):
         t_in_t[half] = t_in[half].T
         t_out[half] = t_out_t[half].T
-    q_inner[...] = (
-        diag[inner, :] * t[inner, :] + dot(part(local, inner), t[...]) - dot(t_in, other_t[outer, :])
-    )
+    pull = dot(t_in, other_t[outer, :])
+    pull_in[...] = pull
+    q_inner[...] = diag[inner, :] * t[inner, :] + dot(part(local, inner), t[...]) - pull
 
 
 def image_kernel(local, q_inner, got, w_inner):
@@ -157,7 +150,7 @@
 
 
 def moment_kernel(
-    local, diag, t_in_t, t_out, t_out_t, t, q_outer, push, got, w_inner, r, w, moments, edge, edge_r
+    local, diag, t_in_t, t_out, t_out_t, t, q_outer, pull_in, push, got, w_inner, r, w, moments, edge, edge_r
 ):
     tile = t_out.shape[-1]
     half = tile // 2
@@ -200,6 +193,9 @@
     r_ay = total(r_now * a_y + y * w_now) + total(y_outer * pull_r)
     r_ay -= weight * total(r_outer * pull_y + y_outer * pull_r)
     r_ar = r_w + (1.0 - weight) * total(r_outer * pull_r)
+    surplus = jnp.where(side == 0, -1.0, 1.0)
+    r_ay += surplus * total((w_inner[...] - shift * t[inner, :]) * pull_in[...])
+    r_ar += surplus * total(t[inner, :] * pull_in[...])
     moments[...] = jnp.concatenate([r_r, r_w, total(y * y), y_ay, r_ay, r_ar, shift, shift], axis=0)
     edge[...] = dot(t_in_t, w_inner[...] - shift * r[inner, :])
     edge_r[...] = dot(t_in_t, r[inner, :])
@@ -207,11 +203,12 @@
 
 def share_kernel(moments, edge, edge_r, other_t, other_w, out):
     outer, _ = outer_block(edge.shape[0])
+    weight = jnp.where(lax.rem(place(), 2) == 0, 2.0, 0.0)
     y_there = other_w[...] - moments[6:7, :] * other_t[outer, :]
     y_ay = jnp.sum(edge[...] * y_there, axis=0, keepdims=True)
     r_ay = jnp.sum(edge_r[...] * y_there, axis=0, keepdims=True)
     row = index_of(moments.shape, 0)
-    total = moments[...] - jnp.where(row == 3, y_ay, 0.0) - jnp.where(row == 4, r_ay, 0.0)
+    total = moments[...] - weight * (jnp.where(row == 3, y_ay, 0.0) + jnp.where(row == 4, r_ay, 0.0))
     for pair in range(out.shape[1]):
         out[:, pair] = jnp.broadcast_to(total[None, 2 * pair : 2 * pair + 2], out[:, pair].shape)
 
@@ -262,24 +259,24 @@
     square, sending = (jnp.bfloat16, 2, tile, tile), (single, 3 * tile + 8, columns)
 
     other_x = lax.ppermute(warm_start, AXES, partner)
-    local, diag, t_in, t_out_t, base, push, q_base, send = call(
+    local, diag, t_in, t_out_t, base, push, send = call(
         local_kernel,
-        [(jnp.bfloat16, 2, rows, rows), field, square, square, field, block, block, sending],
+        [(jnp.bfloat16, 2, rows, rows), field, square, square, field, block, sending],
         block_cols, step_tiles, mass, warm_start, source_ids, first=True,
     )
     t, q_outer, send = call(
-        start_kernel, [field, block, sending], local, t_in, base, q_base, other_x, send, aliases={5: 2}
+        start_kernel, [field, block, sending], local, diag, t_in, base, other_x, send, aliases={5: 2}
     )
     got = lax.ppermute(send, AXES, across)
     other_t = lax.ppermute(t, AXES, partner)
-    q_inner, t_in_t, t_out = call(
-        inner_kernel, [block, square, square], local, diag, t_in, t_out_t, t, other_t
+    q_inner, pull_in, t_in_t, t_out = call(
+        inner_kernel, [block, block, square, square], local, diag, t_in, t_out_t, t, other_t
     )
     w_inner = call(image_kernel, [block], local, q_inner, got)
-    other_w = lax.ppermute(w_inner, AXES, partner)
+    other_w = lax.ppermute(w_inner, AXES, partner[1::2])
     r, w, moments, edge, edge_r = call(
         moment_kernel, [field, field, (single, 8, columns), block, block],
-        local, diag, t_in_t, t_out, t_out_t, t, q_outer, push, got, w_inner,
+        local, diag, t_in_t, t_out, t_out_t, t, q_outer, pull_in, push, got, w_inner,
     )
     shares = call(share_kernel, [(single, devices, 3, 2, columns)], moments, edge, edge_r, other_t, other_w)
     shares = lax.all_to_all(shares, AXES, 0, 0)

time: 27.1 us -> 28.7 us (1.059)
  waiting for transfers between devices: 1.22 us -> 4.52 us
  starting transfers between devices: 8.6 us -> 6.45 us
  blocking collectives: 13.1 us -> 13.6 us
    ppermute x1, waiting for transfers between devices: 0.23 us -> 3.53 us  [body(): other_w = lax.ppermute(w_inner, AXES, partner[1::2])]
    ppermute x1, starting transfers between devices: 3.55 us -> 1.29 us  [body(): other_w = lax.ppermute(w_inner, AXES, partner[1::2])]
    all_to_all x1, blocking collectives: 13.1 us -> 13.6 us  [body(): shares = lax.all_to_all(shares, AXES, 0, 0)]
  transfers between devices with their start and end apart: 4 -> 4, of which waited for: 2 -> 2; matrix products, arithmetic and copies ran while one was open for 0% -> 0% of each run, Pallas kernels for 9% -> 8%
where the time goes in v7:
time: 28.7 us; the launch traced here: 28.5 us
  blocking collectives  13.6 us (47%)
  starting transfers between devices  6.45 us (22%)
  waiting for transfers between devices  4.52 us (16%)
  Pallas kernels  3.87 us (13%)
    all_to_all x1, blocking collectives, body(): shares = lax.all_to_all(shares, AXES, 0, 0)  13.6 us
    ppermute x1, starting transfers between devices, body(): other_t = lax.ppermute(t, AXES, partner)  3.99 us
    pallas_call x7, Pallas kernels, call(): pl.pallas_call(kernel, out_shape=outs if len(outs) > 1 else outs[0], in_s...  3.87 us
    ppermute x1, waiting for transfers between devices, body(): other_w = lax.ppermute(w_inner, AXES, partner[1::2])  3.53 us
    ppermute x1, starting transfers between devices, body(): other_w = lax.ppermute(w_inner, AXES, partner[1::2])  1.29 us
    ppermute x1, waiting for transfers between devices, body(): other_t = lax.ppermute(t, AXES, partner)  0.99 us
    ppermute x1, starting transfers between devices, body(): got = lax.ppermute(send, AXES, across)  0.67 us
  transfers between devices with their start and end apart: 4, of which 2 were waited for; matrix products, arithmetic and copies ran while one was open for 0% of the time, Pallas kernels for 8%

profile of v7, /device:TPU:0, one launch (start us, length us, event | category | flops | bytes accessed | tf_op | source)
XLA Modules:
  0.0 28.5 jit_solution(2684538767223919720)
XLA Ops:
  0.0 0.5 %collective-permute-start = (f32[256,128]{1,0:T(8,128)}, f32[256,128]{1,0:T(8,128)S(1)}, u32[]{:S(2)}, u32[]{:S(2)}) collective-permute-start(f32[256,128]{1,0:T(8,128)} %x.3), channel_id=1, source_target_pairs={{0,1},{1,0},{2,3},{3,2},{4,5},{5,4},{6,7},{7,6},{8,9},{9,8},{10,11... | collective-permute-start | bytes 393224 | tf_op jit(solution)/shard_map/ppermute | solution.py:261
  0.5 1.4 %local_kernel.1 = (bf16[2,256,256]{2,1,0:T(8,128)(2,1)S(1)}, f32[256,128]{1,0:T(8,128)S(1)}, bf16[2,128,128]{2,1,0:T(8,128)(2,1)S(1)}, bf16[2,128,128]{2,1,0:T(8...) custom-call(s32[2,3]{1,0:T(2,128)} %cols.1, f32[2,3,128,128]{3,2,1,0:T(8,128)} %tiles.1, ...), custom_call_target="tpu_custom_call" | custom-call | tf_op jit(solution)/shard_map/local_kernel/pallas_call | solution.py:239
  1.9 0.0 collective-permute-done.other_x
  1.9 0.6 %start_kernel.1 = (f32[256,128]{1,0:T(8,128)S(1)}, f32[128,128]{1,0:T(8,128)S(1)}, f32[392,128]{1,0:T(8,128)S(1)}) custom-call(bf16[2,256,256]{2,1,0:T(8,128)(2,1)S(1)} %get-tuple-element.24.local, f32[256,128]{1,0:T(8,128)S(1)} %get-tuple-element.25.diag, bf16[2,128,128]{2,1,0:T(8,128)(2,1)S(1)} %get-tuple-element.26.t_in, ...), custom_call_target="tpu_custom_call", output_to_operand_aliasing={{2}: (5, {})} | custom-call | tf_op jit(solution)/shard_map/start_kernel/pallas_call | solution.py:239
  2.5 0.7 %collective-permute-start.2 = (f32[392,128]{1,0:T(8,128)S(1)}, f32[392,128]{1,0:T(8,128)S(1)}, u32[]{:S(2)}, u32[]{:S(2)}) collective-permute-start(f32[392,128]{1,0:T(8,128)S(1)} %get-tuple-element.36), channel_id=1, source_target_pairs={{1,2},{3,4},{5,6},{7,8},{9,10},{11,12},{13,14},{2,1},{4,3},{6,5},{... | collective-permute-start | bytes 602120 | tf_op jit(solution)/shard_map/ppermute | solution.py:270
  3.2 4.0 %collective-permute-start.1 = (f32[256,128]{1,0:T(8,128)S(1)}, f32[256,128]{1,0:T(8,128)S(1)}, u32[]{:S(2)}, u32[]{:S(2)}) collective-permute-start(f32[256,128]{1,0:T(8,128)S(1)} %get-tuple-element.30.t), channel_id=1, source_target_pairs={{0,1},{1,0},{2,3},{3,2},{4,5},{5,4},{6,7},{7,6},{8,9},{9,8},{10,11... | collective-permute-start | bytes 393224 | tf_op jit(solution)/shard_map/ppermute | solution.py:271
  7.2 1.0 %collective-permute-done.1.other_t = f32[256,128]{1,0:T(8,128)S(1)} collective-permute-done((f32[256,128]{1,0:T(8,128)S(1)}, f32[256,128]{1,0:T(8,128)S(1)}, u32[]{:S(2)}, u32[]{:S(2)}) %collective-permute-start.1) | collective-permute-done | bytes 131104 | tf_op jit(solution)/shard_map/ppermute | solution.py:271
  8.2 0.2 inner_kernel.1
  8.4 0.0 collective-permute-done.2.got
  8.4 0.2 image_kernel.1.w_inner
  8.6 1.3 %collective-permute-start.3 = (f32[128,128]{1,0:T(8,128)S(1)}, f32[128,128]{1,0:T(8,128)S(1)}, u32[]{:S(2)}, u32[]{:S(2)}) collective-permute-start(f32[128,128]{1,0:T(8,128)S(1)} %image_kernel.1.w_inner), channel_id=1, source_target_pairs={{1,0},{3,2},{5,4},{7,6},{9,8},{11,10},{13,12},{15,14},{17,16},{19,... | collective-permute-start | bytes 196616 | tf_op jit(solution)/shard_map/ppermute | solution.py:276
  9.9 0.7 %moment_kernel.1 = (f32[256,128]{1,0:T(8,128)S(1)}, f32[256,128]{1,0:T(8,128)S(1)}, f32[8,128]{1,0:T(8,128)S(1)}, f32[128,128]{1,0:T(8,128)S(1)}, f32[128,128]{1,0:T(8,128)S(1)}) custom-call(bf16[2,256,256]{2,1,0:T(8,128)(2,1)S(1)} %get-tuple-element.24.local, f32[256,128]{1,0:T(8,128)S(1)} %get-tuple-element.25.diag, ...), custom_call_target="tpu_custom_call" | custom-call | tf_op jit(solution)/shard_map/moment_kernel/pallas_call | solution.py:239
  10.6 3.5 %collective-permute-done.3.other_w = f32[128,128]{1,0:T(8,128)S(1)} collective-permute-done((f32[128,128]{1,0:T(8,128)S(1)}, f32[128,128]{1,0:T(8,128)S(1)}, u32[]{:S(2)}, u32[]{:S(2)}) %collective-permute-start.3) | collective-permute-done | bytes 65568 | tf_op jit(solution)/shard_map/ppermute | solution.py:276
  14.1 0.0 copy-start
  14.1 13.6 %all_to_all.5.shares = f32[16,3,2,128]{3,2,1,0:T(2,128)S(1)} all-to-all(f32[16,3,2,128]{3,2,1,0:T(2,128)S(1)} %share_kernel.1), channel_id=1, replica_groups=mesh['groups'=2,'patch'=8,'sub'=2] {'patch','sub'}, dimensions={0} | all-to-all | bytes 98304 | tf_op jit(solution)/shard_map/all_to_all | solution.py:282
  27.7 0.0 copy-done
  27.7 0.8 %finish_kernel.1 = f32[256,128]{1,0:T(8,128)} custom-call(f32[16,3,2,128]{3,2,1,0:T(2,128)S(1)} %all_to_all.5.shares, f32[256,128]{1,0:T(8,128)S(1)} %copy-done, f32[256,128]{1,0:T(8,128)S(1)} %get-tuple-element.41.r, f32[256,128]{1,0:T(8,128)S(1)} %get-tuple-element.42.w), custom_call_target="tpu_custom_call" | custom-call | tf_op jit(solution)/shard_map/finish_kernel/pallas_call | solution.py:239
  (1 shorter events, 0.0 us)
Async XLA Ops:
  0.0 1.9 %collective-permute-start = (f32[256,128]{1,0:T(8,128)}, f32[256,128]{1,0:T(8,128)S(1)}, u32[]{:S(2)}, u32[]{:S(2)}) collective-permute-start(f32[256,128]{1,0:T(8,128)} %x.3), channel_id=1, source_target_pairs={{0,1},{1,0},{2,3},{3,2},{4,5},{5,4},{6,7},{7,6},{8,9},{9,8},{10,11... | collective-permute-start | bytes 393224 | tf_op jit(solution)/shard_map/ppermute | solution.py:261
  2.5 5.9 %collective-permute-start.2 = (f32[392,128]{1,0:T(8,128)S(1)}, f32[392,128]{1,0:T(8,128)S(1)}, u32[]{:S(2)}, u32[]{:S(2)}) collective-permute-start(f32[392,128]{1,0:T(8,128)S(1)} %get-tuple-element.36), channel_id=1, source_target_pairs={{1,2},{3,4},{5,6},{7,8},{9,10},{11,12},{13,14},{2,1},{4,3},{6,5},{... | collective-permute-start | bytes 602120 | tf_op jit(solution)/shard_map/ppermute | solution.py:270
  3.2 5.0 %collective-permute-start.1 = (f32[256,128]{1,0:T(8,128)S(1)}, f32[256,128]{1,0:T(8,128)S(1)}, u32[]{:S(2)}, u32[]{:S(2)}) collective-permute-start(f32[256,128]{1,0:T(8,128)S(1)} %get-tuple-element.30.t), channel_id=1, source_target_pairs={{0,1},{1,0},{2,3},{3,2},{4,5},{5,4},{6,7},{7,6},{8,9},{9,8},{10,11... | collective-permute-start | bytes 393224 | tf_op jit(solution)/shard_map/ppermute | solution.py:271
  8.6 5.5 %collective-permute-start.3 = (f32[128,128]{1,0:T(8,128)S(1)}, f32[128,128]{1,0:T(8,128)S(1)}, u32[]{:S(2)}, u32[]{:S(2)}) collective-permute-start(f32[128,128]{1,0:T(8,128)S(1)} %image_kernel.1.w_inner), channel_id=1, source_target_pairs={{1,0},{3,2},{5,4},{7,6},{9,8},{11,10},{13,12},{15,14},{17,16},{19,... | collective-permute-start | bytes 196616 | tf_op jit(solution)/shard_map/ppermute | solution.py:276
  14.1 13.6 %copy-start = (f32[256,128]{1,0:T(8,128)S(1)}, f32[256,128]{1,0:T(8,128)}, u32[]{:S(2)}) copy-start(f32[256,128]{1,0:T(8,128)} %x.3) | copy-start | bytes 393220

commit v8 on v6

--- a/solution.py
+++ b/solution.py
@@ -48,7 +48,7 @@
 
 
 def local_kernel(
-    cols, tiles, mass, x, sources, local, diag, t_in, t_out_t, base, push, q_base, send
+    cols, tiles, mass, x, sources, local, diag, t_in, t_out_t, base, push, send
 ):
     tile = tiles.shape[-1]
     half = tile // 2
@@ -87,7 +87,6 @@
     rhs = jnp.where(vertices == sources[...][None, :], 1.0, 0.0)
     base[...] = rhs - diag[...] * x[...] - dot(local, x[...])
     push[...] = dot(t_out_t, x[outer, :])
-    q_base[...] = diag[outer, :] * base[outer, :] + dot(part(local, outer), base[...])
     send[0:tile, :] = base[outer, :]
     send[tile : 2 * tile, :] = push[...]
     own = jnp.where(side == 0, owns[0], owns[1])
@@ -116,28 +115,22 @@
     return pl.ds(pl.multiple_of(side * tile, tile), tile)
 
 
-def inner_columns(tile):
-    side = lax.rem(place(), 2)
-    return pl.ds(pl.multiple_of((1 - side) * tile, tile), tile)
-
-
 def part(pair, *index):
     return pair[(0, *index)], pair[(1, *index)]
 
 
-def start_kernel(local, t_in, base, q_base, other_x, send_in, t, q_outer, send):
+def start_kernel(local, diag, t_in, base, other_x, send_in, t, q_outer, send):
     tile = t_in.shape[-1]
     half = tile // 2
     side = lax.rem(place(), 2)
     outer, inner = outer_block(tile)
-    pull = dot(t_in, other_x[outer, :])
-    q = q_base[...] + dot(part(local, outer, inner_columns(tile)), pull)
+    t[outer, :] = base[outer, :]
+    t[inner, :] = base[inner, :] + dot(t_in, other_x[outer, :])
+    q = diag[outer, :] * base[outer, :] + dot(part(local, outer), t[...])
     turned = jnp.where(side == 0, flip(q), q)
     first_half = index_of((half, tile), 1) < half
     send[2 * tile : 2 * tile + half, :] = jnp.where(first_half, turned[:half], flip(turned[half:]))
     q_outer[...] = q
-    t[outer, :] = base[outer, :]
-    t[inner, :] = base[inner, :] + pull
 
 
 def inner_kernel(local, diag, t_in, t_out_t, t, other_t, q_inner, t_in_t, t_out):
@@ -256,19 +249,19 @@
     devices = lax.axis_size("patch") * lax.axis_size("sub")
     partner = [(i, i ^ 1) for i in range(devices)]
     across = [(i, i + 1) for i in range(1, devices - 1, 2)]
-    across += [(j, i) for i, j in across]
+    across += [(j, i) for i, j in across] + [(0, 0), (devices - 1, devices - 1)]
     single = jnp.float32
     field, block = (single, rows, columns), (single, tile, columns)
     square, sending = (jnp.bfloat16, 2, tile, tile), (single, 3 * tile + 8, columns)
 
     other_x = lax.ppermute(warm_start, AXES, partner)
-    local, diag, t_in, t_out_t, base, push, q_base, send = call(
+    local, diag, t_in, t_out_t, base, push, send = call(
         local_kernel,
-        [(jnp.bfloat16, 2, rows, rows), field, square, square, field, block, block, sending],
+        [(jnp.bfloat16, 2, rows, rows), field, square, square, field, block, sending],
         block_cols, step_tiles, mass, warm_start, source_ids, first=True,
     )
     t, q_outer, send = call(
-        start_kernel, [field, block, sending], local, t_in, base, q_base, other_x, send, aliases={5: 2}
+        start_kernel, [field, block, sending], local, diag, t_in, base, other_x, send, aliases={5: 2}
     )
     got = lax.ppermute(send, AXES, across)
     other_t = lax.ppermute(t, AXES, partner)

time: 27.1 us -> 27 us (level)
  no operation moved by 1% of the time
where the time goes in v8:
time: 27 us; the launch traced here: 26.8 us
  blocking collectives  13 us (48%)
  starting transfers between devices  8.7 us (32%)
  Pallas kernels  3.86 us (14%)
  waiting for transfers between devices  1.22 us (5%)
    all_to_all x1, blocking collectives, body(): shares = lax.all_to_all(shares, AXES, 0, 0)  13 us
    ppermute x1, starting transfers between devices, body(): other_t = lax.ppermute(t, AXES, partner)  3.99 us
    pallas_call x7, Pallas kernels, call(): pl.pallas_call(kernel, out_shape=outs if len(outs) > 1 else outs[0], in_s...  3.86 us
    ppermute x1, starting transfers between devices, body(): other_w = lax.ppermute(w_inner, AXES, partner)  3.54 us
    ppermute x1, waiting for transfers between devices, body(): other_t = lax.ppermute(t, AXES, partner)  0.99 us
    ppermute x1, starting transfers between devices, body(): got = lax.ppermute(send, AXES, across)  0.67 us
  transfers between devices with their start and end apart: 4, of which 2 were waited for; matrix products, arithmetic and copies ran while one was open for 0% of the time, Pallas kernels for 9%

profile of v8, /device:TPU:0, one launch (start us, length us, event | category | flops | bytes accessed | tf_op | source)
XLA Modules:
  0.0 26.8 jit_solution(6783260883193395295)
XLA Ops:
  0.0 0.5 %collective-permute-start = (f32[256,128]{1,0:T(8,128)}, f32[256,128]{1,0:T(8,128)S(1)}, u32[]{:S(2)}, u32[]{:S(2)}) collective-permute-start(f32[256,128]{1,0:T(8,128)} %x.3), channel_id=1, source_target_pairs={{0,1},{1,0},{2,3},{3,2},{4,5},{5,4},{6,7},{7,6},{8,9},{9,8},{10,11... | collective-permute-start | bytes 393224 | tf_op jit(solution)/shard_map/ppermute | solution.py:257
  0.5 1.4 %local_kernel.1 = (bf16[2,256,256]{2,1,0:T(8,128)(2,1)S(1)}, f32[256,128]{1,0:T(8,128)S(1)}, bf16[2,128,128]{2,1,0:T(8,128)(2,1)S(1)}, bf16[2,128,128]{2,1,0:T(8...) custom-call(s32[2,3]{1,0:T(2,128)} %cols.1, f32[2,3,128,128]{3,2,1,0:T(8,128)} %tiles.1, ...), custom_call_target="tpu_custom_call" | custom-call | tf_op jit(solution)/shard_map/local_kernel/pallas_call | solution.py:235
  1.9 0.0 collective-permute-done.other_x
  1.9 0.6 %start_kernel.1 = (f32[256,128]{1,0:T(8,128)S(1)}, f32[128,128]{1,0:T(8,128)S(1)}, f32[392,128]{1,0:T(8,128)S(1)}) custom-call(bf16[2,256,256]{2,1,0:T(8,128)(2,1)S(1)} %get-tuple-element.23.local, f32[256,128]{1,0:T(8,128)S(1)} %get-tuple-element.24.diag, bf16[2,128,128]{2,1,0:T(8,128)(2,1)S(1)} %get-tuple-element.25.t_in, ...), custom_call_target="tpu_custom_call", output_to_operand_aliasing={{2}: (5, {})} | custom-call | tf_op jit(solution)/shard_map/start_kernel/pallas_call | solution.py:235
  2.5 0.7 %collective-permute-start.2 = (f32[392,128]{1,0:T(8,128)S(1)}, f32[392,128]{1,0:T(8,128)S(1)}, u32[]{:S(2)}, u32[]{:S(2)}) collective-permute-start(f32[392,128]{1,0:T(8,128)S(1)} %get-tuple-element.34), channel_id=1, source_target_pairs={{1,2},{3,4},{5,6},{7,8},{9,10},{11,12},{13,14},{2,1},{4,3},{6,5},{... | collective-permute-start | bytes 602120 | tf_op jit(solution)/shard_map/ppermute | solution.py:266
  3.2 4.0 %collective-permute-start.1 = (f32[256,128]{1,0:T(8,128)S(1)}, f32[256,128]{1,0:T(8,128)S(1)}, u32[]{:S(2)}, u32[]{:S(2)}) collective-permute-start(f32[256,128]{1,0:T(8,128)S(1)} %get-tuple-element.29.t), channel_id=1, source_target_pairs={{0,1},{1,0},{2,3},{3,2},{4,5},{5,4},{6,7},{7,6},{8,9},{9,8},{10,11... | collective-permute-start | bytes 393224 | tf_op jit(solution)/shard_map/ppermute | solution.py:267
  7.2 1.0 %collective-permute-done.1.other_t = f32[256,128]{1,0:T(8,128)S(1)} collective-permute-done((f32[256,128]{1,0:T(8,128)S(1)}, f32[256,128]{1,0:T(8,128)S(1)}, u32[]{:S(2)}, u32[]{:S(2)}) %collective-permute-start.1) | collective-permute-done | bytes 131104 | tf_op jit(solution)/shard_map/ppermute | solution.py:267
  8.2 0.2 inner_kernel.1
  8.4 0.0 collective-permute-done.2.got
  8.4 0.2 image_kernel.1.w_inner
  8.6 3.5 %collective-permute-start.3 = (f32[128,128]{1,0:T(8,128)S(1)}, f32[128,128]{1,0:T(8,128)S(1)}, u32[]{:S(2)}, u32[]{:S(2)}) collective-permute-start(f32[128,128]{1,0:T(8,128)S(1)} %image_kernel.1.w_inner), channel_id=1, source_target_pairs={{0,1},{1,0},{2,3},{3,2},{4,5},{5,4},{6,7},{7,6},{8,9},{9,8},{10,11... | collective-permute-start | bytes 196616 | tf_op jit(solution)/shard_map/ppermute | solution.py:272
  12.1 0.7 %moment_kernel.1 = (f32[256,128]{1,0:T(8,128)S(1)}, f32[256,128]{1,0:T(8,128)S(1)}, f32[8,128]{1,0:T(8,128)S(1)}, f32[128,128]{1,0:T(8,128)S(1)}, f32[128,128]{1,0:T(8,128)S(1)}) custom-call(bf16[2,256,256]{2,1,0:T(8,128)(2,1)S(1)} %get-tuple-element.23.local, f32[256,128]{1,0:T(8,128)S(1)} %get-tuple-element.24.diag, ...), custom_call_target="tpu_custom_call" | custom-call | tf_op jit(solution)/shard_map/moment_kernel/pallas_call | solution.py:235
  12.8 0.2 collective-permute-done.3.other_w
  13.0 0.0 copy-start
  13.1 13.0 %all_to_all.5.shares = f32[16,3,2,128]{3,2,1,0:T(2,128)S(1)} all-to-all(f32[16,3,2,128]{3,2,1,0:T(2,128)S(1)} %share_kernel.1), channel_id=1, replica_groups=mesh['groups'=2,'patch'=8,'sub'=2] {'patch','sub'}, dimensions={0} | all-to-all | bytes 98304 | tf_op jit(solution)/shard_map/all_to_all | solution.py:278
  26.0 0.0 copy-done
  26.0 0.8 %finish_kernel.1 = f32[256,128]{1,0:T(8,128)} custom-call(f32[16,3,2,128]{3,2,1,0:T(2,128)S(1)} %all_to_all.5.shares, f32[256,128]{1,0:T(8,128)S(1)} %copy-done, f32[256,128]{1,0:T(8,128)S(1)} %get-tuple-element.39.r, f32[256,128]{1,0:T(8,128)S(1)} %get-tuple-element.40.w), custom_call_target="tpu_custom_call" | custom-call | tf_op jit(solution)/shard_map/finish_kernel/pallas_call | solution.py:235
  (1 shorter events, 0.0 us)
Async XLA Ops:
  0.0 1.9 %collective-permute-start = (f32[256,128]{1,0:T(8,128)}, f32[256,128]{1,0:T(8,128)S(1)}, u32[]{:S(2)}, u32[]{:S(2)}) collective-permute-start(f32[256,128]{1,0:T(8,128)} %x.3), channel_id=1, source_target_pairs={{0,1},{1,0},{2,3},{3,2},{4,5},{5,4},{6,7},{7,6},{8,9},{9,8},{10,11... | collective-permute-start | bytes 393224 | tf_op jit(solution)/shard_map/ppermute | solution.py:257
  2.5 5.9 %collective-permute-start.2 = (f32[392,128]{1,0:T(8,128)S(1)}, f32[392,128]{1,0:T(8,128)S(1)}, u32[]{:S(2)}, u32[]{:S(2)}) collective-permute-start(f32[392,128]{1,0:T(8,128)S(1)} %get-tuple-element.34), channel_id=1, source_target_pairs={{1,2},{3,4},{5,6},{7,8},{9,10},{11,12},{13,14},{2,1},{4,3},{6,5},{... | collective-permute-start | bytes 602120 | tf_op jit(solution)/shard_map/ppermute | solution.py:266
  3.2 5.0 %collective-permute-start.1 = (f32[256,128]{1,0:T(8,128)S(1)}, f32[256,128]{1,0:T(8,128)S(1)}, u32[]{:S(2)}, u32[]{:S(2)}) collective-permute-start(f32[256,128]{1,0:T(8,128)S(1)} %get-tuple-element.29.t), channel_id=1, source_target_pairs={{0,1},{1,0},{2,3},{3,2},{4,5},{5,4},{6,7},{7,6},{8,9},{9,8},{10,11... | collective-permute-start | bytes 393224 | tf_op jit(solution)/shard_map/ppermute | solution.py:267
  8.6 4.4 %collective-permute-start.3 = (f32[128,128]{1,0:T(8,128)S(1)}, f32[128,128]{1,0:T(8,128)S(1)}, u32[]{:S(2)}, u32[]{:S(2)}) collective-permute-start(f32[128,128]{1,0:T(8,128)S(1)} %image_kernel.1.w_inner), channel_id=1, source_target_pairs={{0,1},{1,0},{2,3},{3,2},{4,5},{5,4},{6,7},{7,6},{8,9},{9,8},{10,11... | collective-permute-start | bytes 196616 | tf_op jit(solution)/shard_map/ppermute | solution.py:272
  13.0 13.0 %copy-start = (f32[256,128]{1,0:T(8,128)S(1)}, f32[256,128]{1,0:T(8,128)}, u32[]{:S(2)}) copy-start(f32[256,128]{1,0:T(8,128)} %x.3) | copy-start | bytes 393220

commit v9 on v8

--- a/solution.py
+++ b/solution.py
@@ -248,8 +248,13 @@
     assert block_cols.shape[0] == 2 and columns == tile
     devices = lax.axis_size("patch") * lax.axis_size("sub")
     partner = [(i, i ^ 1) for i in range(devices)]
-    across = [(i, i + 1) for i in range(1, devices - 1, 2)]
-    across += [(j, i) for i, j in across] + [(0, 0), (devices - 1, devices - 1)]
+    groups = lax.axis_size("groups")
+    across = []
+    for group in range(groups):
+        here, there = group * devices, (group + 1) % groups * devices
+        for i in range(1, devices - 1, 2):
+            across += [(here + i, here + i + 1), (here + i + 1, here + i)]
+        across += [(here, there), (here + devices - 1, there + devices - 1)]
     single = jnp.float32
     field, block = (single, rows, columns), (single, tile, columns)
     square, sending = (jnp.bfloat16, 2, tile, tile), (single, 3 * tile + 8, columns)
@@ -263,7 +268,7 @@
     t, q_outer, send = call(
         start_kernel, [field, block, sending], local, diag, t_in, base, other_x, send, aliases={5: 2}
     )
-    got = lax.ppermute(send, AXES, across)
+    got = lax.ppermute(send, ("groups",) + AXES, across)
     other_t = lax.ppermute(t, AXES, partner)
     q_inner, t_in_t, t_out = call(
         inner_kernel, [block, square, square], local, diag, t_in, t_out_t, t, other_t

time: 27 us -> 25.1 us (0.930)
  starting transfers between devices: 8.7 us -> 4.51 us
  waiting for transfers between devices: 1.22 us -> 3.58 us
    ppermute x1, starting transfers between devices: 3.99 us -> 0.09 us  [body(): other_t = lax.ppermute(t, AXES, partner)]
    ppermute x1, starting transfers between devices: 3.54 us -> 1.27 us  [body(): other_w = lax.ppermute(w_inner, AXES, partner)]
    ppermute x1, waiting for transfers between devices: 0.01 us -> 2.1 us  [body(): got = lax.ppermute(send, ('groups',) + AXES, across)]
    ppermute x1, starting transfers between devices: 0.67 us -> 2.67 us  [body(): got = lax.ppermute(send, ('groups',) + AXES, across)]
    ppermute x1, waiting for transfers between devices: 0.99 us -> 1.26 us  [body(): other_t = lax.ppermute(t, AXES, partner)]
  transfers between devices with their start and end apart: 4 -> 4, of which waited for: 2 -> 3; matrix products, arithmetic and copies ran while one was open for 0% -> 0% of each run, Pallas kernels for 9% -> 9%
where the time goes in v9:
time: 25.1 us; the launch traced here: 25 us
  blocking collectives  13 us (52%)
  starting transfers between devices  4.51 us (18%)
  Pallas kernels  3.87 us (15%)
  waiting for transfers between devices  3.58 us (14%)
    all_to_all x1, blocking collectives, body(): shares = lax.all_to_all(shares, AXES, 0, 0)  13 us
    pallas_call x7, Pallas kernels, call(): pl.pallas_call(kernel, out_shape=outs if len(outs) > 1 else outs[0], in_s...  3.87 us
    ppermute x1, starting transfers between devices, body(): got = lax.ppermute(send, ('groups',) + AXES, across)  2.67 us
    ppermute x1, waiting for transfers between devices, body(): got = lax.ppermute(send, ('groups',) + AXES, across)  2.1 us
    ppermute x1, starting transfers between devices, body(): other_w = lax.ppermute(w_inner, AXES, partner)  1.27 us
    ppermute x1, waiting for transfers between devices, body(): other_t = lax.ppermute(t, AXES, partner)  1.26 us
  transfers between devices with their start and end apart: 4, of which 3 were waited for; matrix products, arithmetic and copies ran while one was open for 0% of the time, Pallas kernels for 9%

profile of v9, /device:TPU:0, one launch (start us, length us, event | category | flops | bytes accessed | tf_op | source)
XLA Modules:
  0.0 25.0 jit_solution(13352331021219716561)
XLA Ops:
  0.0 0.5 %collective-permute-start = (f32[256,128]{1,0:T(8,128)}, f32[256,128]{1,0:T(8,128)S(1)}, u32[]{:S(2)}, u32[]{:S(2)}) collective-permute-start(f32[256,128]{1,0:T(8,128)} %x.3), channel_id=1, source_target_pairs={{0,1},{1,0},{2,3},{3,2},{4,5},{5,4},{6,7},{7,6},{8,9},{9,8},{10,11... | collective-permute-start | bytes 393224 | tf_op jit(solution)/shard_map/ppermute | solution.py:262
  0.5 1.4 %local_kernel.1 = (bf16[2,256,256]{2,1,0:T(8,128)(2,1)S(1)}, f32[256,128]{1,0:T(8,128)S(1)}, bf16[2,128,128]{2,1,0:T(8,128)(2,1)S(1)}, bf16[2,128,128]{2,1,0:T(8...) custom-call(s32[2,3]{1,0:T(2,128)} %cols.1, f32[2,3,128,128]{3,2,1,0:T(8,128)} %tiles.1, ...), custom_call_target="tpu_custom_call" | custom-call | tf_op jit(solution)/shard_map/local_kernel/pallas_call | solution.py:235
  1.9 0.0 collective-permute-done.other_x
  1.9 0.6 %start_kernel.1 = (f32[256,128]{1,0:T(8,128)S(1)}, f32[128,128]{1,0:T(8,128)S(1)}, f32[392,128]{1,0:T(8,128)S(1)}) custom-call(bf16[2,256,256]{2,1,0:T(8,128)(2,1)S(1)} %get-tuple-element.23.local, f32[256,128]{1,0:T(8,128)S(1)} %get-tuple-element.24.diag, bf16[2,128,128]{2,1,0:T(8,128)(2,1)S(1)} %get-tuple-element.25.t_in, ...), custom_call_target="tpu_custom_call", output_to_operand_aliasing={{2}: (5, {})} | custom-call | tf_op jit(solution)/shard_map/start_kernel/pallas_call | solution.py:235
  2.5 2.7 %collective-permute-start.2 = (f32[392,128]{1,0:T(8,128)S(1)}, f32[392,128]{1,0:T(8,128)S(1)}, u32[]{:S(2)}, u32[]{:S(2)}) collective-permute-start(f32[392,128]{1,0:T(8,128)S(1)} %get-tuple-element.34), channel_id=1, source_target_pairs={{1,2},{2,1},{3,4},{4,3},{5,6},{6,5},{7,8},{8,7},{9,10},{10,9},{11,... | collective-permute-start | bytes 602120 | tf_op jit(solution)/shard_map/ppermute | solution.py:271
  5.2 0.1 collective-permute-start.1
  5.3 1.3 %collective-permute-done.1.other_t = f32[256,128]{1,0:T(8,128)S(1)} collective-permute-done((f32[256,128]{1,0:T(8,128)S(1)}, f32[256,128]{1,0:T(8,128)S(1)}, u32[]{:S(2)}, u32[]{:S(2)}) %collective-permute-start.1) | collective-permute-done | bytes 131104 | tf_op jit(solution)/shard_map/ppermute | solution.py:272
  6.5 0.2 inner_kernel.1
  6.8 2.1 %collective-permute-done.2.got = f32[392,128]{1,0:T(8,128)S(1)} collective-permute-done((f32[392,128]{1,0:T(8,128)S(1)}, f32[392,128]{1,0:T(8,128)S(1)}, u32[]{:S(2)}, u32[]{:S(2)}) %collective-permute-start.2) | collective-permute-done | bytes 200736 | tf_op jit(solution)/shard_map/ppermute | solution.py:271
  8.9 0.2 image_kernel.1.w_inner
  9.0 1.3 %collective-permute-start.3 = (f32[128,128]{1,0:T(8,128)S(1)}, f32[128,128]{1,0:T(8,128)S(1)}, u32[]{:S(2)}, u32[]{:S(2)}) collective-permute-start(f32[128,128]{1,0:T(8,128)S(1)} %image_kernel.1.w_inner), channel_id=1, source_target_pairs={{0,1},{1,0},{2,3},{3,2},{4,5},{5,4},{6,7},{7,6},{8,9},{9,8},{10,11... | collective-permute-start | bytes 196616 | tf_op jit(solution)/shard_map/ppermute | solution.py:277
  10.3 0.7 %moment_kernel.1 = (f32[256,128]{1,0:T(8,128)S(1)}, f32[256,128]{1,0:T(8,128)S(1)}, f32[8,128]{1,0:T(8,128)S(1)}, f32[128,128]{1,0:T(8,128)S(1)}, f32[128,128]{1,0:T(8,128)S(1)}) custom-call(bf16[2,256,256]{2,1,0:T(8,128)(2,1)S(1)} %get-tuple-element.23.local, f32[256,128]{1,0:T(8,128)S(1)} %get-tuple-element.24.diag, ...), custom_call_target="tpu_custom_call" | custom-call | tf_op jit(solution)/shard_map/moment_kernel/pallas_call | solution.py:235
  11.0 0.2 collective-permute-done.3.other_w
  11.2 0.0 copy-start
  11.3 13.0 %all_to_all.5.shares = f32[16,3,2,128]{3,2,1,0:T(2,128)S(1)} all-to-all(f32[16,3,2,128]{3,2,1,0:T(2,128)S(1)} %share_kernel.1), channel_id=1, replica_groups=mesh['groups'=2,'patch'=8,'sub'=2] {'patch','sub'}, dimensions={0} | all-to-all | bytes 98304 | tf_op jit(solution)/shard_map/all_to_all | solution.py:283
  24.2 0.0 copy-done
  24.2 0.8 %finish_kernel.1 = f32[256,128]{1,0:T(8,128)} custom-call(f32[16,3,2,128]{3,2,1,0:T(2,128)S(1)} %all_to_all.5.shares, f32[256,128]{1,0:T(8,128)S(1)} %copy-done, f32[256,128]{1,0:T(8,128)S(1)} %get-tuple-element.39.r, f32[256,128]{1,0:T(8,128)S(1)} %get-tuple-element.40.w), custom_call_target="tpu_custom_call" | custom-call | tf_op jit(solution)/shard_map/finish_kernel/pallas_call | solution.py:235
  (1 shorter events, 0.0 us)
Async XLA Ops:
  0.0 1.9 %collective-permute-start = (f32[256,128]{1,0:T(8,128)}, f32[256,128]{1,0:T(8,128)S(1)}, u32[]{:S(2)}, u32[]{:S(2)}) collective-permute-start(f32[256,128]{1,0:T(8,128)} %x.3), channel_id=1, source_target_pairs={{0,1},{1,0},{2,3},{3,2},{4,5},{5,4},{6,7},{7,6},{8,9},{9,8},{10,11... | collective-permute-start | bytes 393224 | tf_op jit(solution)/shard_map/ppermute | solution.py:262
  2.5 6.4 %collective-permute-start.2 = (f32[392,128]{1,0:T(8,128)S(1)}, f32[392,128]{1,0:T(8,128)S(1)}, u32[]{:S(2)}, u32[]{:S(2)}) collective-permute-start(f32[392,128]{1,0:T(8,128)S(1)} %get-tuple-element.34), channel_id=1, source_target_pairs={{1,2},{2,1},{3,4},{4,3},{5,6},{6,5},{7,8},{8,7},{9,10},{10,9},{11,... | collective-permute-start | bytes 602120 | tf_op jit(solution)/shard_map/ppermute | solution.py:271
  5.2 1.3 %collective-permute-start.1 = (f32[256,128]{1,0:T(8,128)S(1)}, f32[256,128]{1,0:T(8,128)S(1)}, u32[]{:S(2)}, u32[]{:S(2)}) collective-permute-start(f32[256,128]{1,0:T(8,128)S(1)} %get-tuple-element.29.t), channel_id=1, source_target_pairs={{0,1},{1,0},{2,3},{3,2},{4,5},{5,4},{6,7},{7,6},{8,9},{9,8},{10,11... | collective-permute-start | bytes 393224 | tf_op jit(solution)/shard_map/ppermute | solution.py:272
  9.0 2.2 %collective-permute-start.3 = (f32[128,128]{1,0:T(8,128)S(1)}, f32[128,128]{1,0:T(8,128)S(1)}, u32[]{:S(2)}, u32[]{:S(2)}) collective-permute-start(f32[128,128]{1,0:T(8,128)S(1)} %image_kernel.1.w_inner), channel_id=1, source_target_pairs={{0,1},{1,0},{2,3},{3,2},{4,5},{5,4},{6,7},{7,6},{8,9},{9,8},{10,11... | collective-permute-start | bytes 196616 | tf_op jit(solution)/shard_map/ppermute | solution.py:277
  11.2 13.0 %copy-start = (f32[256,128]{1,0:T(8,128)S(1)}, f32[256,128]{1,0:T(8,128)}, u32[]{:S(2)}) copy-start(f32[256,128]{1,0:T(8,128)} %x.3) | copy-start | bytes 393220

commit v10 on v9

--- a/solution.py
+++ b/solution.py
@@ -1,5 +1,3 @@
-import functools
-
 import jax
 import jax.numpy as jnp
 from jax import lax
@@ -7,10 +5,10 @@
 from jax.experimental.pallas import tpu as pltpu
 from jax.sharding import PartitionSpec as P
 
+
 AXES = ("patch", "sub")
 LEAST_EIGENVALUE = 0.0999
 VMEM = pl.BlockSpec(memory_space=pltpu.VMEM)
-SMEM = pl.BlockSpec(memory_space=pltpu.SMEM)
 
 
 def halves(a):
@@ -47,54 +45,115 @@
     return lax.broadcasted_iota(jnp.int32, shape, dimension)
 
 
-def local_kernel(
-    cols, tiles, mass, x, sources, local, diag, t_in, t_out_t, base, push, send
+def outer_kernel(
+    cols_there, tiles_there, mass_there, x_there, sources_there,
+    local_outer, diag_outer, t_out_t, x, tiles_inner, names, mass_inner, send,
+    cols, tiles, mass, sources, arrived,
 ):
     tile = tiles.shape[-1]
     half = tile // 2
-    slots = tiles.shape[1]
+    slots = tiles.shape[0]
     position = place()
     side = lax.rem(position, 2)
     first = position * 2
-    above, below = first - 1, first + 2
+    moves = (
+        (cols_there, cols),
+        (tiles_there.at[side], tiles),
+        (x_there, x),
+        (mass_there, mass),
+        (sources_there, sources),
+        (tiles_there.at[1 - side], tiles_inner),
+    )
+    copies = [pltpu.make_async_copy(start, end, arrived.at[i]) for i, (start, end) in enumerate(moves)]
+    for copy in copies:
+        copy.start()
+    for copy in copies[:-1]:
+        copy.wait()
     eye = index_of((tile, tile), 0) == index_of((tile, tile), 1)
-
-    def toward(row, block, sign=1.0):
+    outer, _ = outer_block(tile)
+
+    def toward(block, sign=1.0):
         slot, scale = jnp.int32(0), 0.0
         for k in range(slots):
-            named = cols[row, k] == block
+            named = cols[side, k] == block
             slot, scale = jnp.where(named, k, slot), jnp.where(named, sign, scale)
-        return scale * tiles[row, slot]
-
-    owns = []
-    for row in range(2):
-        here, there = pl.ds(row * tile, tile), pl.ds((1 - row) * tile, tile)
-        whole, own = tiles[row, 0], jnp.where(cols[row, 0] == first + row, tiles[row, 0], 0.0)
+        return scale * tiles[slot]
+
+    whole, own = tiles[0], jnp.where(cols[side, 0] == first + side, tiles[0], 0.0)
+    for k in range(1, slots):
+        whole += tiles[k]
+        own += jnp.where(cols[side, k] == first + side, tiles[k], 0.0)
+    masses = mass[0:tile][None, :], mass[tile : 2 * tile][None, :]
+    mass_here = jnp.where(side == 0, masses[0], masses[1])
+    total = jnp.sum(whole + jnp.where(eye, mass_here, 0.0), axis=1, keepdims=True)
+    diag_outer[...] = jnp.broadcast_to(total, diag_outer.shape)
+    cross = toward(first + 1 - side, -1.0)
+    store_halves(local_outer, (slice(None), slice(0, tile)), jnp.where(side == 0, -own, cross))
+    store_halves(local_outer, (slice(None), slice(tile, 2 * tile)), jnp.where(side == 0, cross, -own))
+    store_halves(t_out_t, (slice(None),), toward(jnp.where(side == 0, first - 1, first + 2)).T)
+    vertices = (first + side) * tile + index_of((tile, x.shape[1]), 0)
+    rhs = jnp.where(vertices == sources[...][None, :], 1.0, 0.0)
+    send[0:tile, :] = rhs - total * x[outer, :] - dot(local_outer, x[...])
+    send[tile : 2 * tile, :] = dot(t_out_t, x[outer, :])
+    above_diagonal = index_of((half, tile), 1) > index_of((half, tile), 0)
+    send[2 * tile : 2 * tile + half, :] = jnp.where(above_diagonal, own[:half], flip(own[half:]))
+    diagonal = jnp.sum(jnp.where(eye, total, 0.0), axis=0, keepdims=True)
+    send[2 * tile + half :, :] = jnp.broadcast_to(diagonal, (8, tile))
+    mass_inner[...] = jnp.broadcast_to(jnp.where(side == 0, masses[1], masses[0]), mass_inner.shape)
+    row = index_of(names.shape, 0)
+    named = jnp.broadcast_to(sources[...][None, :], names.shape)
+    for k in range(slots):
+        named = jnp.where(row == k, cols[1 - side, k], named)
+    names[...] = named
+    copies[-1].wait()
+
+
+def store_halves(pair, index, value):
+    pair[(0, *index)], pair[(1, *index)] = halves(value)
+
+
+def inner_row_kernel(
+    local_outer, diag_outer, x, tiles, names, mass_inner, other_x, send,
+    local, diag, t_in, t, q_outer, q_send,
+):
+    tile = tiles.shape[-1]
+    half = tile // 2
+    slots = tiles.shape[0]
+    position = place()
+    side = lax.rem(position, 2)
+    first = position * 2
+    outer, inner = outer_block(tile)
+    eye = index_of((tile, tile), 0) == index_of((tile, tile), 1)
+
+    def toward(block):
+        total = jnp.where(names[0:1, :] == block, tiles[0], 0.0)
         for k in range(1, slots):
-            whole += tiles[row, k]
-            own += jnp.where(cols[row, k] == first + row, tiles[row, k], 0.0)
-        masses = mass[here][None, :]
-        total = jnp.sum(whole + jnp.where(eye, masses, 0.0), axis=1, keepdims=True)
-        diag[here, :] = jnp.broadcast_to(total, (tile, x.shape[1]))
-        local[0, here, here], local[1, here, here] = halves(-own)
-        local[0, here, there], local[1, here, there] = halves(toward(row, first + 1 - row, -1.0))
-        owns.append(own)
-    outer, _ = outer_block(tile)
-    outward_t = toward(side, jnp.where(side == 0, above, below)).T
-    t_in[0], t_in[1] = halves(toward(1 - side, jnp.where(side == 0, below, above)))
-    t_out_t[0], t_out_t[1] = halves(outward_t)
-    vertices = position * (2 * tile) + index_of(x.shape, 0)
-    rhs = jnp.where(vertices == sources[...][None, :], 1.0, 0.0)
-    base[...] = rhs - diag[...] * x[...] - dot(local, x[...])
-    push[...] = dot(t_out_t, x[outer, :])
-    send[0:tile, :] = base[outer, :]
-    send[tile : 2 * tile, :] = push[...]
-    own = jnp.where(side == 0, owns[0], owns[1])
-    above_diagonal = index_of((half, tile), 1) > index_of((half, tile), 0)
-    packed = send.at[2 * tile + half :]
-    packed[0:half, :] = jnp.where(above_diagonal, own[:half], flip(own[half:]))
-    diagonal = jnp.sum(jnp.where(eye, diag[outer, :], 0.0), axis=0, keepdims=True)
-    packed[half:, :] = jnp.broadcast_to(diagonal, (8, tile))
+            total += jnp.where(names[k : k + 1, :] == block, tiles[k], 0.0)
+        return total
+
+    whole = tiles[0]
+    for k in range(1, slots):
+        whole += tiles[k]
+    total = jnp.sum(whole + jnp.where(eye, mass_inner[0:1, :], 0.0), axis=1, keepdims=True)
+    diag[outer, :] = diag_outer[...]
+    diag[inner, :] = jnp.broadcast_to(total, diag_outer.shape)
+    own, cross = -toward(first + 1 - side), -toward(first + side)
+    store_halves(local, (inner, slice(0, tile)), jnp.where(side == 0, cross, own))
+    store_halves(local, (inner, slice(tile, 2 * tile)), jnp.where(side == 0, own, cross))
+    for k in range(2):
+        local[k, outer, :] = local_outer[k]
+    store_halves(t_in, (slice(None),), toward(jnp.where(side == 0, first + 2, first - 1)))
+    vertices = (first + 1 - side) * tile + index_of((tile, x.shape[1]), 0)
+    rhs = jnp.where(vertices == names[slots : slots + 1, :], 1.0, 0.0)
+    t[outer, :] = send[0:tile, :]
+    t[inner, :] = (
+        rhs - total * x[inner, :] - dot(part(local, inner), x[...]) + dot(t_in, other_x[outer, :])
+    )
+    q = diag_outer[...] * send[0:tile, :] + dot(local_outer, t[...])
+    q_outer[...] = q
+    turned = jnp.where(side == 0, flip(q), q)
+    first_half = index_of((half, tile), 1) < half
+    q_send[...] = jnp.where(first_half, turned[:half], flip(turned[half:]))
 
 
 def unpack(packed):
@@ -119,20 +178,6 @@
     return pair[(0, *index)], pair[(1, *index)]
 
 
-def start_kernel(local, diag, t_in, base, other_x, send_in, t, q_outer, send):
-    tile = t_in.shape[-1]
-    half = tile // 2
-    side = lax.rem(place(), 2)
-    outer, inner = outer_block(tile)
-    t[outer, :] = base[outer, :]
-    t[inner, :] = base[inner, :] + dot(t_in, other_x[outer, :])
-    q = diag[outer, :] * base[outer, :] + dot(part(local, outer), t[...])
-    turned = jnp.where(side == 0, flip(q), q)
-    first_half = index_of((half, tile), 1) < half
-    send[2 * tile : 2 * tile + half, :] = jnp.where(first_half, turned[:half], flip(turned[half:]))
-    q_outer[...] = q
-
-
 def inner_kernel(local, diag, t_in, t_out_t, t, other_t, q_inner, t_in_t, t_out):
     outer, inner = outer_block(t_in.shape[-1])
     for half in range(2):
@@ -150,7 +195,7 @@
 
 
 def moment_kernel(
-    local, diag, t_in_t, t_out, t_out_t, t, q_outer, push, got, w_inner, r, w, moments, edge, edge_r
+    local, diag, t_in_t, t_out, t_out_t, t, q_outer, send, got, got_q, w_inner, r, w, moments, edge, edge_r
 ):
     tile = t_out.shape[-1]
     half = tile // 2
@@ -160,7 +205,7 @@
     def total(value):
         return jnp.sum(value, axis=0, keepdims=True)
 
-    push_here, push_there = got[tile : 2 * tile, :], push[...]
+    push_here, push_there = got[tile : 2 * tile, :], send[tile : 2 * tile, :]
     r_outer, r_there = t[outer, :] + push_here, got[0:tile, :] + push_there
     pull_r = dot(t_out, r_there)
     w_outer = (
@@ -178,12 +223,12 @@
     shift = jnp.where(r_r > 0, r_w / r_r, 0.0)
     y = w_now - shift * r_now
     y_outer = w_outer - shift * r_outer
-    q_half = got[2 * tile : 2 * tile + half, :]
+    q_half = got_q[...]
     q_flip = flip(q_half)
     q_there = jnp.concatenate(
         [jnp.where(side == 0, q_half, q_flip), jnp.where(side == 0, q_flip, q_half)], axis=0
     )
-    own_there, diag_there = unpack(got[2 * tile + half :, :])
+    own_there, diag_there = unpack(got[2 * tile :, :])
     w_there = q_there + diag_there * push_there - dot(halves(own_there), push_there) - dot(t_out_t, r_outer)
     pull_y = dot(t_out, w_there - shift * r_there)
     mine = (index_of((1, r_now.shape[1]), 1) >= half) == (side == 1)
@@ -224,22 +269,15 @@
     out[...] = x[...] + (first + step * (1.0 + ratio)) * r[...] - (step * first) * w[...]
 
 
-def call(kernel, shapes, *operands, first=False, last=False, aliases={}):
+def call(kernel, shapes, *operands, last=False):
     place_out = jax.ShapeDtypeStruct if last else pltpu.VMEM
     outs = [place_out(shape[1:], shape[0]) for shape in shapes]
-    in_specs, placed = [], []
-    for operand in operands:
-        scalars = operand.dtype == jnp.int32 and operand.ndim > 1
-        in_specs.append(SMEM if scalars else VMEM)
-        placed.append(operand if first else pltpu.with_memory_space_constraint(operand, pltpu.VMEM))
     return pl.pallas_call(
         kernel,
         out_shape=outs if len(outs) > 1 else outs[0],
-        in_specs=in_specs,
+        in_specs=[VMEM] * len(operands),
         out_specs=[VMEM] * len(outs) if len(outs) > 1 else VMEM,
-        input_output_aliases=aliases,
-        name=kernel.__name__,
-    )(*placed)
+    )(*[pltpu.with_memory_space_constraint(operand, pltpu.VMEM) for operand in operands])
 
 
 def body(block_cols, step_tiles, mass, warm_start, source_ids):
@@ -255,20 +293,37 @@
         for i in range(1, devices - 1, 2):
             across += [(here + i, here + i + 1), (here + i + 1, here + i)]
         across += [(here, there), (here + devices - 1, there + devices - 1)]
-    single = jnp.float32
+    single, slots = jnp.float32, block_cols.shape[1]
+    assert slots < 8
     field, block = (single, rows, columns), (single, tile, columns)
-    square, sending = (jnp.bfloat16, 2, tile, tile), (single, 3 * tile + 8, columns)
+    square, halfway = (jnp.bfloat16, 2, tile, tile), (single, tile // 2, columns)
 
     other_x = lax.ppermute(warm_start, AXES, partner)
-    local, diag, t_in, t_out_t, base, push, send = call(
-        local_kernel,
-        [(jnp.bfloat16, 2, rows, rows), field, square, square, field, block, sending],
-        block_cols, step_tiles, mass, warm_start, source_ids, first=True,
-    )
-    t, q_outer, send = call(
-        start_kernel, [field, block, sending], local, diag, t_in, base, other_x, send, aliases={5: 2}
-    )
+    results = [
+        (jnp.bfloat16, 2, tile, rows), block, square, field, (single, slots, tile, tile),
+        (jnp.int32, 8, tile), (single, 8, tile), (single, 2 * tile + tile // 2 + 8, columns),
+    ]
+    local_outer, diag_outer, t_out_t, x, tiles_inner, names, mass_inner, send = pl.pallas_call(
+        outer_kernel,
+        out_shape=[pltpu.VMEM(shape[1:], shape[0]) for shape in results],
+        in_specs=[pl.BlockSpec(memory_space=pl.ANY)] * 5,
+        out_specs=[VMEM] * len(results),
+        scratch_shapes=[
+            pltpu.SMEM(block_cols.shape, jnp.int32),
+            pltpu.VMEM((slots, tile, tile), single),
+            pltpu.VMEM(mass.shape, single),
+            pltpu.VMEM(source_ids.shape, jnp.int32),
+            pltpu.SemaphoreType.DMA((6,)),
+        ],
+        name="outer_kernel",
+    )(block_cols, step_tiles, mass, warm_start, source_ids)
     got = lax.ppermute(send, ("groups",) + AXES, across)
+    local, diag, t_in, t, q_outer, q_send = call(
+        inner_row_kernel,
+        [(jnp.bfloat16, 2, rows, rows), field, square, field, block, halfway],
+        local_outer, diag_outer, x, tiles_inner, names, mass_inner, other_x, send,
+    )
+    got_q = lax.ppermute(q_send, ("groups",) + AXES, across)
     other_t = lax.ppermute(t, AXES, partner)
     q_inner, t_in_t, t_out = call(
         inner_kernel, [block, square, square], local, diag, t_in, t_out_t, t, other_t
@@ -277,11 +332,11 @@
     other_w = lax.ppermute(w_inner, AXES, partner)
     r, w, moments, edge, edge_r = call(
         moment_kernel, [field, field, (single, 8, columns), block, block],
-        local, diag, t_in_t, t_out, t_out_t, t, q_outer, push, got, w_inner,
+        local, diag, t_in_t, t_out, t_out_t, t, q_outer, send, got, got_q, w_inner,
     )
     shares = call(share_kernel, [(single, devices, 3, 2, columns)], moments, edge, edge_r, other_t, other_w)
     shares = lax.all_to_all(shares, AXES, 0, 0)
-    return call(finish_kernel, [field], shares, warm_start, r, w, last=True)
+    return call(finish_kernel, [field], shares, x, r, w, last=True)
 
 
 def solution(mesh):

time: 25.1 us -> 27.7 us (1.10)
  blocking collectives: 13 us -> 14 us
  starting transfers between devices: 4.51 us -> 5.41 us
  waiting for transfers between devices: 3.58 us -> 4.2 us
    ppermute x0 -> x1, starting transfers between devices: none -> 2.05 us  [body(): got_q = lax.ppermute(q_send, ('groups',) + AXES, across)]
    ppermute x0 -> x1, waiting for transfers between devices: none -> 1.89 us  [body(): got_q = lax.ppermute(q_send, ('groups',) + AXES, across)]
    pallas_call x0 -> x1, Pallas kernels: none -> 1.35 us  [body(): pl.pallas_call(outer_kernel, out_shape=[pltpu.VMEM(shape[1:], shape[0]) f...]
    pallas_call x7 -> x6, Pallas kernels: 3.87 us -> 2.53 us  [call(): pl.pallas_call(kernel, out_shape=outs if len(outs) > 1 else outs[0], in_s...]
    ppermute x1, starting transfers between devices: 1.27 us -> 0.15 us  [body(): other_w = lax.ppermute(w_inner, AXES, partner)]
    ppermute x1, waiting for transfers between devices: 2.1 us -> 1.04 us  [body(): got = lax.ppermute(send, ('groups',) + AXES, across)]
    all_to_all x1, blocking collectives: 13 us -> 14 us  [body(): shares = lax.all_to_all(shares, AXES, 0, 0)]
  transfers between devices with their start and end apart: 4 -> 5, of which waited for: 3 -> 3; matrix products, arithmetic and copies ran while one was open for 0% -> 0% of each run, Pallas kernels for 9% -> 11%
where the time goes in v10:
time: 27.7 us; the launch traced here: 27.5 us
  blocking collectives  14 us (51%)
  starting transfers between devices  5.41 us (20%)
  waiting for transfers between devices  4.2 us (15%)
  Pallas kernels  3.88 us (14%)
    all_to_all x1, blocking collectives, body(): shares = lax.all_to_all(shares, AXES, 0, 0)  14 us
    ppermute x1, starting transfers between devices, body(): got = lax.ppermute(send, ('groups',) + AXES, across)  2.57 us
    pallas_call x6, Pallas kernels, call(): pl.pallas_call(kernel, out_shape=outs if len(outs) > 1 else outs[0], in_s...  2.53 us
    ppermute x1, starting transfers between devices, body(): got_q = lax.ppermute(q_send, ('groups',) + AXES, across)  2.05 us
    ppermute x1, waiting for transfers between devices, body(): got_q = lax.ppermute(q_send, ('groups',) + AXES, across)  1.89 us
    pallas_call x1, Pallas kernels, body(): pl.pallas_call(outer_kernel, out_shape=[pltpu.VMEM(shape[1:], shape[0]) f...  1.35 us
    ppermute x1, waiting for transfers between devices, body(): other_t = lax.ppermute(t, AXES, partner)  1.26 us
    ppermute x1, waiting for transfers between devices, body(): got = lax.ppermute(send, ('groups',) + AXES, across)  1.04 us
  transfers between devices with their start and end apart: 5, of which 3 were waited for; matrix products, arithmetic and copies ran while one was open for 0% of the time, Pallas kernels for 11%

profile of v10, /device:TPU:0, one launch (start us, length us, event | category | flops | bytes accessed | tf_op | source)
XLA Modules:
  0.0 27.5 jit_solution(1221289589790380889)
XLA Ops:
  0.0 0.5 %collective-permute-start = (f32[256,128]{1,0:T(8,128)}, f32[256,128]{1,0:T(8,128)S(1)}, u32[]{:S(2)}, u32[]{:S(2)}) collective-permute-start(f32[256,128]{1,0:T(8,128)} %x_there.1), channel_id=1, source_target_pairs={{0,1},{1,0},{2,3},{3,2},{4,5},{5,4},{6,7},{7,6},{8,9},{9,8},{10,11... | collective-permute-start | bytes 393224 | tf_op jit(solution)/shard_map/ppermute | solution.py:301
  0.5 1.4 %outer_kernel.1 = (bf16[2,128,256]{2,1,0:T(8,128)(2,1)S(1)}, f32[128,128]{1,0:T(8,128)S(1)}, bf16[2,128,128]{2,1,0:T(8,128)(2,1)S(1)}, f32[256,128]{1,0:T(8,128)...) custom-call(s32[2,3]{1,0:T(2,128)} %cols_there.1, ...), custom_call_target="tpu_custom_call" | custom-call | tf_op jit(solution)/shard_map/outer_kernel/pallas_call | solution.py:306
  1.9 2.6 %collective-permute-start.2 = (f32[328,128]{1,0:T(8,128)S(1)}, f32[328,128]{1,0:T(8,128)S(1)}, u32[]{:S(2)}, u32[]{:S(2)}) collective-permute-start(f32[328,128]{1,0:T(8,128)S(1)} %get-tuple-element.33.send), channel_id=1, source_target_pairs={{1,2},{2,1},{3,4},{4,3},{5,6},{6,5},{7,8},{8,7},{9,10},{10,9},{11,... | collective-permute-start | bytes 503816 | tf_op jit(solution)/shard_map/ppermute | solution.py:320
  4.4 0.0 collective-permute-done.other_x
  4.4 0.6 %shard_map.55 = (bf16[2,256,256]{2,1,0:T(8,128)(2,1)S(1)}, f32[256,128]{1,0:T(8,128)S(1)}, bf16[2,128,128]{2,1,0:T(8,128)(2,1)S(1)}, f32[256,128]{1,0:T(8,128)S(...) custom-call(bf16[2,128,256]{2,1,0:T(8,128)(2,1)S(1)} %get-tuple-element.27.local_outer, ...), custom_call_target="tpu_custom_call" | custom-call | tf_op jit(solution)/shard_map/pallas_call | solution.py:275
  5.1 0.1 collective-permute-start.1
  5.2 1.3 %collective-permute-done.1.other_t = f32[256,128]{1,0:T(8,128)S(1)} collective-permute-done((f32[256,128]{1,0:T(8,128)S(1)}, f32[256,128]{1,0:T(8,128)S(1)}, u32[]{:S(2)}, u32[]{:S(2)}) %collective-permute-start.1) | collective-permute-done | bytes 131104 | tf_op jit(solution)/shard_map/ppermute | solution.py:327
  6.5 0.2 shard_map.56
  6.7 1.0 %collective-permute-done.2.got = f32[328,128]{1,0:T(8,128)S(1)} collective-permute-done((f32[328,128]{1,0:T(8,128)S(1)}, f32[328,128]{1,0:T(8,128)S(1)}, u32[]{:S(2)}, u32[]{:S(2)}) %collective-permute-start.2) | collective-permute-done | bytes 167968 | tf_op jit(solution)/shard_map/ppermute | solution.py:320
  7.8 0.2 shard_map.57.w_inner
  7.9 0.2 collective-permute-start.4
  8.1 2.0 %collective-permute-start.3 = (f32[64,128]{1,0:T(8,128)S(1)}, f32[64,128]{1,0:T(8,128)S(1)}, u32[]{:S(2)}, u32[]{:S(2)}) collective-permute-start(f32[64,128]{1,0:T(8,128)S(1)} %get-tuple-element.42), channel_id=1, source_target_pairs={{1,2},{2,1},{3,4},{4,3},{5,6},{6,5},{7,8},{8,7},{9,10},{10,9},{11,... | collective-permute-start | bytes 98312 | tf_op jit(solution)/shard_map/ppermute | solution.py:326
  10.1 1.9 %collective-permute-done.3.got_q = f32[64,128]{1,0:T(8,128)S(1)} collective-permute-done((f32[64,128]{1,0:T(8,128)S(1)}, f32[64,128]{1,0:T(8,128)S(1)}, u32[]{:S(2)}, u32[]{:S(2)}) %collective-permute-start.3) | collective-permute-done | bytes 32800 | tf_op jit(solution)/shard_map/ppermute | solution.py:326
  12.0 0.7 %shard_map.58 = (f32[256,128]{1,0:T(8,128)S(1)}, f32[256,128]{1,0:T(8,128)S(1)}, f32[8,128]{1,0:T(8,128)S(1)}, f32[128,128]{1,0:T(8,128)S(1)}, f32[128,128]{1,0:T(8,128)S(1)}) custom-call(bf16[2,256,256]{2,1,0:T(8,128)(2,1)S(1)} %get-tuple-element.34.local, f32[256,128]{1,0:T(8,128)S(1)} %get-tuple-element.35.diag, ...), custom_call_target="tpu_custom_call" | custom-call | tf_op jit(solution)/shard_map/pallas_call | solution.py:275
  12.7 0.0 collective-permute-done.4.other_w
  12.7 0.1 shard_map.59
  12.8 14.0 %all_to_all.5.shares = f32[16,3,2,128]{3,2,1,0:T(2,128)S(1)} all-to-all(f32[16,3,2,128]{3,2,1,0:T(2,128)S(1)} %shard_map.59), channel_id=1, replica_groups=mesh['groups'=2,'patch'=8,'sub'=2] {'patch','sub'}, dimensions={0} | all-to-all | bytes 98304 | tf_op jit(solution)/shard_map/all_to_all | solution.py:338
  26.8 0.8 %shard_map.60 = f32[256,128]{1,0:T(8,128)} custom-call(f32[16,3,2,128]{3,2,1,0:T(2,128)S(1)} %all_to_all.5.shares, f32[256,128]{1,0:T(8,128)S(1)} %get-tuple-element.29.x, f32[256,128]{1,0:T(8,128)S(1)} %get-tuple-element.47.r, f32[256,128]{1,0:T(8,128)S(1)} %get-tuple-element.48.w), custom_call_target="tpu_custom_call" | custom-call | tf_op jit(solution)/shard_map/pallas_call | solution.py:275
Async XLA Ops:
  0.0 4.4 %collective-permute-start = (f32[256,128]{1,0:T(8,128)}, f32[256,128]{1,0:T(8,128)S(1)}, u32[]{:S(2)}, u32[]{:S(2)}) collective-permute-start(f32[256,128]{1,0:T(8,128)} %x_there.1), channel_id=1, source_target_pairs={{0,1},{1,0},{2,3},{3,2},{4,5},{5,4},{6,7},{7,6},{8,9},{9,8},{10,11... | collective-permute-start | bytes 393224 | tf_op jit(solution)/shard_map/ppermute | solution.py:301
  1.9 5.9 %collective-permute-start.2 = (f32[328,128]{1,0:T(8,128)S(1)}, f32[328,128]{1,0:T(8,128)S(1)}, u32[]{:S(2)}, u32[]{:S(2)}) collective-permute-start(f32[328,128]{1,0:T(8,128)S(1)} %get-tuple-element.33.send), channel_id=1, source_target_pairs={{1,2},{2,1},{3,4},{4,3},{5,6},{6,5},{7,8},{8,7},{9,10},{10,9},{11,... | collective-permute-start | bytes 503816 | tf_op jit(solution)/shard_map/ppermute | solution.py:320
  5.1 1.4 %collective-permute-start.1 = (f32[256,128]{1,0:T(8,128)S(1)}, f32[256,128]{1,0:T(8,128)S(1)}, u32[]{:S(2)}, u32[]{:S(2)}) collective-permute-start(f32[256,128]{1,0:T(8,128)S(1)} %get-tuple-element.38.t), channel_id=1, source_target_pairs={{0,1},{1,0},{2,3},{3,2},{4,5},{5,4},{6,7},{7,6},{8,9},{9,8},{10,11... | collective-permute-start | bytes 393224 | tf_op jit(solution)/shard_map/ppermute | solution.py:327
  7.9 4.8 %collective-permute-start.4 = (f32[128,128]{1,0:T(8,128)S(1)}, f32[128,128]{1,0:T(8,128)S(1)}, u32[]{:S(2)}, u32[]{:S(2)}) collective-permute-start(f32[128,128]{1,0:T(8,128)S(1)} %shard_map.57.w_inner), channel_id=1, source_target_pairs={{0,1},{1,0},{2,3},{3,2},{4,5},{5,4},{6,7},{7,6},{8,9},{9,8},{10,11... | collective-permute-start | bytes 196616 | tf_op jit(solution)/shard_map/ppermute | solution.py:332
  8.1 3.9 %collective-permute-start.3 = (f32[64,128]{1,0:T(8,128)S(1)}, f32[64,128]{1,0:T(8,128)S(1)}, u32[]{:S(2)}, u32[]{:S(2)}) collective-permute-start(f32[64,128]{1,0:T(8,128)S(1)} %get-tuple-element.42), channel_id=1, source_target_pairs={{1,2},{2,1},{3,4},{4,3},{5,6},{6,5},{7,8},{8,7},{9,10},{10,9},{11,... | collective-permute-start | bytes 98312 | tf_op jit(solution)/shard_map/ppermute | solution.py:326

commit v11 on v10

v11 whole, which is shorter than its diff:
```python
import jax
import jax.numpy as jnp
from jax import lax
from jax.experimental import pallas as pl
from jax.experimental.pallas import tpu as pltpu
from jax.sharding import PartitionSpec as P


AXES = ("patch", "sub")
LEAST_EIGENVALUE = 0.0999
VMEM = pl.BlockSpec(memory_space=pltpu.VMEM)


def halves(a):
    high = a.astype(jnp.bfloat16)
    return high, (a - high.astype(jnp.float32)).astype(jnp.bfloat16)


def dot(a, b):
    a_high, a_low = a[0], a[1]
    b_high, b_low = halves(b)

    def product(p, q):
        return jnp.dot(p, q, preferred_element_type=jnp.float32)

    return product(a_high, b_high) + (product(a_high, b_low) + product(a_low, b_high))


def place():
    return lax.axis_index("patch") * lax.axis_size("sub") + lax.axis_index("sub")


def outer_block(tile):
    side = lax.rem(place(), 2)
    outer = pl.ds(pl.multiple_of(side * tile, tile), tile)
    inner = pl.ds(pl.multiple_of((1 - side) * tile, tile), tile)
    return outer, inner


def flip(x):
    return pltpu.roll(x, x.shape[1] // 2, 1)


def index_of(shape, dimension):
    return lax.broadcasted_iota(jnp.int32, shape, dimension)


def push_kernel(
    cols_there, tiles_there, mass_there, x_there, sources_there,
    push, t_out_t, x, tiles_outer, tiles_inner, names, masses,
    cols, mass, sources, arrived,
):
    tile = tiles_outer.shape[-1]
    slots = tiles_outer.shape[0]
    position = place()
    side = lax.rem(position, 2)
    moves = (
        (cols_there, cols),
        (tiles_there.at[side], tiles_outer),
        (x_there, x),
        (mass_there, mass),
        (sources_there, sources),
        (tiles_there.at[1 - side], tiles_inner),
    )
    copies = [pltpu.make_async_copy(start, end, arrived.at[i]) for i, (start, end) in enumerate(moves)]
    for copy in copies:
        copy.start()
    for copy in copies[:3]:
        copy.wait()
    outer, _ = outer_block(tile)
    beyond = 2 * position + jnp.where(side == 0, -1, 2)
    slot, scale = jnp.int32(0), 0.0
    for k in range(slots):
        named = cols[side, k] == beyond
        slot, scale = jnp.where(named, k, slot), jnp.where(named, 1.0, scale)
    store_halves(t_out_t, (slice(None),), (scale * tiles_outer[slot]).T)
    push[...] = dot(t_out_t, x[outer, :])
    for copy in copies[3:]:
        copy.wait()
    row = index_of(names.shape, 0)
    named = jnp.broadcast_to(sources[...][None, :], names.shape)
    for k in range(slots):
        named = jnp.where(row == k, cols[side, k], named)
        named = jnp.where(row == 8 + k, cols[1 - side, k], named)
    names[...] = named
    first, second = mass[0:tile][None, :], mass[tile : 2 * tile][None, :]
    masses[0:8, :] = jnp.broadcast_to(jnp.where(side == 0, first, second), (8, tile))
    masses[8:16, :] = jnp.broadcast_to(jnp.where(side == 0, second, first), (8, tile))


def toward(tiles, names, block):
    total = jnp.where(names[0:1, :] == block, tiles[0], 0.0)
    for k in range(1, tiles.shape[0]):
        total += jnp.where(names[k : k + 1, :] == block, tiles[k], 0.0)
    return total


def row_sums(tiles, masses):
    tile = tiles.shape[-1]
    whole = tiles[0]
    for k in range(1, tiles.shape[0]):
        whole += tiles[k]
    eye = index_of((tile, tile), 0) == index_of((tile, tile), 1)
    return jnp.sum(whole + jnp.where(eye, masses[0:1, :], 0.0), axis=1, keepdims=True)


def right_side(names, block, shape):
    vertices = block * shape[0] + index_of(shape, 0)
    return jnp.where(vertices == names[7:8, :], 1.0, 0.0)


def outer_kernel(x, tiles, names, masses, local_outer, diag_outer, send):
    tile = tiles.shape[-1]
    half = tile // 2
    position = place()
    side = lax.rem(position, 2)
    first = position * 2
    outer, _ = outer_block(tile)
    names, masses = names[0:8, :], masses[0:8, :]
    total = row_sums(tiles, masses)
    diag_outer[...] = jnp.broadcast_to(total, diag_outer.shape)
    own, cross = toward(tiles, names, first + side), toward(tiles, names, first + 1 - side)
    store_halves(local_outer, (slice(None), slice(0, tile)), jnp.where(side == 0, -own, -cross))
    store_halves(local_outer, (slice(None), slice(tile, 2 * tile)), jnp.where(side == 0, -cross, -own))
    x_outer = x[outer, :]
    send[0:tile, :] = (
        right_side(names, first + side, x_outer.shape) - total * x_outer - dot(local_outer, x[...])
    )
    above_diagonal = index_of((half, tile), 1) > index_of((half, tile), 0)
    send[tile : tile + half, :] = jnp.where(above_diagonal, own[:half], flip(own[half:]))
    eye = index_of((tile, tile), 0) == index_of((tile, tile), 1)
    diagonal = jnp.sum(jnp.where(eye, total, 0.0), axis=0, keepdims=True)
    send[tile + half :, :] = jnp.broadcast_to(diagonal, (8, tile))


def store_halves(pair, index, value):
    pair[(0, *index)], pair[(1, *index)] = halves(value)


def inner_row_kernel(
    local_outer, diag_outer, x, tiles, names, masses, other_x, send,
    local, diag, t_in, t, q_outer, q_send,
):
    tile = tiles.shape[-1]
    half = tile // 2
    position = place()
    side = lax.rem(position, 2)
    first = position * 2
    outer, inner = outer_block(tile)
    names, masses = names[8:16, :], masses[8:16, :]
    total = row_sums(tiles, masses)
    diag[outer, :] = diag_outer[...]
    diag[inner, :] = jnp.broadcast_to(total, diag_outer.shape)
    own, cross = toward(tiles, names, first + 1 - side), toward(tiles, names, first + side)
    store_halves(local, (inner, slice(0, tile)), jnp.where(side == 0, -cross, -own))
    store_halves(local, (inner, slice(tile, 2 * tile)), jnp.where(side == 0, -own, -cross))
    for k in range(2):
        local[k, outer, :] = local_outer[k]
    store_halves(t_in, (slice(None),), toward(tiles, names, jnp.where(side == 0, first + 2, first - 1)))
    x_inner = x[inner, :]
    t[outer, :] = send[0:tile, :]
    t[inner, :] = (
        right_side(names, first + 1 - side, x_inner.shape)
        - total * x_inner
        - dot(part(local, inner), x[...])
        + dot(t_in, other_x[outer, :])
    )
    q = diag_outer[...] * send[0:tile, :] + dot(local_outer, t[...])
    q_outer[...] = q
    turned = jnp.where(side == 0, flip(q), q)
    first_half = index_of((half, tile), 1) < half
    q_send[...] = jnp.where(first_half, turned[:half], flip(turned[half:]))


def unpack(packed):
    tile = packed.shape[1]
    half = tile // 2
    rows = packed[0:half, :]
    row, column = index_of((half, tile), 0), index_of((half, tile), 1)
    upper = jnp.where(column > row, rows, 0.0)
    lower = flip(jnp.where(column < row, rows, 0.0))
    triangles = jnp.concatenate([upper, lower], axis=0)
    eye = index_of((tile, tile), 0) == index_of((tile, tile), 1)
    diagonal = jnp.sum(jnp.where(eye, packed[half : half + 1, :], 0.0), axis=1, keepdims=True)
    return triangles + triangles.T, diagonal


def outer_columns(tile):
    side = lax.rem(place(), 2)
    return pl.ds(pl.multiple_of(side * tile, tile), tile)


def part(pair, *index):
    return pair[(0, *index)], pair[(1, *index)]


def inner_kernel(local, diag, t_in, t_out_t, t, other_t, q_inner, t_in_t, t_out):
    outer, inner = outer_block(t_in.shape[-1])
    for half in range(2):
        t_in_t[half] = t_in[half].T
        t_out[half] = t_out_t[half].T
    q_inner[...] = (
        diag[inner, :] * t[inner, :] + dot(part(local, inner), t[...]) - dot(t_in, other_t[outer, :])
    )


def image_kernel(local, q_inner, push_here, w_inner):
    tile = q_inner.shape[0]
    _, inner = outer_block(tile)
    w_inner[...] = q_inner[...] + dot(part(local, inner, outer_columns(tile)), push_here[...])


def total(value):
    return jnp.sum(value, axis=0, keepdims=True)


def moment_kernel(
    local, diag, t_in_t, t_out, t, q_outer, push_here, push_there, got, w_inner,
    r, w, y_outer, pull_r, moments, edge, edge_r,
):
    tile = t_out.shape[-1]
    outer, inner = outer_block(tile)
    r_outer = t[outer, :] + push_here[...]
    pull = dot(t_out, got[0:tile, :] + push_there[...])
    w_outer = (
        q_outer[...]
        + diag[outer, :] * push_here[...]
        + dot(part(local, outer, outer_columns(tile)), push_here[...])
        - pull
    )
    r[outer, :] = r_outer
    r[inner, :] = t[inner, :]
    w[outer, :] = w_outer
    w[inner, :] = w_inner[...]
    w_now, r_now = w[...], r[...]
    r_r, r_w = total(r_now * r_now), total(r_now * w_now)
    shift = jnp.where(r_r > 0, r_w / r_r, 0.0)
    y = w_now - shift * r_now
    y_out = w_outer - shift * r_outer
    a_y = diag[...] * y + dot(local, y)
    r_ay = total(r_now * a_y + y * w_now) + total(y_out * pull)
    r_ar = r_w + total(r_outer * pull)
    y_outer[...] = y_out
    pull_r[...] = pull
    moments[...] = jnp.concatenate([r_r, r_w, total(y * y), total(y * a_y), r_ay, r_ar, shift, shift], axis=0)
    edge[...] = dot(t_in_t, w_inner[...] - shift * r[inner, :])
    edge_r[...] = dot(t_in_t, r[inner, :])


def share_kernel(
    moments, edge, edge_r, y_outer, pull_r, r, t_out, t_out_t, push_there, got, got_q, other_t, other_w, out
):
    tile = t_out.shape[-1]
    half = tile // 2
    side = lax.rem(place(), 2)
    outer, _ = outer_block(tile)
    shift = moments[6:7, :]
    q_half = got_q[...]
    q_flip = flip(q_half)
    q_there = jnp.concatenate(
        [jnp.where(side == 0, q_half, q_flip), jnp.where(side == 0, q_flip, q_half)], axis=0
    )
    own_there, diag_there = unpack(got[tile:, :])
    r_outer, r_there = r[outer, :], got[0:tile, :] + push_there[...]
    w_there = (
        q_there
        + diag_there * push_there[...]
        - dot(halves(own_there), push_there[...])
        - dot(t_out_t, r_outer)
    )
    pull_y = dot(t_out, w_there - shift * r_there)
    mine = (index_of(shift.shape, 1) >= half) == (side == 1)
    weight = jnp.where(mine, 2.0, 0.0)
    y_partner = other_w[...] - shift * other_t[outer, :]
    y_ay = total(edge[...] * y_partner) + weight * total(y_outer[...] * pull_y)
    r_ay = total(edge_r[...] * y_partner)
    r_ay += weight * total(r_outer * pull_y + y_outer[...] * pull_r[...])
    r_ar = weight * total(r_outer * pull_r[...])
    row = index_of(moments.shape, 0)
    sums = moments[...]
    for place_of, value in ((3, y_ay), (4, r_ay), (5, r_ar)):
        sums -= jnp.where(row == place_of, value, 0.0)
    for pair in range(out.shape[1]):
        out[:, pair] = jnp.broadcast_to(sums[None, 2 * pair : 2 * pair + 2], out[:, pair].shape)


def finish_kernel(shares, x, r, w, out):
    r_rs, r_ws, spreads, y_ay, r_ay, r_ar = [shares[:, row // 2, row % 2, :] for row in range(6)]
    r_r = jnp.sum(r_rs, axis=0, keepdims=True)
    r_w = jnp.sum(r_ws, axis=0, keepdims=True)
    theta = r_w / r_r
    off = jnp.where(r_rs > 0, r_ws / r_rs, 0.0) - theta
    spread = jnp.sum(spreads + r_rs * off * off, axis=0, keepdims=True)
    energy = jnp.sum(y_ay + off * (r_ay + off * r_ar), axis=0, keepdims=True)
    ratio = spread / (theta * theta * r_r)
    energy = jnp.maximum(energy - ratio * theta * spread, LEAST_EIGENVALUE * spread * (1.0 + ratio))
    step = jnp.where(spread > 0, spread / energy, 0.0)
    first = 1.0 / theta
    out[...] = x[...] + (first + step * (1.0 + ratio)) * r[...] - (step * first) * w[...]


def call(kernel, shapes, *operands, last=False):
    place_out = jax.ShapeDtypeStruct if last else pltpu.VMEM
    outs = [place_out(shape[1:], shape[0]) for shape in shapes]
    return pl.pallas_call(
        kernel,
        out_shape=outs if len(outs) > 1 else outs[0],
        in_specs=[VMEM] * len(operands),
        out_specs=[VMEM] * len(outs) if len(outs) > 1 else VMEM,
    )(*[pltpu.with_memory_space_constraint(operand, pltpu.VMEM) for operand in operands])


def body(block_cols, step_tiles, mass, warm_start, source_ids):
    tile = step_tiles.shape[-1]
    rows, columns = warm_start.shape
    assert block_cols.shape[0] == 2 and columns == tile
    devices = lax.axis_size("patch") * lax.axis_size("sub")
    partner = [(i, i ^ 1) for i in range(devices)]
    groups = lax.axis_size("groups")
    across = []
    for group in range(groups):
        here, there = group * devices, (group + 1) % groups * devices
        for i in range(1, devices - 1, 2):
            across += [(here + i, here + i + 1), (here + i + 1, here + i)]
        across += [(here, there), (here + devices - 1, there + devices - 1)]
    single, slots = jnp.float32, block_cols.shape[1]
    assert slots < 8
    field, block = (single, rows, columns), (single, tile, columns)
    square, halfway = (jnp.bfloat16, 2, tile, tile), (single, tile // 2, columns)
    tiles = (single, slots, tile, tile)

    def exchange(value):
        return lax.ppermute(value, ("groups",) + AXES, across)

    other_x = lax.ppermute(warm_start, AXES, partner)
    results = [block, square, field, tiles, tiles, (jnp.int32, 16, tile), (single, 16, tile)]
    push_there, t_out_t, x, tiles_outer, tiles_inner, names, masses = pl.pallas_call(
        push_kernel,
        out_shape=[pltpu.VMEM(shape[1:], shape[0]) for shape in results],
        in_specs=[pl.BlockSpec(memory_space=pl.ANY)] * 5,
        out_specs=[VMEM] * len(results),
        scratch_shapes=[
            pltpu.SMEM(block_cols.shape, jnp.int32),
            pltpu.VMEM(mass.shape, single),
            pltpu.VMEM(source_ids.shape, jnp.int32),
            pltpu.SemaphoreType.DMA((6,)),
        ],
        name="push_kernel",
    )(block_cols, step_tiles, mass, warm_start, source_ids)
    push_here = exchange(push_there)
    local_outer, diag_outer, send = call(
        outer_kernel,
        [(jnp.bfloat16, 2, tile, rows), block, (single, tile + tile // 2 + 8, columns)],
        x, tiles_outer, names, masses,
    )
    got = exchange(send)
    local, diag, t_in, t, q_outer, q_send = call(
        inner_row_kernel,
        [(jnp.bfloat16, 2, rows, rows), field, square, field, block, halfway],
        local_outer, diag_outer, x, tiles_inner, names, masses, other_x, send,
    )
    got_q = exchange(q_send)
    other_t = lax.ppermute(t, AXES, partner)
    q_inner, t_in_t, t_out = call(
        inner_kernel, [block, square, square], local, diag, t_in, t_out_t, t, other_t
    )
    w_inner = call(image_kernel, [block], local, q_inner, push_here)
    other_w = lax.ppermute(w_inner, AXES, partner)
    r, w, y_outer, pull_r, moments, edge, edge_r = call(
        moment_kernel, [field, field, block, block, (single, 8, columns), block, block],
        local, diag, t_in_t, t_out, t, q_outer, push_here, push_there, got, w_inner,
    )
    shares = call(
        share_kernel, [(single, devices, 3, 2, columns)],
        moments, edge, edge_r, y_outer, pull_r, r, t_out, t_out_t, push_there, got, got_q, other_t, other_w,
    )
    shares = lax.all_to_all(shares, AXES, 0, 0)
    return call(finish_kernel, [field], shares, x, r, w, last=True)


def solution(mesh):
    in_specs = (
        P(("groups", "patch", "sub"), None),
        P(("groups", "patch", "sub"), None, None, None),
        P(("groups", "patch", "sub")),
        P(("groups", "patch", "sub"), None),
        P("groups"),
    )
    out_specs = P(("groups", "patch", "sub"), None)
    return jax.shard_map(body, mesh=mesh, in_specs=in_specs, out_specs=out_specs, check_vma=False)
```

time: 27.7 us -> 26.6 us (0.960)
  blocking collectives: 14 us -> 12.8 us
  waiting for transfers between devices: 4.2 us -> 3.26 us
  Pallas kernels: 3.88 us -> 4.54 us
  starting transfers between devices: 5.41 us -> 5.76 us
    ppermute x1, waiting for transfers between devices: 1.26 us -> 0.01 us  [body(): other_t = lax.ppermute(t, AXES, partner)]
    all_to_all x1, blocking collectives: 14 us -> 12.8 us  [body(): shares = lax.all_to_all(shares, AXES, 0, 0)]
    pallas_call x6 -> x7, Pallas kernels: 2.53 us -> 3.22 us  [call(): pl.pallas_call(kernel, out_shape=outs if len(outs) > 1 else outs[0], in_s...]
    ppermute x2 -> x3, starting transfers between devices: 4.62 us -> 5.03 us  [exchange(): return lax.ppermute(value, ('groups',) + AXES, across)]
    ppermute x2 -> x3, waiting for transfers between devices: 2.93 us -> 3.25 us  [exchange(): return lax.ppermute(value, ('groups',) + AXES, across)]
  transfers between devices with their start and end apart: 5 -> 6, of which waited for: 3 -> 3; matrix products, arithmetic and copies ran while one was open for 0% -> 0% of each run, Pallas kernels for 11% -> 10%
where the time goes in v11:
time: 26.6 us; the launch traced here: 26.4 us
  blocking collectives  12.8 us (48%)
  starting transfers between devices  5.76 us (22%)
  Pallas kernels  4.54 us (17%)
  waiting for transfers between devices  3.26 us (12%)
    all_to_all x1, blocking collectives, body(): shares = lax.all_to_all(shares, AXES, 0, 0)  12.8 us
    ppermute x3, starting transfers between devices, exchange(): return lax.ppermute(value, ('groups',) + AXES, across)  5.03 us
    ppermute x3, waiting for transfers between devices, exchange(): return lax.ppermute(value, ('groups',) + AXES, across)  3.25 us
    pallas_call x7, Pallas kernels, call(): pl.pallas_call(kernel, out_shape=outs if len(outs) > 1 else outs[0], in_s...  3.22 us
    pallas_call x1, Pallas kernels, body(): pl.pallas_call(push_kernel, out_shape=[pltpu.VMEM(shape[1:], shape[0]) fo...  1.32 us
  transfers between devices with their start and end apart: 6, of which 3 were waited for; matrix products, arithmetic and copies ran while one was open for 0% of the time, Pallas kernels for 10%

profile of v11, /device:TPU:0, one launch (start us, length us, event | category | flops | bytes accessed | tf_op | source)
XLA Modules:
  0.0 26.4 jit_solution(6592466707585962567)
XLA Ops:
  0.0 0.5 %collective-permute-start = (f32[256,128]{1,0:T(8,128)}, f32[256,128]{1,0:T(8,128)S(1)}, u32[]{:S(2)}, u32[]{:S(2)}) collective-permute-start(f32[256,128]{1,0:T(8,128)} %x_there.1), channel_id=1, source_target_pairs={{0,1},{1,0},{2,3},{3,2},{4,5},{5,4},{6,7},{7,6},{8,9},{9,8},{10,11... | collective-permute-start | bytes 393224 | tf_op jit(solution)/shard_map/ppermute | solution.py:335
  0.5 1.3 %push_kernel.1 = (f32[128,128]{1,0:T(8,128)S(1)}, bf16[2,128,128]{2,1,0:T(8,128)(2,1)S(1)}, f32[256,128]{1,0:T(8,128)S(1)}, f32[3,128,128]{2,1,0:T(8,128)S(1)}, ...) custom-call(s32[2,3]{1,0:T(2,128)} %cols_there.1, f32[2,3,128,128]{3,2,1,0:T(8,128)} %tiles_there.1, ...), custom_call_target="tpu_custom_call" | custom-call | tf_op jit(solution)/shard_map/push_kernel/pallas_call | solution.py:337
  1.8 0.2 shard_map.55
  2.1 0.0 collective-permute-done.other_x
  2.1 0.7 %shard_map.56 = (bf16[2,256,256]{2,1,0:T(8,128)(2,1)S(1)}, f32[256,128]{1,0:T(8,128)S(1)}, bf16[2,128,128]{2,1,0:T(8,128)(2,1)S(1)}, f32[256,128]{1,0:T(8,128)S(...) custom-call(bf16[2,128,256]{2,1,0:T(8,128)(2,1)S(1)} %get-tuple-element.35.local_outer, ...), custom_call_target="tpu_custom_call" | custom-call | tf_op jit(solution)/shard_map/pallas_call | solution.py:305
  2.7 0.1 collective-permute-start.1
  2.8 3.0 %collective-permute-start.2 = (f32[128,128]{1,0:T(8,128)S(1)}, f32[128,128]{1,0:T(8,128)S(1)}, u32[]{:S(2)}, u32[]{:S(2)}) collective-permute-start(f32[128,128]{1,0:T(8,128)S(1)} %get-tuple-element.47.push_there), channel_id=1, source_target_pairs={{1,2},{2,1},{3,4},{4,3},{5,6},{6,5},{7,8},{8,7},{9,10},{10,9},{11,... | collective-permute-start | bytes 196616 | tf_op jit(solution)/shard_map/ppermute | solution.py:333
  5.8 0.0 collective-permute-start.3
  5.8 0.0 collective-permute-done.1.other_t
  5.8 0.2 shard_map.57
  6.1 2.0 %collective-permute-done.2.push_here = f32[128,128]{1,0:T(8,128)S(1)} collective-permute-done((f32[128,128]{1,0:T(8,128)S(1)}, f32[128,128]{1,0:T(8,128)S(1)}, u32[]{:S(2)}, u32[]{:S(2)}) %collective-permute-start.2) | collective-permute-done | bytes 65568 | tf_op jit(solution)/shard_map/ppermute | solution.py:333
  8.1 0.2 shard_map.58.w_inner
  8.2 0.2 collective-permute-start.5
  8.4 2.0 %collective-permute-start.4 = (f32[64,128]{1,0:T(8,128)S(1)}, f32[64,128]{1,0:T(8,128)S(1)}, u32[]{:S(2)}, u32[]{:S(2)}) collective-permute-start(f32[64,128]{1,0:T(8,128)S(1)} %get-tuple-element.55), channel_id=1, source_target_pairs={{1,2},{2,1},{3,4},{4,3},{5,6},{6,5},{7,8},{8,7},{9,10},{10,9},{11,... | collective-permute-start | bytes 98312 | tf_op jit(solution)/shard_map/ppermute | solution.py:333
  10.4 0.1 collective-permute-done.3.got
  10.5 0.6 %shard_map.59 = (f32[256,128]{1,0:T(8,128)S(1)}, f32[256,128]{1,0:T(8,128)S(1)}, f32[128,128]{1,0:T(8,128)S(1)}, f32[128,128]{1,0:T(8,128)S(1)}, f32[8,128]{1,0:...) custom-call(bf16[2,256,256]{2,1,0:T(8,128)(2,1)S(1)} %get-tuple-element.39.local, ...), custom_call_target="tpu_custom_call" | custom-call | tf_op jit(solution)/shard_map/pallas_call | solution.py:305
  11.1 1.2 %collective-permute-done.4.got_q = f32[64,128]{1,0:T(8,128)S(1)} collective-permute-done((f32[64,128]{1,0:T(8,128)S(1)}, f32[64,128]{1,0:T(8,128)S(1)}, u32[]{:S(2)}, u32[]{:S(2)}) %collective-permute-start.4) | collective-permute-done | bytes 32800 | tf_op jit(solution)/shard_map/ppermute | solution.py:333
  12.3 0.0 collective-permute-done.5.other_w
  12.3 0.5 %shard_map.60 = f32[16,3,2,128]{3,2,1,0:T(2,128)S(1)} custom-call(f32[8,128]{1,0:T(8,128)S(1)} %get-tuple-element.49.moments, f32[128,128]{1,0:T(8,128)S(1)} %get-tuple-element.50.edge, f32[128,128]{1,0:T(8,128)S(1)} %get-tuple-element.51.edge_r, f32[128,128]{1,0:T(8,128)S(1)} %get-tuple-element.52.y_outer, f32[128,128]{1,0:T(8,128)S(1)} %get-tuple-element.53.pull_r, ...), custom_call_target="tpu_custom_call" | custom-call | tf_op jit(solution)/shard_map/pallas_call | solution.py:305
  12.8 12.8 %all_to_all.5.shares = f32[16,3,2,128]{3,2,1,0:T(2,128)S(1)} all-to-all(f32[16,3,2,128]{3,2,1,0:T(2,128)S(1)} %shard_map.60), channel_id=1, replica_groups=mesh['groups'=2,'patch'=8,'sub'=2] {'patch','sub'}, dimensions={0} | all-to-all | bytes 98304 | tf_op jit(solution)/shard_map/all_to_all | solution.py:377
  25.7 0.8 %shard_map.61 = f32[256,128]{1,0:T(8,128)} custom-call(f32[16,3,2,128]{3,2,1,0:T(2,128)S(1)} %all_to_all.5.shares, f32[256,128]{1,0:T(8,128)S(1)} %get-tuple-element.31.x, f32[256,128]{1,0:T(8,128)S(1)} %get-tuple-element.54.r, f32[256,128]{1,0:T(8,128)S(1)} %get-tuple-element.56.w), custom_call_target="tpu_custom_call" | custom-call | tf_op jit(solution)/shard_map/pallas_call | solution.py:305
Async XLA Ops:
  0.0 2.1 %collective-permute-start = (f32[256,128]{1,0:T(8,128)}, f32[256,128]{1,0:T(8,128)S(1)}, u32[]{:S(2)}, u32[]{:S(2)}) collective-permute-start(f32[256,128]{1,0:T(8,128)} %x_there.1), channel_id=1, source_target_pairs={{0,1},{1,0},{2,3},{3,2},{4,5},{5,4},{6,7},{7,6},{8,9},{9,8},{10,11... | collective-permute-start | bytes 393224 | tf_op jit(solution)/shard_map/ppermute | solution.py:335
  2.7 3.1 %collective-permute-start.1 = (f32[256,128]{1,0:T(8,128)S(1)}, f32[256,128]{1,0:T(8,128)S(1)}, u32[]{:S(2)}, u32[]{:S(2)}) collective-permute-start(f32[256,128]{1,0:T(8,128)S(1)} %get-tuple-element.43.t), channel_id=1, source_target_pairs={{0,1},{1,0},{2,3},{3,2},{4,5},{5,4},{6,7},{7,6},{8,9},{9,8},{10,11... | collective-permute-start | bytes 393224 | tf_op jit(solution)/shard_map/ppermute | solution.py:363
  2.8 5.2 %collective-permute-start.2 = (f32[128,128]{1,0:T(8,128)S(1)}, f32[128,128]{1,0:T(8,128)S(1)}, u32[]{:S(2)}, u32[]{:S(2)}) collective-permute-start(f32[128,128]{1,0:T(8,128)S(1)} %get-tuple-element.47.push_there), channel_id=1, source_target_pairs={{1,2},{2,1},{3,4},{4,3},{5,6},{6,5},{7,8},{8,7},{9,10},{10,9},{11,... | collective-permute-start | bytes 196616 | tf_op jit(solution)/shard_map/ppermute | solution.py:333
  5.8 4.7 %collective-permute-start.3 = (f32[200,128]{1,0:T(8,128)S(1)}, f32[200,128]{1,0:T(8,128)S(1)}, u32[]{:S(2)}, u32[]{:S(2)}) collective-permute-start(f32[200,128]{1,0:T(8,128)S(1)} %get-tuple-element.38.send), channel_id=1, source_target_pairs={{1,2},{2,1},{3,4},{4,3},{5,6},{6,5},{7,8},{8,7},{9,10},{10,9},{11,... | collective-permute-start | bytes 307208 | tf_op jit(solution)/shard_map/ppermute | solution.py:333
  8.2 4.1 %collective-permute-start.5 = (f32[128,128]{1,0:T(8,128)S(1)}, f32[128,128]{1,0:T(8,128)S(1)}, u32[]{:S(2)}, u32[]{:S(2)}) collective-permute-start(f32[128,128]{1,0:T(8,128)S(1)} %shard_map.58.w_inner), channel_id=1, source_target_pairs={{0,1},{1,0},{2,3},{3,2},{4,5},{5,4},{6,7},{7,6},{8,9},{9,8},{10,11... | collective-permute-start | bytes 196616 | tf_op jit(solution)/shard_map/ppermute | solution.py:368
  8.4 3.9 %collective-permute-start.4 = (f32[64,128]{1,0:T(8,128)S(1)}, f32[64,128]{1,0:T(8,128)S(1)}, u32[]{:S(2)}, u32[]{:S(2)}) collective-permute-start(f32[64,128]{1,0:T(8,128)S(1)} %get-tuple-element.55), channel_id=1, source_target_pairs={{1,2},{2,1},{3,4},{4,3},{5,6},{6,5},{7,8},{8,7},{9,10},{10,9},{11,... | collective-permute-start | bytes 98312 | tf_op jit(solution)/shard_map/ppermute | solution.py:333

commit v12 on v10

v12 whole, which is shorter than its diff:
```python
import jax
import jax.numpy as jnp
from jax import lax
from jax.experimental import pallas as pl
from jax.experimental.pallas import tpu as pltpu
from jax.sharding import PartitionSpec as P


AXES = ("patch", "sub")
LEAST_EIGENVALUE = 0.0999
VMEM = pl.BlockSpec(memory_space=pltpu.VMEM)


def halves(a):
    high = a.astype(jnp.bfloat16)
    return high, (a - high.astype(jnp.float32)).astype(jnp.bfloat16)


def dot(a, b):
    a_high, a_low = a[0], a[1]
    b_high, b_low = halves(b)

    def product(p, q):
        return jnp.dot(p, q, preferred_element_type=jnp.float32)

    return product(a_high, b_high) + (product(a_high, b_low) + product(a_low, b_high))


def place():
    return lax.axis_index("patch") * lax.axis_size("sub") + lax.axis_index("sub")


def outer_block(tile):
    side = lax.rem(place(), 2)
    outer = pl.ds(pl.multiple_of(side * tile, tile), tile)
    inner = pl.ds(pl.multiple_of((1 - side) * tile, tile), tile)
    return outer, inner


def flip(x):
    return pltpu.roll(x, x.shape[1] // 2, 1)


def index_of(shape, dimension):
    return lax.broadcasted_iota(jnp.int32, shape, dimension)


def toward(tiles, names, block):
    total = jnp.where(names[0:1, :] == block, tiles[0], 0.0)
    for k in range(1, tiles.shape[0]):
        total += jnp.where(names[k : k + 1, :] == block, tiles[k], 0.0)
    return total


def row_sums(tiles, masses):
    tile = tiles.shape[-1]
    whole = tiles[0]
    for k in range(1, tiles.shape[0]):
        whole += tiles[k]
    eye = index_of((tile, tile), 0) == index_of((tile, tile), 1)
    return jnp.sum(whole + jnp.where(eye, masses[0:1, :], 0.0), axis=1, keepdims=True)


def right_side(names, block, shape):
    vertices = block * shape[0] + index_of(shape, 0)
    return jnp.where(vertices == names[7:8, :], 1.0, 0.0)


def outer_kernel(
    cols_there, tiles_there, mass_there, x_there, sources_there,
    local_outer, diag_outer, t_out_t, x, tiles_inner, names, masses, send, packed,
    cols, tiles, mass, sources, arrived,
):
    tile = tiles.shape[-1]
    half = tile // 2
    slots = tiles.shape[0]
    position = place()
    side = lax.rem(position, 2)
    first = position * 2
    moves = (
        (cols_there, cols),
        (tiles_there.at[side], tiles),
        (x_there, x),
        (mass_there, mass),
        (sources_there, sources),
        (tiles_there.at[1 - side], tiles_inner),
    )
    copies = [pltpu.make_async_copy(start, end, arrived.at[i]) for i, (start, end) in enumerate(moves)]
    for copy in copies:
        copy.start()
    for copy in copies[:-1]:
        copy.wait()
    eye = index_of((tile, tile), 0) == index_of((tile, tile), 1)
    outer, _ = outer_block(tile)
    row = index_of(names.shape, 0)
    named = jnp.broadcast_to(sources[...][None, :], names.shape)
    for k in range(slots):
        named = jnp.where(row == k, cols[1 - side, k], named)
    names[...] = named
    mass_0, mass_1 = mass[0:tile][None, :], mass[tile : 2 * tile][None, :]
    masses[...] = jnp.broadcast_to(jnp.where(side == 0, mass_1, mass_0), masses.shape)

    def one_toward(block):
        slot, scale = jnp.int32(0), 0.0
        for k in range(slots):
            found = cols[side, k] == block
            slot, scale = jnp.where(found, k, slot), jnp.where(found, 1.0, scale)
        return scale * tiles[slot]

    own = jnp.where(cols[side, 0] == first + side, tiles[0], 0.0)
    for k in range(1, slots):
        own += jnp.where(cols[side, k] == first + side, tiles[k], 0.0)
    cross = one_toward(first + 1 - side)
    total = row_sums(tiles, jnp.where(side == 0, mass_0, mass_1))
    diag_outer[...] = jnp.broadcast_to(total, diag_outer.shape)
    store_halves(local_outer, (slice(None), slice(0, tile)), jnp.where(side == 0, -own, -cross))
    store_halves(local_outer, (slice(None), slice(tile, 2 * tile)), jnp.where(side == 0, -cross, -own))
    store_halves(t_out_t, (slice(None),), one_toward(jnp.where(side == 0, first - 1, first + 2)).T)
    x_outer = x[outer, :]
    send[0:tile, :] = (
        right_side(named, first + side, x_outer.shape) - total * x_outer - dot(local_outer, x[...])
    )
    send[tile:, :] = dot(t_out_t, x_outer)
    above_diagonal = index_of((half, tile), 1) > index_of((half, tile), 0)
    packed[0:half, :] = jnp.where(above_diagonal, own[:half], flip(own[half:]))
    diagonal = jnp.sum(jnp.where(eye, total, 0.0), axis=0, keepdims=True)
    packed[half:, :] = jnp.broadcast_to(diagonal, (8, tile))
    copies[-1].wait()


def store_halves(pair, index, value):
    pair[(0, *index)], pair[(1, *index)] = halves(value)


def inner_row_kernel(
    local_outer, diag_outer, x, tiles, names, masses, other_x, send, packed,
    local, diag, t_in, t, q_outer, send_late,
):
    tile = tiles.shape[-1]
    half = tile // 2
    position = place()
    side = lax.rem(position, 2)
    first = position * 2
    outer, inner = outer_block(tile)
    total = row_sums(tiles, masses)
    diag[outer, :] = diag_outer[...]
    diag[inner, :] = jnp.broadcast_to(total, diag_outer.shape)
    own, cross = toward(tiles, names, first + 1 - side), toward(tiles, names, first + side)
    store_halves(local, (inner, slice(0, tile)), jnp.where(side == 0, -cross, -own))
    store_halves(local, (inner, slice(tile, 2 * tile)), jnp.where(side == 0, -own, -cross))
    for k in range(2):
        local[k, outer, :] = local_outer[k]
    store_halves(t_in, (slice(None),), toward(tiles, names, jnp.where(side == 0, first + 2, first - 1)))
    x_inner = x[inner, :]
    t[outer, :] = send[0:tile, :]
    t[inner, :] = (
        right_side(names, first + 1 - side, x_inner.shape)
        - total * x_inner
        - dot(part(local, inner), x[...])
        + dot(t_in, other_x[outer, :])
    )
    q = diag_outer[...] * send[0:tile, :] + dot(local_outer, t[...])
    q_outer[...] = q
    turned = jnp.where(side == 0, flip(q), q)
    first_half = index_of((half, tile), 1) < half
    send_late[0:half, :] = jnp.where(first_half, turned[:half], flip(turned[half:]))
    send_late[half:, :] = packed[...]


def unpack(packed):
    tile = packed.shape[1]
    half = tile // 2
    rows = packed[0:half, :]
    row, column = index_of((half, tile), 0), index_of((half, tile), 1)
    upper = jnp.where(column > row, rows, 0.0)
    lower = flip(jnp.where(column < row, rows, 0.0))
    triangles = jnp.concatenate([upper, lower], axis=0)
    eye = index_of((tile, tile), 0) == index_of((tile, tile), 1)
    diagonal = jnp.sum(jnp.where(eye, packed[half : half + 1, :], 0.0), axis=1, keepdims=True)
    return triangles + triangles.T, diagonal


def outer_columns(tile):
    side = lax.rem(place(), 2)
    return pl.ds(pl.multiple_of(side * tile, tile), tile)


def part(pair, *index):
    return pair[(0, *index)], pair[(1, *index)]


def inner_kernel(local, diag, t_in, t_out_t, t, other_t, q_inner, t_in_t, t_out):
    outer, inner = outer_block(t_in.shape[-1])
    for half in range(2):
        t_in_t[half] = t_in[half].T
        t_out[half] = t_out_t[half].T
    q_inner[...] = (
        diag[inner, :] * t[inner, :] + dot(part(local, inner), t[...]) - dot(t_in, other_t[outer, :])
    )


def image_kernel(local, q_inner, got, w_inner):
    tile = q_inner.shape[0]
    _, inner = outer_block(tile)
    w_inner[...] = q_inner[...] + dot(part(local, inner, outer_columns(tile)), got[tile:, :])


def total(value):
    return jnp.sum(value, axis=0, keepdims=True)


def moment_kernel(
    local, diag, t_in_t, t_out, t_out_t, t, q_outer, send, got, w_inner,
    r, w, there, edge_y_out, edge_r_out, moments, edge_y_in, edge_r_in,
):
    tile = t_out.shape[-1]
    outer, inner = outer_block(tile)
    push_here, push_there = got[tile:, :], send[tile:, :]
    r_outer, r_there = t[outer, :] + push_here, got[0:tile, :] + push_there
    pull = dot(t_out, r_there)
    w_outer = (
        q_outer[...]
        + diag[outer, :] * push_here
        + dot(part(local, outer, outer_columns(tile)), push_here)
        - pull
    )
    r[outer, :] = r_outer
    r[inner, :] = t[inner, :]
    w[outer, :] = w_outer
    w[inner, :] = w_inner[...]
    w_now, r_now = w[...], r[...]
    r_r, r_w = total(r_now * r_now), total(r_now * w_now)
    shift = jnp.where(r_r > 0, r_w / r_r, 0.0)
    y = w_now - shift * r_now
    y_outer = w_outer - shift * r_outer
    a_y = diag[...] * y + dot(local, y)
    y_pull, r_pull = total(y_outer * pull), total(r_outer * pull)
    r_ay = total(r_now * a_y + y * w_now) + y_pull
    moments[...] = jnp.concatenate(
        [r_r, r_w, total(y * y), total(y * a_y), r_ay, r_w + r_pull, shift, y_pull, r_pull]
        + [shift] * (moments.shape[0] - 9),
        axis=0,
    )
    back = dot(t_out_t, r_outer)
    edge_r_out[...] = back
    edge_y_out[...] = dot(t_out_t, y_outer)
    there[...] = -back - shift * r_there
    edge_y_in[...] = dot(t_in_t, w_inner[...] - shift * r[inner, :])
    edge_r_in[...] = dot(t_in_t, r[inner, :])


def share_kernel(
    moments, edge_y_in, edge_r_in, edge_y_out, edge_r_out, there, send, got, other_t, other_w, out
):
    tile = there.shape[0]
    half = tile // 2
    side = lax.rem(place(), 2)
    outer, _ = outer_block(tile)
    shift = moments[6:7, :]
    q_half = got[0:half, :]
    q_flip = flip(q_half)
    q_there = jnp.concatenate(
        [jnp.where(side == 0, q_half, q_flip), jnp.where(side == 0, q_flip, q_half)], axis=0
    )
    own_there, diag_there = unpack(got[half:, :])
    push_there = send[tile:, :]
    y_there = q_there + there[...] + diag_there * push_there - dot(halves(own_there), push_there)
    mine = (index_of(shift.shape, 1) >= half) == (side == 1)
    weight = jnp.where(mine, 2.0, 0.0)
    y_partner = other_w[...] - shift * other_t[outer, :]
    y_ay = total(edge_y_in[...] * y_partner) + weight * total(edge_y_out[...] * y_there)
    r_ay = total(edge_r_in[...] * y_partner)
    r_ay += weight * (total(edge_r_out[...] * y_there) + moments[7:8, :])
    r_ar = weight * moments[8:9, :]
    sums = moments[0:8, :]
    row = index_of(sums.shape, 0)
    for place_of, value in ((3, y_ay), (4, r_ay), (5, r_ar)):
        sums -= jnp.where(row == place_of, value, 0.0)
    for pair in range(out.shape[1]):
        out[:, pair] = jnp.broadcast_to(sums[None, 2 * pair : 2 * pair + 2], out[:, pair].shape)


def finish_kernel(shares, x, r, w, out):
    r_rs, r_ws, spreads, y_ay, r_ay, r_ar = [shares[:, row // 2, row % 2, :] for row in range(6)]
    r_r = jnp.sum(r_rs, axis=0, keepdims=True)
    r_w = jnp.sum(r_ws, axis=0, keepdims=True)
    theta = r_w / r_r
    off = jnp.where(r_rs > 0, r_ws / r_rs, 0.0) - theta
    spread = jnp.sum(spreads + r_rs * off * off, axis=0, keepdims=True)
    energy = jnp.sum(y_ay + off * (r_ay + off * r_ar), axis=0, keepdims=True)
    ratio = spread / (theta * theta * r_r)
    energy = jnp.maximum(energy - ratio * theta * spread, LEAST_EIGENVALUE * spread * (1.0 + ratio))
    step = jnp.where(spread > 0, spread / energy, 0.0)
    first = 1.0 / theta
    out[...] = x[...] + (first + step * (1.0 + ratio)) * r[...] - (step * first) * w[...]


def call(kernel, shapes, *operands, last=False):
    place_out = jax.ShapeDtypeStruct if last else pltpu.VMEM
    outs = [place_out(shape[1:], shape[0]) for shape in shapes]
    return pl.pallas_call(
        kernel,
        out_shape=outs if len(outs) > 1 else outs[0],
        in_specs=[VMEM] * len(operands),
        out_specs=[VMEM] * len(outs) if len(outs) > 1 else VMEM,
    )(*[pltpu.with_memory_space_constraint(operand, pltpu.VMEM) for operand in operands])


def body(block_cols, step_tiles, mass, warm_start, source_ids):
    tile = step_tiles.shape[-1]
    rows, columns = warm_start.shape
    assert block_cols.shape[0] == 2 and columns == tile
    devices = lax.axis_size("patch") * lax.axis_size("sub")
    partner = [(i, i ^ 1) for i in range(devices)]
    groups = lax.axis_size("groups")
    across = []
    for group in range(groups):
        here, there = group * devices, (group + 1) % groups * devices
        for i in range(1, devices - 1, 2):
            across += [(here + i, here + i + 1), (here + i + 1, here + i)]
        across += [(here, there), (here + devices - 1, there + devices - 1)]
    single, slots = jnp.float32, block_cols.shape[1]
    assert slots < 8
    field, block = (single, rows, columns), (single, tile, columns)
    square, late = (jnp.bfloat16, 2, tile, tile), tile // 2 + 8

    def exchange(value):
        return lax.ppermute(value, ("groups",) + AXES, across)

    other_x = lax.ppermute(warm_start, AXES, partner)
    results = [
        (jnp.bfloat16, 2, tile, rows), block, square, field, (single, slots, tile, tile),
        (jnp.int32, 8, tile), (single, 8, tile), (single, 2 * tile, columns), (single, late, columns),
    ]
    local_outer, diag_outer, t_out_t, x, tiles_inner, names, masses, send, packed = pl.pallas_call(
        outer_kernel,
        out_shape=[pltpu.VMEM(shape[1:], shape[0]) for shape in results],
        in_specs=[pl.BlockSpec(memory_space=pl.ANY)] * 5,
        out_specs=[VMEM] * len(results),
        scratch_shapes=[
            pltpu.SMEM(block_cols.shape, jnp.int32),
            pltpu.VMEM((slots, tile, tile), single),
            pltpu.VMEM(mass.shape, single),
            pltpu.VMEM(source_ids.shape, jnp.int32),
            pltpu.SemaphoreType.DMA((6,)),
        ],
        name="outer_kernel",
    )(block_cols, step_tiles, mass, warm_start, source_ids)
    got = exchange(send)
    local, diag, t_in, t, q_outer, send_late = call(
        inner_row_kernel,
        [(jnp.bfloat16, 2, rows, rows), field, square, field, block, (single, tile // 2 + late, columns)],
        local_outer, diag_outer, x, tiles_inner, names, masses, other_x, send, packed,
    )
    got_late = exchange(send_late)
    other_t = lax.ppermute(t, AXES, partner)
    q_inner, t_in_t, t_out = call(
        inner_kernel, [block, square, square], local, diag, t_in, t_out_t, t, other_t
    )
    w_inner = call(image_kernel, [block], local, q_inner, got)
    other_w = lax.ppermute(w_inner, AXES, partner)
    r, w, there, edge_y_out, edge_r_out, moments, edge_y_in, edge_r_in = call(
        moment_kernel, [field, field, block, block, block, (single, 16, columns), block, block],
        local, diag, t_in_t, t_out, t_out_t, t, q_outer, send, got, w_inner,
    )
    shares = call(
        share_kernel, [(single, devices, 3, 2, columns)],
        moments, edge_y_in, edge_r_in, edge_y_out, edge_r_out, there, send, got_late, other_t, other_w,
    )
    shares = lax.all_to_all(shares, AXES, 0, 0)
    return call(finish_kernel, [field], shares, x, r, w, last=True)


def solution(mesh):
    in_specs = (
        P(("groups", "patch", "sub"), None),
        P(("groups", "patch", "sub"), None, None, None),
        P(("groups", "patch", "sub")),
        P(("groups", "patch", "sub"), None),
        P("groups"),
    )
    out_specs = P(("groups", "patch", "sub"), None)
    return jax.shard_map(body, mesh=mesh, in_specs=in_specs, out_specs=out_specs, check_vma=False)
```

time: 27.7 us -> 24.8 us (0.90)
  starting transfers between devices: 5.41 us -> 3.74 us
  waiting for transfers between devices: 4.2 us -> 3.17 us
  blocking collectives: 14 us -> 13.5 us
  Pallas kernels: 3.88 us -> 4.16 us
    ppermute x2, starting transfers between devices: 4.62 us -> 2.85 us  [exchange(): return lax.ppermute(value, ('groups',) + AXES, across)]
    ppermute x1, waiting for transfers between devices: 1.26 us -> 0.01 us  [body(): other_t = lax.ppermute(t, AXES, partner)]
    all_to_all x1, blocking collectives: 14 us -> 13.5 us  [body(): shares = lax.all_to_all(shares, AXES, 0, 0)]
    pallas_call x6, Pallas kernels: 2.53 us -> 2.81 us  [call(): pl.pallas_call(kernel, out_shape=outs if len(outs) > 1 else outs[0], in_s...]
  transfers between devices with their start and end apart: 5 -> 5, of which waited for: 3 -> 3; matrix products, arithmetic and copies ran while one was open for 0% -> 0% of each run, Pallas kernels for 11% -> 10%
where the time goes in v12:
time: 24.8 us; the launch traced here: 24.7 us
  blocking collectives  13.5 us (54%)
  Pallas kernels  4.16 us (17%)
  starting transfers between devices  3.74 us (15%)
  waiting for transfers between devices  3.17 us (13%)
    all_to_all x1, blocking collectives, body(): shares = lax.all_to_all(shares, AXES, 0, 0)  13.5 us
    ppermute x2, waiting for transfers between devices, exchange(): return lax.ppermute(value, ('groups',) + AXES, across)  3.03 us
    ppermute x2, starting transfers between devices, exchange(): return lax.ppermute(value, ('groups',) + AXES, across)  2.85 us
    pallas_call x6, Pallas kernels, call(): pl.pallas_call(kernel, out_shape=outs if len(outs) > 1 else outs[0], in_s...  2.81 us
    pallas_call x1, Pallas kernels, body(): pl.pallas_call(outer_kernel, out_shape=[pltpu.VMEM(shape[1:], shape[0]) f...  1.35 us
  transfers between devices with their start and end apart: 5, of which 3 were waited for; matrix products, arithmetic and copies ran while one was open for 0% of the time, Pallas kernels for 10%

profile of v12, /device:TPU:0, one launch (start us, length us, event | category | flops | bytes accessed | tf_op | source)
XLA Modules:
  0.0 24.7 jit_solution(9885291267649377177)
XLA Ops:
  0.0 0.5 %collective-permute-start = (f32[256,128]{1,0:T(8,128)}, f32[256,128]{1,0:T(8,128)S(1)}, u32[]{:S(2)}, u32[]{:S(2)}) collective-permute-start(f32[256,128]{1,0:T(8,128)} %x_there.1), channel_id=1, source_target_pairs={{0,1},{1,0},{2,3},{3,2},{4,5},{5,4},{6,7},{7,6},{8,9},{9,8},{10,11... | collective-permute-start | bytes 393224 | tf_op jit(solution)/shard_map/ppermute | solution.py:330
  0.5 1.3 %outer_kernel.1 = (bf16[2,128,256]{2,1,0:T(8,128)(2,1)S(1)}, f32[128,128]{1,0:T(8,128)S(1)}, bf16[2,128,128]{2,1,0:T(8,128)(2,1)S(1)}, f32[256,128]{1,0:T(8,128)...) custom-call(s32[2,3]{1,0:T(2,128)} %cols_there.1, ...), custom_call_target="tpu_custom_call" | custom-call | tf_op jit(solution)/shard_map/outer_kernel/pallas_call | solution.py:335
  1.9 0.0 collective-permute-done.other_x
  1.9 0.7 %shard_map.55 = (bf16[2,256,256]{2,1,0:T(8,128)(2,1)S(1)}, f32[256,128]{1,0:T(8,128)S(1)}, bf16[2,128,128]{2,1,0:T(8,128)(2,1)S(1)}, f32[256,128]{1,0:T(8,128)S(...) custom-call(bf16[2,128,256]{2,1,0:T(8,128)(2,1)S(1)} %get-tuple-element.31.local_outer, ...), custom_call_target="tpu_custom_call" | custom-call | tf_op jit(solution)/shard_map/pallas_call | solution.py:301
  2.5 0.2 collective-permute-start.1
  2.8 2.8 %collective-permute-start.2 = (f32[256,128]{1,0:T(8,128)S(1)}, f32[256,128]{1,0:T(8,128)S(1)}, u32[]{:S(2)}, u32[]{:S(2)}) collective-permute-start(f32[256,128]{1,0:T(8,128)S(1)} %get-tuple-element.37.send), channel_id=1, source_target_pairs={{1,2},{2,1},{3,4},{4,3},{5,6},{6,5},{7,8},{8,7},{9,10},{10,9},{11,... | collective-permute-start | bytes 393224 | tf_op jit(solution)/shard_map/ppermute | solution.py:328
  5.6 0.0 collective-permute-start.3
  5.6 0.0 collective-permute-done.1.other_t
  5.6 0.2 shard_map.56
  5.9 2.7 %collective-permute-done.2.got = f32[256,128]{1,0:T(8,128)S(1)} collective-permute-done((f32[256,128]{1,0:T(8,128)S(1)}, f32[256,128]{1,0:T(8,128)S(1)}, u32[]{:S(2)}, u32[]{:S(2)}) %collective-permute-start.2) | collective-permute-done | bytes 131104 | tf_op jit(solution)/shard_map/ppermute | solution.py:328
  8.5 0.2 shard_map.57.w_inner
  8.7 0.2 collective-permute-start.4
  8.9 0.7 %shard_map.58 = (f32[256,128]{1,0:T(8,128)S(1)}, f32[256,128]{1,0:T(8,128)S(1)}, f32[128,128]{1,0:T(8,128)S(1)}, f32[128,128]{1,0:T(8,128)S(1)}, f32[128,128]{1,...) custom-call(bf16[2,256,256]{2,1,0:T(8,128)(2,1)S(1)} %get-tuple-element.39.local, ...), custom_call_target="tpu_custom_call" | custom-call | tf_op jit(solution)/shard_map/pallas_call | solution.py:301
  9.5 0.4 %collective-permute-done.3.got = f32[136,128]{1,0:T(8,128)S(1)} collective-permute-done((f32[136,128]{1,0:T(8,128)S(1)}, f32[136,128]{1,0:T(8,128)S(1)}, u32[]{:S(2)}, u32[]{:S(2)}) %collective-permute-start.3) | collective-permute-done | bytes 69664 | tf_op jit(solution)/shard_map/ppermute | solution.py:328
  9.9 0.1 collective-permute-done.4.other_w
  10.0 0.3 %shard_map.59 = f32[16,3,2,128]{3,2,1,0:T(2,128)S(1)} custom-call(f32[16,128]{1,0:T(8,128)S(1)} %get-tuple-element.48.moments, f32[128,128]{1,0:T(8,128)S(1)} %get-tuple-element.49.edge_y_in, f32[128,128]{1,0:T(8,128)S(1)} %get-tuple-element.50.edge_r_in, f32[128,128]{1,0:T(8,128)S(1)} %get-tuple-element.51.edge_y_out, ...), custom_call_target="tpu_custom_call" | custom-call | tf_op jit(solution)/shard_map/pallas_call | solution.py:301
  10.4 13.5 %all_to_all.5.shares = f32[16,3,2,128]{3,2,1,0:T(2,128)S(1)} all-to-all(f32[16,3,2,128]{3,2,1,0:T(2,128)S(1)} %shard_map.59), channel_id=1, replica_groups=mesh['groups'=2,'patch'=8,'sub'=2] {'patch','sub'}, dimensions={0} | all-to-all | bytes 98304 | tf_op jit(solution)/shard_map/all_to_all | solution.py:370
  23.9 0.8 %shard_map.60 = f32[256,128]{1,0:T(8,128)} custom-call(f32[16,3,2,128]{3,2,1,0:T(2,128)S(1)} %all_to_all.5.shares, f32[256,128]{1,0:T(8,128)S(1)} %get-tuple-element.33.x, f32[256,128]{1,0:T(8,128)S(1)} %get-tuple-element.55.r, f32[256,128]{1,0:T(8,128)S(1)} %get-tuple-element.56.w), custom_call_target="tpu_custom_call" | custom-call | tf_op jit(solution)/shard_map/pallas_call | solution.py:301
Async XLA Ops:
  0.0 1.9 %collective-permute-start = (f32[256,128]{1,0:T(8,128)}, f32[256,128]{1,0:T(8,128)S(1)}, u32[]{:S(2)}, u32[]{:S(2)}) collective-permute-start(f32[256,128]{1,0:T(8,128)} %x_there.1), channel_id=1, source_target_pairs={{0,1},{1,0},{2,3},{3,2},{4,5},{5,4},{6,7},{7,6},{8,9},{9,8},{10,11... | collective-permute-start | bytes 393224 | tf_op jit(solution)/shard_map/ppermute | solution.py:330
  2.5 3.1 %collective-permute-start.1 = (f32[256,128]{1,0:T(8,128)S(1)}, f32[256,128]{1,0:T(8,128)S(1)}, u32[]{:S(2)}, u32[]{:S(2)}) collective-permute-start(f32[256,128]{1,0:T(8,128)S(1)} %get-tuple-element.43.t), channel_id=1, source_target_pairs={{0,1},{1,0},{2,3},{3,2},{4,5},{5,4},{6,7},{7,6},{8,9},{9,8},{10,11... | collective-permute-start | bytes 393224 | tf_op jit(solution)/shard_map/ppermute | solution.py:356
  2.8 5.8 %collective-permute-start.2 = (f32[256,128]{1,0:T(8,128)S(1)}, f32[256,128]{1,0:T(8,128)S(1)}, u32[]{:S(2)}, u32[]{:S(2)}) collective-permute-start(f32[256,128]{1,0:T(8,128)S(1)} %get-tuple-element.37.send), channel_id=1, source_target_pairs={{1,2},{2,1},{3,4},{4,3},{5,6},{6,5},{7,8},{8,7},{9,10},{10,9},{11,... | collective-permute-start | bytes 393224 | tf_op jit(solution)/shard_map/ppermute | solution.py:328
  5.6 4.3 %collective-permute-start.3 = (f32[136,128]{1,0:T(8,128)S(1)}, f32[136,128]{1,0:T(8,128)S(1)}, u32[]{:S(2)}, u32[]{:S(2)}) collective-permute-start(f32[136,128]{1,0:T(8,128)S(1)} %get-tuple-element.54), channel_id=1, source_target_pairs={{1,2},{2,1},{3,4},{4,3},{5,6},{6,5},{7,8},{8,7},{9,10},{10,9},{11,... | collective-permute-start | bytes 208904 | tf_op jit(solution)/shard_map/ppermute | solution.py:328
  8.7 1.3 %collective-permute-start.4 = (f32[128,128]{1,0:T(8,128)S(1)}, f32[128,128]{1,0:T(8,128)S(1)}, u32[]{:S(2)}, u32[]{:S(2)}) collective-permute-start(f32[128,128]{1,0:T(8,128)S(1)} %shard_map.57.w_inner), channel_id=1, source_target_pairs={{0,1},{1,0},{2,3},{3,2},{4,5},{5,4},{6,7},{7,6},{8,9},{9,8},{10,11... | collective-permute-start | bytes 196616 | tf_op jit(solution)/shard_map/ppermute | solution.py:361

commit v13 on v12

--- a/solution.py
+++ b/solution.py
@@ -68,7 +68,7 @@
 
 def outer_kernel(
     cols_there, tiles_there, mass_there, x_there, sources_there,
-    local_outer, diag_outer, t_out_t, x, tiles_inner, names, masses, send, packed,
+    local_outer, diag_outer, t_out_t, x, tiles_inner, names, masses, push, send,
     cols, tiles, mass, sources, arrived,
 ):
     tile = tiles.shape[-1]
@@ -120,11 +120,11 @@
     send[0:tile, :] = (
         right_side(named, first + side, x_outer.shape) - total * x_outer - dot(local_outer, x[...])
     )
-    send[tile:, :] = dot(t_out_t, x_outer)
+    push[...] = dot(t_out_t, x_outer)
     above_diagonal = index_of((half, tile), 1) > index_of((half, tile), 0)
-    packed[0:half, :] = jnp.where(above_diagonal, own[:half], flip(own[half:]))
+    send[tile : tile + half, :] = jnp.where(above_diagonal, own[:half], flip(own[half:]))
     diagonal = jnp.sum(jnp.where(eye, total, 0.0), axis=0, keepdims=True)
-    packed[half:, :] = jnp.broadcast_to(diagonal, (8, tile))
+    send[tile + half :, :] = jnp.broadcast_to(diagonal, (8, tile))
     copies[-1].wait()
 
 
@@ -133,8 +133,8 @@
 
 
 def inner_row_kernel(
-    local_outer, diag_outer, x, tiles, names, masses, other_x, send, packed,
-    local, diag, t_in, t, q_outer, send_late,
+    local_outer, diag_outer, x, tiles, names, masses, other_x, send,
+    local, diag, t_in, t, q_outer, q_send,
 ):
     tile = tiles.shape[-1]
     half = tile // 2
@@ -163,8 +163,7 @@
     q_outer[...] = q
     turned = jnp.where(side == 0, flip(q), q)
     first_half = index_of((half, tile), 1) < half
-    send_late[0:half, :] = jnp.where(first_half, turned[:half], flip(turned[half:]))
-    send_late[half:, :] = packed[...]
+    q_send[...] = jnp.where(first_half, turned[:half], flip(turned[half:]))
 
 
 def unpack(packed):
@@ -199,10 +198,10 @@
     )
 
 
-def image_kernel(local, q_inner, got, w_inner):
+def image_kernel(local, q_inner, push_here, w_inner):
     tile = q_inner.shape[0]
     _, inner = outer_block(tile)
-    w_inner[...] = q_inner[...] + dot(part(local, inner, outer_columns(tile)), got[tile:, :])
+    w_inner[...] = q_inner[...] + dot(part(local, inner, outer_columns(tile)), push_here[...])
 
 
 def total(value):
@@ -210,12 +209,12 @@
 
 
 def moment_kernel(
-    local, diag, t_in_t, t_out, t_out_t, t, q_outer, send, got, w_inner,
+    local, diag, t_in_t, t_out, t_out_t, t, q_outer, push_here, push_there, got, w_inner,
     r, w, there, edge_y_out, edge_r_out, moments, edge_y_in, edge_r_in,
 ):
     tile = t_out.shape[-1]
     outer, inner = outer_block(tile)
-    push_here, push_there = got[tile:, :], send[tile:, :]
+    push_here, push_there = push_here[...], push_there[...]
     r_outer, r_there = t[outer, :] + push_here, got[0:tile, :] + push_there
     pull = dot(t_out, r_there)
     w_outer = (
@@ -244,27 +243,26 @@
     back = dot(t_out_t, r_outer)
     edge_r_out[...] = back
     edge_y_out[...] = dot(t_out_t, y_outer)
-    there[...] = -back - shift * r_there
+    own_there, diag_there = unpack(got[tile:, :])
+    there[...] = diag_there * push_there - dot(halves(own_there), push_there) - back - shift * r_there
     edge_y_in[...] = dot(t_in_t, w_inner[...] - shift * r[inner, :])
     edge_r_in[...] = dot(t_in_t, r[inner, :])
 
 
 def share_kernel(
-    moments, edge_y_in, edge_r_in, edge_y_out, edge_r_out, there, send, got, other_t, other_w, out
+    moments, edge_y_in, edge_r_in, edge_y_out, edge_r_out, there, got_q, other_t, other_w, out
 ):
     tile = there.shape[0]
     half = tile // 2
     side = lax.rem(place(), 2)
     outer, _ = outer_block(tile)
     shift = moments[6:7, :]
-    q_half = got[0:half, :]
+    q_half = got_q[...]
     q_flip = flip(q_half)
     q_there = jnp.concatenate(
         [jnp.where(side == 0, q_half, q_flip), jnp.where(side == 0, q_flip, q_half)], axis=0
     )
-    own_there, diag_there = unpack(got[half:, :])
-    push_there = send[tile:, :]
-    y_there = q_there + there[...] + diag_there * push_there - dot(halves(own_there), push_there)
+    y_there = q_there + there[...]
     mine = (index_of(shift.shape, 1) >= half) == (side == 1)
     weight = jnp.where(mine, 2.0, 0.0)
     y_partner = other_w[...] - shift * other_t[outer, :]
@@ -322,7 +320,7 @@
     single, slots = jnp.float32, block_cols.shape[1]
     assert slots < 8
     field, block = (single, rows, columns), (single, tile, columns)
-    square, late = (jnp.bfloat16, 2, tile, tile), tile // 2 + 8
+    square, halfway = (jnp.bfloat16, 2, tile, tile), (single, tile // 2, columns)
 
     def exchange(value):
         return lax.ppermute(value, ("groups",) + AXES, across)
@@ -330,9 +328,9 @@
     other_x = lax.ppermute(warm_start, AXES, partner)
     results = [
         (jnp.bfloat16, 2, tile, rows), block, square, field, (single, slots, tile, tile),
-        (jnp.int32, 8, tile), (single, 8, tile), (single, 2 * tile, columns), (single, late, columns),
+        (jnp.int32, 8, tile), (single, 8, tile), block, (single, tile + tile // 2 + 8, columns),
     ]
-    local_outer, diag_outer, t_out_t, x, tiles_inner, names, masses, send, packed = pl.pallas_call(
+    local_outer, diag_outer, t_out_t, x, tiles_inner, names, masses, push_there, send = pl.pallas_call(
         outer_kernel,
         out_shape=[pltpu.VMEM(shape[1:], shape[0]) for shape in results],
         in_specs=[pl.BlockSpec(memory_space=pl.ANY)] * 5,
@@ -346,26 +344,27 @@
         ],
         name="outer_kernel",
     )(block_cols, step_tiles, mass, warm_start, source_ids)
+    push_here = exchange(push_there)
     got = exchange(send)
-    local, diag, t_in, t, q_outer, send_late = call(
+    local, diag, t_in, t, q_outer, q_send = call(
         inner_row_kernel,
-        [(jnp.bfloat16, 2, rows, rows), field, square, field, block, (single, tile // 2 + late, columns)],
-        local_outer, diag_outer, x, tiles_inner, names, masses, other_x, send, packed,
-    )
-    got_late = exchange(send_late)
+        [(jnp.bfloat16, 2, rows, rows), field, square, field, block, halfway],
+        local_outer, diag_outer, x, tiles_inner, names, masses, other_x, send,
+    )
+    got_q = exchange(q_send)
     other_t = lax.ppermute(t, AXES, partner)
     q_inner, t_in_t, t_out = call(
         inner_kernel, [block, square, square], local, diag, t_in, t_out_t, t, other_t
     )
-    w_inner = call(image_kernel, [block], local, q_inner, got)
+    w_inner = call(image_kernel, [block], local, q_inner, push_here)
     other_w = lax.ppermute(w_inner, AXES, partner)
     r, w, there, edge_y_out, edge_r_out, moments, edge_y_in, edge_r_in = call(
         moment_kernel, [field, field, block, block, block, (single, 16, columns), block, block],
-        local, diag, t_in_t, t_out, t_out_t, t, q_outer, send, got, w_inner,
+        local, diag, t_in_t, t_out, t_out_t, t, q_outer, push_here, push_there, got, w_inner,
     )
     shares = call(
         share_kernel, [(single, devices, 3, 2, columns)],
-        moments, edge_y_in, edge_r_in, edge_y_out, edge_r_out, there, send, got_late, other_t, other_w,
+        moments, edge_y_in, edge_r_in, edge_y_out, edge_r_out, there, got_q, other_t, other_w,
     )
     shares = lax.all_to_all(shares, AXES, 0, 0)
     return call(finish_kernel, [field], shares, x, r, w, last=True)

time: 24.8 us -> 26 us (1.048)
  starting transfers between devices: 3.74 us -> 5.76 us
  blocking collectives: 13.5 us -> 12.8 us
    ppermute x2 -> x3, starting transfers between devices: 2.85 us -> 4.87 us  [exchange(): return lax.ppermute(value, ('groups',) + AXES, across)]
    all_to_all x1, blocking collectives: 13.5 us -> 12.8 us  [body(): shares = lax.all_to_all(shares, AXES, 0, 0)]
    ppermute x2 -> x3, waiting for transfers between devices: 3.03 us -> 3.2 us  [exchange(): return lax.ppermute(value, ('groups',) + AXES, across)]
  transfers between devices with their start and end apart: 5 -> 6, of which waited for: 3 -> 3; matrix products, arithmetic and copies ran while one was open for 0% -> 0% of each run, Pallas kernels for 10% -> 9%
where the time goes in v13:
time: 26 us; the launch traced here: 25.8 us
  blocking collectives  12.8 us (49%)
  starting transfers between devices  5.76 us (22%)
  Pallas kernels  3.95 us (15%)
  waiting for transfers between devices  3.21 us (12%)
    all_to_all x1, blocking collectives, body(): shares = lax.all_to_all(shares, AXES, 0, 0)  12.8 us
    ppermute x3, starting transfers between devices, exchange(): return lax.ppermute(value, ('groups',) + AXES, across)  4.87 us
    ppermute x3, waiting for transfers between devices, exchange(): return lax.ppermute(value, ('groups',) + AXES, across)  3.2 us
    pallas_call x6, Pallas kernels, call(): pl.pallas_call(kernel, out_shape=outs if len(outs) > 1 else outs[0], in_s...  2.6 us
    pallas_call x1, Pallas kernels, body(): pl.pallas_call(outer_kernel, out_shape=[pltpu.VMEM(shape[1:], shape[0]) f...  1.35 us
  transfers between devices with their start and end apart: 6, of which 3 were waited for; matrix products, arithmetic and copies ran while one was open for 0% of the time, Pallas kernels for 9%

profile of v13, /device:TPU:0, one launch (start us, length us, event | category | flops | bytes accessed | tf_op | source)
XLA Modules:
  0.0 25.8 jit_solution(12626496931219243484)
XLA Ops:
  0.0 0.5 %collective-permute-start = (f32[256,128]{1,0:T(8,128)}, f32[256,128]{1,0:T(8,128)S(1)}, u32[]{:S(2)}, u32[]{:S(2)}) collective-permute-start(f32[256,128]{1,0:T(8,128)} %x_there.1), channel_id=1, source_target_pairs={{0,1},{1,0},{2,3},{3,2},{4,5},{5,4},{6,7},{7,6},{8,9},{9,8},{10,11... | collective-permute-start | bytes 393224 | tf_op jit(solution)/shard_map/ppermute | solution.py:328
  0.5 1.3 %outer_kernel.1 = (bf16[2,128,256]{2,1,0:T(8,128)(2,1)S(1)}, f32[128,128]{1,0:T(8,128)S(1)}, bf16[2,128,128]{2,1,0:T(8,128)(2,1)S(1)}, f32[256,128]{1,0:T(8,128)...) custom-call(s32[2,3]{1,0:T(2,128)} %cols_there.1, ...), custom_call_target="tpu_custom_call" | custom-call | tf_op jit(solution)/shard_map/outer_kernel/pallas_call | solution.py:333
  1.9 0.0 collective-permute-done.other_x
  1.9 0.7 %shard_map.55 = (bf16[2,256,256]{2,1,0:T(8,128)(2,1)S(1)}, f32[256,128]{1,0:T(8,128)S(1)}, bf16[2,128,128]{2,1,0:T(8,128)(2,1)S(1)}, f32[256,128]{1,0:T(8,128)S(...) custom-call(bf16[2,128,256]{2,1,0:T(8,128)(2,1)S(1)} %get-tuple-element.31.local_outer, ...), custom_call_target="tpu_custom_call" | custom-call | tf_op jit(solution)/shard_map/pallas_call | solution.py:299
  2.5 0.2 collective-permute-start.1
  2.8 2.8 %collective-permute-start.2 = (f32[128,128]{1,0:T(8,128)S(1)}, f32[128,128]{1,0:T(8,128)S(1)}, u32[]{:S(2)}, u32[]{:S(2)}) collective-permute-start(f32[128,128]{1,0:T(8,128)S(1)} %get-tuple-element.46.push_there), channel_id=1, source_target_pairs={{1,2},{2,1},{3,4},{4,3},{5,6},{6,5},{7,8},{8,7},{9,10},{10,9},{11,... | collective-permute-start | bytes 196616 | tf_op jit(solution)/shard_map/ppermute | solution.py:326
  5.6 0.0 collective-permute-start.3
  5.6 0.0 collective-permute-done.1.other_t
  5.6 0.2 shard_map.56
  5.9 2.0 %collective-permute-done.2.push_here = f32[128,128]{1,0:T(8,128)S(1)} collective-permute-done((f32[128,128]{1,0:T(8,128)S(1)}, f32[128,128]{1,0:T(8,128)S(1)}, u32[]{:S(2)}, u32[]{:S(2)}) %collective-permute-start.2) | collective-permute-done | bytes 65568 | tf_op jit(solution)/shard_map/ppermute | solution.py:326
  7.8 0.2 shard_map.57.w_inner
  8.0 0.2 collective-permute-start.5
  8.2 2.0 %collective-permute-start.4 = (f32[64,128]{1,0:T(8,128)S(1)}, f32[64,128]{1,0:T(8,128)S(1)}, u32[]{:S(2)}, u32[]{:S(2)}) collective-permute-start(f32[64,128]{1,0:T(8,128)S(1)} %get-tuple-element.54), channel_id=1, source_target_pairs={{1,2},{2,1},{3,4},{4,3},{5,6},{6,5},{7,8},{8,7},{9,10},{10,9},{11,... | collective-permute-start | bytes 98312 | tf_op jit(solution)/shard_map/ppermute | solution.py:326
  10.2 0.1 collective-permute-done.3.got
  10.3 0.7 %shard_map.58 = (f32[256,128]{1,0:T(8,128)S(1)}, f32[256,128]{1,0:T(8,128)S(1)}, f32[128,128]{1,0:T(8,128)S(1)}, f32[128,128]{1,0:T(8,128)S(1)}, f32[128,128]{1,...) custom-call(bf16[2,256,256]{2,1,0:T(8,128)(2,1)S(1)} %get-tuple-element.38.local, ...), custom_call_target="tpu_custom_call" | custom-call | tf_op jit(solution)/shard_map/pallas_call | solution.py:299
  10.9 1.2 %collective-permute-done.4.got_q = f32[64,128]{1,0:T(8,128)S(1)} collective-permute-done((f32[64,128]{1,0:T(8,128)S(1)}, f32[64,128]{1,0:T(8,128)S(1)}, u32[]{:S(2)}, u32[]{:S(2)}) %collective-permute-start.4) | collective-permute-done | bytes 32800 | tf_op jit(solution)/shard_map/ppermute | solution.py:326
  12.1 0.0 collective-permute-done.5.other_w
  12.1 0.1 shard_map.59
  12.2 12.8 %all_to_all.5.shares = f32[16,3,2,128]{3,2,1,0:T(2,128)S(1)} all-to-all(f32[16,3,2,128]{3,2,1,0:T(2,128)S(1)} %shard_map.59), channel_id=1, replica_groups=mesh['groups'=2,'patch'=8,'sub'=2] {'patch','sub'}, dimensions={0} | all-to-all | bytes 98304 | tf_op jit(solution)/shard_map/all_to_all | solution.py:369
  25.0 0.8 %shard_map.60 = f32[256,128]{1,0:T(8,128)} custom-call(f32[16,3,2,128]{3,2,1,0:T(2,128)S(1)} %all_to_all.5.shares, f32[256,128]{1,0:T(8,128)S(1)} %get-tuple-element.33.x, f32[256,128]{1,0:T(8,128)S(1)} %get-tuple-element.55.r, f32[256,128]{1,0:T(8,128)S(1)} %get-tuple-element.56.w), custom_call_target="tpu_custom_call" | custom-call | tf_op jit(solution)/shard_map/pallas_call | solution.py:299
Async XLA Ops:
  0.0 1.9 %collective-permute-start = (f32[256,128]{1,0:T(8,128)}, f32[256,128]{1,0:T(8,128)S(1)}, u32[]{:S(2)}, u32[]{:S(2)}) collective-permute-start(f32[256,128]{1,0:T(8,128)} %x_there.1), channel_id=1, source_target_pairs={{0,1},{1,0},{2,3},{3,2},{4,5},{5,4},{6,7},{7,6},{8,9},{9,8},{10,11... | collective-permute-start | bytes 393224 | tf_op jit(solution)/shard_map/ppermute | solution.py:328
  2.5 3.1 %collective-permute-start.1 = (f32[256,128]{1,0:T(8,128)S(1)}, f32[256,128]{1,0:T(8,128)S(1)}, u32[]{:S(2)}, u32[]{:S(2)}) collective-permute-start(f32[256,128]{1,0:T(8,128)S(1)} %get-tuple-element.42.t), channel_id=1, source_target_pairs={{0,1},{1,0},{2,3},{3,2},{4,5},{5,4},{6,7},{7,6},{8,9},{9,8},{10,11... | collective-permute-start | bytes 393224 | tf_op jit(solution)/shard_map/ppermute | solution.py:355
  2.8 5.1 %collective-permute-start.2 = (f32[128,128]{1,0:T(8,128)S(1)}, f32[128,128]{1,0:T(8,128)S(1)}, u32[]{:S(2)}, u32[]{:S(2)}) collective-permute-start(f32[128,128]{1,0:T(8,128)S(1)} %get-tuple-element.46.push_there), channel_id=1, source_target_pairs={{1,2},{2,1},{3,4},{4,3},{5,6},{6,5},{7,8},{8,7},{9,10},{10,9},{11,... | collective-permute-start | bytes 196616 | tf_op jit(solution)/shard_map/ppermute | solution.py:326
  5.6 4.7 %collective-permute-start.3 = (f32[200,128]{1,0:T(8,128)S(1)}, f32[200,128]{1,0:T(8,128)S(1)}, u32[]{:S(2)}, u32[]{:S(2)}) collective-permute-start(f32[200,128]{1,0:T(8,128)S(1)} %get-tuple-element.37.send), channel_id=1, source_target_pairs={{1,2},{2,1},{3,4},{4,3},{5,6},{6,5},{7,8},{8,7},{9,10},{10,9},{11,... | collective-permute-start | bytes 307208 | tf_op jit(solution)/shard_map/ppermute | solution.py:326
  8.0 4.1 %collective-permute-start.5 = (f32[128,128]{1,0:T(8,128)S(1)}, f32[128,128]{1,0:T(8,128)S(1)}, u32[]{:S(2)}, u32[]{:S(2)}) collective-permute-start(f32[128,128]{1,0:T(8,128)S(1)} %shard_map.57.w_inner), channel_id=1, source_target_pairs={{0,1},{1,0},{2,3},{3,2},{4,5},{5,4},{6,7},{7,6},{8,9},{9,8},{10,11... | collective-permute-start | bytes 196616 | tf_op jit(solution)/shard_map/ppermute | solution.py:360
  8.2 3.9 %collective-permute-start.4 = (f32[64,128]{1,0:T(8,128)S(1)}, f32[64,128]{1,0:T(8,128)S(1)}, u32[]{:S(2)}, u32[]{:S(2)}) collective-permute-start(f32[64,128]{1,0:T(8,128)S(1)} %get-tuple-element.54), channel_id=1, source_target_pairs={{1,2},{2,1},{3,4},{4,3},{5,6},{6,5},{7,8},{8,7},{9,10},{10,9},{11,... | collective-permute-start | bytes 98312 | tf_op jit(solution)/shard_map/ppermute | solution.py:326

commit v14 on v13

--- a/solution.py
+++ b/solution.py
@@ -68,7 +68,7 @@
 
 def outer_kernel(
     cols_there, tiles_there, mass_there, x_there, sources_there,
-    local_outer, diag_outer, t_out_t, x, tiles_inner, names, masses, push, send,
+    local_outer, diag_outer, t_out_t, x, x_inner, tiles_inner, names, masses, push, send,
     cols, tiles, mass, sources, arrived,
 ):
     tile = tiles.shape[-1]
@@ -91,7 +91,8 @@
     for copy in copies[:-1]:
         copy.wait()
     eye = index_of((tile, tile), 0) == index_of((tile, tile), 1)
-    outer, _ = outer_block(tile)
+    outer, inner = outer_block(tile)
+    x_inner[...] = x[inner, :]
     row = index_of(names.shape, 0)
     named = jnp.broadcast_to(sources[...][None, :], names.shape)
     for k in range(slots):
@@ -134,7 +135,7 @@
 
 def inner_row_kernel(
     local_outer, diag_outer, x, tiles, names, masses, other_x, send,
-    local, diag, t_in, t, q_outer, q_send,
+    local, diag, t_in, t, t_inner, q_outer, q_send,
 ):
     tile = tiles.shape[-1]
     half = tile // 2
@@ -153,12 +154,13 @@
     store_halves(t_in, (slice(None),), toward(tiles, names, jnp.where(side == 0, first + 2, first - 1)))
     x_inner = x[inner, :]
     t[outer, :] = send[0:tile, :]
-    t[inner, :] = (
+    t_inner[...] = (
         right_side(names, first + 1 - side, x_inner.shape)
         - total * x_inner
         - dot(part(local, inner), x[...])
-        + dot(t_in, other_x[outer, :])
-    )
+        + dot(t_in, other_x[...])
+    )
+    t[inner, :] = t_inner[...]
     q = diag_outer[...] * send[0:tile, :] + dot(local_outer, t[...])
     q_outer[...] = q
     turned = jnp.where(side == 0, flip(q), q)
@@ -188,20 +190,18 @@
     return pair[(0, *index)], pair[(1, *index)]
 
 
-def inner_kernel(local, diag, t_in, t_out_t, t, other_t, q_inner, t_in_t, t_out):
-    outer, inner = outer_block(t_in.shape[-1])
+def inner_kernel(local, diag, t_in, t_out_t, t, other_t, push_here, w_inner, t_in_t, t_out):
+    tile = t_in.shape[-1]
+    _, inner = outer_block(tile)
+    w_inner[...] = (
+        diag[inner, :] * t[inner, :]
+        + dot(part(local, inner), t[...])
+        + dot(part(local, inner, outer_columns(tile)), push_here[...])
+        - dot(t_in, other_t[...])
+    )
     for half in range(2):
         t_in_t[half] = t_in[half].T
         t_out[half] = t_out_t[half].T
-    q_inner[...] = (
-        diag[inner, :] * t[inner, :] + dot(part(local, inner), t[...]) - dot(t_in, other_t[outer, :])
-    )
-
-
-def image_kernel(local, q_inner, push_here, w_inner):
-    tile = q_inner.shape[0]
-    _, inner = outer_block(tile)
-    w_inner[...] = q_inner[...] + dot(part(local, inner, outer_columns(tile)), push_here[...])
 
 
 def total(value):
@@ -255,7 +255,6 @@
     tile = there.shape[0]
     half = tile // 2
     side = lax.rem(place(), 2)
-    outer, _ = outer_block(tile)
     shift = moments[6:7, :]
     q_half = got_q[...]
     q_flip = flip(q_half)
@@ -265,7 +264,7 @@
     y_there = q_there + there[...]
     mine = (index_of(shift.shape, 1) >= half) == (side == 1)
     weight = jnp.where(mine, 2.0, 0.0)
-    y_partner = other_w[...] - shift * other_t[outer, :]
+    y_partner = other_w[...] - shift * other_t[...]
     y_ay = total(edge_y_in[...] * y_partner) + weight * total(edge_y_out[...] * y_there)
     r_ay = total(edge_r_in[...] * y_partner)
     r_ay += weight * (total(edge_r_out[...] * y_there) + moments[7:8, :])
@@ -325,12 +324,11 @@
     def exchange(value):
         return lax.ppermute(value, ("groups",) + AXES, across)
 
-    other_x = lax.ppermute(warm_start, AXES, partner)
     results = [
-        (jnp.bfloat16, 2, tile, rows), block, square, field, (single, slots, tile, tile),
+        (jnp.bfloat16, 2, tile, rows), block, square, field, block, (single, slots, tile, tile),
         (jnp.int32, 8, tile), (single, 8, tile), block, (single, tile + tile // 2 + 8, columns),
     ]
-    local_outer, diag_outer, t_out_t, x, tiles_inner, names, masses, push_there, send = pl.pallas_call(
+    local_outer, diag_outer, t_out_t, x, x_inner, tiles_inner, names, masses, push_there, send = pl.pallas_call(
         outer_kernel,
         out_shape=[pltpu.VMEM(shape[1:], shape[0]) for shape in results],
         in_specs=[pl.BlockSpec(memory_space=pl.ANY)] * 5,
@@ -345,18 +343,18 @@
         name="outer_kernel",
     )(block_cols, step_tiles, mass, warm_start, source_ids)
     push_here = exchange(push_there)
+    other_x = lax.ppermute(x_inner, AXES, partner)
     got = exchange(send)
-    local, diag, t_in, t, q_outer, q_send = call(
+    local, diag, t_in, t, t_inner, q_outer, q_send = call(
         inner_row_kernel,
-        [(jnp.bfloat16, 2, rows, rows), field, square, field, block, halfway],
+        [(jnp.bfloat16, 2, rows, rows), field, square, field, block, block, halfway],
         local_outer, diag_outer, x, tiles_inner, names, masses, other_x, send,
     )
     got_q = exchange(q_send)
-    other_t = lax.ppermute(t, AXES, partner)
-    q_inner, t_in_t, t_out = call(
-        inner_kernel, [block, square, square], local, diag, t_in, t_out_t, t, other_t
-    )
-    w_inner = call(image_kernel, [block], local, q_inner, push_here)
+    other_t = lax.ppermute(t_inner, AXES, partner)
+    w_inner, t_in_t, t_out = call(
+        inner_kernel, [block, square, square], local, diag, t_in, t_out_t, t, other_t, push_here
+    )
     other_w = lax.ppermute(w_inner, AXES, partner)
     r, w, there, edge_y_out, edge_r_out, moments, edge_y_in, edge_r_in = call(
         moment_kernel, [field, field, block, block, block, (single, 16, columns), block, block],

time: 26 us -> 25 us (0.962)
  waiting for transfers between devices: 3.21 us -> 1.33 us
  starting transfers between devices: 5.76 us -> 6.93 us
    ppermute x3, waiting for transfers between devices: 3.2 us -> 1.32 us  [exchange(): return lax.ppermute(value, ('groups',) + AXES, across)]
    ppermute x3, starting transfers between devices: 4.87 us -> 6.02 us  [exchange(): return lax.ppermute(value, ('groups',) + AXES, across)]
    pallas_call x6 -> x5, Pallas kernels: 2.6 us -> 2.46 us  [call(): pl.pallas_call(kernel, out_shape=outs if len(outs) > 1 else outs[0], in_s...]
  transfers between devices with their start and end apart: 6 -> 6, of which waited for: 3 -> 2; matrix products, arithmetic and copies ran while one was open for 0% -> 0% of each run, Pallas kernels for 9% -> 6%
where the time goes in v14:
time: 25 us; the launch traced here: 24.8 us
  blocking collectives  12.7 us (51%)
  starting transfers between devices  6.93 us (28%)
  Pallas kernels  3.81 us (15%)
  waiting for transfers between devices  1.33 us (5%)
    all_to_all x1, blocking collectives, body(): shares = lax.all_to_all(shares, AXES, 0, 0)  12.7 us
    ppermute x3, starting transfers between devices, exchange(): return lax.ppermute(value, ('groups',) + AXES, across)  6.02 us
    pallas_call x5, Pallas kernels, call(): pl.pallas_call(kernel, out_shape=outs if len(outs) > 1 else outs[0], in_s...  2.46 us
    pallas_call x1, Pallas kernels, body(): pl.pallas_call(outer_kernel, out_shape=[pltpu.VMEM(shape[1:], shape[0]) f...  1.35 us
    ppermute x3, waiting for transfers between devices, exchange(): return lax.ppermute(value, ('groups',) + AXES, across)  1.32 us
    ppermute x1, starting transfers between devices, body(): other_x = lax.ppermute(x_inner, AXES, partner)  0.56 us
  transfers between devices with their start and end apart: 6, of which 2 were waited for; matrix products, arithmetic and copies ran while one was open for 0% of the time, Pallas kernels for 6%

profile of v14, /device:TPU:0, one launch (start us, length us, event | category | flops | bytes accessed | tf_op | source)
XLA Modules:
  0.0 24.8 jit_solution(14620101157992733102)
XLA Ops:
  0.0 1.3 %outer_kernel.1 = (bf16[2,128,256]{2,1,0:T(8,128)(2,1)S(1)}, f32[128,128]{1,0:T(8,128)S(1)}, bf16[2,128,128]{2,1,0:T(8,128)(2,1)S(1)}, f32[256,128]{1,0:T(8,128)...) custom-call(s32[2,3]{1,0:T(2,128)} %cols_there.1, ...), custom_call_target="tpu_custom_call" | custom-call | tf_op jit(solution)/shard_map/outer_kernel/pallas_call | solution.py:331
  1.4 0.6 %collective-permute-start = (f32[128,128]{1,0:T(8,128)S(1)}, f32[128,128]{1,0:T(8,128)S(1)}, u32[]{:S(2)}, u32[]{:S(2)}) collective-permute-start(f32[128,128]{1,0:T(8,128)S(1)} %get-tuple-element.39), channel_id=1, source_target_pairs={{0,1},{1,0},{2,3},{3,2},{4,5},{5,4},{6,7},{7,6},{8,9},{9,8},{10,11... | collective-permute-start | bytes 196616 | tf_op jit(solution)/shard_map/ppermute | solution.py:346
  1.9 2.6 %collective-permute-start.2 = (f32[128,128]{1,0:T(8,128)S(1)}, f32[128,128]{1,0:T(8,128)S(1)}, u32[]{:S(2)}, u32[]{:S(2)}) collective-permute-start(f32[128,128]{1,0:T(8,128)S(1)} %get-tuple-element.47.push_there), channel_id=1, source_target_pairs={{1,2},{2,1},{3,4},{4,3},{5,6},{6,5},{7,8},{8,7},{9,10},{10,9},{11,... | collective-permute-start | bytes 196616 | tf_op jit(solution)/shard_map/ppermute | solution.py:325
  4.5 0.0 collective-permute-done.other_x
  4.5 0.6 %shard_map.55 = (bf16[2,256,256]{2,1,0:T(8,128)(2,1)S(1)}, f32[256,128]{1,0:T(8,128)S(1)}, bf16[2,128,128]{2,1,0:T(8,128)(2,1)S(1)}, f32[256,128]{1,0:T(8,128)S(...) custom-call(bf16[2,128,256]{2,1,0:T(8,128)(2,1)S(1)} %get-tuple-element.33.local_outer, ...), custom_call_target="tpu_custom_call" | custom-call | tf_op jit(solution)/shard_map/pallas_call | solution.py:298
  5.1 0.1 collective-permute-start.1
  5.3 1.5 %collective-permute-start.3 = (f32[200,128]{1,0:T(8,128)S(1)}, f32[200,128]{1,0:T(8,128)S(1)}, u32[]{:S(2)}, u32[]{:S(2)}) collective-permute-start(f32[200,128]{1,0:T(8,128)S(1)} %get-tuple-element.40.send), channel_id=1, source_target_pairs={{1,2},{2,1},{3,4},{4,3},{5,6},{6,5},{7,8},{8,7},{9,10},{10,9},{11,... | collective-permute-start | bytes 307208 | tf_op jit(solution)/shard_map/ppermute | solution.py:325
  6.8 0.0 collective-permute-done.2.push_here
  6.8 0.0 collective-permute-done.1.other_t
  6.8 0.3 %shard_map.56 = (f32[128,128]{1,0:T(8,128)S(1)}, bf16[2,128,128]{2,1,0:T(8,128)(2,1)S(1)}, bf16[2,128,128]{2,1,0:T(8,128)(2,1)S(1)}) custom-call(bf16[2,256,256]{2,1,0:T(8,128)(2,1)S(1)} %get-tuple-element.41.local, f32[256,128]{1,0:T(8,128)S(1)} %get-tuple-element.42.diag, bf16[2,128,128]{2,1,0:T(8,128)(2,1)S(1)} %get-tuple-element.43.t_in, ...), custom_call_target="tpu_custom_call" | custom-call | tf_op jit(solution)/shard_map/pallas_call | solution.py:298
  7.1 0.2 collective-permute-start.5
  7.3 1.9 %collective-permute-start.4 = (f32[64,128]{1,0:T(8,128)S(1)}, f32[64,128]{1,0:T(8,128)S(1)}, u32[]{:S(2)}, u32[]{:S(2)}) collective-permute-start(f32[64,128]{1,0:T(8,128)S(1)} %get-tuple-element.58), channel_id=1, source_target_pairs={{1,2},{2,1},{3,4},{4,3},{5,6},{6,5},{7,8},{8,7},{9,10},{10,9},{11,... | collective-permute-start | bytes 98312 | tf_op jit(solution)/shard_map/ppermute | solution.py:325
  9.2 0.7 %collective-permute-done.3.got = f32[200,128]{1,0:T(8,128)S(1)} collective-permute-done((f32[200,128]{1,0:T(8,128)S(1)}, f32[200,128]{1,0:T(8,128)S(1)}, u32[]{:S(2)}, u32[]{:S(2)}) %collective-permute-start.3) | collective-permute-done | bytes 102432 | tf_op jit(solution)/shard_map/ppermute | solution.py:325
  10.0 0.7 %shard_map.57 = (f32[256,128]{1,0:T(8,128)S(1)}, f32[256,128]{1,0:T(8,128)S(1)}, f32[128,128]{1,0:T(8,128)S(1)}, f32[128,128]{1,0:T(8,128)S(1)}, f32[128,128]{1,...) custom-call(bf16[2,256,256]{2,1,0:T(8,128)(2,1)S(1)} %get-tuple-element.41.local, ...), custom_call_target="tpu_custom_call" | custom-call | tf_op jit(solution)/shard_map/pallas_call | solution.py:298
  10.6 0.6 %collective-permute-done.4.got_q = f32[64,128]{1,0:T(8,128)S(1)} collective-permute-done((f32[64,128]{1,0:T(8,128)S(1)}, f32[64,128]{1,0:T(8,128)S(1)}, u32[]{:S(2)}, u32[]{:S(2)}) %collective-permute-start.4) | collective-permute-done | bytes 32800 | tf_op jit(solution)/shard_map/ppermute | solution.py:325
  11.2 0.0 collective-permute-done.5.other_w
  11.2 0.1 shard_map.58
  11.3 12.7 %all_to_all.5.shares = f32[16,3,2,128]{3,2,1,0:T(2,128)S(1)} all-to-all(f32[16,3,2,128]{3,2,1,0:T(2,128)S(1)} %shard_map.58), channel_id=1, replica_groups=mesh['groups'=2,'patch'=8,'sub'=2] {'patch','sub'}, dimensions={0} | all-to-all | bytes 98304 | tf_op jit(solution)/shard_map/all_to_all | solution.py:367
  24.1 0.8 %shard_map.59 = f32[256,128]{1,0:T(8,128)} custom-call(f32[16,3,2,128]{3,2,1,0:T(2,128)S(1)} %all_to_all.5.shares, f32[256,128]{1,0:T(8,128)S(1)} %get-tuple-element.35.x, f32[256,128]{1,0:T(8,128)S(1)} %get-tuple-element.59.r, f32[256,128]{1,0:T(8,128)S(1)} %get-tuple-element.60.w), custom_call_target="tpu_custom_call" | custom-call | tf_op jit(solution)/shard_map/pallas_call | solution.py:298
Async XLA Ops:
  1.4 3.1 %collective-permute-start = (f32[128,128]{1,0:T(8,128)S(1)}, f32[128,128]{1,0:T(8,128)S(1)}, u32[]{:S(2)}, u32[]{:S(2)}) collective-permute-start(f32[128,128]{1,0:T(8,128)S(1)} %get-tuple-element.39), channel_id=1, source_target_pairs={{0,1},{1,0},{2,3},{3,2},{4,5},{5,4},{6,7},{7,6},{8,9},{9,8},{10,11... | collective-permute-start | bytes 196616 | tf_op jit(solution)/shard_map/ppermute | solution.py:346
  1.9 4.9 %collective-permute-start.2 = (f32[128,128]{1,0:T(8,128)S(1)}, f32[128,128]{1,0:T(8,128)S(1)}, u32[]{:S(2)}, u32[]{:S(2)}) collective-permute-start(f32[128,128]{1,0:T(8,128)S(1)} %get-tuple-element.47.push_there), channel_id=1, source_target_pairs={{1,2},{2,1},{3,4},{4,3},{5,6},{6,5},{7,8},{8,7},{9,10},{10,9},{11,... | collective-permute-start | bytes 196616 | tf_op jit(solution)/shard_map/ppermute | solution.py:325
  5.1 1.7 %collective-permute-start.1 = (f32[128,128]{1,0:T(8,128)S(1)}, f32[128,128]{1,0:T(8,128)S(1)}, u32[]{:S(2)}, u32[]{:S(2)}) collective-permute-start(f32[128,128]{1,0:T(8,128)S(1)} %get-tuple-element.46), channel_id=1, source_target_pairs={{0,1},{1,0},{2,3},{3,2},{4,5},{5,4},{6,7},{7,6},{8,9},{9,8},{10,11... | collective-permute-start | bytes 196616 | tf_op jit(solution)/shard_map/ppermute | solution.py:354
  5.3 4.7 %collective-permute-start.3 = (f32[200,128]{1,0:T(8,128)S(1)}, f32[200,128]{1,0:T(8,128)S(1)}, u32[]{:S(2)}, u32[]{:S(2)}) collective-permute-start(f32[200,128]{1,0:T(8,128)S(1)} %get-tuple-element.40.send), channel_id=1, source_target_pairs={{1,2},{2,1},{3,4},{4,3},{5,6},{6,5},{7,8},{8,7},{9,10},{10,9},{11,... | collective-permute-start | bytes 307208 | tf_op jit(solution)/shard_map/ppermute | solution.py:325
  7.1 4.1 %collective-permute-start.5 = (f32[128,128]{1,0:T(8,128)S(1)}, f32[128,128]{1,0:T(8,128)S(1)}, u32[]{:S(2)}, u32[]{:S(2)}) collective-permute-start(f32[128,128]{1,0:T(8,128)S(1)} %get-tuple-element.51.w_inner), channel_id=1, source_target_pairs={{0,1},{1,0},{2,3},{3,2},{4,5},{5,4},{6,7},{7,6},{8,9},{9,8},{10,11... | collective-permute-start | bytes 196616 | tf_op jit(solution)/shard_map/ppermute | solution.py:358
  7.3 3.9 %collective-permute-start.4 = (f32[64,128]{1,0:T(8,128)S(1)}, f32[64,128]{1,0:T(8,128)S(1)}, u32[]{:S(2)}, u32[]{:S(2)}) collective-permute-start(f32[64,128]{1,0:T(8,128)S(1)} %get-tuple-element.58), channel_id=1, source_target_pairs={{1,2},{2,1},{3,4},{4,3},{5,6},{6,5},{7,8},{8,7},{9,10},{10,9},{11,... | collective-permute-start | bytes 98312 | tf_op jit(solution)/shard_map/ppermute | solution.py:325

commit v15 on v14

--- a/solution.py
+++ b/solution.py
@@ -161,7 +161,11 @@
         + dot(t_in, other_x[...])
     )
     t[inner, :] = t_inner[...]
-    q = diag_outer[...] * send[0:tile, :] + dot(local_outer, t[...])
+    q = (
+        diag_outer[...] * send[0:tile, :]
+        + dot(part(local_outer, slice(None), outer_columns(tile)), send[0:tile, :])
+        + dot(part(local_outer, slice(None), inner_columns(tile)), t_inner[...])
+    )
     q_outer[...] = q
     turned = jnp.where(side == 0, flip(q), q)
     first_half = index_of((half, tile), 1) < half
@@ -184,6 +188,11 @@
 def outer_columns(tile):
     side = lax.rem(place(), 2)
     return pl.ds(pl.multiple_of(side * tile, tile), tile)
+
+
+def inner_columns(tile):
+    side = lax.rem(place(), 2)
+    return pl.ds(pl.multiple_of((1 - side) * tile, tile), tile)
 
 
 def part(pair, *index):

time: 25 us -> 25 us (level)
  no operation moved by 1% of the time
where the time goes in v15:
time: 25 us; the launch traced here: 24.8 us
  blocking collectives  12.8 us (51%)
  starting transfers between devices  6.98 us (28%)
  Pallas kernels  3.76 us (15%)
  waiting for transfers between devices  1.27 us (5%)
    all_to_all x1, blocking collectives, body(): shares = lax.all_to_all(shares, AXES, 0, 0)  12.8 us
    ppermute x3, starting transfers between devices, exchange(): return lax.ppermute(value, ('groups',) + AXES, across)  6.08 us
    pallas_call x5, Pallas kernels, call(): pl.pallas_call(kernel, out_shape=outs if len(outs) > 1 else outs[0], in_s...  2.41 us
    pallas_call x1, Pallas kernels, body(): pl.pallas_call(outer_kernel, out_shape=[pltpu.VMEM(shape[1:], shape[0]) f...  1.35 us
    ppermute x3, waiting for transfers between devices, exchange(): return lax.ppermute(value, ('groups',) + AXES, across)  1.26 us
    ppermute x1, starting transfers between devices, body(): other_x = lax.ppermute(x_inner, AXES, partner)  0.56 us
  transfers between devices with their start and end apart: 6, of which 2 were waited for; matrix products, arithmetic and copies ran while one was open for 0% of the time, Pallas kernels for 6%

profile of v15, /device:TPU:0, one launch (start us, length us, event | category | flops | bytes accessed | tf_op | source)
XLA Modules:
  0.0 24.8 jit_solution(14182112178597045884)
XLA Ops:
  0.0 1.3 %outer_kernel.1 = (bf16[2,128,256]{2,1,0:T(8,128)(2,1)S(1)}, f32[128,128]{1,0:T(8,128)S(1)}, bf16[2,128,128]{2,1,0:T(8,128)(2,1)S(1)}, f32[256,128]{1,0:T(8,128)...) custom-call(s32[2,3]{1,0:T(2,128)} %cols_there.1, ...), custom_call_target="tpu_custom_call" | custom-call | tf_op jit(solution)/shard_map/outer_kernel/pallas_call | solution.py:340
  1.4 0.6 %collective-permute-start = (f32[128,128]{1,0:T(8,128)S(1)}, f32[128,128]{1,0:T(8,128)S(1)}, u32[]{:S(2)}, u32[]{:S(2)}) collective-permute-start(f32[128,128]{1,0:T(8,128)S(1)} %get-tuple-element.39), channel_id=1, source_target_pairs={{0,1},{1,0},{2,3},{3,2},{4,5},{5,4},{6,7},{7,6},{8,9},{9,8},{10,11... | collective-permute-start | bytes 196616 | tf_op jit(solution)/shard_map/ppermute | solution.py:355
  1.9 2.6 %collective-permute-start.2 = (f32[128,128]{1,0:T(8,128)S(1)}, f32[128,128]{1,0:T(8,128)S(1)}, u32[]{:S(2)}, u32[]{:S(2)}) collective-permute-start(f32[128,128]{1,0:T(8,128)S(1)} %get-tuple-element.47.push_there), channel_id=1, source_target_pairs={{1,2},{2,1},{3,4},{4,3},{5,6},{6,5},{7,8},{8,7},{9,10},{10,9},{11,... | collective-permute-start | bytes 196616 | tf_op jit(solution)/shard_map/ppermute | solution.py:334
  4.5 0.0 collective-permute-done.other_x
  4.5 0.6 %shard_map.55 = (bf16[2,256,256]{2,1,0:T(8,128)(2,1)S(1)}, f32[256,128]{1,0:T(8,128)S(1)}, bf16[2,128,128]{2,1,0:T(8,128)(2,1)S(1)}, f32[256,128]{1,0:T(8,128)S(...) custom-call(bf16[2,128,256]{2,1,0:T(8,128)(2,1)S(1)} %get-tuple-element.33.local_outer, ...), custom_call_target="tpu_custom_call" | custom-call | tf_op jit(solution)/shard_map/pallas_call | solution.py:307
  5.1 0.1 collective-permute-start.1
  5.2 1.5 %collective-permute-start.3 = (f32[200,128]{1,0:T(8,128)S(1)}, f32[200,128]{1,0:T(8,128)S(1)}, u32[]{:S(2)}, u32[]{:S(2)}) collective-permute-start(f32[200,128]{1,0:T(8,128)S(1)} %get-tuple-element.40.send), channel_id=1, source_target_pairs={{1,2},{2,1},{3,4},{4,3},{5,6},{6,5},{7,8},{8,7},{9,10},{10,9},{11,... | collective-permute-start | bytes 307208 | tf_op jit(solution)/shard_map/ppermute | solution.py:334
  6.8 0.0 collective-permute-done.2.push_here
  6.8 0.0 collective-permute-done.1.other_t
  6.8 0.3 %shard_map.56 = (f32[128,128]{1,0:T(8,128)S(1)}, bf16[2,128,128]{2,1,0:T(8,128)(2,1)S(1)}, bf16[2,128,128]{2,1,0:T(8,128)(2,1)S(1)}) custom-call(bf16[2,256,256]{2,1,0:T(8,128)(2,1)S(1)} %get-tuple-element.41.local, f32[256,128]{1,0:T(8,128)S(1)} %get-tuple-element.42.diag, bf16[2,128,128]{2,1,0:T(8,128)(2,1)S(1)} %get-tuple-element.43.t_in, ...), custom_call_target="tpu_custom_call" | custom-call | tf_op jit(solution)/shard_map/pallas_call | solution.py:307
  7.0 0.2 collective-permute-start.5
  7.2 2.0 %collective-permute-start.4 = (f32[64,128]{1,0:T(8,128)S(1)}, f32[64,128]{1,0:T(8,128)S(1)}, u32[]{:S(2)}, u32[]{:S(2)}) collective-permute-start(f32[64,128]{1,0:T(8,128)S(1)} %get-tuple-element.58), channel_id=1, source_target_pairs={{1,2},{2,1},{3,4},{4,3},{5,6},{6,5},{7,8},{8,7},{9,10},{10,9},{11,... | collective-permute-start | bytes 98312 | tf_op jit(solution)/shard_map/ppermute | solution.py:334
  9.2 0.7 %collective-permute-done.3.got = f32[200,128]{1,0:T(8,128)S(1)} collective-permute-done((f32[200,128]{1,0:T(8,128)S(1)}, f32[200,128]{1,0:T(8,128)S(1)}, u32[]{:S(2)}, u32[]{:S(2)}) %collective-permute-start.3) | collective-permute-done | bytes 102432 | tf_op jit(solution)/shard_map/ppermute | solution.py:334
  9.9 0.7 %shard_map.57 = (f32[256,128]{1,0:T(8,128)S(1)}, f32[256,128]{1,0:T(8,128)S(1)}, f32[128,128]{1,0:T(8,128)S(1)}, f32[128,128]{1,0:T(8,128)S(1)}, f32[128,128]{1,...) custom-call(bf16[2,256,256]{2,1,0:T(8,128)(2,1)S(1)} %get-tuple-element.41.local, ...), custom_call_target="tpu_custom_call" | custom-call | tf_op jit(solution)/shard_map/pallas_call | solution.py:307
  10.6 0.6 %collective-permute-done.4.got_q = f32[64,128]{1,0:T(8,128)S(1)} collective-permute-done((f32[64,128]{1,0:T(8,128)S(1)}, f32[64,128]{1,0:T(8,128)S(1)}, u32[]{:S(2)}, u32[]{:S(2)}) %collective-permute-start.4) | collective-permute-done | bytes 32800 | tf_op jit(solution)/shard_map/ppermute | solution.py:334
  11.2 0.0 collective-permute-done.5.other_w
  11.2 0.1 shard_map.58
  11.3 12.8 %all_to_all.5.shares = f32[16,3,2,128]{3,2,1,0:T(2,128)S(1)} all-to-all(f32[16,3,2,128]{3,2,1,0:T(2,128)S(1)} %shard_map.58), channel_id=1, replica_groups=mesh['groups'=2,'patch'=8,'sub'=2] {'patch','sub'}, dimensions={0} | all-to-all | bytes 98304 | tf_op jit(solution)/shard_map/all_to_all | solution.py:376
  24.1 0.8 %shard_map.59 = f32[256,128]{1,0:T(8,128)} custom-call(f32[16,3,2,128]{3,2,1,0:T(2,128)S(1)} %all_to_all.5.shares, f32[256,128]{1,0:T(8,128)S(1)} %get-tuple-element.35.x, f32[256,128]{1,0:T(8,128)S(1)} %get-tuple-element.59.r, f32[256,128]{1,0:T(8,128)S(1)} %get-tuple-element.60.w), custom_call_target="tpu_custom_call" | custom-call | tf_op jit(solution)/shard_map/pallas_call | solution.py:307
Async XLA Ops:
  1.4 3.1 %collective-permute-start = (f32[128,128]{1,0:T(8,128)S(1)}, f32[128,128]{1,0:T(8,128)S(1)}, u32[]{:S(2)}, u32[]{:S(2)}) collective-permute-start(f32[128,128]{1,0:T(8,128)S(1)} %get-tuple-element.39), channel_id=1, source_target_pairs={{0,1},{1,0},{2,3},{3,2},{4,5},{5,4},{6,7},{7,6},{8,9},{9,8},{10,11... | collective-permute-start | bytes 196616 | tf_op jit(solution)/shard_map/ppermute | solution.py:355
  1.9 4.8 %collective-permute-start.2 = (f32[128,128]{1,0:T(8,128)S(1)}, f32[128,128]{1,0:T(8,128)S(1)}, u32[]{:S(2)}, u32[]{:S(2)}) collective-permute-start(f32[128,128]{1,0:T(8,128)S(1)} %get-tuple-element.47.push_there), channel_id=1, source_target_pairs={{1,2},{2,1},{3,4},{4,3},{5,6},{6,5},{7,8},{8,7},{9,10},{10,9},{11,... | collective-permute-start | bytes 196616 | tf_op jit(solution)/shard_map/ppermute | solution.py:334
  5.1 1.7 %collective-permute-start.1 = (f32[128,128]{1,0:T(8,128)S(1)}, f32[128,128]{1,0:T(8,128)S(1)}, u32[]{:S(2)}, u32[]{:S(2)}) collective-permute-start(f32[128,128]{1,0:T(8,128)S(1)} %get-tuple-element.46), channel_id=1, source_target_pairs={{0,1},{1,0},{2,3},{3,2},{4,5},{5,4},{6,7},{7,6},{8,9},{9,8},{10,11... | collective-permute-start | bytes 196616 | tf_op jit(solution)/shard_map/ppermute | solution.py:363
  5.2 4.7 %collective-permute-start.3 = (f32[200,128]{1,0:T(8,128)S(1)}, f32[200,128]{1,0:T(8,128)S(1)}, u32[]{:S(2)}, u32[]{:S(2)}) collective-permute-start(f32[200,128]{1,0:T(8,128)S(1)} %get-tuple-element.40.send), channel_id=1, source_target_pairs={{1,2},{2,1},{3,4},{4,3},{5,6},{6,5},{7,8},{8,7},{9,10},{10,9},{11,... | collective-permute-start | bytes 307208 | tf_op jit(solution)/shard_map/ppermute | solution.py:334
  7.0 4.1 %collective-permute-start.5 = (f32[128,128]{1,0:T(8,128)S(1)}, f32[128,128]{1,0:T(8,128)S(1)}, u32[]{:S(2)}, u32[]{:S(2)}) collective-permute-start(f32[128,128]{1,0:T(8,128)S(1)} %get-tuple-element.51.w_inner), channel_id=1, source_target_pairs={{0,1},{1,0},{2,3},{3,2},{4,5},{5,4},{6,7},{7,6},{8,9},{9,8},{10,11... | collective-permute-start | bytes 196616 | tf_op jit(solution)/shard_map/ppermute | solution.py:367
  7.2 3.9 %collective-permute-start.4 = (f32[64,128]{1,0:T(8,128)S(1)}, f32[64,128]{1,0:T(8,128)S(1)}, u32[]{:S(2)}, u32[]{:S(2)}) collective-permute-start(f32[64,128]{1,0:T(8,128)S(1)} %get-tuple-element.58), channel_id=1, source_target_pairs={{1,2},{2,1},{3,4},{4,3},{5,6},{6,5},{7,8},{8,7},{9,10},{10,9},{11,... | collective-permute-start | bytes 98312 | tf_op jit(solution)/shard_map/ppermute | solution.py:334

commit v16 on v15

--- a/solution.py
+++ b/solution.py
@@ -217,23 +217,28 @@
     return jnp.sum(value, axis=0, keepdims=True)
 
 
+def residual_kernel(local, diag, t_in_t, t_out_t, t, q_outer, push_here, r, w_outer, edge_r_out, edge_r_in):
+    tile = t_in_t.shape[-1]
+    outer, inner = outer_block(tile)
+    push = push_here[...]
+    r_outer = t[outer, :] + push
+    r[outer, :] = r_outer
+    r[inner, :] = t[inner, :]
+    w_outer[...] = q_outer[...] + diag[outer, :] * push + dot(part(local, outer, outer_columns(tile)), push)
+    edge_r_out[...] = dot(t_out_t, r_outer)
+    edge_r_in[...] = dot(t_in_t, t[inner, :])
+
+
 def moment_kernel(
-    local, diag, t_in_t, t_out, t_out_t, t, q_outer, push_here, push_there, got, w_inner,
-    r, w, there, edge_y_out, edge_r_out, moments, edge_y_in, edge_r_in,
+    local, diag, t_in_t, t_out, t_out_t, r, w_local, edge_r_out, push_there, got, w_inner,
+    w, there, edge_y_out, moments, edge_y_in,
 ):
     tile = t_out.shape[-1]
     outer, inner = outer_block(tile)
-    push_here, push_there = push_here[...], push_there[...]
-    r_outer, r_there = t[outer, :] + push_here, got[0:tile, :] + push_there
+    push = push_there[...]
+    r_outer, r_there = r[outer, :], got[0:tile, :] + push
     pull = dot(t_out, r_there)
-    w_outer = (
-        q_outer[...]
-        + diag[outer, :] * push_here
-        + dot(part(local, outer, outer_columns(tile)), push_here)
-        - pull
-    )
-    r[outer, :] = r_outer
-    r[inner, :] = t[inner, :]
+    w_outer = w_local[...] - pull
     w[outer, :] = w_outer
     w[inner, :] = w_inner[...]
     w_now, r_now = w[...], r[...]
@@ -249,13 +254,10 @@
         + [shift] * (moments.shape[0] - 9),
         axis=0,
     )
-    back = dot(t_out_t, r_outer)
-    edge_r_out[...] = back
     edge_y_out[...] = dot(t_out_t, y_outer)
     own_there, diag_there = unpack(got[tile:, :])
-    there[...] = diag_there * push_there - dot(halves(own_there), push_there) - back - shift * r_there
+    there[...] = diag_there * push - dot(halves(own_there), push) - edge_r_out[...] - shift * r_there
     edge_y_in[...] = dot(t_in_t, w_inner[...] - shift * r[inner, :])
-    edge_r_in[...] = dot(t_in_t, r[inner, :])
 
 
 def share_kernel(
@@ -365,9 +367,13 @@
         inner_kernel, [block, square, square], local, diag, t_in, t_out_t, t, other_t, push_here
     )
     other_w = lax.ppermute(w_inner, AXES, partner)
-    r, w, there, edge_y_out, edge_r_out, moments, edge_y_in, edge_r_in = call(
-        moment_kernel, [field, field, block, block, block, (single, 16, columns), block, block],
-        local, diag, t_in_t, t_out, t_out_t, t, q_outer, push_here, push_there, got, w_inner,
+    r, w_local, edge_r_out, edge_r_in = call(
+        residual_kernel, [field, block, block, block],
+        local, diag, t_in_t, t_out_t, t, q_outer, push_here,
+    )
+    w, there, edge_y_out, moments, edge_y_in = call(
+        moment_kernel, [field, block, block, (single, 16, columns), block],
+        local, diag, t_in_t, t_out, t_out_t, r, w_local, edge_r_out, push_there, got, w_inner,
     )
     shares = call(
         share_kernel, [(single, devices, 3, 2, columns)],

time: 25 us -> 25 us (level)
    pallas_call x5 -> x6, Pallas kernels: 2.41 us -> 2.54 us  [call(): pl.pallas_call(kernel, out_shape=outs if len(outs) > 1 else outs[0], in_s...]
  transfers between devices with their start and end apart: 6 -> 6, of which waited for: 2 -> 2; matrix products, arithmetic and copies ran while one was open for 0% -> 0% of each run, Pallas kernels for 6% -> 7%
where the time goes in v16:
time: 25 us; the launch traced here: 24.8 us
  blocking collectives  12.8 us (51%)
  starting transfers between devices  6.98 us (28%)
  Pallas kernels  3.88 us (16%)
  waiting for transfers between devices  1.12 us (4%)
    all_to_all x1, blocking collectives, body(): shares = lax.all_to_all(shares, AXES, 0, 0)  12.8 us
    ppermute x3, starting transfers between devices, exchange(): return lax.ppermute(value, ('groups',) + AXES, across)  6.08 us
    pallas_call x6, Pallas kernels, call(): pl.pallas_call(kernel, out_shape=outs if len(outs) > 1 else outs[0], in_s...  2.54 us
    pallas_call x1, Pallas kernels, body(): pl.pallas_call(outer_kernel, out_shape=[pltpu.VMEM(shape[1:], shape[0]) f...  1.35 us
    ppermute x3, waiting for transfers between devices, exchange(): return lax.ppermute(value, ('groups',) + AXES, across)  1.11 us
    ppermute x1, starting transfers between devices, body(): other_x = lax.ppermute(x_inner, AXES, partner)  0.56 us
  transfers between devices with their start and end apart: 6, of which 2 were waited for; matrix products, arithmetic and copies ran while one was open for 0% of the time, Pallas kernels for 7%

profile of v16, /device:TPU:0, one launch (start us, length us, event | category | flops | bytes accessed | tf_op | source)
XLA Modules:
  0.0 24.8 jit_solution(9729458636981289225)
XLA Ops:
  0.0 1.3 %outer_kernel.1 = (bf16[2,128,256]{2,1,0:T(8,128)(2,1)S(1)}, f32[128,128]{1,0:T(8,128)S(1)}, bf16[2,128,128]{2,1,0:T(8,128)(2,1)S(1)}, f32[256,128]{1,0:T(8,128)...) custom-call(s32[2,3]{1,0:T(2,128)} %cols_there.1, ...), custom_call_target="tpu_custom_call" | custom-call | tf_op jit(solution)/shard_map/outer_kernel/pallas_call | solution.py:342
  1.4 0.6 %collective-permute-start = (f32[128,128]{1,0:T(8,128)S(1)}, f32[128,128]{1,0:T(8,128)S(1)}, u32[]{:S(2)}, u32[]{:S(2)}) collective-permute-start(f32[128,128]{1,0:T(8,128)S(1)} %get-tuple-element.40), channel_id=1, source_target_pairs={{0,1},{1,0},{2,3},{3,2},{4,5},{5,4},{6,7},{7,6},{8,9},{9,8},{10,11... | collective-permute-start | bytes 196616 | tf_op jit(solution)/shard_map/ppermute | solution.py:357
  1.9 2.6 %collective-permute-start.2 = (f32[128,128]{1,0:T(8,128)S(1)}, f32[128,128]{1,0:T(8,128)S(1)}, u32[]{:S(2)}, u32[]{:S(2)}) collective-permute-start(f32[128,128]{1,0:T(8,128)S(1)} %get-tuple-element.48.push_there), channel_id=1, source_target_pairs={{1,2},{2,1},{3,4},{4,3},{5,6},{6,5},{7,8},{8,7},{9,10},{10,9},{11,... | collective-permute-start | bytes 196616 | tf_op jit(solution)/shard_map/ppermute | solution.py:336
  4.5 0.0 collective-permute-done.other_x
  4.5 0.6 %shard_map.55 = (bf16[2,256,256]{2,1,0:T(8,128)(2,1)S(1)}, f32[256,128]{1,0:T(8,128)S(1)}, bf16[2,128,128]{2,1,0:T(8,128)(2,1)S(1)}, f32[256,128]{1,0:T(8,128)S(...) custom-call(bf16[2,128,256]{2,1,0:T(8,128)(2,1)S(1)} %get-tuple-element.34.local_outer, ...), custom_call_target="tpu_custom_call" | custom-call | tf_op jit(solution)/shard_map/pallas_call | solution.py:309
  5.1 0.1 collective-permute-start.1
  5.2 1.5 %collective-permute-start.3 = (f32[200,128]{1,0:T(8,128)S(1)}, f32[200,128]{1,0:T(8,128)S(1)}, u32[]{:S(2)}, u32[]{:S(2)}) collective-permute-start(f32[200,128]{1,0:T(8,128)S(1)} %get-tuple-element.41.send), channel_id=1, source_target_pairs={{1,2},{2,1},{3,4},{4,3},{5,6},{6,5},{7,8},{8,7},{9,10},{10,9},{11,... | collective-permute-start | bytes 307208 | tf_op jit(solution)/shard_map/ppermute | solution.py:336
  6.8 0.0 collective-permute-done.2.push_here
  6.8 0.0 collective-permute-done.1.other_t
  6.8 0.3 %shard_map.56 = (f32[128,128]{1,0:T(8,128)S(1)}, bf16[2,128,128]{2,1,0:T(8,128)(2,1)S(1)}, bf16[2,128,128]{2,1,0:T(8,128)(2,1)S(1)}) custom-call(bf16[2,256,256]{2,1,0:T(8,128)(2,1)S(1)} %get-tuple-element.42.local, f32[256,128]{1,0:T(8,128)S(1)} %get-tuple-element.43.diag, bf16[2,128,128]{2,1,0:T(8,128)(2,1)S(1)} %get-tuple-element.44.t_in, ...), custom_call_target="tpu_custom_call" | custom-call | tf_op jit(solution)/shard_map/pallas_call | solution.py:309
  7.0 0.2 collective-permute-start.5
  7.2 2.0 %collective-permute-start.4 = (f32[64,128]{1,0:T(8,128)S(1)}, f32[64,128]{1,0:T(8,128)S(1)}, u32[]{:S(2)}, u32[]{:S(2)}) collective-permute-start(f32[64,128]{1,0:T(8,128)S(1)} %get-tuple-element.61), channel_id=1, source_target_pairs={{1,2},{2,1},{3,4},{4,3},{5,6},{6,5},{7,8},{8,7},{9,10},{10,9},{11,... | collective-permute-start | bytes 98312 | tf_op jit(solution)/shard_map/ppermute | solution.py:336
  9.2 0.2 shard_map.57
  9.5 0.4 %collective-permute-done.3.got = f32[200,128]{1,0:T(8,128)S(1)} collective-permute-done((f32[200,128]{1,0:T(8,128)S(1)}, f32[200,128]{1,0:T(8,128)S(1)}, u32[]{:S(2)}, u32[]{:S(2)}) %collective-permute-start.3) | collective-permute-done | bytes 102432 | tf_op jit(solution)/shard_map/ppermute | solution.py:336
  9.9 0.6 %shard_map.58 = (f32[256,128]{1,0:T(8,128)S(1)}, f32[128,128]{1,0:T(8,128)S(1)}, f32[128,128]{1,0:T(8,128)S(1)}, f32[16,128]{1,0:T(8,128)S(1)}, f32[128,128]{1,0:T(8,128)S(1)}) custom-call(bf16[2,256,256]{2,1,0:T(8,128)(2,1)S(1)} %get-tuple-element.42.local, f32[256,128]{1,0:T(8,128)S(1)} %get-tuple-element.43.diag, ...), custom_call_target="tpu_custom_call" | custom-call | tf_op jit(solution)/shard_map/pallas_call | solution.py:309
  10.5 0.7 %collective-permute-done.4.got_q = f32[64,128]{1,0:T(8,128)S(1)} collective-permute-done((f32[64,128]{1,0:T(8,128)S(1)}, f32[64,128]{1,0:T(8,128)S(1)}, u32[]{:S(2)}, u32[]{:S(2)}) %collective-permute-start.4) | collective-permute-done | bytes 32800 | tf_op jit(solution)/shard_map/ppermute | solution.py:336
  11.2 0.0 collective-permute-done.5.other_w
  11.2 0.1 shard_map.59
  11.3 12.8 %all_to_all.5.shares = f32[16,3,2,128]{3,2,1,0:T(2,128)S(1)} all-to-all(f32[16,3,2,128]{3,2,1,0:T(2,128)S(1)} %shard_map.59), channel_id=1, replica_groups=mesh['groups'=2,'patch'=8,'sub'=2] {'patch','sub'}, dimensions={0} | all-to-all | bytes 98304 | tf_op jit(solution)/shard_map/all_to_all | solution.py:382
  24.0 0.8 %shard_map.60 = f32[256,128]{1,0:T(8,128)} custom-call(f32[16,3,2,128]{3,2,1,0:T(2,128)S(1)} %all_to_all.5.shares, f32[256,128]{1,0:T(8,128)S(1)} %get-tuple-element.36.x, f32[256,128]{1,0:T(8,128)S(1)} %get-tuple-element.52.r, f32[256,128]{1,0:T(8,128)S(1)} %get-tuple-element.62.w), custom_call_target="tpu_custom_call" | custom-call | tf_op jit(solution)/shard_map/pallas_call | solution.py:309
Async XLA Ops:
  1.4 3.1 %collective-permute-start = (f32[128,128]{1,0:T(8,128)S(1)}, f32[128,128]{1,0:T(8,128)S(1)}, u32[]{:S(2)}, u32[]{:S(2)}) collective-permute-start(f32[128,128]{1,0:T(8,128)S(1)} %get-tuple-element.40), channel_id=1, source_target_pairs={{0,1},{1,0},{2,3},{3,2},{4,5},{5,4},{6,7},{7,6},{8,9},{9,8},{10,11... | collective-permute-start | bytes 196616 | tf_op jit(solution)/shard_map/ppermute | solution.py:357
  1.9 4.8 %collective-permute-start.2 = (f32[128,128]{1,0:T(8,128)S(1)}, f32[128,128]{1,0:T(8,128)S(1)}, u32[]{:S(2)}, u32[]{:S(2)}) collective-permute-start(f32[128,128]{1,0:T(8,128)S(1)} %get-tuple-element.48.push_there), channel_id=1, source_target_pairs={{1,2},{2,1},{3,4},{4,3},{5,6},{6,5},{7,8},{8,7},{9,10},{10,9},{11,... | collective-permute-start | bytes 196616 | tf_op jit(solution)/shard_map/ppermute | solution.py:336
  5.1 1.7 %collective-permute-start.1 = (f32[128,128]{1,0:T(8,128)S(1)}, f32[128,128]{1,0:T(8,128)S(1)}, u32[]{:S(2)}, u32[]{:S(2)}) collective-permute-start(f32[128,128]{1,0:T(8,128)S(1)} %get-tuple-element.47), channel_id=1, source_target_pairs={{0,1},{1,0},{2,3},{3,2},{4,5},{5,4},{6,7},{7,6},{8,9},{9,8},{10,11... | collective-permute-start | bytes 196616 | tf_op jit(solution)/shard_map/ppermute | solution.py:365
  5.2 4.7 %collective-permute-start.3 = (f32[200,128]{1,0:T(8,128)S(1)}, f32[200,128]{1,0:T(8,128)S(1)}, u32[]{:S(2)}, u32[]{:S(2)}) collective-permute-start(f32[200,128]{1,0:T(8,128)S(1)} %get-tuple-element.41.send), channel_id=1, source_target_pairs={{1,2},{2,1},{3,4},{4,3},{5,6},{6,5},{7,8},{8,7},{9,10},{10,9},{11,... | collective-permute-start | bytes 307208 | tf_op jit(solution)/shard_map/ppermute | solution.py:336
  7.0 4.1 %collective-permute-start.5 = (f32[128,128]{1,0:T(8,128)S(1)}, f32[128,128]{1,0:T(8,128)S(1)}, u32[]{:S(2)}, u32[]{:S(2)}) collective-permute-start(f32[128,128]{1,0:T(8,128)S(1)} %get-tuple-element.55.w_inner), channel_id=1, source_target_pairs={{0,1},{1,0},{2,3},{3,2},{4,5},{5,4},{6,7},{7,6},{8,9},{9,8},{10,11... | collective-permute-start | bytes 196616 | tf_op jit(solution)/shard_map/ppermute | solution.py:369
  7.2 3.9 %collective-permute-start.4 = (f32[64,128]{1,0:T(8,128)S(1)}, f32[64,128]{1,0:T(8,128)S(1)}, u32[]{:S(2)}, u32[]{:S(2)}) collective-permute-start(f32[64,128]{1,0:T(8,128)S(1)} %get-tuple-element.61), channel_id=1, source_target_pairs={{1,2},{2,1},{3,4},{4,3},{5,6},{6,5},{7,8},{8,7},{9,10},{10,9},{11,... | collective-permute-start | bytes 98312 | tf_op jit(solution)/shard_map/ppermute | solution.py:336

commit v17 on v16

--- a/solution.py
+++ b/solution.py
@@ -31,7 +31,7 @@
 
 
 def outer_block(tile):
-    side = lax.rem(place(), 2)
+    side = lax.axis_index("sub")
     outer = pl.ds(pl.multiple_of(side * tile, tile), tile)
     inner = pl.ds(pl.multiple_of((1 - side) * tile, tile), tile)
     return outer, inner
@@ -75,7 +75,7 @@
     half = tile // 2
     slots = tiles.shape[0]
     position = place()
-    side = lax.rem(position, 2)
+    side = lax.axis_index("sub")
     first = position * 2
     moves = (
         (cols_there, cols),
@@ -140,7 +140,7 @@
     tile = tiles.shape[-1]
     half = tile // 2
     position = place()
-    side = lax.rem(position, 2)
+    side = lax.axis_index("sub")
     first = position * 2
     outer, inner = outer_block(tile)
     total = row_sums(tiles, masses)
@@ -186,12 +186,12 @@
 
 
 def outer_columns(tile):
-    side = lax.rem(place(), 2)
+    side = lax.axis_index("sub")
     return pl.ds(pl.multiple_of(side * tile, tile), tile)
 
 
 def inner_columns(tile):
-    side = lax.rem(place(), 2)
+    side = lax.axis_index("sub")
     return pl.ds(pl.multiple_of((1 - side) * tile, tile), tile)
 
 
@@ -265,7 +265,7 @@
 ):
     tile = there.shape[0]
     half = tile // 2
-    side = lax.rem(place(), 2)
+    side = lax.axis_index("sub")
     shift = moments[6:7, :]
     q_half = got_q[...]
     q_flip = flip(q_half)
@@ -317,7 +317,7 @@
 def body(block_cols, step_tiles, mass, warm_start, source_ids):
     tile = step_tiles.shape[-1]
     rows, columns = warm_start.shape
-    assert block_cols.shape[0] == 2 and columns == tile
+    assert block_cols.shape[0] == 2 and columns == tile and lax.axis_size("sub") == 2
     devices = lax.axis_size("patch") * lax.axis_size("sub")
     partner = [(i, i ^ 1) for i in range(devices)]
     groups = lax.axis_size("groups")

time: 25 us -> 25 us (level)
  no operation moved by 1% of the time
where the time goes in v17:
time: 25 us; the launch traced here: 24.8 us
  blocking collectives  12.8 us (51%)
  starting transfers between devices  6.98 us (28%)
  Pallas kernels  3.89 us (16%)
  waiting for transfers between devices  1.12 us (4%)
    all_to_all x1, blocking collectives, body(): shares = lax.all_to_all(shares, AXES, 0, 0)  12.8 us
    ppermute x3, starting transfers between devices, exchange(): return lax.ppermute(value, ('groups',) + AXES, across)  6.07 us
    pallas_call x6, Pallas kernels, call(): pl.pallas_call(kernel, out_shape=outs if len(outs) > 1 else outs[0], in_s...  2.54 us
    pallas_call x1, Pallas kernels, body(): pl.pallas_call(outer_kernel, out_shape=[pltpu.VMEM(shape[1:], shape[0]) f...  1.35 us
    ppermute x3, waiting for transfers between devices, exchange(): return lax.ppermute(value, ('groups',) + AXES, across)  1.11 us
    ppermute x1, starting transfers between devices, body(): other_x = lax.ppermute(x_inner, AXES, partner)  0.56 us
  transfers between devices with their start and end apart: 6, of which 2 were waited for; matrix products, arithmetic and copies ran while one was open for 0% of the time, Pallas kernels for 7%

profile of v17, /device:TPU:0, one launch (start us, length us, event | category | flops | bytes accessed | tf_op | source)
XLA Modules:
  0.0 24.8 jit_solution(3538083092109615789)
XLA Ops:
  0.0 1.3 %outer_kernel.1 = (bf16[2,128,256]{2,1,0:T(8,128)(2,1)S(1)}, f32[128,128]{1,0:T(8,128)S(1)}, bf16[2,128,128]{2,1,0:T(8,128)(2,1)S(1)}, f32[256,128]{1,0:T(8,128)...) custom-call(s32[2,3]{1,0:T(2,128)} %cols_there.1, ...), custom_call_target="tpu_custom_call" | custom-call | tf_op jit(solution)/shard_map/outer_kernel/pallas_call | solution.py:342
  1.4 0.6 %collective-permute-start = (f32[128,128]{1,0:T(8,128)S(1)}, f32[128,128]{1,0:T(8,128)S(1)}, u32[]{:S(2)}, u32[]{:S(2)}) collective-permute-start(f32[128,128]{1,0:T(8,128)S(1)} %get-tuple-element.40), channel_id=1, source_target_pairs={{0,1},{1,0},{2,3},{3,2},{4,5},{5,4},{6,7},{7,6},{8,9},{9,8},{10,11... | collective-permute-start | bytes 196616 | tf_op jit(solution)/shard_map/ppermute | solution.py:357
  1.9 2.6 %collective-permute-start.2 = (f32[128,128]{1,0:T(8,128)S(1)}, f32[128,128]{1,0:T(8,128)S(1)}, u32[]{:S(2)}, u32[]{:S(2)}) collective-permute-start(f32[128,128]{1,0:T(8,128)S(1)} %get-tuple-element.48.push_there), channel_id=1, source_target_pairs={{1,2},{2,1},{3,4},{4,3},{5,6},{6,5},{7,8},{8,7},{9,10},{10,9},{11,... | collective-permute-start | bytes 196616 | tf_op jit(solution)/shard_map/ppermute | solution.py:336
  4.5 0.0 collective-permute-done.other_x
  4.5 0.6 %shard_map.55 = (bf16[2,256,256]{2,1,0:T(8,128)(2,1)S(1)}, f32[256,128]{1,0:T(8,128)S(1)}, bf16[2,128,128]{2,1,0:T(8,128)(2,1)S(1)}, f32[256,128]{1,0:T(8,128)S(...) custom-call(bf16[2,128,256]{2,1,0:T(8,128)(2,1)S(1)} %get-tuple-element.34.local_outer, ...), custom_call_target="tpu_custom_call" | custom-call | tf_op jit(solution)/shard_map/pallas_call | solution.py:309
  5.1 0.1 collective-permute-start.1
  5.2 1.5 %collective-permute-start.3 = (f32[200,128]{1,0:T(8,128)S(1)}, f32[200,128]{1,0:T(8,128)S(1)}, u32[]{:S(2)}, u32[]{:S(2)}) collective-permute-start(f32[200,128]{1,0:T(8,128)S(1)} %get-tuple-element.41.send), channel_id=1, source_target_pairs={{1,2},{2,1},{3,4},{4,3},{5,6},{6,5},{7,8},{8,7},{9,10},{10,9},{11,... | collective-permute-start | bytes 307208 | tf_op jit(solution)/shard_map/ppermute | solution.py:336
  6.8 0.0 collective-permute-done.2.push_here
  6.8 0.0 collective-permute-done.1.other_t
  6.8 0.3 %shard_map.56 = (f32[128,128]{1,0:T(8,128)S(1)}, bf16[2,128,128]{2,1,0:T(8,128)(2,1)S(1)}, bf16[2,128,128]{2,1,0:T(8,128)(2,1)S(1)}) custom-call(bf16[2,256,256]{2,1,0:T(8,128)(2,1)S(1)} %get-tuple-element.42.local, f32[256,128]{1,0:T(8,128)S(1)} %get-tuple-element.43.diag, bf16[2,128,128]{2,1,0:T(8,128)(2,1)S(1)} %get-tuple-element.44.t_in, ...), custom_call_target="tpu_custom_call" | custom-call | tf_op jit(solution)/shard_map/pallas_call | solution.py:309
  7.0 0.2 collective-permute-start.5
  7.2 2.0 %collective-permute-start.4 = (f32[64,128]{1,0:T(8,128)S(1)}, f32[64,128]{1,0:T(8,128)S(1)}, u32[]{:S(2)}, u32[]{:S(2)}) collective-permute-start(f32[64,128]{1,0:T(8,128)S(1)} %get-tuple-element.61), channel_id=1, source_target_pairs={{1,2},{2,1},{3,4},{4,3},{5,6},{6,5},{7,8},{8,7},{9,10},{10,9},{11,... | collective-permute-start | bytes 98312 | tf_op jit(solution)/shard_map/ppermute | solution.py:336
  9.2 0.2 shard_map.57
  9.5 0.4 %collective-permute-done.3.got = f32[200,128]{1,0:T(8,128)S(1)} collective-permute-done((f32[200,128]{1,0:T(8,128)S(1)}, f32[200,128]{1,0:T(8,128)S(1)}, u32[]{:S(2)}, u32[]{:S(2)}) %collective-permute-start.3) | collective-permute-done | bytes 102432 | tf_op jit(solution)/shard_map/ppermute | solution.py:336
  9.9 0.6 %shard_map.58 = (f32[256,128]{1,0:T(8,128)S(1)}, f32[128,128]{1,0:T(8,128)S(1)}, f32[128,128]{1,0:T(8,128)S(1)}, f32[16,128]{1,0:T(8,128)S(1)}, f32[128,128]{1,0:T(8,128)S(1)}) custom-call(bf16[2,256,256]{2,1,0:T(8,128)(2,1)S(1)} %get-tuple-element.42.local, f32[256,128]{1,0:T(8,128)S(1)} %get-tuple-element.43.diag, ...), custom_call_target="tpu_custom_call" | custom-call | tf_op jit(solution)/shard_map/pallas_call | solution.py:309
  10.5 0.7 %collective-permute-done.4.got_q = f32[64,128]{1,0:T(8,128)S(1)} collective-permute-done((f32[64,128]{1,0:T(8,128)S(1)}, f32[64,128]{1,0:T(8,128)S(1)}, u32[]{:S(2)}, u32[]{:S(2)}) %collective-permute-start.4) | collective-permute-done | bytes 32800 | tf_op jit(solution)/shard_map/ppermute | solution.py:336
  11.2 0.0 collective-permute-done.5.other_w
  11.2 0.1 shard_map.59
  11.3 12.8 %all_to_all.5.shares = f32[16,3,2,128]{3,2,1,0:T(2,128)S(1)} all-to-all(f32[16,3,2,128]{3,2,1,0:T(2,128)S(1)} %shard_map.59), channel_id=1, replica_groups=mesh['groups'=2,'patch'=8,'sub'=2] {'patch','sub'}, dimensions={0} | all-to-all | bytes 98304 | tf_op jit(solution)/shard_map/all_to_all | solution.py:382
  24.0 0.8 %shard_map.60 = f32[256,128]{1,0:T(8,128)} custom-call(f32[16,3,2,128]{3,2,1,0:T(2,128)S(1)} %all_to_all.5.shares, f32[256,128]{1,0:T(8,128)S(1)} %get-tuple-element.36.x, f32[256,128]{1,0:T(8,128)S(1)} %get-tuple-element.52.r, f32[256,128]{1,0:T(8,128)S(1)} %get-tuple-element.62.w), custom_call_target="tpu_custom_call" | custom-call | tf_op jit(solution)/shard_map/pallas_call | solution.py:309
Async XLA Ops:
  1.4 3.1 %collective-permute-start = (f32[128,128]{1,0:T(8,128)S(1)}, f32[128,128]{1,0:T(8,128)S(1)}, u32[]{:S(2)}, u32[]{:S(2)}) collective-permute-start(f32[128,128]{1,0:T(8,128)S(1)} %get-tuple-element.40), channel_id=1, source_target_pairs={{0,1},{1,0},{2,3},{3,2},{4,5},{5,4},{6,7},{7,6},{8,9},{9,8},{10,11... | collective-permute-start | bytes 196616 | tf_op jit(solution)/shard_map/ppermute | solution.py:357
  1.9 4.8 %collective-permute-start.2 = (f32[128,128]{1,0:T(8,128)S(1)}, f32[128,128]{1,0:T(8,128)S(1)}, u32[]{:S(2)}, u32[]{:S(2)}) collective-permute-start(f32[128,128]{1,0:T(8,128)S(1)} %get-tuple-element.48.push_there), channel_id=1, source_target_pairs={{1,2},{2,1},{3,4},{4,3},{5,6},{6,5},{7,8},{8,7},{9,10},{10,9},{11,... | collective-permute-start | bytes 196616 | tf_op jit(solution)/shard_map/ppermute | solution.py:336
  5.1 1.7 %collective-permute-start.1 = (f32[128,128]{1,0:T(8,128)S(1)}, f32[128,128]{1,0:T(8,128)S(1)}, u32[]{:S(2)}, u32[]{:S(2)}) collective-permute-start(f32[128,128]{1,0:T(8,128)S(1)} %get-tuple-element.47), channel_id=1, source_target_pairs={{0,1},{1,0},{2,3},{3,2},{4,5},{5,4},{6,7},{7,6},{8,9},{9,8},{10,11... | collective-permute-start | bytes 196616 | tf_op jit(solution)/shard_map/ppermute | solution.py:365
  5.2 4.7 %collective-permute-start.3 = (f32[200,128]{1,0:T(8,128)S(1)}, f32[200,128]{1,0:T(8,128)S(1)}, u32[]{:S(2)}, u32[]{:S(2)}) collective-permute-start(f32[200,128]{1,0:T(8,128)S(1)} %get-tuple-element.41.send), channel_id=1, source_target_pairs={{1,2},{2,1},{3,4},{4,3},{5,6},{6,5},{7,8},{8,7},{9,10},{10,9},{11,... | collective-permute-start | bytes 307208 | tf_op jit(solution)/shard_map/ppermute | solution.py:336
  7.0 4.1 %collective-permute-start.5 = (f32[128,128]{1,0:T(8,128)S(1)}, f32[128,128]{1,0:T(8,128)S(1)}, u32[]{:S(2)}, u32[]{:S(2)}) collective-permute-start(f32[128,128]{1,0:T(8,128)S(1)} %get-tuple-element.55.w_inner), channel_id=1, source_target_pairs={{0,1},{1,0},{2,3},{3,2},{4,5},{5,4},{6,7},{7,6},{8,9},{9,8},{10,11... | collective-permute-start | bytes 196616 | tf_op jit(solution)/shard_map/ppermute | solution.py:369
  7.2 3.9 %collective-permute-start.4 = (f32[64,128]{1,0:T(8,128)S(1)}, f32[64,128]{1,0:T(8,128)S(1)}, u32[]{:S(2)}, u32[]{:S(2)}) collective-permute-start(f32[64,128]{1,0:T(8,128)S(1)} %get-tuple-element.61), channel_id=1, source_target_pairs={{1,2},{2,1},{3,4},{4,3},{5,6},{6,5},{7,8},{8,7},{9,10},{10,9},{11,... | collective-permute-start | bytes 98312 | tf_op jit(solution)/shard_map/ppermute | solution.py:336

commit v18 on v17

--- a/solution.py
+++ b/solution.py
@@ -68,7 +68,7 @@
 
 def outer_kernel(
     cols_there, tiles_there, mass_there, x_there, sources_there,
-    local_outer, diag_outer, t_out_t, x, x_inner, tiles_inner, names, masses, push, send,
+    local_outer, diag_outer, t_out_t, x, tiles_inner, names, masses, push, send,
     cols, tiles, mass, sources, arrived,
 ):
     tile = tiles.shape[-1]
@@ -91,8 +91,7 @@
     for copy in copies[:-1]:
         copy.wait()
     eye = index_of((tile, tile), 0) == index_of((tile, tile), 1)
-    outer, inner = outer_block(tile)
-    x_inner[...] = x[inner, :]
+    outer, _ = outer_block(tile)
     row = index_of(names.shape, 0)
     named = jnp.broadcast_to(sources[...][None, :], names.shape)
     for k in range(slots):
@@ -158,7 +157,7 @@
         right_side(names, first + 1 - side, x_inner.shape)
         - total * x_inner
         - dot(part(local, inner), x[...])
-        + dot(t_in, other_x[...])
+        + dot(t_in, other_x[outer, :])
     )
     t[inner, :] = t_inner[...]
     q = (
@@ -335,11 +334,12 @@
     def exchange(value):
         return lax.ppermute(value, ("groups",) + AXES, across)
 
+    other_x = lax.ppermute(warm_start, AXES, partner)
     results = [
-        (jnp.bfloat16, 2, tile, rows), block, square, field, block, (single, slots, tile, tile),
+        (jnp.bfloat16, 2, tile, rows), block, square, field, (single, slots, tile, tile),
         (jnp.int32, 8, tile), (single, 8, tile), block, (single, tile + tile // 2 + 8, columns),
     ]
-    local_outer, diag_outer, t_out_t, x, x_inner, tiles_inner, names, masses, push_there, send = pl.pallas_call(
+    local_outer, diag_outer, t_out_t, x, tiles_inner, names, masses, push_there, send = pl.pallas_call(
         outer_kernel,
         out_shape=[pltpu.VMEM(shape[1:], shape[0]) for shape in results],
         in_specs=[pl.BlockSpec(memory_space=pl.ANY)] * 5,
@@ -354,7 +354,6 @@
         name="outer_kernel",
     )(block_cols, step_tiles, mass, warm_start, source_ids)
     push_here = exchange(push_there)
-    other_x = lax.ppermute(x_inner, AXES, partner)
     got = exchange(send)
     local, diag, t_in, t, t_inner, q_outer, q_send = call(
         inner_row_kernel,

time: 25 us -> 25 us (level)
  transfers between devices with their start and end apart: 6 -> 6, of which waited for: 2 -> 2; matrix products, arithmetic and copies ran while one was open for 0% -> 0% of each run, Pallas kernels for 7% -> 12%
where the time goes in v18:
time: 25 us; the launch traced here: 24.8 us
  blocking collectives  12.8 us (51%)
  starting transfers between devices  6.9 us (28%)
  Pallas kernels  3.89 us (16%)
  waiting for transfers between devices  1.13 us (5%)
    all_to_all x1, blocking collectives, body(): shares = lax.all_to_all(shares, AXES, 0, 0)  12.8 us
    ppermute x3, starting transfers between devices, exchange(): return lax.ppermute(value, ('groups',) + AXES, across)  6.06 us
    pallas_call x6, Pallas kernels, call(): pl.pallas_call(kernel, out_shape=outs if len(outs) > 1 else outs[0], in_s...  2.54 us
    pallas_call x1, Pallas kernels, body(): pl.pallas_call(outer_kernel, out_shape=[pltpu.VMEM(shape[1:], shape[0]) f...  1.35 us
    ppermute x3, waiting for transfers between devices, exchange(): return lax.ppermute(value, ('groups',) + AXES, across)  1.12 us
  transfers between devices with their start and end apart: 6, of which 2 were waited for; matrix products, arithmetic and copies ran while one was open for 0% of the time, Pallas kernels for 12%

profile of v18, /device:TPU:0, one launch (start us, length us, event | category | flops | bytes accessed | tf_op | source)
XLA Modules:
  0.0 24.8 jit_solution(7539496551821004957)
XLA Ops:
  0.0 0.5 %collective-permute-start = (f32[256,128]{1,0:T(8,128)}, f32[256,128]{1,0:T(8,128)S(1)}, u32[]{:S(2)}, u32[]{:S(2)}) collective-permute-start(f32[256,128]{1,0:T(8,128)} %x_there.1), channel_id=1, source_target_pairs={{0,1},{1,0},{2,3},{3,2},{4,5},{5,4},{6,7},{7,6},{8,9},{9,8},{10,11... | collective-permute-start | bytes 393224 | tf_op jit(solution)/shard_map/ppermute | solution.py:337
  0.5 1.3 %outer_kernel.1 = (bf16[2,128,256]{2,1,0:T(8,128)(2,1)S(1)}, f32[128,128]{1,0:T(8,128)S(1)}, bf16[2,128,128]{2,1,0:T(8,128)(2,1)S(1)}, f32[256,128]{1,0:T(8,128)...) custom-call(s32[2,3]{1,0:T(2,128)} %cols_there.1, ...), custom_call_target="tpu_custom_call" | custom-call | tf_op jit(solution)/shard_map/outer_kernel/pallas_call | solution.py:342
  1.8 2.6 %collective-permute-start.2 = (f32[128,128]{1,0:T(8,128)S(1)}, f32[128,128]{1,0:T(8,128)S(1)}, u32[]{:S(2)}, u32[]{:S(2)}) collective-permute-start(f32[128,128]{1,0:T(8,128)S(1)} %get-tuple-element.46.push_there), channel_id=1, source_target_pairs={{1,2},{2,1},{3,4},{4,3},{5,6},{6,5},{7,8},{8,7},{9,10},{10,9},{11,... | collective-permute-start | bytes 196616 | tf_op jit(solution)/shard_map/ppermute | solution.py:335
  4.4 0.0 collective-permute-done.other_x
  4.4 0.6 %shard_map.55 = (bf16[2,256,256]{2,1,0:T(8,128)(2,1)S(1)}, f32[256,128]{1,0:T(8,128)S(1)}, bf16[2,128,128]{2,1,0:T(8,128)(2,1)S(1)}, f32[256,128]{1,0:T(8,128)S(...) custom-call(bf16[2,128,256]{2,1,0:T(8,128)(2,1)S(1)} %get-tuple-element.33.local_outer, ...), custom_call_target="tpu_custom_call" | custom-call | tf_op jit(solution)/shard_map/pallas_call | solution.py:308
  5.0 0.1 collective-permute-start.1
  5.2 1.5 %collective-permute-start.3 = (f32[200,128]{1,0:T(8,128)S(1)}, f32[200,128]{1,0:T(8,128)S(1)}, u32[]{:S(2)}, u32[]{:S(2)}) collective-permute-start(f32[200,128]{1,0:T(8,128)S(1)} %get-tuple-element.39.send), channel_id=1, source_target_pairs={{1,2},{2,1},{3,4},{4,3},{5,6},{6,5},{7,8},{8,7},{9,10},{10,9},{11,... | collective-permute-start | bytes 307208 | tf_op jit(solution)/shard_map/ppermute | solution.py:335
  6.7 0.0 collective-permute-done.2.push_here
  6.7 0.0 collective-permute-done.1.other_t
  6.7 0.3 %shard_map.56 = (f32[128,128]{1,0:T(8,128)S(1)}, bf16[2,128,128]{2,1,0:T(8,128)(2,1)S(1)}, bf16[2,128,128]{2,1,0:T(8,128)(2,1)S(1)}) custom-call(bf16[2,256,256]{2,1,0:T(8,128)(2,1)S(1)} %get-tuple-element.40.local, f32[256,128]{1,0:T(8,128)S(1)} %get-tuple-element.41.diag, bf16[2,128,128]{2,1,0:T(8,128)(2,1)S(1)} %get-tuple-element.42.t_in, ...), custom_call_target="tpu_custom_call" | custom-call | tf_op jit(solution)/shard_map/pallas_call | solution.py:308
  7.0 0.2 collective-permute-start.5
  7.2 2.0 %collective-permute-start.4 = (f32[64,128]{1,0:T(8,128)S(1)}, f32[64,128]{1,0:T(8,128)S(1)}, u32[]{:S(2)}, u32[]{:S(2)}) collective-permute-start(f32[64,128]{1,0:T(8,128)S(1)} %get-tuple-element.59), channel_id=1, source_target_pairs={{1,2},{2,1},{3,4},{4,3},{5,6},{6,5},{7,8},{8,7},{9,10},{10,9},{11,... | collective-permute-start | bytes 98312 | tf_op jit(solution)/shard_map/ppermute | solution.py:335
  9.1 0.2 shard_map.57
  9.4 0.4 %collective-permute-done.3.got = f32[200,128]{1,0:T(8,128)S(1)} collective-permute-done((f32[200,128]{1,0:T(8,128)S(1)}, f32[200,128]{1,0:T(8,128)S(1)}, u32[]{:S(2)}, u32[]{:S(2)}) %collective-permute-start.3) | collective-permute-done | bytes 102432 | tf_op jit(solution)/shard_map/ppermute | solution.py:335
  9.8 0.6 %shard_map.58 = (f32[256,128]{1,0:T(8,128)S(1)}, f32[128,128]{1,0:T(8,128)S(1)}, f32[128,128]{1,0:T(8,128)S(1)}, f32[16,128]{1,0:T(8,128)S(1)}, f32[128,128]{1,0:T(8,128)S(1)}) custom-call(bf16[2,256,256]{2,1,0:T(8,128)(2,1)S(1)} %get-tuple-element.40.local, f32[256,128]{1,0:T(8,128)S(1)} %get-tuple-element.41.diag, ...), custom_call_target="tpu_custom_call" | custom-call | tf_op jit(solution)/shard_map/pallas_call | solution.py:308
  10.4 0.7 %collective-permute-done.4.got_q = f32[64,128]{1,0:T(8,128)S(1)} collective-permute-done((f32[64,128]{1,0:T(8,128)S(1)}, f32[64,128]{1,0:T(8,128)S(1)}, u32[]{:S(2)}, u32[]{:S(2)}) %collective-permute-start.4) | collective-permute-done | bytes 32800 | tf_op jit(solution)/shard_map/ppermute | solution.py:335
  11.1 0.0 collective-permute-done.5.other_w
  11.1 0.1 shard_map.59
  11.2 12.8 %all_to_all.5.shares = f32[16,3,2,128]{3,2,1,0:T(2,128)S(1)} all-to-all(f32[16,3,2,128]{3,2,1,0:T(2,128)S(1)} %shard_map.59), channel_id=1, replica_groups=mesh['groups'=2,'patch'=8,'sub'=2] {'patch','sub'}, dimensions={0} | all-to-all | bytes 98304 | tf_op jit(solution)/shard_map/all_to_all | solution.py:381
  24.0 0.8 %shard_map.60 = f32[256,128]{1,0:T(8,128)} custom-call(f32[16,3,2,128]{3,2,1,0:T(2,128)S(1)} %all_to_all.5.shares, f32[256,128]{1,0:T(8,128)S(1)} %get-tuple-element.35.x, f32[256,128]{1,0:T(8,128)S(1)} %get-tuple-element.50.r, f32[256,128]{1,0:T(8,128)S(1)} %get-tuple-element.60.w), custom_call_target="tpu_custom_call" | custom-call | tf_op jit(solution)/shard_map/pallas_call | solution.py:308
Async XLA Ops:
  0.0 4.4 %collective-permute-start = (f32[256,128]{1,0:T(8,128)}, f32[256,128]{1,0:T(8,128)S(1)}, u32[]{:S(2)}, u32[]{:S(2)}) collective-permute-start(f32[256,128]{1,0:T(8,128)} %x_there.1), channel_id=1, source_target_pairs={{0,1},{1,0},{2,3},{3,2},{4,5},{5,4},{6,7},{7,6},{8,9},{9,8},{10,11... | collective-permute-start | bytes 393224 | tf_op jit(solution)/shard_map/ppermute | solution.py:337
  1.8 4.8 %collective-permute-start.2 = (f32[128,128]{1,0:T(8,128)S(1)}, f32[128,128]{1,0:T(8,128)S(1)}, u32[]{:S(2)}, u32[]{:S(2)}) collective-permute-start(f32[128,128]{1,0:T(8,128)S(1)} %get-tuple-element.46.push_there), channel_id=1, source_target_pairs={{1,2},{2,1},{3,4},{4,3},{5,6},{6,5},{7,8},{8,7},{9,10},{10,9},{11,... | collective-permute-start | bytes 196616 | tf_op jit(solution)/shard_map/ppermute | solution.py:335
  5.0 1.7 %collective-permute-start.1 = (f32[128,128]{1,0:T(8,128)S(1)}, f32[128,128]{1,0:T(8,128)S(1)}, u32[]{:S(2)}, u32[]{:S(2)}) collective-permute-start(f32[128,128]{1,0:T(8,128)S(1)} %get-tuple-element.45), channel_id=1, source_target_pairs={{0,1},{1,0},{2,3},{3,2},{4,5},{5,4},{6,7},{7,6},{8,9},{9,8},{10,11... | collective-permute-start | bytes 196616 | tf_op jit(solution)/shard_map/ppermute | solution.py:364
  5.2 4.7 %collective-permute-start.3 = (f32[200,128]{1,0:T(8,128)S(1)}, f32[200,128]{1,0:T(8,128)S(1)}, u32[]{:S(2)}, u32[]{:S(2)}) collective-permute-start(f32[200,128]{1,0:T(8,128)S(1)} %get-tuple-element.39.send), channel_id=1, source_target_pairs={{1,2},{2,1},{3,4},{4,3},{5,6},{6,5},{7,8},{8,7},{9,10},{10,9},{11,... | collective-permute-start | bytes 307208 | tf_op jit(solution)/shard_map/ppermute | solution.py:335
  7.0 4.1 %collective-permute-start.5 = (f32[128,128]{1,0:T(8,128)S(1)}, f32[128,128]{1,0:T(8,128)S(1)}, u32[]{:S(2)}, u32[]{:S(2)}) collective-permute-start(f32[128,128]{1,0:T(8,128)S(1)} %get-tuple-element.53.w_inner), channel_id=1, source_target_pairs={{0,1},{1,0},{2,3},{3,2},{4,5},{5,4},{6,7},{7,6},{8,9},{9,8},{10,11... | collective-permute-start | bytes 196616 | tf_op jit(solution)/shard_map/ppermute | solution.py:368
  7.2 3.9 %collective-permute-start.4 = (f32[64,128]{1,0:T(8,128)S(1)}, f32[64,128]{1,0:T(8,128)S(1)}, u32[]{:S(2)}, u32[]{:S(2)}) collective-permute-start(f32[64,128]{1,0:T(8,128)S(1)} %get-tuple-element.59), channel_id=1, source_target_pairs={{1,2},{2,1},{3,4},{4,3},{5,6},{6,5},{7,8},{8,7},{9,10},{10,9},{11,... | collective-permute-start | bytes 98312 | tf_op jit(solution)/shard_map/ppermute | solution.py:335

commit v19 on v18

--- a/solution.py
+++ b/solution.py
@@ -288,7 +288,9 @@
 
 
 def finish_kernel(shares, x, r, w, out):
-    r_rs, r_ws, spreads, y_ay, r_ay, r_ar = [shares[:, row // 2, row % 2, :] for row in range(6)]
+    devices = shares.shape[0] // lax.axis_size("groups")
+    mine = pl.ds(lax.axis_index("groups") * devices, devices)
+    r_rs, r_ws, spreads, y_ay, r_ay, r_ar = [shares[mine, row // 2, row % 2, :] for row in range(6)]
     r_r = jnp.sum(r_rs, axis=0, keepdims=True)
     r_w = jnp.sum(r_ws, axis=0, keepdims=True)
     theta = r_w / r_r
@@ -375,10 +377,10 @@
         local, diag, t_in_t, t_out, t_out_t, r, w_local, edge_r_out, push_there, got, w_inner,
     )
     shares = call(
-        share_kernel, [(single, devices, 3, 2, columns)],
+        share_kernel, [(single, groups * devices, 3, 2, columns)],
         moments, edge_y_in, edge_r_in, edge_y_out, edge_r_out, there, got_q, other_t, other_w,
     )
-    shares = lax.all_to_all(shares, AXES, 0, 0)
+    shares = lax.all_to_all(shares, ("groups",) + AXES, 0, 0)
     return call(finish_kernel, [field], shares, x, r, w, last=True)
 
 

time: 25 us -> 25.9 us (1.036)
  blocking collectives: 12.8 us -> 13.8 us
    all_to_all x1, blocking collectives: 12.8 us -> 13.8 us  [body(): shares = lax.all_to_all(shares, ('groups',) + AXES, 0, 0)]
where the time goes in v19:
time: 25.9 us; the launch traced here: 25.8 us
  blocking collectives  13.8 us (53%)
  starting transfers between devices  6.9 us (27%)
  Pallas kernels  3.89 us (15%)
  waiting for transfers between devices  1.13 us (4%)
    all_to_all x1, blocking collectives, body(): shares = lax.all_to_all(shares, ('groups',) + AXES, 0, 0)  13.8 us
    ppermute x3, starting transfers between devices, exchange(): return lax.ppermute(value, ('groups',) + AXES, across)  6.06 us
    pallas_call x6, Pallas kernels, call(): pl.pallas_call(kernel, out_shape=outs if len(outs) > 1 else outs[0], in_s...  2.54 us
    pallas_call x1, Pallas kernels, body(): pl.pallas_call(outer_kernel, out_shape=[pltpu.VMEM(shape[1:], shape[0]) f...  1.35 us
    ppermute x3, waiting for transfers between devices, exchange(): return lax.ppermute(value, ('groups',) + AXES, across)  1.12 us
  transfers between devices with their start and end apart: 6, of which 2 were waited for; matrix products, arithmetic and copies ran while one was open for 0% of the time, Pallas kernels for 12%

profile of v19, /device:TPU:0, one launch (start us, length us, event | category | flops | bytes accessed | tf_op | source)
XLA Modules:
  0.0 25.8 jit_solution(17330491329696079019)
XLA Ops:
  0.0 0.5 %collective-permute-start = (f32[256,128]{1,0:T(8,128)}, f32[256,128]{1,0:T(8,128)S(1)}, u32[]{:S(2)}, u32[]{:S(2)}) collective-permute-start(f32[256,128]{1,0:T(8,128)} %x_there.1), channel_id=1, source_target_pairs={{0,1},{1,0},{2,3},{3,2},{4,5},{5,4},{6,7},{7,6},{8,9},{9,8},{10,11... | collective-permute-start | bytes 393224 | tf_op jit(solution)/shard_map/ppermute | solution.py:339
  0.5 1.3 %outer_kernel.1 = (bf16[2,128,256]{2,1,0:T(8,128)(2,1)S(1)}, f32[128,128]{1,0:T(8,128)S(1)}, bf16[2,128,128]{2,1,0:T(8,128)(2,1)S(1)}, f32[256,128]{1,0:T(8,128)...) custom-call(s32[2,3]{1,0:T(2,128)} %cols_there.1, ...), custom_call_target="tpu_custom_call" | custom-call | tf_op jit(solution)/shard_map/outer_kernel/pallas_call | solution.py:344
  1.8 2.6 %collective-permute-start.2 = (f32[128,128]{1,0:T(8,128)S(1)}, f32[128,128]{1,0:T(8,128)S(1)}, u32[]{:S(2)}, u32[]{:S(2)}) collective-permute-start(f32[128,128]{1,0:T(8,128)S(1)} %get-tuple-element.46.push_there), channel_id=1, source_target_pairs={{1,2},{2,1},{3,4},{4,3},{5,6},{6,5},{7,8},{8,7},{9,10},{10,9},{11,... | collective-permute-start | bytes 196616 | tf_op jit(solution)/shard_map/ppermute | solution.py:337
  4.4 0.0 collective-permute-done.other_x
  4.4 0.6 %shard_map.55 = (bf16[2,256,256]{2,1,0:T(8,128)(2,1)S(1)}, f32[256,128]{1,0:T(8,128)S(1)}, bf16[2,128,128]{2,1,0:T(8,128)(2,1)S(1)}, f32[256,128]{1,0:T(8,128)S(...) custom-call(bf16[2,128,256]{2,1,0:T(8,128)(2,1)S(1)} %get-tuple-element.33.local_outer, ...), custom_call_target="tpu_custom_call" | custom-call | tf_op jit(solution)/shard_map/pallas_call | solution.py:310
  5.0 0.1 collective-permute-start.1
  5.2 1.5 %collective-permute-start.3 = (f32[200,128]{1,0:T(8,128)S(1)}, f32[200,128]{1,0:T(8,128)S(1)}, u32[]{:S(2)}, u32[]{:S(2)}) collective-permute-start(f32[200,128]{1,0:T(8,128)S(1)} %get-tuple-element.39.send), channel_id=1, source_target_pairs={{1,2},{2,1},{3,4},{4,3},{5,6},{6,5},{7,8},{8,7},{9,10},{10,9},{11,... | collective-permute-start | bytes 307208 | tf_op jit(solution)/shard_map/ppermute | solution.py:337
  6.7 0.0 collective-permute-done.2.push_here
  6.7 0.0 collective-permute-done.1.other_t
  6.7 0.3 %shard_map.56 = (f32[128,128]{1,0:T(8,128)S(1)}, bf16[2,128,128]{2,1,0:T(8,128)(2,1)S(1)}, bf16[2,128,128]{2,1,0:T(8,128)(2,1)S(1)}) custom-call(bf16[2,256,256]{2,1,0:T(8,128)(2,1)S(1)} %get-tuple-element.40.local, f32[256,128]{1,0:T(8,128)S(1)} %get-tuple-element.41.diag, bf16[2,128,128]{2,1,0:T(8,128)(2,1)S(1)} %get-tuple-element.42.t_in, ...), custom_call_target="tpu_custom_call" | custom-call | tf_op jit(solution)/shard_map/pallas_call | solution.py:310
  7.0 0.2 collective-permute-start.5
  7.2 2.0 %collective-permute-start.4 = (f32[64,128]{1,0:T(8,128)S(1)}, f32[64,128]{1,0:T(8,128)S(1)}, u32[]{:S(2)}, u32[]{:S(2)}) collective-permute-start(f32[64,128]{1,0:T(8,128)S(1)} %get-tuple-element.59), channel_id=1, source_target_pairs={{1,2},{2,1},{3,4},{4,3},{5,6},{6,5},{7,8},{8,7},{9,10},{10,9},{11,... | collective-permute-start | bytes 98312 | tf_op jit(solution)/shard_map/ppermute | solution.py:337
  9.1 0.2 shard_map.57
  9.4 0.4 %collective-permute-done.3.got = f32[200,128]{1,0:T(8,128)S(1)} collective-permute-done((f32[200,128]{1,0:T(8,128)S(1)}, f32[200,128]{1,0:T(8,128)S(1)}, u32[]{:S(2)}, u32[]{:S(2)}) %collective-permute-start.3) | collective-permute-done | bytes 102432 | tf_op jit(solution)/shard_map/ppermute | solution.py:337
  9.8 0.6 %shard_map.58 = (f32[256,128]{1,0:T(8,128)S(1)}, f32[128,128]{1,0:T(8,128)S(1)}, f32[128,128]{1,0:T(8,128)S(1)}, f32[16,128]{1,0:T(8,128)S(1)}, f32[128,128]{1,0:T(8,128)S(1)}) custom-call(bf16[2,256,256]{2,1,0:T(8,128)(2,1)S(1)} %get-tuple-element.40.local, f32[256,128]{1,0:T(8,128)S(1)} %get-tuple-element.41.diag, ...), custom_call_target="tpu_custom_call" | custom-call | tf_op jit(solution)/shard_map/pallas_call | solution.py:310
  10.4 0.7 %collective-permute-done.4.got_q = f32[64,128]{1,0:T(8,128)S(1)} collective-permute-done((f32[64,128]{1,0:T(8,128)S(1)}, f32[64,128]{1,0:T(8,128)S(1)}, u32[]{:S(2)}, u32[]{:S(2)}) %collective-permute-start.4) | collective-permute-done | bytes 32800 | tf_op jit(solution)/shard_map/ppermute | solution.py:337
  11.1 0.0 collective-permute-done.5.other_w
  11.1 0.1 shard_map.59
  11.2 13.8 %all_to_all.5.shares = f32[32,3,2,128]{3,2,1,0:T(2,128)S(1)} all-to-all(f32[32,3,2,128]{3,2,1,0:T(2,128)S(1)} %shard_map.59), channel_id=1, replica_groups=mesh['groups'=2,'patch'=8,'sub'=2] {'groups','patch','sub'}, dimensions={0} | all-to-all | bytes 196608 | tf_op jit(solution)/shard_map/all_to_all | solution.py:383
  25.0 0.8 %shard_map.60 = f32[256,128]{1,0:T(8,128)} custom-call(f32[32,3,2,128]{3,2,1,0:T(2,128)S(1)} %all_to_all.5.shares, f32[256,128]{1,0:T(8,128)S(1)} %get-tuple-element.35.x, f32[256,128]{1,0:T(8,128)S(1)} %get-tuple-element.50.r, f32[256,128]{1,0:T(8,128)S(1)} %get-tuple-element.60.w), custom_call_target="tpu_custom_call" | custom-call | tf_op jit(solution)/shard_map/pallas_call | solution.py:310
Async XLA Ops:
  0.0 4.4 %collective-permute-start = (f32[256,128]{1,0:T(8,128)}, f32[256,128]{1,0:T(8,128)S(1)}, u32[]{:S(2)}, u32[]{:S(2)}) collective-permute-start(f32[256,128]{1,0:T(8,128)} %x_there.1), channel_id=1, source_target_pairs={{0,1},{1,0},{2,3},{3,2},{4,5},{5,4},{6,7},{7,6},{8,9},{9,8},{10,11... | collective-permute-start | bytes 393224 | tf_op jit(solution)/shard_map/ppermute | solution.py:339
  1.8 4.8 %collective-permute-start.2 = (f32[128,128]{1,0:T(8,128)S(1)}, f32[128,128]{1,0:T(8,128)S(1)}, u32[]{:S(2)}, u32[]{:S(2)}) collective-permute-start(f32[128,128]{1,0:T(8,128)S(1)} %get-tuple-element.46.push_there), channel_id=1, source_target_pairs={{1,2},{2,1},{3,4},{4,3},{5,6},{6,5},{7,8},{8,7},{9,10},{10,9},{11,... | collective-permute-start | bytes 196616 | tf_op jit(solution)/shard_map/ppermute | solution.py:337
  5.0 1.7 %collective-permute-start.1 = (f32[128,128]{1,0:T(8,128)S(1)}, f32[128,128]{1,0:T(8,128)S(1)}, u32[]{:S(2)}, u32[]{:S(2)}) collective-permute-start(f32[128,128]{1,0:T(8,128)S(1)} %get-tuple-element.45), channel_id=1, source_target_pairs={{0,1},{1,0},{2,3},{3,2},{4,5},{5,4},{6,7},{7,6},{8,9},{9,8},{10,11... | collective-permute-start | bytes 196616 | tf_op jit(solution)/shard_map/ppermute | solution.py:366
  5.2 4.7 %collective-permute-start.3 = (f32[200,128]{1,0:T(8,128)S(1)}, f32[200,128]{1,0:T(8,128)S(1)}, u32[]{:S(2)}, u32[]{:S(2)}) collective-permute-start(f32[200,128]{1,0:T(8,128)S(1)} %get-tuple-element.39.send), channel_id=1, source_target_pairs={{1,2},{2,1},{3,4},{4,3},{5,6},{6,5},{7,8},{8,7},{9,10},{10,9},{11,... | collective-permute-start | bytes 307208 | tf_op jit(solution)/shard_map/ppermute | solution.py:337
  7.0 4.1 %collective-permute-start.5 = (f32[128,128]{1,0:T(8,128)S(1)}, f32[128,128]{1,0:T(8,128)S(1)}, u32[]{:S(2)}, u32[]{:S(2)}) collective-permute-start(f32[128,128]{1,0:T(8,128)S(1)} %get-tuple-element.53.w_inner), channel_id=1, source_target_pairs={{0,1},{1,0},{2,3},{3,2},{4,5},{5,4},{6,7},{7,6},{8,9},{9,8},{10,11... | collective-permute-start | bytes 196616 | tf_op jit(solution)/shard_map/ppermute | solution.py:370
  7.2 3.9 %collective-permute-start.4 = (f32[64,128]{1,0:T(8,128)S(1)}, f32[64,128]{1,0:T(8,128)S(1)}, u32[]{:S(2)}, u32[]{:S(2)}) collective-permute-start(f32[64,128]{1,0:T(8,128)S(1)} %get-tuple-element.59), channel_id=1, source_target_pairs={{1,2},{2,1},{3,4},{4,3},{5,6},{6,5},{7,8},{8,7},{9,10},{10,9},{11,... | collective-permute-start | bytes 98312 | tf_op jit(solution)/shard_map/ppermute | solution.py:337

commit v20 on v17

--- a/solution.py
+++ b/solution.py
@@ -144,20 +144,17 @@
     first = position * 2
     outer, inner = outer_block(tile)
     total = row_sums(tiles, masses)
-    diag[outer, :] = diag_outer[...]
-    diag[inner, :] = jnp.broadcast_to(total, diag_outer.shape)
+    diag[...] = jnp.broadcast_to(total, diag.shape)
     own, cross = toward(tiles, names, first + 1 - side), toward(tiles, names, first + side)
-    store_halves(local, (inner, slice(0, tile)), jnp.where(side == 0, -cross, -own))
-    store_halves(local, (inner, slice(tile, 2 * tile)), jnp.where(side == 0, -own, -cross))
-    for k in range(2):
-        local[k, outer, :] = local_outer[k]
+    store_halves(local, (slice(None), slice(0, tile)), jnp.where(side == 0, -cross, -own))
+    store_halves(local, (slice(None), slice(tile, 2 * tile)), jnp.where(side == 0, -own, -cross))
     store_halves(t_in, (slice(None),), toward(tiles, names, jnp.where(side == 0, first + 2, first - 1)))
     x_inner = x[inner, :]
     t[outer, :] = send[0:tile, :]
     t_inner[...] = (
         right_side(names, first + 1 - side, x_inner.shape)
         - total * x_inner
-        - dot(part(local, inner), x[...])
+        - dot(local, x[...])
         + dot(t_in, other_x[...])
     )
     t[inner, :] = t_inner[...]
@@ -203,9 +200,9 @@
     tile = t_in.shape[-1]
     _, inner = outer_block(tile)
     w_inner[...] = (
-        diag[inner, :] * t[inner, :]
-        + dot(part(local, inner), t[...])
-        + dot(part(local, inner, outer_columns(tile)), push_here[...])
+        diag[...] * t[inner, :]
+        + dot(local, t[...])
+        + dot(part(local, slice(None), outer_columns(tile)), push_here[...])
         - dot(t_in, other_t[...])
     )
     for half in range(2):
@@ -224,13 +221,15 @@
     r_outer = t[outer, :] + push
     r[outer, :] = r_outer
     r[inner, :] = t[inner, :]
-    w_outer[...] = q_outer[...] + diag[outer, :] * push + dot(part(local, outer, outer_columns(tile)), push)
+    w_outer[...] = (
+        q_outer[...] + diag[...] * push + dot(part(local, slice(None), outer_columns(tile)), push)
+    )
     edge_r_out[...] = dot(t_out_t, r_outer)
     edge_r_in[...] = dot(t_in_t, t[inner, :])
 
 
 def moment_kernel(
-    local, diag, t_in_t, t_out, t_out_t, r, w_local, edge_r_out, push_there, got, w_inner,
+    local_outer, diag_outer, local_inner, diag_inner, t_in_t, t_out, t_out_t, r, w_local, edge_r_out, push_there, got, w_inner,
     w, there, edge_y_out, moments, edge_y_in,
 ):
     tile = t_out.shape[-1]
@@ -246,39 +245,44 @@
     shift = jnp.where(r_r > 0, r_w / r_r, 0.0)
     y = w_now - shift * r_now
     y_outer = w_outer - shift * r_outer
-    a_y = diag[...] * y + dot(local, y)
+    y_inner = w_inner[...] - shift * r[inner, :]
+    a_outer = diag_outer[...] * y_outer + dot(local_outer, y)
+    a_inner = diag_inner[...] * y_inner + dot(local_inner, y)
+    y_ay = total(y_outer * a_outer + y_inner * a_inner)
     y_pull, r_pull = total(y_outer * pull), total(r_outer * pull)
-    r_ay = total(r_now * a_y + y * w_now) + y_pull
+    r_ay = total(y * w_now) + total(r_outer * a_outer + r[inner, :] * a_inner) + y_pull
     moments[...] = jnp.concatenate(
-        [r_r, r_w, total(y * y), total(y * a_y), r_ay, r_w + r_pull, shift, y_pull, r_pull]
+        [r_r, r_w, total(y * y), y_ay, r_ay, r_w + r_pull, shift, y_pull, r_pull]
         + [shift] * (moments.shape[0] - 9),
         axis=0,
     )
     edge_y_out[...] = dot(t_out_t, y_outer)
     own_there, diag_there = unpack(got[tile:, :])
     there[...] = diag_there * push - dot(halves(own_there), push) - edge_r_out[...] - shift * r_there
-    edge_y_in[...] = dot(t_in_t, w_inner[...] - shift * r[inner, :])
-
-
-def share_kernel(
-    moments, edge_y_in, edge_r_in, edge_y_out, edge_r_out, there, got_q, other_t, other_w, out
-):
+    edge_y_in[...] = dot(t_in_t, y_inner)
+
+
+def partner_kernel(moments, edge_y_in, edge_r_in, other_t, other_w, sums):
+    y_partner = other_w[...] - moments[6:7, :] * other_t[...]
+    row = index_of(moments.shape, 0)
+    y_ay = jnp.where(row == 3, total(edge_y_in[...] * y_partner), 0.0)
+    sums[...] = moments[...] - y_ay - jnp.where(row == 4, total(edge_r_in[...] * y_partner), 0.0)
+
+
+def share_kernel(moments, edge_y_out, edge_r_out, there, got_q, out):
     tile = there.shape[0]
     half = tile // 2
     side = lax.axis_index("sub")
-    shift = moments[6:7, :]
     q_half = got_q[...]
     q_flip = flip(q_half)
     q_there = jnp.concatenate(
         [jnp.where(side == 0, q_half, q_flip), jnp.where(side == 0, q_flip, q_half)], axis=0
     )
     y_there = q_there + there[...]
-    mine = (index_of(shift.shape, 1) >= half) == (side == 1)
+    mine = (index_of((1, out.shape[-1]), 1) >= half) == (side == 1)
     weight = jnp.where(mine, 2.0, 0.0)
-    y_partner = other_w[...] - shift * other_t[...]
-    y_ay = total(edge_y_in[...] * y_partner) + weight * total(edge_y_out[...] * y_there)
-    r_ay = total(edge_r_in[...] * y_partner)
-    r_ay += weight * (total(edge_r_out[...] * y_there) + moments[7:8, :])
+    y_ay = weight * total(edge_y_out[...] * y_there)
+    r_ay = weight * (total(edge_r_out[...] * y_there) + moments[7:8, :])
     r_ar = weight * moments[8:9, :]
     sums = moments[0:8, :]
     row = index_of(sums.shape, 0)
@@ -356,28 +360,30 @@
     push_here = exchange(push_there)
     other_x = lax.ppermute(x_inner, AXES, partner)
     got = exchange(send)
-    local, diag, t_in, t, t_inner, q_outer, q_send = call(
+    local_inner, diag_inner, t_in, t, t_inner, q_outer, q_send = call(
         inner_row_kernel,
-        [(jnp.bfloat16, 2, rows, rows), field, square, field, block, block, halfway],
+        [(jnp.bfloat16, 2, tile, rows), block, square, field, block, block, halfway],
         local_outer, diag_outer, x, tiles_inner, names, masses, other_x, send,
     )
     got_q = exchange(q_send)
     other_t = lax.ppermute(t_inner, AXES, partner)
     w_inner, t_in_t, t_out = call(
-        inner_kernel, [block, square, square], local, diag, t_in, t_out_t, t, other_t, push_here
+        inner_kernel, [block, square, square], local_inner, diag_inner, t_in, t_out_t, t, other_t, push_here
     )
     other_w = lax.ppermute(w_inner, AXES, partner)
     r, w_local, edge_r_out, edge_r_in = call(
         residual_kernel, [field, block, block, block],
-        local, diag, t_in_t, t_out_t, t, q_outer, push_here,
+        local_outer, diag_outer, t_in_t, t_out_t, t, q_outer, push_here,
     )
     w, there, edge_y_out, moments, edge_y_in = call(
         moment_kernel, [field, block, block, (single, 16, columns), block],
-        local, diag, t_in_t, t_out, t_out_t, r, w_local, edge_r_out, push_there, got, w_inner,
+        local_outer, diag_outer, local_inner, diag_inner, t_in_t, t_out, t_out_t, r, w_local, edge_r_out, push_there, got, w_inner,
+    )
+    moments = call(
+        partner_kernel, [(single, 16, columns)], moments, edge_y_in, edge_r_in, other_t, other_w
     )
     shares = call(
-        share_kernel, [(single, devices, 3, 2, columns)],
-        moments, edge_y_in, edge_r_in, edge_y_out, edge_r_out, there, got_q, other_t, other_w,
+        share_kernel, [(single, devices, 3, 2, columns)], moments, edge_y_out, edge_r_out, there, got_q
     )
     shares = lax.all_to_all(shares, AXES, 0, 0)
     return call(finish_kernel, [field], shares, x, r, w, last=True)

time: 25 us -> 25 us (level)
    pallas_call x6 -> x7, Pallas kernels: 2.54 us -> 2.59 us  [call(): pl.pallas_call(kernel, out_shape=outs if len(outs) > 1 else outs[0], in_s...]
where the time goes in v20:
time: 25 us; the launch traced here: 24.8 us
  blocking collectives  12.8 us (51%)
  starting transfers between devices  6.98 us (28%)
  Pallas kernels  3.94 us (16%)
  waiting for transfers between devices  1.06 us (4%)
    all_to_all x1, blocking collectives, body(): shares = lax.all_to_all(shares, AXES, 0, 0)  12.8 us
    ppermute x3, starting transfers between devices, exchange(): return lax.ppermute(value, ('groups',) + AXES, across)  6.07 us
    pallas_call x7, Pallas kernels, call(): pl.pallas_call(kernel, out_shape=outs if len(outs) > 1 else outs[0], in_s...  2.59 us
    pallas_call x1, Pallas kernels, body(): pl.pallas_call(outer_kernel, out_shape=[pltpu.VMEM(shape[1:], shape[0]) f...  1.35 us
    ppermute x3, waiting for transfers between devices, exchange(): return lax.ppermute(value, ('groups',) + AXES, across)  1.05 us
    ppermute x1, starting transfers between devices, body(): other_x = lax.ppermute(x_inner, AXES, partner)  0.56 us
  transfers between devices with their start and end apart: 6, of which 2 were waited for; matrix products, arithmetic and copies ran while one was open for 0% of the time, Pallas kernels for 7%

profile of v20, /device:TPU:0, one launch (start us, length us, event | category | flops | bytes accessed | tf_op | source)
XLA Modules:
  0.0 24.8 jit_solution(16835720908743171186)
XLA Ops:
  0.0 1.4 %outer_kernel.1 = (bf16[2,128,256]{2,1,0:T(8,128)(2,1)S(1)}, f32[128,128]{1,0:T(8,128)S(1)}, bf16[2,128,128]{2,1,0:T(8,128)(2,1)S(1)}, f32[256,128]{1,0:T(8,128)...) custom-call(s32[2,3]{1,0:T(2,128)} %cols_there.1, ...), custom_call_target="tpu_custom_call" | custom-call | tf_op jit(solution)/shard_map/outer_kernel/pallas_call | solution.py:346
  1.4 0.6 %collective-permute-start = (f32[128,128]{1,0:T(8,128)S(1)}, f32[128,128]{1,0:T(8,128)S(1)}, u32[]{:S(2)}, u32[]{:S(2)}) collective-permute-start(f32[128,128]{1,0:T(8,128)S(1)} %get-tuple-element.40), channel_id=1, source_target_pairs={{0,1},{1,0},{2,3},{3,2},{4,5},{5,4},{6,7},{7,6},{8,9},{9,8},{10,11... | collective-permute-start | bytes 196616 | tf_op jit(solution)/shard_map/ppermute | solution.py:361
  1.9 2.6 %collective-permute-start.2 = (f32[128,128]{1,0:T(8,128)S(1)}, f32[128,128]{1,0:T(8,128)S(1)}, u32[]{:S(2)}, u32[]{:S(2)}) collective-permute-start(f32[128,128]{1,0:T(8,128)S(1)} %get-tuple-element.48.push_there), channel_id=1, source_target_pairs={{1,2},{2,1},{3,4},{4,3},{5,6},{6,5},{7,8},{8,7},{9,10},{10,9},{11,... | collective-permute-start | bytes 196616 | tf_op jit(solution)/shard_map/ppermute | solution.py:340
  4.5 0.0 collective-permute-done.other_x
  4.5 0.6 %shard_map.55 = (bf16[2,128,256]{2,1,0:T(8,128)(2,1)S(1)}, f32[128,128]{1,0:T(8,128)S(1)}, bf16[2,128,128]{2,1,0:T(8,128)(2,1)S(1)}, f32[256,128]{1,0:T(8,128)S(...) custom-call(bf16[2,128,256]{2,1,0:T(8,128)(2,1)S(1)} %get-tuple-element.34.local_outer.local, ...), custom_call_target="tpu_custom_call" | custom-call | tf_op jit(solution)/shard_map/pallas_call | solution.py:313
  5.1 0.1 collective-permute-start.1
  5.2 1.5 %collective-permute-start.3 = (f32[200,128]{1,0:T(8,128)S(1)}, f32[200,128]{1,0:T(8,128)S(1)}, u32[]{:S(2)}, u32[]{:S(2)}) collective-permute-start(f32[200,128]{1,0:T(8,128)S(1)} %get-tuple-element.41.send), channel_id=1, source_target_pairs={{1,2},{2,1},{3,4},{4,3},{5,6},{6,5},{7,8},{8,7},{9,10},{10,9},{11,... | collective-permute-start | bytes 307208 | tf_op jit(solution)/shard_map/ppermute | solution.py:340
  6.8 0.0 collective-permute-done.2.push_here
  6.8 0.0 collective-permute-done.1.other_t
  6.8 0.3 %shard_map.56 = (f32[128,128]{1,0:T(8,128)S(1)}, bf16[2,128,128]{2,1,0:T(8,128)(2,1)S(1)}, bf16[2,128,128]{2,1,0:T(8,128)(2,1)S(1)}) custom-call(bf16[2,128,256]{2,1,0:T(8,128)(2,1)S(1)} %get-tuple-element.42.local.local_inner, f32[128,128]{1,0:T(8,128)S(1)} %get-tuple-element.43.diag.diag_inner, bf16[2,128,128]{2,1,0:T(8,128)(2,1)S(1)} %get-tuple-element.44.t_in, ...), custom_call_target="tpu_custom_call" | custom-call | tf_op jit(solution)/shard_map/pallas_call | solution.py:313
  7.0 0.2 collective-permute-start.4
  7.3 2.0 %collective-permute-start.5 = (f32[64,128]{1,0:T(8,128)S(1)}, f32[64,128]{1,0:T(8,128)S(1)}, u32[]{:S(2)}, u32[]{:S(2)}) collective-permute-start(f32[64,128]{1,0:T(8,128)S(1)} %get-tuple-element.61), channel_id=1, source_target_pairs={{1,2},{2,1},{3,4},{4,3},{5,6},{6,5},{7,8},{8,7},{9,10},{10,9},{11,... | collective-permute-start | bytes 98312 | tf_op jit(solution)/shard_map/ppermute | solution.py:340
  9.2 0.2 shard_map.57
  9.5 0.4 %collective-permute-done.3.got = f32[200,128]{1,0:T(8,128)S(1)} collective-permute-done((f32[200,128]{1,0:T(8,128)S(1)}, f32[200,128]{1,0:T(8,128)S(1)}, u32[]{:S(2)}, u32[]{:S(2)}) %collective-permute-start.3) | collective-permute-done | bytes 102432 | tf_op jit(solution)/shard_map/ppermute | solution.py:340
  9.9 0.6 %shard_map.58 = (f32[256,128]{1,0:T(8,128)S(1)}, f32[128,128]{1,0:T(8,128)S(1)}, f32[128,128]{1,0:T(8,128)S(1)}, f32[16,128]{1,0:T(8,128)S(1)}, f32[128,128]{1,0:T(8,128)S(1)}) custom-call(bf16[2,128,256]{2,1,0:T(8,128)(2,1)S(1)} %get-tuple-element.34.local_outer.local, f32[128,128]{1,0:T(8,128)S(1)} %get-tuple-element.35.diag_outer.diag, ...), custom_call_target="tpu_custom_call" | custom-call | tf_op jit(solution)/shard_map/pallas_call | solution.py:313
  10.5 0.0 collective-permute-done.4.other_w
  10.5 0.6 %collective-permute-done.5.got_q = f32[64,128]{1,0:T(8,128)S(1)} collective-permute-done((f32[64,128]{1,0:T(8,128)S(1)}, f32[64,128]{1,0:T(8,128)S(1)}, u32[]{:S(2)}, u32[]{:S(2)}) %collective-permute-start.5) | collective-permute-done | bytes 32800 | tf_op jit(solution)/shard_map/ppermute | solution.py:340
  11.2 0.1 shard_map.60
  11.3 12.8 %all_to_all.5.shares = f32[16,3,2,128]{3,2,1,0:T(2,128)S(1)} all-to-all(f32[16,3,2,128]{3,2,1,0:T(2,128)S(1)} %shard_map.60), channel_id=1, replica_groups=mesh['groups'=2,'patch'=8,'sub'=2] {'patch','sub'}, dimensions={0} | all-to-all | bytes 98304 | tf_op jit(solution)/shard_map/all_to_all | solution.py:388
  24.1 0.8 %shard_map.61 = f32[256,128]{1,0:T(8,128)} custom-call(f32[16,3,2,128]{3,2,1,0:T(2,128)S(1)} %all_to_all.5.shares, f32[256,128]{1,0:T(8,128)S(1)} %get-tuple-element.36.x, f32[256,128]{1,0:T(8,128)S(1)} %get-tuple-element.52.r, f32[256,128]{1,0:T(8,128)S(1)} %get-tuple-element.62.w), custom_call_target="tpu_custom_call" | custom-call | tf_op jit(solution)/shard_map/pallas_call | solution.py:313
  (1 shorter events, 0.0 us)
Async XLA Ops:
  1.4 3.1 %collective-permute-start = (f32[128,128]{1,0:T(8,128)S(1)}, f32[128,128]{1,0:T(8,128)S(1)}, u32[]{:S(2)}, u32[]{:S(2)}) collective-permute-start(f32[128,128]{1,0:T(8,128)S(1)} %get-tuple-element.40), channel_id=1, source_target_pairs={{0,1},{1,0},{2,3},{3,2},{4,5},{5,4},{6,7},{7,6},{8,9},{9,8},{10,11... | collective-permute-start | bytes 196616 | tf_op jit(solution)/shard_map/ppermute | solution.py:361
  1.9 4.8 %collective-permute-start.2 = (f32[128,128]{1,0:T(8,128)S(1)}, f32[128,128]{1,0:T(8,128)S(1)}, u32[]{:S(2)}, u32[]{:S(2)}) collective-permute-start(f32[128,128]{1,0:T(8,128)S(1)} %get-tuple-element.48.push_there), channel_id=1, source_target_pairs={{1,2},{2,1},{3,4},{4,3},{5,6},{6,5},{7,8},{8,7},{9,10},{10,9},{11,... | collective-permute-start | bytes 196616 | tf_op jit(solution)/shard_map/ppermute | solution.py:340
  5.1 1.7 %collective-permute-start.1 = (f32[128,128]{1,0:T(8,128)S(1)}, f32[128,128]{1,0:T(8,128)S(1)}, u32[]{:S(2)}, u32[]{:S(2)}) collective-permute-start(f32[128,128]{1,0:T(8,128)S(1)} %get-tuple-element.47), channel_id=1, source_target_pairs={{0,1},{1,0},{2,3},{3,2},{4,5},{5,4},{6,7},{7,6},{8,9},{9,8},{10,11... | collective-permute-start | bytes 196616 | tf_op jit(solution)/shard_map/ppermute | solution.py:369
  5.2 4.7 %collective-permute-start.3 = (f32[200,128]{1,0:T(8,128)S(1)}, f32[200,128]{1,0:T(8,128)S(1)}, u32[]{:S(2)}, u32[]{:S(2)}) collective-permute-start(f32[200,128]{1,0:T(8,128)S(1)} %get-tuple-element.41.send), channel_id=1, source_target_pairs={{1,2},{2,1},{3,4},{4,3},{5,6},{6,5},{7,8},{8,7},{9,10},{10,9},{11,... | collective-permute-start | bytes 307208 | tf_op jit(solution)/shard_map/ppermute | solution.py:340
  7.0 3.5 %collective-permute-start.4 = (f32[128,128]{1,0:T(8,128)S(1)}, f32[128,128]{1,0:T(8,128)S(1)}, u32[]{:S(2)}, u32[]{:S(2)}) collective-permute-start(f32[128,128]{1,0:T(8,128)S(1)} %get-tuple-element.55.w_inner), channel_id=1, source_target_pairs={{0,1},{1,0},{2,3},{3,2},{4,5},{5,4},{6,7},{7,6},{8,9},{9,8},{10,11... | collective-permute-start | bytes 196616 | tf_op jit(solution)/shard_map/ppermute | solution.py:373
  7.3 3.9 %collective-permute-start.5 = (f32[64,128]{1,0:T(8,128)S(1)}, f32[64,128]{1,0:T(8,128)S(1)}, u32[]{:S(2)}, u32[]{:S(2)}) collective-permute-start(f32[64,128]{1,0:T(8,128)S(1)} %get-tuple-element.61), channel_id=1, source_target_pairs={{1,2},{2,1},{3,4},{4,3},{5,6},{6,5},{7,8},{8,7},{9,10},{10,9},{11,... | collective-permute-start | bytes 98312 | tf_op jit(solution)/shard_map/ppermute | solution.py:340

commit v21 on v17

--- a/solution.py
+++ b/solution.py
@@ -288,7 +288,7 @@
         out[:, pair] = jnp.broadcast_to(sums[None, 2 * pair : 2 * pair + 2], out[:, pair].shape)
 
 
-def finish_kernel(shares, x, r, w, out):
+def finish_kernel(shares, x, r, w, out_there, out, left):
     r_rs, r_ws, spreads, y_ay, r_ay, r_ar = [shares[:, row // 2, row % 2, :] for row in range(6)]
     r_r = jnp.sum(r_rs, axis=0, keepdims=True)
     r_w = jnp.sum(r_ws, axis=0, keepdims=True)
@@ -300,12 +300,20 @@
     energy = jnp.maximum(energy - ratio * theta * spread, LEAST_EIGENVALUE * spread * (1.0 + ratio))
     step = jnp.where(spread > 0, spread / energy, 0.0)
     first = 1.0 / theta
-    out[...] = x[...] + (first + step * (1.0 + ratio)) * r[...] - (step * first) * w[...]
-
-
-def call(kernel, shapes, *operands, last=False):
-    place_out = jax.ShapeDtypeStruct if last else pltpu.VMEM
-    outs = [place_out(shape[1:], shape[0]) for shape in shapes]
+    by_r, by_w = first + step * (1.0 + ratio), step * first
+    rows = out.shape[0] // 2
+    copies = []
+    for half in range(2):
+        here = pl.ds(half * rows, rows)
+        out[here, :] = x[here, :] + by_r * r[here, :] - by_w * w[here, :]
+        copies.append(pltpu.make_async_copy(out.at[here], out_there.at[here], left.at[half]))
+        copies[half].start()
+    for copy in copies:
+        copy.wait()
+
+
+def call(kernel, shapes, *operands):
+    outs = [pltpu.VMEM(shape[1:], shape[0]) for shape in shapes]
     return pl.pallas_call(
         kernel,
         out_shape=outs if len(outs) > 1 else outs[0],
@@ -380,7 +388,14 @@
         moments, edge_y_in, edge_r_in, edge_y_out, edge_r_out, there, got_q, other_t, other_w,
     )
     shares = lax.all_to_all(shares, AXES, 0, 0)
-    return call(finish_kernel, [field], shares, x, r, w, last=True)
+    return pl.pallas_call(
+        finish_kernel,
+        out_shape=jax.ShapeDtypeStruct((rows, columns), single),
+        in_specs=[VMEM] * 4,
+        out_specs=pl.BlockSpec(memory_space=pl.ANY),
+        scratch_shapes=[pltpu.VMEM((rows, columns), single), pltpu.SemaphoreType.DMA((2,))],
+        name="finish_kernel",
+    )(*[pltpu.with_memory_space_constraint(operand, pltpu.VMEM) for operand in (shares, x, r, w)])
 
 
 def solution(mesh):

time: 25 us -> 25 us (level)
    pallas_call x6 -> x5, Pallas kernels: 2.54 us -> 1.79 us  [call(): pl.pallas_call(kernel, out_shape=outs if len(outs) > 1 else outs[0], in_s...]
    pallas_call x0 -> x1, Pallas kernels: none -> 0.76 us  [body(): pl.pallas_call(finish_kernel, out_shape=jax.ShapeDtypeStruct((rows, colum...]
where the time goes in v21:
time: 25 us; the launch traced here: 24.8 us
  blocking collectives  12.8 us (51%)
  starting transfers between devices  6.98 us (28%)
  Pallas kernels  3.89 us (16%)
  waiting for transfers between devices  1.12 us (4%)
    all_to_all x1, blocking collectives, body(): shares = lax.all_to_all(shares, AXES, 0, 0)  12.8 us
    ppermute x3, starting transfers between devices, exchange(): return lax.ppermute(value, ('groups',) + AXES, across)  6.07 us
    pallas_call x5, Pallas kernels, call(): pl.pallas_call(kernel, out_shape=outs if len(outs) > 1 else outs[0], in_s...  1.79 us
    pallas_call x1, Pallas kernels, body(): pl.pallas_call(outer_kernel, out_shape=[pltpu.VMEM(shape[1:], shape[0]) f...  1.35 us
    ppermute x3, waiting for transfers between devices, exchange(): return lax.ppermute(value, ('groups',) + AXES, across)  1.11 us
    pallas_call x1, Pallas kernels, body(): pl.pallas_call(finish_kernel, out_shape=jax.ShapeDtypeStruct((rows, colum...  0.76 us
    ppermute x1, starting transfers between devices, body(): other_x = lax.ppermute(x_inner, AXES, partner)  0.56 us
  transfers between devices with their start and end apart: 6, of which 2 were waited for; matrix products, arithmetic and copies ran while one was open for 0% of the time, Pallas kernels for 7%

profile of v21, /device:TPU:0, one launch (start us, length us, event | category | flops | bytes accessed | tf_op | source)
XLA Modules:
  0.0 24.8 jit_solution(123936821031391090)
XLA Ops:
  0.0 1.3 %outer_kernel.1 = (bf16[2,128,256]{2,1,0:T(8,128)(2,1)S(1)}, f32[128,128]{1,0:T(8,128)S(1)}, bf16[2,128,128]{2,1,0:T(8,128)(2,1)S(1)}, f32[256,128]{1,0:T(8,128)...) custom-call(s32[2,3]{1,0:T(2,128)} %cols_there.1, ...), custom_call_target="tpu_custom_call" | custom-call | tf_op jit(solution)/shard_map/outer_kernel/pallas_call | solution.py:350
  1.4 0.6 %collective-permute-start = (f32[128,128]{1,0:T(8,128)S(1)}, f32[128,128]{1,0:T(8,128)S(1)}, u32[]{:S(2)}, u32[]{:S(2)}) collective-permute-start(f32[128,128]{1,0:T(8,128)S(1)} %get-tuple-element.40), channel_id=1, source_target_pairs={{0,1},{1,0},{2,3},{3,2},{4,5},{5,4},{6,7},{7,6},{8,9},{9,8},{10,11... | collective-permute-start | bytes 196616 | tf_op jit(solution)/shard_map/ppermute | solution.py:365
  1.9 2.6 %collective-permute-start.2 = (f32[128,128]{1,0:T(8,128)S(1)}, f32[128,128]{1,0:T(8,128)S(1)}, u32[]{:S(2)}, u32[]{:S(2)}) collective-permute-start(f32[128,128]{1,0:T(8,128)S(1)} %get-tuple-element.48.push_there), channel_id=1, source_target_pairs={{1,2},{2,1},{3,4},{4,3},{5,6},{6,5},{7,8},{8,7},{9,10},{10,9},{11,... | collective-permute-start | bytes 196616 | tf_op jit(solution)/shard_map/ppermute | solution.py:344
  4.5 0.0 collective-permute-done.other_x
  4.5 0.6 %shard_map.55 = (bf16[2,256,256]{2,1,0:T(8,128)(2,1)S(1)}, f32[256,128]{1,0:T(8,128)S(1)}, bf16[2,128,128]{2,1,0:T(8,128)(2,1)S(1)}, f32[256,128]{1,0:T(8,128)S(...) custom-call(bf16[2,128,256]{2,1,0:T(8,128)(2,1)S(1)} %get-tuple-element.34.local_outer, ...), custom_call_target="tpu_custom_call" | custom-call | tf_op jit(solution)/shard_map/pallas_call | solution.py:317
  5.1 0.1 collective-permute-start.1
  5.2 1.5 %collective-permute-start.3 = (f32[200,128]{1,0:T(8,128)S(1)}, f32[200,128]{1,0:T(8,128)S(1)}, u32[]{:S(2)}, u32[]{:S(2)}) collective-permute-start(f32[200,128]{1,0:T(8,128)S(1)} %get-tuple-element.41.send), channel_id=1, source_target_pairs={{1,2},{2,1},{3,4},{4,3},{5,6},{6,5},{7,8},{8,7},{9,10},{10,9},{11,... | collective-permute-start | bytes 307208 | tf_op jit(solution)/shard_map/ppermute | solution.py:344
  6.8 0.0 collective-permute-done.2.push_here
  6.8 0.0 collective-permute-done.1.other_t
  6.8 0.3 %shard_map.56 = (f32[128,128]{1,0:T(8,128)S(1)}, bf16[2,128,128]{2,1,0:T(8,128)(2,1)S(1)}, bf16[2,128,128]{2,1,0:T(8,128)(2,1)S(1)}) custom-call(bf16[2,256,256]{2,1,0:T(8,128)(2,1)S(1)} %get-tuple-element.42.local, f32[256,128]{1,0:T(8,128)S(1)} %get-tuple-element.43.diag, bf16[2,128,128]{2,1,0:T(8,128)(2,1)S(1)} %get-tuple-element.44.t_in, ...), custom_call_target="tpu_custom_call" | custom-call | tf_op jit(solution)/shard_map/pallas_call | solution.py:317
  7.0 0.2 collective-permute-start.5
  7.2 2.0 %collective-permute-start.4 = (f32[64,128]{1,0:T(8,128)S(1)}, f32[64,128]{1,0:T(8,128)S(1)}, u32[]{:S(2)}, u32[]{:S(2)}) collective-permute-start(f32[64,128]{1,0:T(8,128)S(1)} %get-tuple-element.61), channel_id=1, source_target_pairs={{1,2},{2,1},{3,4},{4,3},{5,6},{6,5},{7,8},{8,7},{9,10},{10,9},{11,... | collective-permute-start | bytes 98312 | tf_op jit(solution)/shard_map/ppermute | solution.py:344
  9.2 0.2 shard_map.57
  9.5 0.4 %collective-permute-done.3.got = f32[200,128]{1,0:T(8,128)S(1)} collective-permute-done((f32[200,128]{1,0:T(8,128)S(1)}, f32[200,128]{1,0:T(8,128)S(1)}, u32[]{:S(2)}, u32[]{:S(2)}) %collective-permute-start.3) | collective-permute-done | bytes 102432 | tf_op jit(solution)/shard_map/ppermute | solution.py:344
  9.9 0.6 %shard_map.58 = (f32[256,128]{1,0:T(8,128)S(1)}, f32[128,128]{1,0:T(8,128)S(1)}, f32[128,128]{1,0:T(8,128)S(1)}, f32[16,128]{1,0:T(8,128)S(1)}, f32[128,128]{1,0:T(8,128)S(1)}) custom-call(bf16[2,256,256]{2,1,0:T(8,128)(2,1)S(1)} %get-tuple-element.42.local, f32[256,128]{1,0:T(8,128)S(1)} %get-tuple-element.43.diag, ...), custom_call_target="tpu_custom_call" | custom-call | tf_op jit(solution)/shard_map/pallas_call | solution.py:317
  10.5 0.7 %collective-permute-done.4.got_q = f32[64,128]{1,0:T(8,128)S(1)} collective-permute-done((f32[64,128]{1,0:T(8,128)S(1)}, f32[64,128]{1,0:T(8,128)S(1)}, u32[]{:S(2)}, u32[]{:S(2)}) %collective-permute-start.4) | collective-permute-done | bytes 32800 | tf_op jit(solution)/shard_map/ppermute | solution.py:344
  11.2 0.0 collective-permute-done.5.other_w
  11.2 0.1 shard_map.59
  11.3 12.8 %all_to_all.5.shares = f32[16,3,2,128]{3,2,1,0:T(2,128)S(1)} all-to-all(f32[16,3,2,128]{3,2,1,0:T(2,128)S(1)} %shard_map.59), channel_id=1, replica_groups=mesh['groups'=2,'patch'=8,'sub'=2] {'patch','sub'}, dimensions={0} | all-to-all | bytes 98304 | tf_op jit(solution)/shard_map/all_to_all | solution.py:390
  24.0 0.8 %finish_kernel.1 = f32[256,128]{1,0:T(8,128)} custom-call(f32[16,3,2,128]{3,2,1,0:T(2,128)S(1)} %all_to_all.5.shares, f32[256,128]{1,0:T(8,128)S(1)} %get-tuple-element.36.x, f32[256,128]{1,0:T(8,128)S(1)} %get-tuple-element.52.r, f32[256,128]{1,0:T(8,128)S(1)} %get-tuple-element.62.w), custom_call_target="tpu_custom_call" | custom-call | tf_op jit(solution)/shard_map/finish_kernel/pallas_call | solution.py:391
Async XLA Ops:
  1.4 3.1 %collective-permute-start = (f32[128,128]{1,0:T(8,128)S(1)}, f32[128,128]{1,0:T(8,128)S(1)}, u32[]{:S(2)}, u32[]{:S(2)}) collective-permute-start(f32[128,128]{1,0:T(8,128)S(1)} %get-tuple-element.40), channel_id=1, source_target_pairs={{0,1},{1,0},{2,3},{3,2},{4,5},{5,4},{6,7},{7,6},{8,9},{9,8},{10,11... | collective-permute-start | bytes 196616 | tf_op jit(solution)/shard_map/ppermute | solution.py:365
  1.9 4.8 %collective-permute-start.2 = (f32[128,128]{1,0:T(8,128)S(1)}, f32[128,128]{1,0:T(8,128)S(1)}, u32[]{:S(2)}, u32[]{:S(2)}) collective-permute-start(f32[128,128]{1,0:T(8,128)S(1)} %get-tuple-element.48.push_there), channel_id=1, source_target_pairs={{1,2},{2,1},{3,4},{4,3},{5,6},{6,5},{7,8},{8,7},{9,10},{10,9},{11,... | collective-permute-start | bytes 196616 | tf_op jit(solution)/shard_map/ppermute | solution.py:344
  5.1 1.7 %collective-permute-start.1 = (f32[128,128]{1,0:T(8,128)S(1)}, f32[128,128]{1,0:T(8,128)S(1)}, u32[]{:S(2)}, u32[]{:S(2)}) collective-permute-start(f32[128,128]{1,0:T(8,128)S(1)} %get-tuple-element.47), channel_id=1, source_target_pairs={{0,1},{1,0},{2,3},{3,2},{4,5},{5,4},{6,7},{7,6},{8,9},{9,8},{10,11... | collective-permute-start | bytes 196616 | tf_op jit(solution)/shard_map/ppermute | solution.py:373
  5.2 4.7 %collective-permute-start.3 = (f32[200,128]{1,0:T(8,128)S(1)}, f32[200,128]{1,0:T(8,128)S(1)}, u32[]{:S(2)}, u32[]{:S(2)}) collective-permute-start(f32[200,128]{1,0:T(8,128)S(1)} %get-tuple-element.41.send), channel_id=1, source_target_pairs={{1,2},{2,1},{3,4},{4,3},{5,6},{6,5},{7,8},{8,7},{9,10},{10,9},{11,... | collective-permute-start | bytes 307208 | tf_op jit(solution)/shard_map/ppermute | solution.py:344
  7.0 4.1 %collective-permute-start.5 = (f32[128,128]{1,0:T(8,128)S(1)}, f32[128,128]{1,0:T(8,128)S(1)}, u32[]{:S(2)}, u32[]{:S(2)}) collective-permute-start(f32[128,128]{1,0:T(8,128)S(1)} %get-tuple-element.55.w_inner), channel_id=1, source_target_pairs={{0,1},{1,0},{2,3},{3,2},{4,5},{5,4},{6,7},{7,6},{8,9},{9,8},{10,11... | collective-permute-start | bytes 196616 | tf_op jit(solution)/shard_map/ppermute | solution.py:377
  7.2 3.9 %collective-permute-start.4 = (f32[64,128]{1,0:T(8,128)S(1)}, f32[64,128]{1,0:T(8,128)S(1)}, u32[]{:S(2)}, u32[]{:S(2)}) collective-permute-start(f32[64,128]{1,0:T(8,128)S(1)} %get-tuple-element.61), channel_id=1, source_target_pairs={{1,2},{2,1},{3,4},{4,3},{5,6},{6,5},{7,8},{8,7},{9,10},{10,9},{11,... | collective-permute-start | bytes 98312 | tf_op jit(solution)/shard_map/ppermute | solution.py:344

commit v22 on v17

--- a/solution.py
+++ b/solution.py
@@ -68,7 +68,7 @@
 
 def outer_kernel(
     cols_there, tiles_there, mass_there, x_there, sources_there,
-    local_outer, diag_outer, t_out_t, x, x_inner, tiles_inner, names, masses, push, send,
+    local_outer, diag_outer, t_out_t, x, x_inner, names, masses, push, send,
     cols, tiles, mass, sources, arrived,
 ):
     tile = tiles.shape[-1]
@@ -83,12 +83,11 @@
         (x_there, x),
         (mass_there, mass),
         (sources_there, sources),
-        (tiles_there.at[1 - side], tiles_inner),
     )
     copies = [pltpu.make_async_copy(start, end, arrived.at[i]) for i, (start, end) in enumerate(moves)]
     for copy in copies:
         copy.start()
-    for copy in copies[:-1]:
+    for copy in copies:
         copy.wait()
     eye = index_of((tile, tile), 0) == index_of((tile, tile), 1)
     outer, inner = outer_block(tile)
@@ -126,7 +125,6 @@
     send[tile : tile + half, :] = jnp.where(above_diagonal, own[:half], flip(own[half:]))
     diagonal = jnp.sum(jnp.where(eye, total, 0.0), axis=0, keepdims=True)
     send[tile + half :, :] = jnp.broadcast_to(diagonal, (8, tile))
-    copies[-1].wait()
 
 
 def store_halves(pair, index, value):
@@ -134,9 +132,10 @@
 
 
 def inner_row_kernel(
-    local_outer, diag_outer, x, tiles, names, masses, other_x, send,
+    local_outer, diag_outer, x, all_tiles, names, masses, other_x, send,
     local, diag, t_in, t, t_inner, q_outer, q_send,
 ):
+    tiles = all_tiles.at[1 - lax.axis_index("sub")]
     tile = tiles.shape[-1]
     half = tile // 2
     position = place()
@@ -336,10 +335,10 @@
         return lax.ppermute(value, ("groups",) + AXES, across)
 
     results = [
-        (jnp.bfloat16, 2, tile, rows), block, square, field, block, (single, slots, tile, tile),
+        (jnp.bfloat16, 2, tile, rows), block, square, field, block,
         (jnp.int32, 8, tile), (single, 8, tile), block, (single, tile + tile // 2 + 8, columns),
     ]
-    local_outer, diag_outer, t_out_t, x, x_inner, tiles_inner, names, masses, push_there, send = pl.pallas_call(
+    local_outer, diag_outer, t_out_t, x, x_inner, names, masses, push_there, send = pl.pallas_call(
         outer_kernel,
         out_shape=[pltpu.VMEM(shape[1:], shape[0]) for shape in results],
         in_specs=[pl.BlockSpec(memory_space=pl.ANY)] * 5,
@@ -349,7 +348,7 @@
             pltpu.VMEM((slots, tile, tile), single),
             pltpu.VMEM(mass.shape, single),
             pltpu.VMEM(source_ids.shape, jnp.int32),
-            pltpu.SemaphoreType.DMA((6,)),
+            pltpu.SemaphoreType.DMA((5,)),
         ],
         name="outer_kernel",
     )(block_cols, step_tiles, mass, warm_start, source_ids)
@@ -359,7 +358,7 @@
     local, diag, t_in, t, t_inner, q_outer, q_send = call(
         inner_row_kernel,
         [(jnp.bfloat16, 2, rows, rows), field, square, field, block, block, halfway],
-        local_outer, diag_outer, x, tiles_inner, names, masses, other_x, send,
+        local_outer, diag_outer, x, step_tiles, names, masses, other_x, send,
     )
     got_q = exchange(q_send)
     other_t = lax.ppermute(t_inner, AXES, partner)

time: 25 us -> 25 us (level)
  no operation moved by 1% of the time
where the time goes in v22:
time: 25 us; the launch traced here: 24.9 us
  blocking collectives  12.8 us (51%)
  starting transfers between devices  6.98 us (28%)
  Pallas kernels  3.94 us (16%)
  waiting for transfers between devices  1.11 us (4%)
    all_to_all x1, blocking collectives, body(): shares = lax.all_to_all(shares, AXES, 0, 0)  12.8 us
    ppermute x3, starting transfers between devices, exchange(): return lax.ppermute(value, ('groups',) + AXES, across)  6.07 us
    pallas_call x6, Pallas kernels, call(): pl.pallas_call(kernel, out_shape=outs if len(outs) > 1 else outs[0], in_s...  2.55 us
    pallas_call x1, Pallas kernels, body(): pl.pallas_call(outer_kernel, out_shape=[pltpu.VMEM(shape[1:], shape[0]) f...  1.39 us
    ppermute x3, waiting for transfers between devices, exchange(): return lax.ppermute(value, ('groups',) + AXES, across)  1.11 us
    ppermute x1, starting transfers between devices, body(): other_x = lax.ppermute(x_inner, AXES, partner)  0.56 us
  transfers between devices with their start and end apart: 6, of which 2 were waited for; matrix products, arithmetic and copies ran while one was open for 0% of the time, Pallas kernels for 7%

profile of v22, /device:TPU:0, one launch (start us, length us, event | category | flops | bytes accessed | tf_op | source)
XLA Modules:
  0.0 24.9 jit_solution(379673658235797204)
XLA Ops:
  0.0 0.0 copy-start
  0.0 1.4 %outer_kernel.1 = (bf16[2,128,256]{2,1,0:T(8,128)(2,1)S(1)}, f32[128,128]{1,0:T(8,128)S(1)}, bf16[2,128,128]{2,1,0:T(8,128)(2,1)S(1)}, f32[256,128]{1,0:T(8,128)...) custom-call(s32[2,3]{1,0:T(2,128)} %cols_there.1, ...), custom_call_target="tpu_custom_call" | custom-call | tf_op jit(solution)/shard_map/outer_kernel/pallas_call | solution.py:341
  1.4 0.6 %collective-permute-start = (f32[128,128]{1,0:T(8,128)S(1)}, f32[128,128]{1,0:T(8,128)S(1)}, u32[]{:S(2)}, u32[]{:S(2)}) collective-permute-start(f32[128,128]{1,0:T(8,128)S(1)} %get-tuple-element.38), channel_id=1, source_target_pairs={{0,1},{1,0},{2,3},{3,2},{4,5},{5,4},{6,7},{7,6},{8,9},{9,8},{10,11... | collective-permute-start | bytes 196616 | tf_op jit(solution)/shard_map/ppermute | solution.py:356
  2.0 2.6 %collective-permute-start.2 = (f32[128,128]{1,0:T(8,128)S(1)}, f32[128,128]{1,0:T(8,128)S(1)}, u32[]{:S(2)}, u32[]{:S(2)}) collective-permute-start(f32[128,128]{1,0:T(8,128)S(1)} %get-tuple-element.46.push_there), channel_id=1, source_target_pairs={{1,2},{2,1},{3,4},{4,3},{5,6},{6,5},{7,8},{8,7},{9,10},{10,9},{11,... | collective-permute-start | bytes 196616 | tf_op jit(solution)/shard_map/ppermute | solution.py:335
  4.5 0.0 collective-permute-done.other_x
  4.5 0.0 copy-done
  4.5 0.6 %shard_map.55 = (bf16[2,256,256]{2,1,0:T(8,128)(2,1)S(1)}, f32[256,128]{1,0:T(8,128)S(1)}, bf16[2,128,128]{2,1,0:T(8,128)(2,1)S(1)}, f32[256,128]{1,0:T(8,128)S(...) custom-call(bf16[2,128,256]{2,1,0:T(8,128)(2,1)S(1)} %get-tuple-element.33.local_outer, ...), custom_call_target="tpu_custom_call" | custom-call | tf_op jit(solution)/shard_map/pallas_call | solution.py:308
  5.1 0.1 collective-permute-start.1
  5.3 1.5 %collective-permute-start.3 = (f32[200,128]{1,0:T(8,128)S(1)}, f32[200,128]{1,0:T(8,128)S(1)}, u32[]{:S(2)}, u32[]{:S(2)}) collective-permute-start(f32[200,128]{1,0:T(8,128)S(1)} %get-tuple-element.39.send), channel_id=1, source_target_pairs={{1,2},{2,1},{3,4},{4,3},{5,6},{6,5},{7,8},{8,7},{9,10},{10,9},{11,... | collective-permute-start | bytes 307208 | tf_op jit(solution)/shard_map/ppermute | solution.py:335
  6.8 0.0 collective-permute-done.2.push_here
  6.8 0.0 collective-permute-done.1.other_t
  6.8 0.3 %shard_map.56 = (f32[128,128]{1,0:T(8,128)S(1)}, bf16[2,128,128]{2,1,0:T(8,128)(2,1)S(1)}, bf16[2,128,128]{2,1,0:T(8,128)(2,1)S(1)}) custom-call(bf16[2,256,256]{2,1,0:T(8,128)(2,1)S(1)} %get-tuple-element.40.local, f32[256,128]{1,0:T(8,128)S(1)} %get-tuple-element.41.diag, bf16[2,128,128]{2,1,0:T(8,128)(2,1)S(1)} %get-tuple-element.42.t_in, ...), custom_call_target="tpu_custom_call" | custom-call | tf_op jit(solution)/shard_map/pallas_call | solution.py:308
  7.1 0.2 collective-permute-start.5
  7.3 2.0 %collective-permute-start.4 = (f32[64,128]{1,0:T(8,128)S(1)}, f32[64,128]{1,0:T(8,128)S(1)}, u32[]{:S(2)}, u32[]{:S(2)}) collective-permute-start(f32[64,128]{1,0:T(8,128)S(1)} %get-tuple-element.59), channel_id=1, source_target_pairs={{1,2},{2,1},{3,4},{4,3},{5,6},{6,5},{7,8},{8,7},{9,10},{10,9},{11,... | collective-permute-start | bytes 98312 | tf_op jit(solution)/shard_map/ppermute | solution.py:335
  9.3 0.2 shard_map.57
  9.5 0.4 %collective-permute-done.3.got = f32[200,128]{1,0:T(8,128)S(1)} collective-permute-done((f32[200,128]{1,0:T(8,128)S(1)}, f32[200,128]{1,0:T(8,128)S(1)}, u32[]{:S(2)}, u32[]{:S(2)}) %collective-permute-start.3) | collective-permute-done | bytes 102432 | tf_op jit(solution)/shard_map/ppermute | solution.py:335
  9.9 0.6 %shard_map.58 = (f32[256,128]{1,0:T(8,128)S(1)}, f32[128,128]{1,0:T(8,128)S(1)}, f32[128,128]{1,0:T(8,128)S(1)}, f32[16,128]{1,0:T(8,128)S(1)}, f32[128,128]{1,0:T(8,128)S(1)}) custom-call(bf16[2,256,256]{2,1,0:T(8,128)(2,1)S(1)} %get-tuple-element.40.local, f32[256,128]{1,0:T(8,128)S(1)} %get-tuple-element.41.diag, ...), custom_call_target="tpu_custom_call" | custom-call | tf_op jit(solution)/shard_map/pallas_call | solution.py:308
  10.5 0.7 %collective-permute-done.4.got_q = f32[64,128]{1,0:T(8,128)S(1)} collective-permute-done((f32[64,128]{1,0:T(8,128)S(1)}, f32[64,128]{1,0:T(8,128)S(1)}, u32[]{:S(2)}, u32[]{:S(2)}) %collective-permute-start.4) | collective-permute-done | bytes 32800 | tf_op jit(solution)/shard_map/ppermute | solution.py:335
  11.2 0.0 collective-permute-done.5.other_w
  11.2 0.1 shard_map.59
  11.3 12.8 %all_to_all.5.shares = f32[16,3,2,128]{3,2,1,0:T(2,128)S(1)} all-to-all(f32[16,3,2,128]{3,2,1,0:T(2,128)S(1)} %shard_map.59), channel_id=1, replica_groups=mesh['groups'=2,'patch'=8,'sub'=2] {'patch','sub'}, dimensions={0} | all-to-all | bytes 98304 | tf_op jit(solution)/shard_map/all_to_all | solution.py:381
  24.1 0.8 %shard_map.60 = f32[256,128]{1,0:T(8,128)} custom-call(f32[16,3,2,128]{3,2,1,0:T(2,128)S(1)} %all_to_all.5.shares, f32[256,128]{1,0:T(8,128)S(1)} %get-tuple-element.35.x, f32[256,128]{1,0:T(8,128)S(1)} %get-tuple-element.50.r, f32[256,128]{1,0:T(8,128)S(1)} %get-tuple-element.60.w), custom_call_target="tpu_custom_call" | custom-call | tf_op jit(solution)/shard_map/pallas_call | solution.py:308
Async XLA Ops:
  0.0 4.5 %copy-start = (f32[2,3,128,128]{3,2,1,0:T(8,128)S(1)}, f32[2,3,128,128]{3,2,1,0:T(8,128)}, u32[]{:S(2)}) copy-start(f32[2,3,128,128]{3,2,1,0:T(8,128)} %all_tiles.1) | copy-start | bytes 1179652
  1.4 3.1 %collective-permute-start = (f32[128,128]{1,0:T(8,128)S(1)}, f32[128,128]{1,0:T(8,128)S(1)}, u32[]{:S(2)}, u32[]{:S(2)}) collective-permute-start(f32[128,128]{1,0:T(8,128)S(1)} %get-tuple-element.38), channel_id=1, source_target_pairs={{0,1},{1,0},{2,3},{3,2},{4,5},{5,4},{6,7},{7,6},{8,9},{9,8},{10,11... | collective-permute-start | bytes 196616 | tf_op jit(solution)/shard_map/ppermute | solution.py:356
  2.0 4.8 %collective-permute-start.2 = (f32[128,128]{1,0:T(8,128)S(1)}, f32[128,128]{1,0:T(8,128)S(1)}, u32[]{:S(2)}, u32[]{:S(2)}) collective-permute-start(f32[128,128]{1,0:T(8,128)S(1)} %get-tuple-element.46.push_there), channel_id=1, source_target_pairs={{1,2},{2,1},{3,4},{4,3},{5,6},{6,5},{7,8},{8,7},{9,10},{10,9},{11,... | collective-permute-start | bytes 196616 | tf_op jit(solution)/shard_map/ppermute | solution.py:335
  5.1 1.7 %collective-permute-start.1 = (f32[128,128]{1,0:T(8,128)S(1)}, f32[128,128]{1,0:T(8,128)S(1)}, u32[]{:S(2)}, u32[]{:S(2)}) collective-permute-start(f32[128,128]{1,0:T(8,128)S(1)} %get-tuple-element.45), channel_id=1, source_target_pairs={{0,1},{1,0},{2,3},{3,2},{4,5},{5,4},{6,7},{7,6},{8,9},{9,8},{10,11... | collective-permute-start | bytes 196616 | tf_op jit(solution)/shard_map/ppermute | solution.py:364
  5.3 4.7 %collective-permute-start.3 = (f32[200,128]{1,0:T(8,128)S(1)}, f32[200,128]{1,0:T(8,128)S(1)}, u32[]{:S(2)}, u32[]{:S(2)}) collective-permute-start(f32[200,128]{1,0:T(8,128)S(1)} %get-tuple-element.39.send), channel_id=1, source_target_pairs={{1,2},{2,1},{3,4},{4,3},{5,6},{6,5},{7,8},{8,7},{9,10},{10,9},{11,... | collective-permute-start | bytes 307208 | tf_op jit(solution)/shard_map/ppermute | solution.py:335
  7.1 4.1 %collective-permute-start.5 = (f32[128,128]{1,0:T(8,128)S(1)}, f32[128,128]{1,0:T(8,128)S(1)}, u32[]{:S(2)}, u32[]{:S(2)}) collective-permute-start(f32[128,128]{1,0:T(8,128)S(1)} %get-tuple-element.53.w_inner), channel_id=1, source_target_pairs={{0,1},{1,0},{2,3},{3,2},{4,5},{5,4},{6,7},{7,6},{8,9},{9,8},{10,11... | collective-permute-start | bytes 196616 | tf_op jit(solution)/shard_map/ppermute | solution.py:368
  7.3 3.9 %collective-permute-start.4 = (f32[64,128]{1,0:T(8,128)S(1)}, f32[64,128]{1,0:T(8,128)S(1)}, u32[]{:S(2)}, u32[]{:S(2)}) collective-permute-start(f32[64,128]{1,0:T(8,128)S(1)} %get-tuple-element.59), channel_id=1, source_target_pairs={{1,2},{2,1},{3,4},{4,3},{5,6},{6,5},{7,8},{8,7},{9,10},{10,9},{11,... | collective-permute-start | bytes 98312 | tf_op jit(solution)/shard_map/ppermute | solution.py:335
